TPU v7x, 32 devices: a whole 2x2x4 slice. The times are simulated.
32 devices in a mesh: grp: 4 (over y, x), tile: 8 (over z, core).
Axes of the slice: x: 2, y: 2, z: 4, core: 2. Of those that a mesh axis runs over, the one named last changes fastest.
Arguments:
- base_rhs: float32 [1024, 4096], P('grp', 'tile'), may hold values from -6 to 6
- depth: float32 [1024, 4096], P('grp', 'tile'), may hold values from 0.25 to 2
- ssh_prev: float32 [1024, 4096], P('grp', 'tile'), may hold values from -6 to 6
- currents: float32 [2, 1024, 4096], P(None, 'grp', 'tile'), may hold values from -3 to 3
- land_blocks: int32 [128, 512], P('grp', 'tile'), may hold values 0 or 1
- ice_thick: float32 [2, 256, 4096], P(None, 'grp', 'tile'), may hold values from 0.25 to 4
- ice_blocks: int32 [2, 32, 512], P(None, 'grp', 'tile'), may hold values 0 or 1
- ice_vel: float32 [2, 2, 256, 4096], P(None, None, 'grp', 'tile'), may hold values from -3 to 3
- ice_stress: float32 [3, 2, 256, 4096], P(None, None, 'grp', 'tile'), may hold values from -5 to 5
- wind: float32 [2, 2, 256, 4096], P(None, None, 'grp', 'tile'), may hold values from -6 to 6
Outputs:
- ssh: float32 [1024, 4096], P('grp', 'tile')
- ice_vel_out: float32 [2, 2, 256, 4096], P(None, None, 'grp', 'tile')
- ice_stress_out: float32 [3, 2, 256, 4096], P(None, None, 'grp', 'tile')
All inputs are finite; a program needn't handle non-finite values. No bound on the sum of `land_blocks` or of `ice_blocks` on one device may be relied on, other than what follows from the above.
Results may differ from a plain program's by a relative error of at most 0.0001.
Values sent between devices are 32-bit elements; how exact they have to be, the bound alone decides.
No kernel may reach another device: no remote copies, remote signals or barrier semaphores. Data moves between devices by JAX's collectives and lax.ppermute only.
A program may use at most 64 MiB of HBM per device.

v0:
```python
import jax
import jax.numpy as jnp
from jax import lax
from jax.sharding import PartitionSpec as P

BS = 8
NSUB = 8
ITERS = 3


DAMP = 0.05
RELAX = 0.2
STRENGTH = 0.5
DRAG = 1.0
STEP = 0.5


def extended(array, sides, width):
    for axis, dim in sides:
        devices, length = (lax.axis_size(axis), array.shape[dim])
        up = [(i, (i + 1) % devices) for i in range(devices - 1)]
        down = [(j, i) for i, j in up]
        last = lax.slice_in_dim(array, length - width, length, axis=dim)
        first = lax.slice_in_dim(array, 0, width, axis=dim)
        before = lax.ppermute(last, axis, up)
        after = lax.ppermute(first, axis, down)
        array = jnp.concatenate([before, array, after], axis=dim)
    return array


def passed_along(array, axis, by):
    devices = lax.axis_size(axis)
    pairs = [(i, i + by) for i in range(devices) if 0 <= i + by < devices]
    return lax.ppermute(array, axis, pairs)


def strain_rates(u_pad, v_pad):
    du_dx = u_pad[..., 1:, :-1] - u_pad[..., :-1, :-1]
    du_dy = u_pad[..., :-1, 1:] - u_pad[..., :-1, :-1]
    dv_dx = v_pad[..., 1:, :-1] - v_pad[..., :-1, :-1]
    dv_dy = v_pad[..., :-1, 1:] - v_pad[..., :-1, :-1]
    return (du_dx + dv_dy, du_dx - dv_dy, du_dy + dv_dx)


def relax_stress(previous, strength, div_rate, tens_rate, shear_rate):
    deformation = jnp.sqrt(
        div_rate * div_rate + tens_rate * tens_rate + shear_rate * shear_rate + 1.0
    )
    relax_scale = 1.0 / (1.0 + RELAX)
    div_part = (previous[0] + RELAX * strength * (div_rate / deformation - 1.0)) * relax_scale
    tens_part = (previous[1] + RELAX * strength * tens_rate / deformation) * relax_scale
    shear_part = (previous[2] + RELAX * strength * shear_rate / deformation) * relax_scale
    return jnp.stack([div_part, tens_part, shear_part])


def along_rows(field):
    return field[..., 1:, 1:] - field[..., :-1, 1:]


def along_cols(field):
    return field[..., 1:, 1:] - field[..., 1:, :-1]


def stress_force(stress_pad):
    force_x = 0.5 * along_rows(stress_pad[0] + stress_pad[1]) + along_cols(stress_pad[2])
    force_y = 0.5 * along_cols(stress_pad[0] - stress_pad[1]) + along_rows(stress_pad[2])
    return jnp.stack([force_x, force_y])


def momentum(velocity, force, ice_mass, ice_cover, wind, ocean_flow):
    return (
        ice_cover
        * (ice_mass * velocity + STEP * (force + wind + DRAG * ocean_flow))
        / (ice_mass + STEP * DRAG)
    )


def face_weights(depth_pad):
    centre = depth_pad[1:-1, 1:-1]
    return (
        centre * depth_pad[2:, 1:-1],
        centre * depth_pad[:-2, 1:-1],
        centre * depth_pad[1:-1, 2:],
        centre * depth_pad[1:-1, :-2],
    )


def apply_operator(field_pad, weights):
    field = field_pad[1:-1, 1:-1]
    north_weight, south_weight, east_weight, west_weight = weights
    return (
        DAMP * field
        + north_weight * (field - field_pad[2:, 1:-1])
        + south_weight * (field - field_pad[:-2, 1:-1])
        + east_weight * (field - field_pad[1:-1, 2:])
        + west_weight * (field - field_pad[1:-1, :-2])
    )


def expand(blocks):
    return jnp.repeat(jnp.repeat(blocks, BS, axis=-2), BS, axis=-1).astype(jnp.float32)


def operate(field, weights):
    field_pad = extended(field, (("grp", 0), ("tile", 1)), 1)
    return apply_operator(field_pad, weights)


def forward_edges(velocity):
    row_in = passed_along(velocity[:, :, :1, :], "grp", -1)
    col_in = passed_along(velocity[:, :, :, :1], "tile", -1)
    taller = jnp.concatenate([velocity, row_in], axis=2)
    col_tall = jnp.pad(col_in, ((0, 0), (0, 0), (0, 1), (0, 0)))
    return jnp.concatenate([taller, col_tall], axis=3)


def backward_edges(stress):
    row_in = passed_along(stress[:, :, -1:, :], "grp", 1)
    col_in = passed_along(stress[:, :, :, -1:], "tile", 1)
    taller = jnp.concatenate([row_in, stress], axis=2)
    col_tall = jnp.pad(col_in, ((0, 0), (0, 0), (1, 0), (0, 0)))
    return jnp.concatenate([col_tall, taller], axis=3)


def pair_sums(residual, precond, applied):
    return lax.psum((jnp.sum(residual * precond), jnp.sum(precond * applied)), ("grp", "tile"))


def shards(
    base_rhs,
    depth,
    ssh_prev,
    currents,
    land_blocks,
    ice_thick,
    ice_blocks,
    ice_vel,
    ice_stress,
    wind,
):
    groups = lax.axis_size("grp")
    grp_index = lax.axis_index("grp")
    ocean_cols = base_rhs.shape[1]
    ice_rows = ice_thick.shape[1]
    cap_rows = ice_rows * groups
    wet_cells = expand(land_blocks)
    ice_cover = expand(ice_blocks)
    at_north = (grp_index == 0).astype(jnp.float32)
    at_south = (grp_index == groups - 1).astype(jnp.float32)
    outgoing = jnp.stack([currents * at_north, currents * at_south], axis=1)
    outgoing = outgoing.reshape(2, 2, groups, ice_rows, ocean_cols)
    incoming = lax.all_to_all(outgoing, "grp", split_axis=2, concat_axis=2, tiled=True)
    ocean_flow = jnp.sum(incoming, axis=2)
    strength = STRENGTH * ice_thick * ice_cover
    ice_mass = ice_thick * ice_cover + 1.0
    velocity = ice_vel
    stress = ice_stress
    for subcycle in range(NSUB):
        vel_pad = forward_edges(velocity)
        div_rate, tens_rate, shear_rate = strain_rates(vel_pad[0], vel_pad[1])
        stress = relax_stress(stress, strength, div_rate, tens_rate, shear_rate)
        stress_pad = backward_edges(stress)
        velocity = momentum(
            velocity, stress_force(stress_pad), ice_mass, ice_cover, wind, ocean_flow
        )
    ice_drag = DRAG * ice_cover * (velocity - ocean_flow)
    empty_slot = jnp.zeros_like(ice_drag[:, 0])
    parcel = jnp.stack([ice_drag[:, 0]] + [empty_slot] * (groups - 2) + [ice_drag[:, 1]], axis=1)
    returned = lax.all_to_all(parcel, "grp", split_axis=1, concat_axis=1, tiled=True).reshape(
        2, cap_rows, ocean_cols
    )
    ocean_drag = jnp.where(
        grp_index == 0, returned, jnp.where(grp_index == groups - 1, returned, 0.0)
    )
    forcing_pad = extended(
        jnp.stack([ocean_drag[0], ocean_drag[1], depth * wet_cells]), (("grp", 1), ("tile", 2)), 1
    )
    spread = (
        forcing_pad[0, 1:-1, 1:-1]
        - forcing_pad[0, :-2, 1:-1]
        + (forcing_pad[1, 1:-1, 1:-1] - forcing_pad[1, 1:-1, :-2])
    )
    forcing = wet_cells * (base_rhs + spread)
    weights = face_weights(forcing_pad[2])
    diagonal = DAMP + weights[0] + weights[1] + weights[2] + weights[3]
    solution = ssh_prev
    residual = forcing - operate(solution, weights)
    precond = residual / diagonal
    applied = operate(precond, weights)
    precond_norm, curvature_sum = pair_sums(residual, precond, applied)
    step_size = precond_norm / curvature_sum
    direction = precond
    search_image = applied
    for iteration in range(ITERS):
        solution = solution + step_size * direction
        residual = residual - step_size * search_image
        if iteration + 1 < ITERS:
            precond = residual / diagonal
            applied = operate(precond, weights)
            norm_next, curvature_sum = pair_sums(residual, precond, applied)
            beta_ratio = norm_next / precond_norm
            step_size = norm_next / (curvature_sum - beta_ratio * norm_next / step_size)
            direction = precond + beta_ratio * direction
            search_image = applied + beta_ratio * search_image
            precond_norm = norm_next
    return (solution, velocity, stress)


def solution(mesh):
    return jax.shard_map(
        shards,
        mesh=mesh,
        in_specs=(
            P("grp", "tile"),
            P("grp", "tile"),
            P("grp", "tile"),
            P(None, "grp", "tile"),
            P("grp", "tile"),
            P(None, "grp", "tile"),
            P(None, "grp", "tile"),
            P(None, None, "grp", "tile"),
            P(None, None, "grp", "tile"),
            P(None, None, "grp", "tile"),
        ),
        out_specs=(P("grp", "tile"), P(None, None, "grp", "tile"), P(None, None, "grp", "tile")),
        check_vma=False,
    )
```

profile of v0, /device:TPU:0, one launch (start us, length us, event | category | flops | bytes accessed | tf_op | source)
XLA Modules:
  0.0 449.4 jit_solution(3022196357651030177)
XLA Ops:
  8.3 6.5 %all-to-all-start = ((f32[2,2,4,64,512]{4,3,0,1,2:T(8,128)}), f32[2,2,4,64,512]{4,3,0,1,2:T(8,128)}, u32[]{:S(2)}, u32[]{:S(2)}) async-start(f32[2,2,4,64,512]{4,3,0,1,2:T(8,128)} %copy.184), calls=%async_computation | async-start | bytes 4194304 | tf_op jit(solution)/shard_map/all_to_all | solution.py:152
  17.2 3.9 collective-permute-start.3
  21.2 2.5 collective-permute-start.2
  23.7 15.0 %collective-permute-done.3 = f32[3,2,1,512]{3,1,2,0:T(2,128)S(1)} collective-permute-done((f32[3,2,1,512]{3,1,2,0:T(2,128)S(1)}, f32[3,2,1,512]{3,1,2,0:T(2,128)S(1)}, u32[]{:S(2)}, u32[]{:S(2)}) %collective-permute-start.3) | collective-permute-done | bytes 12320 | tf_op jit(solution)/shard_map/ppermute | solution.py:34
  48.1 2.9 collective-permute-done.4
  51.9 3.8 collective-permute-start.7
  55.9 4.8 %collective-permute-start.6 = (f32[3,2,64,1]{3,2,1,0:T(8,128)S(1)}, f32[3,2,64,1]{3,2,1,0:T(8,128)S(1)}, u32[]{:S(2)}, u32[]{:S(2)}) collective-permute-start(f32[3,2,64,1]{3,2,1,0:T(8,128)S(1)} %pad_maximum_fusion.52), channel_id=1, source_target_pairs={{0,1},{1,2},{2,3},{3,4},{4,5},{5,6},{6,7},{8,9},{9,10},{10,11},{11... | collective-permute-start | bytes 4616 | tf_op jit(solution)/shard_map/ppermute | solution.py:34
  65.6 3.4 collective-permute-done.8
  69.9 4.8 %collective-permute-start.11 = (f32[3,2,1,512]{3,1,2,0:T(2,128)S(1)}, f32[3,2,1,512]{3,1,2,0:T(2,128)S(1)}, u32[]{:S(2)}, u32[]{:S(2)}) collective-permute-start(f32[3,2,1,512]{3,1,2,0:T(2,128)S(1)} %copy.198), channel_id=1, source_target_pairs={{0,8},{8,16},{16,24},{1,9},{9,17},{17,25},{2,10},{10,18},{18,26},{... | collective-permute-start | bytes 36872 | tf_op jit(solution)/shard_map/ppermute | solution.py:34
  74.8 5.9 %collective-permute-start.10 = (f32[3,2,64,1]{3,2,1,0:T(8,128)S(1)}, f32[3,2,64,1]{3,2,1,0:T(8,128)S(1)}, u32[]{:S(2)}, u32[]{:S(2)}) collective-permute-start(f32[3,2,64,1]{3,2,1,0:T(8,128)S(1)} %pad_maximum_fusion.51), channel_id=1, source_target_pairs={{0,1},{1,2},{2,3},{3,4},{4,5},{5,6},{6,7},{8,9},{9,10},{10,11},{11... | collective-permute-start | bytes 4616 | tf_op jit(solution)/shard_map/ppermute | solution.py:34
  85.6 3.8 collective-permute-done.12
  90.3 4.8 %collective-permute-start.15 = (f32[3,2,1,512]{3,1,2,0:T(2,128)S(1)}, f32[3,2,1,512]{3,1,2,0:T(2,128)S(1)}, u32[]{:S(2)}, u32[]{:S(2)}) collective-permute-start(f32[3,2,1,512]{3,1,2,0:T(2,128)S(1)} %copy.205), channel_id=1, source_target_pairs={{0,8},{8,16},{16,24},{1,9},{9,17},{17,25},{2,10},{10,18},{18,26},{... | collective-permute-start | bytes 36872 | tf_op jit(solution)/shard_map/ppermute | solution.py:34
  95.3 5.9 %collective-permute-start.14 = (f32[3,2,64,1]{3,2,1,0:T(8,128)S(1)}, f32[3,2,64,1]{3,2,1,0:T(8,128)S(1)}, u32[]{:S(2)}, u32[]{:S(2)}) collective-permute-start(f32[3,2,64,1]{3,2,1,0:T(8,128)S(1)} %pad_maximum_fusion.50), channel_id=1, source_target_pairs={{0,1},{1,2},{2,3},{3,4},{4,5},{5,6},{6,7},{8,9},{9,10},{10,11},{11... | collective-permute-start | bytes 4616 | tf_op jit(solution)/shard_map/ppermute | solution.py:34
  106.3 3.6 collective-permute-done.16
  110.8 4.8 %collective-permute-start.19 = (f32[3,2,1,512]{3,1,2,0:T(2,128)S(1)}, f32[3,2,1,512]{3,1,2,0:T(2,128)S(1)}, u32[]{:S(2)}, u32[]{:S(2)}) collective-permute-start(f32[3,2,1,512]{3,1,2,0:T(2,128)S(1)} %copy.212), channel_id=1, source_target_pairs={{0,8},{8,16},{16,24},{1,9},{9,17},{17,25},{2,10},{10,18},{18,26},{... | collective-permute-start | bytes 36872 | tf_op jit(solution)/shard_map/ppermute | solution.py:34
  115.7 5.9 %collective-permute-start.18 = (f32[3,2,64,1]{3,2,1,0:T(8,128)S(1)}, f32[3,2,64,1]{3,2,1,0:T(8,128)S(1)}, u32[]{:S(2)}, u32[]{:S(2)}) collective-permute-start(f32[3,2,64,1]{3,2,1,0:T(8,128)S(1)} %pad_maximum_fusion.49), channel_id=1, source_target_pairs={{0,1},{1,2},{2,3},{3,4},{4,5},{5,6},{6,7},{8,9},{9,10},{10,11},{11... | collective-permute-start | bytes 4616 | tf_op jit(solution)/shard_map/ppermute | solution.py:34
  126.5 3.8 collective-permute-done.20
  131.2 4.8 %collective-permute-start.23 = (f32[3,2,1,512]{3,1,2,0:T(2,128)S(1)}, f32[3,2,1,512]{3,1,2,0:T(2,128)S(1)}, u32[]{:S(2)}, u32[]{:S(2)}) collective-permute-start(f32[3,2,1,512]{3,1,2,0:T(2,128)S(1)} %copy.219), channel_id=1, source_target_pairs={{0,8},{8,16},{16,24},{1,9},{9,17},{17,25},{2,10},{10,18},{18,26},{... | collective-permute-start | bytes 36872 | tf_op jit(solution)/shard_map/ppermute | solution.py:34
  136.1 5.9 %collective-permute-start.22 = (f32[3,2,64,1]{3,2,1,0:T(8,128)S(1)}, f32[3,2,64,1]{3,2,1,0:T(8,128)S(1)}, u32[]{:S(2)}, u32[]{:S(2)}) collective-permute-start(f32[3,2,64,1]{3,2,1,0:T(8,128)S(1)} %pad_maximum_fusion.48), channel_id=1, source_target_pairs={{0,1},{1,2},{2,3},{3,4},{4,5},{5,6},{6,7},{8,9},{9,10},{10,11},{11... | collective-permute-start | bytes 4616 | tf_op jit(solution)/shard_map/ppermute | solution.py:34
  147.0 3.8 collective-permute-done.24
  151.6 4.8 %collective-permute-start.27 = (f32[3,2,1,512]{3,1,2,0:T(2,128)S(1)}, f32[3,2,1,512]{3,1,2,0:T(2,128)S(1)}, u32[]{:S(2)}, u32[]{:S(2)}) collective-permute-start(f32[3,2,1,512]{3,1,2,0:T(2,128)S(1)} %copy.226), channel_id=1, source_target_pairs={{0,8},{8,16},{16,24},{1,9},{9,17},{17,25},{2,10},{10,18},{18,26},{... | collective-permute-start | bytes 36872 | tf_op jit(solution)/shard_map/ppermute | solution.py:34
  156.6 5.9 %collective-permute-start.26 = (f32[3,2,64,1]{3,2,1,0:T(8,128)S(1)}, f32[3,2,64,1]{3,2,1,0:T(8,128)S(1)}, u32[]{:S(2)}, u32[]{:S(2)}) collective-permute-start(f32[3,2,64,1]{3,2,1,0:T(8,128)S(1)} %pad_maximum_fusion.47), channel_id=1, source_target_pairs={{0,1},{1,2},{2,3},{3,4},{4,5},{5,6},{6,7},{8,9},{9,10},{10,11},{11... | collective-permute-start | bytes 4616 | tf_op jit(solution)/shard_map/ppermute | solution.py:34
  167.4 3.8 collective-permute-done.28
  172.2 4.8 %collective-permute-start.31 = (f32[3,2,1,512]{3,1,2,0:T(2,128)S(1)}, f32[3,2,1,512]{3,1,2,0:T(2,128)S(1)}, u32[]{:S(2)}, u32[]{:S(2)}) collective-permute-start(f32[3,2,1,512]{3,1,2,0:T(2,128)S(1)} %copy.235), channel_id=1, source_target_pairs={{0,8},{8,16},{16,24},{1,9},{9,17},{17,25},{2,10},{10,18},{18,26},{... | collective-permute-start | bytes 36872 | tf_op jit(solution)/shard_map/ppermute | solution.py:34
  177.1 5.9 %collective-permute-start.30 = (f32[3,2,64,1]{3,2,1,0:T(8,128)S(1)}, f32[3,2,64,1]{3,2,1,0:T(8,128)S(1)}, u32[]{:S(2)}, u32[]{:S(2)}) collective-permute-start(f32[3,2,64,1]{3,2,1,0:T(8,128)S(1)} %slice.1123), channel_id=1, source_target_pairs={{0,1},{1,2},{2,3},{3,4},{4,5},{5,6},{6,7},{8,9},{9,10},{10,11},{11... | collective-permute-start | bytes 4616 | tf_op jit(solution)/shard_map/ppermute | solution.py:34
  187.3 4.3 all-to-all-start.1
  192.0 14.2 %all-to-all-done.1 = f32[2,4,64,512]{3,2,0,1:T(8,128)S(1)} async-done(((f32[2,4,64,512]{3,2,0,1:T(8,128)}), f32[2,4,64,512]{3,2,0,1:T(8,128)S(1)}, u32[]{:S(2)}, u32[]{:S(2)}) %all-to-all-start.1) | async-done | bytes 1048608 | tf_op jit(solution)/shard_map/all_to_all | solution.py:169
  211.1 4.5 %collective-permute-start.32 = (f32[3,1,512]{2,1,0:T(1,128)S(1)}, f32[3,1,512]{2,1,0:T(1,128)S(1)}, u32[]{:S(2)}, u32[]{:S(2)}) collective-permute-start(f32[3,1,512]{2,1,0:T(1,128)S(1)} %copy.243), channel_id=1, source_target_pairs={{0,8},{8,16},{16,24},{1,9},{9,17},{17,25},{2,10},{10,18},{18,26},{... | collective-permute-start | bytes 18440 | tf_op jit(solution)/shard_map/ppermute | solution.py:25
  219.4 5.6 %collective-permute-start.37 = (f32[1,512]{0,1:T(8,128)}, f32[1,512]{0,1:T(8,128)}, u32[]{:S(2)}, u32[]{:S(2)}) collective-permute-start(f32[1,512]{0,1:T(8,128)} %copy.253), channel_id=1, source_target_pairs={{0,8},{8,16},{16,24},{1,9},{9,17},{17,25},{2,10},{10,18},{18,26},{... | collective-permute-start | bytes 6152 | tf_op jit(solution)/shard_map/ppermute | solution.py:25
  229.2 3.0 collective-permute-start.34
  234.3 5.2 %collective-permute-start.39 = (f32[258,1]{0,1:T(1,128)S(1)}, f32[258,1]{0,1:T(1,128)S(1)}, u32[]{:S(2)}, u32[]{:S(2)}) collective-permute-start(f32[258,1]{0,1:T(1,128)S(1)} %get-tuple-element.110), channel_id=1, source_target_pairs={{0,1},{1,2},{2,3},{3,4},{4,5},{5,6},{6,7},{8,9},{9,10},{10,11},{11... | collective-permute-start | bytes 3104 | tf_op jit(solution)/shard_map/ppermute | solution.py:25
  240.4 3.3 fusion.160
  243.8 3.9 collective-permute-start.41
  249.1 4.7 %collective-permute-done.41 = f32[1,512]{0,1:T(8,128)S(1)} collective-permute-done((f32[1,512]{0,1:T(8,128)S(1)}, f32[1,512]{0,1:T(8,128)S(1)}, u32[]{:S(2)}, u32[]{:S(2)}) %collective-permute-start.41) | collective-permute-done | bytes 2080 | tf_op jit(solution)/shard_map/ppermute | solution.py:25
  253.8 6.3 %collective-permute-done.40 = f32[1,512]{0,1:T(8,128)S(1)} collective-permute-done((f32[1,512]{0,1:T(8,128)S(1)}, f32[1,512]{0,1:T(8,128)S(1)}, u32[]{:S(2)}, u32[]{:S(2)}) %collective-permute-start.40) | collective-permute-done | bytes 2080 | tf_op jit(solution)/shard_map/ppermute | solution.py:26
  261.4 3.1 collective-permute-start.43
  266.7 42.6 %all-reduce.18 = (f32[]{:T(128)}, f32[]{:T(128)}) all-reduce(f32[]{:T(128)} %get-tuple-element.20, f32[]{:T(128)} %get-tuple-element.19), channel_id=1, replica_groups=mesh['grp'=4,'tile'=8] {'grp','tile'}, use_global_device_ids=true, to_apply=%region_2.3 | all-reduce | flops 2 | bytes 16 | tf_op jit(solution)/shard_map/psum | solution.py:126
  311.0 4.3 collective-permute-start.45
  316.6 2.6 collective-permute-done.45
  319.2 7.3 %collective-permute-done.44 = f32[1,512]{0,1:T(8,128)S(1)} collective-permute-done((f32[1,512]{0,1:T(8,128)S(1)}, f32[1,512]{0,1:T(8,128)S(1)}, u32[]{:S(2)}, u32[]{:S(2)}) %collective-permute-start.44) | collective-permute-done | bytes 2080 | tf_op jit(solution)/shard_map/ppermute | solution.py:26
  327.8 3.0 collective-permute-start.47
  331.7 2.1 multiply_reduce_fusion.1
  333.8 40.1 %all-reduce.17 = (f32[]{:T(128)}, f32[]{:T(128)}) all-reduce(f32[]{:T(128)} %get-tuple-element.18, f32[]{:T(128)} %get-tuple-element.17), channel_id=1, replica_groups=mesh['grp'=4,'tile'=8] {'grp','tile'}, use_global_device_ids=true, to_apply=%region_6.7 | all-reduce | flops 2 | bytes 16 | tf_op jit(solution)/shard_map/psum | solution.py:126
  380.0 4.3 collective-permute-start.49
  385.6 4.1 collective-permute-done.49
  389.7 7.5 %collective-permute-done.48 = f32[1,512]{0,1:T(8,128)S(1)} collective-permute-done((f32[1,512]{0,1:T(8,128)S(1)}, f32[1,512]{0,1:T(8,128)S(1)}, u32[]{:S(2)}, u32[]{:S(2)}) %collective-permute-start.48) | collective-permute-done | bytes 2080 | tf_op jit(solution)/shard_map/ppermute | solution.py:26
  398.7 3.0 collective-permute-start.51
  403.9 40.4 %all-reduce.16 = (f32[]{:T(128)}, f32[]{:T(128)}) all-reduce(f32[]{:T(128)} %get-tuple-element.16, f32[]{:T(128)} %get-tuple-element.15), channel_id=1, replica_groups=mesh['grp'=4,'tile'=8] {'grp','tile'}, use_global_device_ids=true, to_apply=%region_10.11 | all-reduce | flops 2 | bytes 16 | tf_op jit(solution)/shard_map/psum | solution.py:126
  (298 shorter events, 91.6 us)
Async XLA Ops:
  1.5 13.7 %collective-permute-start = (f32[2,2,1,512]{3,1,2,0:T(2,128)S(1)}, f32[2,2,1,512]{3,1,2,0:T(2,128)S(1)}, u32[]{:S(2)}, u32[]{:S(2)}) collective-permute-start(f32[2,2,1,512]{3,1,2,0:T(2,128)S(1)} %copy.263), channel_id=1, source_target_pairs={{8,0},{16,8},{24,16},{9,1},{17,9},{25,17},{10,2},{18,10},{26,18},{... | collective-permute-start | bytes 24584 | tf_op jit(solution)/shard_map/ppermute | solution.py:34
  3.7 11.5 %collective-permute-start.1 = (f32[2,2,64,1]{3,2,1,0:T(8,128)S(1)}, f32[2,2,64,1]{3,2,1,0:T(8,128)S(1)}, u32[]{:S(2)}, u32[]{:S(2)}) collective-permute-start(f32[2,2,64,1]{3,2,1,0:T(8,128)S(1)} %slice.750), channel_id=1, source_target_pairs={{1,0},{2,1},{3,2},{4,3},{5,4},{6,5},{7,6},{9,8},{10,9},{11,10},{12... | collective-permute-start | bytes 3080 | tf_op jit(solution)/shard_map/ppermute | solution.py:34
  8.3 33.9 %all-to-all-start = ((f32[2,2,4,64,512]{4,3,0,1,2:T(8,128)}), f32[2,2,4,64,512]{4,3,0,1,2:T(8,128)}, u32[]{:S(2)}, u32[]{:S(2)}) async-start(f32[2,2,4,64,512]{4,3,0,1,2:T(8,128)} %copy.184), calls=%async_computation | async-start | bytes 4194304 | tf_op jit(solution)/shard_map/all_to_all | solution.py:152
  17.2 21.6 %collective-permute-start.3 = (f32[3,2,1,512]{3,1,2,0:T(2,128)S(1)}, f32[3,2,1,512]{3,1,2,0:T(2,128)S(1)}, u32[]{:S(2)}, u32[]{:S(2)}) collective-permute-start(f32[3,2,1,512]{3,1,2,0:T(2,128)S(1)} %copy.182), channel_id=1, source_target_pairs={{0,8},{8,16},{16,24},{1,9},{9,17},{17,25},{2,10},{10,18},{18,26},{... | collective-permute-start | bytes 36872 | tf_op jit(solution)/shard_map/ppermute | solution.py:34
  21.2 17.5 %collective-permute-start.2 = (f32[3,2,64,1]{3,2,1,0:T(8,128)S(1)}, f32[3,2,64,1]{3,2,1,0:T(8,128)S(1)}, u32[]{:S(2)}, u32[]{:S(2)}) collective-permute-start(f32[3,2,64,1]{3,2,1,0:T(8,128)S(1)} %pad_maximum_fusion.53), channel_id=1, source_target_pairs={{0,1},{1,2},{2,3},{3,4},{4,5},{5,6},{6,7},{8,9},{9,10},{10,11},{11... | collective-permute-start | bytes 4616 | tf_op jit(solution)/shard_map/ppermute | solution.py:34
  45.5 5.5 %collective-permute-start.4 = (f32[2,2,1,512]{3,1,2,0:T(2,128)S(1)}, f32[2,2,1,512]{3,1,2,0:T(2,128)S(1)}, u32[]{:S(2)}, u32[]{:S(2)}) collective-permute-start(f32[2,2,1,512]{3,1,2,0:T(2,128)S(1)} %copy.189), channel_id=1, source_target_pairs={{8,0},{16,8},{24,16},{9,1},{17,9},{25,17},{10,2},{18,10},{26,18},{... | collective-permute-start | bytes 24584 | tf_op jit(solution)/shard_map/ppermute | solution.py:34
  51.9 8.8 %collective-permute-start.7 = (f32[3,2,1,512]{3,1,2,0:T(2,128)S(1)}, f32[3,2,1,512]{3,1,2,0:T(2,128)S(1)}, u32[]{:S(2)}, u32[]{:S(2)}) collective-permute-start(f32[3,2,1,512]{3,1,2,0:T(2,128)S(1)} %copy.191), channel_id=1, source_target_pairs={{0,8},{8,16},{16,24},{1,9},{9,17},{17,25},{2,10},{10,18},{18,26},{... | collective-permute-start | bytes 36872 | tf_op jit(solution)/shard_map/ppermute | solution.py:34
  55.9 5.9 %collective-permute-start.6 = (f32[3,2,64,1]{3,2,1,0:T(8,128)S(1)}, f32[3,2,64,1]{3,2,1,0:T(8,128)S(1)}, u32[]{:S(2)}, u32[]{:S(2)}) collective-permute-start(f32[3,2,64,1]{3,2,1,0:T(8,128)S(1)} %pad_maximum_fusion.52), channel_id=1, source_target_pairs={{0,1},{1,2},{2,3},{3,4},{4,5},{5,6},{6,7},{8,9},{9,10},{10,11},{11... | collective-permute-start | bytes 4616 | tf_op jit(solution)/shard_map/ppermute | solution.py:34
  63.0 6.0 %collective-permute-start.8 = (f32[2,2,1,512]{3,1,2,0:T(2,128)S(1)}, f32[2,2,1,512]{3,1,2,0:T(2,128)S(1)}, u32[]{:S(2)}, u32[]{:S(2)}) collective-permute-start(f32[2,2,1,512]{3,1,2,0:T(2,128)S(1)} %copy.196), channel_id=1, source_target_pairs={{8,0},{16,8},{24,16},{9,1},{17,9},{25,17},{10,2},{18,10},{26,18},{... | collective-permute-start | bytes 24584 | tf_op jit(solution)/shard_map/ppermute | solution.py:34
  64.3 4.7 %collective-permute-start.9 = (f32[2,2,64,1]{3,2,1,0:T(8,128)S(1)}, f32[2,2,64,1]{3,2,1,0:T(8,128)S(1)}, u32[]{:S(2)}, u32[]{:S(2)}) collective-permute-start(f32[2,2,64,1]{3,2,1,0:T(8,128)S(1)} %slice.1014), channel_id=1, source_target_pairs={{1,0},{2,1},{3,2},{4,3},{5,4},{6,5},{7,6},{9,8},{10,9},{11,10},{12... | collective-permute-start | bytes 3080 | tf_op jit(solution)/shard_map/ppermute | solution.py:34
  69.9 10.8 %collective-permute-start.11 = (f32[3,2,1,512]{3,1,2,0:T(2,128)S(1)}, f32[3,2,1,512]{3,1,2,0:T(2,128)S(1)}, u32[]{:S(2)}, u32[]{:S(2)}) collective-permute-start(f32[3,2,1,512]{3,1,2,0:T(2,128)S(1)} %copy.198), channel_id=1, source_target_pairs={{0,8},{8,16},{16,24},{1,9},{9,17},{17,25},{2,10},{10,18},{18,26},{... | collective-permute-start | bytes 36872 | tf_op jit(solution)/shard_map/ppermute | solution.py:34
  74.8 6.9 %collective-permute-start.10 = (f32[3,2,64,1]{3,2,1,0:T(8,128)S(1)}, f32[3,2,64,1]{3,2,1,0:T(8,128)S(1)}, u32[]{:S(2)}, u32[]{:S(2)}) collective-permute-start(f32[3,2,64,1]{3,2,1,0:T(8,128)S(1)} %pad_maximum_fusion.51), channel_id=1, source_target_pairs={{0,1},{1,2},{2,3},{3,4},{4,5},{5,6},{6,7},{8,9},{9,10},{10,11},{11... | collective-permute-start | bytes 4616 | tf_op jit(solution)/shard_map/ppermute | solution.py:34
  83.0 6.4 %collective-permute-start.12 = (f32[2,2,1,512]{3,1,2,0:T(2,128)S(1)}, f32[2,2,1,512]{3,1,2,0:T(2,128)S(1)}, u32[]{:S(2)}, u32[]{:S(2)}) collective-permute-start(f32[2,2,1,512]{3,1,2,0:T(2,128)S(1)} %copy.203), channel_id=1, source_target_pairs={{8,0},{16,8},{24,16},{9,1},{17,9},{25,17},{10,2},{18,10},{26,18},{... | collective-permute-start | bytes 24584 | tf_op jit(solution)/shard_map/ppermute | solution.py:34
  84.3 5.1 %collective-permute-start.13 = (f32[2,2,64,1]{3,2,1,0:T(8,128)S(1)}, f32[2,2,64,1]{3,2,1,0:T(8,128)S(1)}, u32[]{:S(2)}, u32[]{:S(2)}) collective-permute-start(f32[2,2,64,1]{3,2,1,0:T(8,128)S(1)} %slice.1034), channel_id=1, source_target_pairs={{1,0},{2,1},{3,2},{4,3},{5,4},{6,5},{7,6},{9,8},{10,9},{11,10},{12... | collective-permute-start | bytes 3080 | tf_op jit(solution)/shard_map/ppermute | solution.py:34
  90.3 10.8 %collective-permute-start.15 = (f32[3,2,1,512]{3,1,2,0:T(2,128)S(1)}, f32[3,2,1,512]{3,1,2,0:T(2,128)S(1)}, u32[]{:S(2)}, u32[]{:S(2)}) collective-permute-start(f32[3,2,1,512]{3,1,2,0:T(2,128)S(1)} %copy.205), channel_id=1, source_target_pairs={{0,8},{8,16},{16,24},{1,9},{9,17},{17,25},{2,10},{10,18},{18,26},{... | collective-permute-start | bytes 36872 | tf_op jit(solution)/shard_map/ppermute | solution.py:34
  95.3 6.9 %collective-permute-start.14 = (f32[3,2,64,1]{3,2,1,0:T(8,128)S(1)}, f32[3,2,64,1]{3,2,1,0:T(8,128)S(1)}, u32[]{:S(2)}, u32[]{:S(2)}) collective-permute-start(f32[3,2,64,1]{3,2,1,0:T(8,128)S(1)} %pad_maximum_fusion.50), channel_id=1, source_target_pairs={{0,1},{1,2},{2,3},{3,4},{4,5},{5,6},{6,7},{8,9},{9,10},{10,11},{11... | collective-permute-start | bytes 4616 | tf_op jit(solution)/shard_map/ppermute | solution.py:34
  103.5 6.4 %collective-permute-start.16 = (f32[2,2,1,512]{3,1,2,0:T(2,128)S(1)}, f32[2,2,1,512]{3,1,2,0:T(2,128)S(1)}, u32[]{:S(2)}, u32[]{:S(2)}) collective-permute-start(f32[2,2,1,512]{3,1,2,0:T(2,128)S(1)} %copy.210), channel_id=1, source_target_pairs={{8,0},{16,8},{24,16},{9,1},{17,9},{25,17},{10,2},{18,10},{26,18},{... | collective-permute-start | bytes 24584 | tf_op jit(solution)/shard_map/ppermute | solution.py:34
  104.8 5.1 %collective-permute-start.17 = (f32[2,2,64,1]{3,2,1,0:T(8,128)S(1)}, f32[2,2,64,1]{3,2,1,0:T(8,128)S(1)}, u32[]{:S(2)}, u32[]{:S(2)}) collective-permute-start(f32[2,2,64,1]{3,2,1,0:T(8,128)S(1)} %slice.1054), channel_id=1, source_target_pairs={{1,0},{2,1},{3,2},{4,3},{5,4},{6,5},{7,6},{9,8},{10,9},{11,10},{12... | collective-permute-start | bytes 3080 | tf_op jit(solution)/shard_map/ppermute | solution.py:34
  110.8 10.8 %collective-permute-start.19 = (f32[3,2,1,512]{3,1,2,0:T(2,128)S(1)}, f32[3,2,1,512]{3,1,2,0:T(2,128)S(1)}, u32[]{:S(2)}, u32[]{:S(2)}) collective-permute-start(f32[3,2,1,512]{3,1,2,0:T(2,128)S(1)} %copy.212), channel_id=1, source_target_pairs={{0,8},{8,16},{16,24},{1,9},{9,17},{17,25},{2,10},{10,18},{18,26},{... | collective-permute-start | bytes 36872 | tf_op jit(solution)/shard_map/ppermute | solution.py:34
  115.7 6.9 %collective-permute-start.18 = (f32[3,2,64,1]{3,2,1,0:T(8,128)S(1)}, f32[3,2,64,1]{3,2,1,0:T(8,128)S(1)}, u32[]{:S(2)}, u32[]{:S(2)}) collective-permute-start(f32[3,2,64,1]{3,2,1,0:T(8,128)S(1)} %pad_maximum_fusion.49), channel_id=1, source_target_pairs={{0,1},{1,2},{2,3},{3,4},{4,5},{5,6},{6,7},{8,9},{9,10},{10,11},{11... | collective-permute-start | bytes 4616 | tf_op jit(solution)/shard_map/ppermute | solution.py:34
  123.9 6.4 %collective-permute-start.20 = (f32[2,2,1,512]{3,1,2,0:T(2,128)S(1)}, f32[2,2,1,512]{3,1,2,0:T(2,128)S(1)}, u32[]{:S(2)}, u32[]{:S(2)}) collective-permute-start(f32[2,2,1,512]{3,1,2,0:T(2,128)S(1)} %copy.217), channel_id=1, source_target_pairs={{8,0},{16,8},{24,16},{9,1},{17,9},{25,17},{10,2},{18,10},{26,18},{... | collective-permute-start | bytes 24584 | tf_op jit(solution)/shard_map/ppermute | solution.py:34
  125.2 5.1 %collective-permute-start.21 = (f32[2,2,64,1]{3,2,1,0:T(8,128)S(1)}, f32[2,2,64,1]{3,2,1,0:T(8,128)S(1)}, u32[]{:S(2)}, u32[]{:S(2)}) collective-permute-start(f32[2,2,64,1]{3,2,1,0:T(8,128)S(1)} %slice.1074), channel_id=1, source_target_pairs={{1,0},{2,1},{3,2},{4,3},{5,4},{6,5},{7,6},{9,8},{10,9},{11,10},{12... | collective-permute-start | bytes 3080 | tf_op jit(solution)/shard_map/ppermute | solution.py:34
  131.2 10.8 %collective-permute-start.23 = (f32[3,2,1,512]{3,1,2,0:T(2,128)S(1)}, f32[3,2,1,512]{3,1,2,0:T(2,128)S(1)}, u32[]{:S(2)}, u32[]{:S(2)}) collective-permute-start(f32[3,2,1,512]{3,1,2,0:T(2,128)S(1)} %copy.219), channel_id=1, source_target_pairs={{0,8},{8,16},{16,24},{1,9},{9,17},{17,25},{2,10},{10,18},{18,26},{... | collective-permute-start | bytes 36872 | tf_op jit(solution)/shard_map/ppermute | solution.py:34
  136.1 6.9 %collective-permute-start.22 = (f32[3,2,64,1]{3,2,1,0:T(8,128)S(1)}, f32[3,2,64,1]{3,2,1,0:T(8,128)S(1)}, u32[]{:S(2)}, u32[]{:S(2)}) collective-permute-start(f32[3,2,64,1]{3,2,1,0:T(8,128)S(1)} %pad_maximum_fusion.48), channel_id=1, source_target_pairs={{0,1},{1,2},{2,3},{3,4},{4,5},{5,6},{6,7},{8,9},{9,10},{10,11},{11... | collective-permute-start | bytes 4616 | tf_op jit(solution)/shard_map/ppermute | solution.py:34
  144.3 6.4 %collective-permute-start.24 = (f32[2,2,1,512]{3,1,2,0:T(2,128)S(1)}, f32[2,2,1,512]{3,1,2,0:T(2,128)S(1)}, u32[]{:S(2)}, u32[]{:S(2)}) collective-permute-start(f32[2,2,1,512]{3,1,2,0:T(2,128)S(1)} %copy.224), channel_id=1, source_target_pairs={{8,0},{16,8},{24,16},{9,1},{17,9},{25,17},{10,2},{18,10},{26,18},{... | collective-permute-start | bytes 24584 | tf_op jit(solution)/shard_map/ppermute | solution.py:34
  145.7 5.1 %collective-permute-start.25 = (f32[2,2,64,1]{3,2,1,0:T(8,128)S(1)}, f32[2,2,64,1]{3,2,1,0:T(8,128)S(1)}, u32[]{:S(2)}, u32[]{:S(2)}) collective-permute-start(f32[2,2,64,1]{3,2,1,0:T(8,128)S(1)} %slice.1094), channel_id=1, source_target_pairs={{1,0},{2,1},{3,2},{4,3},{5,4},{6,5},{7,6},{9,8},{10,9},{11,10},{12... | collective-permute-start | bytes 3080 | tf_op jit(solution)/shard_map/ppermute | solution.py:34
  151.6 10.8 %collective-permute-start.27 = (f32[3,2,1,512]{3,1,2,0:T(2,128)S(1)}, f32[3,2,1,512]{3,1,2,0:T(2,128)S(1)}, u32[]{:S(2)}, u32[]{:S(2)}) collective-permute-start(f32[3,2,1,512]{3,1,2,0:T(2,128)S(1)} %copy.226), channel_id=1, source_target_pairs={{0,8},{8,16},{16,24},{1,9},{9,17},{17,25},{2,10},{10,18},{18,26},{... | collective-permute-start | bytes 36872 | tf_op jit(solution)/shard_map/ppermute | solution.py:34
  156.6 6.9 %collective-permute-start.26 = (f32[3,2,64,1]{3,2,1,0:T(8,128)S(1)}, f32[3,2,64,1]{3,2,1,0:T(8,128)S(1)}, u32[]{:S(2)}, u32[]{:S(2)}) collective-permute-start(f32[3,2,64,1]{3,2,1,0:T(8,128)S(1)} %pad_maximum_fusion.47), channel_id=1, source_target_pairs={{0,1},{1,2},{2,3},{3,4},{4,5},{5,6},{6,7},{8,9},{9,10},{10,11},{11... | collective-permute-start | bytes 4616 | tf_op jit(solution)/shard_map/ppermute | solution.py:34
  164.8 6.4 %collective-permute-start.28 = (f32[2,2,1,512]{3,1,2,0:T(2,128)S(1)}, f32[2,2,1,512]{3,1,2,0:T(2,128)S(1)}, u32[]{:S(2)}, u32[]{:S(2)}) collective-permute-start(f32[2,2,1,512]{3,1,2,0:T(2,128)S(1)} %copy.232), channel_id=1, source_target_pairs={{8,0},{16,8},{24,16},{9,1},{17,9},{25,17},{10,2},{18,10},{26,18},{... | collective-permute-start | bytes 24584 | tf_op jit(solution)/shard_map/ppermute | solution.py:34
  166.1 5.1 %collective-permute-start.29 = (f32[2,2,64,1]{3,2,0,1:T(8,128)S(1)}, f32[2,2,64,1]{3,2,0,1:T(8,128)S(1)}, u32[]{:S(2)}, u32[]{:S(2)}) collective-permute-start(f32[2,2,64,1]{3,2,0,1:T(8,128)S(1)} %slice.1114), channel_id=1, source_target_pairs={{1,0},{2,1},{3,2},{4,3},{5,4},{6,5},{7,6},{9,8},{10,9},{11,10},{12... | collective-permute-start | bytes 3080 | tf_op jit(solution)/shard_map/ppermute | solution.py:34
  172.2 10.9 %collective-permute-start.31 = (f32[3,2,1,512]{3,1,2,0:T(2,128)S(1)}, f32[3,2,1,512]{3,1,2,0:T(2,128)S(1)}, u32[]{:S(2)}, u32[]{:S(2)}) collective-permute-start(f32[3,2,1,512]{3,1,2,0:T(2,128)S(1)} %copy.235), channel_id=1, source_target_pairs={{0,8},{8,16},{16,24},{1,9},{9,17},{17,25},{2,10},{10,18},{18,26},{... | collective-permute-start | bytes 36872 | tf_op jit(solution)/shard_map/ppermute | solution.py:34
  177.1 6.9 %collective-permute-start.30 = (f32[3,2,64,1]{3,2,1,0:T(8,128)S(1)}, f32[3,2,64,1]{3,2,1,0:T(8,128)S(1)}, u32[]{:S(2)}, u32[]{:S(2)}) collective-permute-start(f32[3,2,64,1]{3,2,1,0:T(8,128)S(1)} %slice.1123), channel_id=1, source_target_pairs={{0,1},{1,2},{2,3},{3,4},{4,5},{5,6},{6,7},{8,9},{9,10},{10,11},{11... | collective-permute-start | bytes 4616 | tf_op jit(solution)/shard_map/ppermute | solution.py:34
  187.3 18.9 %all-to-all-start.1 = ((f32[2,4,64,512]{3,2,0,1:T(8,128)}), f32[2,4,64,512]{3,2,0,1:T(8,128)S(1)}, u32[]{:S(2)}, u32[]{:S(2)}) async-start(f32[2,4,64,512]{3,2,0,1:T(8,128)} %pad_maximum_fusion.1), calls=%async_computation.1 | async-start | bytes 2097152 | tf_op jit(solution)/shard_map/all_to_all | solution.py:169
  209.7 17.6 %collective-permute-start.33 = (f32[3,1,512]{2,1,0:T(1,128)S(1)}, f32[3,1,512]{2,1,0:T(1,128)S(1)}, u32[]{:S(2)}, u32[]{:S(2)}) collective-permute-start(f32[3,1,512]{2,1,0:T(1,128)S(1)} %copy.245), channel_id=1, source_target_pairs={{8,0},{16,8},{24,16},{9,1},{17,9},{25,17},{10,2},{18,10},{26,18},{... | collective-permute-start | bytes 18440 | tf_op jit(solution)/shard_map/ppermute | solution.py:26
  211.1 15.9 %collective-permute-start.32 = (f32[3,1,512]{2,1,0:T(1,128)S(1)}, f32[3,1,512]{2,1,0:T(1,128)S(1)}, u32[]{:S(2)}, u32[]{:S(2)}) collective-permute-start(f32[3,1,512]{2,1,0:T(1,128)S(1)} %copy.243), channel_id=1, source_target_pairs={{0,8},{8,16},{16,24},{1,9},{9,17},{17,25},{2,10},{10,18},{18,26},{... | collective-permute-start | bytes 18440 | tf_op jit(solution)/shard_map/ppermute | solution.py:25
  217.3 14.9 %collective-permute-start.36 = (f32[1,512]{0,1:T(8,128)}, f32[1,512]{0,1:T(8,128)S(1)}, u32[]{:S(2)}, u32[]{:S(2)}) collective-permute-start(f32[1,512]{0,1:T(8,128)} %copy.250), channel_id=1, source_target_pairs={{8,0},{16,8},{24,16},{9,1},{17,9},{25,17},{10,2},{18,10},{26,18},{... | collective-permute-start | bytes 6152 | tf_op jit(solution)/shard_map/ppermute | solution.py:26
  219.4 12.8 %collective-permute-start.37 = (f32[1,512]{0,1:T(8,128)}, f32[1,512]{0,1:T(8,128)}, u32[]{:S(2)}, u32[]{:S(2)}) collective-permute-start(f32[1,512]{0,1:T(8,128)} %copy.253), channel_id=1, source_target_pairs={{0,8},{8,16},{16,24},{1,9},{9,17},{17,25},{2,10},{10,18},{18,26},{... | collective-permute-start | bytes 6152 | tf_op jit(solution)/shard_map/ppermute | solution.py:25
  227.7 11.8 %collective-permute-start.35 = (f32[3,258,1]{1,2,0:T(1,128)S(1)}, f32[3,258,1]{1,2,0:T(1,128)S(1)}, u32[]{:S(2)}, u32[]{:S(2)}) collective-permute-start(f32[3,258,1]{1,2,0:T(1,128)S(1)} %get-tuple-element.57), channel_id=1, source_target_pairs={{1,0},{2,1},{3,2},{4,3},{5,4},{6,5},{7,6},{9,8},{10,9},{11,10},{12... | collective-permute-start | bytes 9296 | tf_op jit(solution)/shard_map/ppermute | solution.py:26
  229.2 10.4 %collective-permute-start.34 = (f32[3,258,1]{1,2,0:T(1,128)S(1)}, f32[3,258,1]{1,2,0:T(1,128)S(1)}, u32[]{:S(2)}, u32[]{:S(2)}) collective-permute-start(f32[3,258,1]{1,2,0:T(1,128)S(1)} %get-tuple-element.58), channel_id=1, source_target_pairs={{0,1},{1,2},{2,3},{3,4},{4,5},{5,6},{6,7},{8,9},{9,10},{10,11},{11... | collective-permute-start | bytes 9296 | tf_op jit(solution)/shard_map/ppermute | solution.py:25
  233.0 6.9 %collective-permute-start.38 = (f32[258,1]{0,1:T(1,128)S(1)}, f32[258,1]{0,1:T(1,128)S(1)}, u32[]{:S(2)}, u32[]{:S(2)}) collective-permute-start(f32[258,1]{0,1:T(1,128)S(1)} %get-tuple-element.109), channel_id=1, source_target_pairs={{1,0},{2,1},{3,2},{4,3},{5,4},{6,5},{7,6},{9,8},{10,9},{11,10},{12... | collective-permute-start | bytes 3104 | tf_op jit(solution)/shard_map/ppermute | solution.py:26
  234.3 6.0 %collective-permute-start.39 = (f32[258,1]{0,1:T(1,128)S(1)}, f32[258,1]{0,1:T(1,128)S(1)}, u32[]{:S(2)}, u32[]{:S(2)}) collective-permute-start(f32[258,1]{0,1:T(1,128)S(1)} %get-tuple-element.110), channel_id=1, source_target_pairs={{0,1},{1,2},{2,3},{3,4},{4,5},{5,6},{6,7},{8,9},{9,10},{10,11},{11... | collective-permute-start | bytes 3104 | tf_op jit(solution)/shard_map/ppermute | solution.py:25
  243.8 9.9 %collective-permute-start.41 = (f32[1,512]{0,1:T(8,128)S(1)}, f32[1,512]{0,1:T(8,128)S(1)}, u32[]{:S(2)}, u32[]{:S(2)}) collective-permute-start(f32[1,512]{0,1:T(8,128)S(1)} %get-tuple-element.131), channel_id=1, source_target_pairs={{0,8},{8,16},{16,24},{1,9},{9,17},{17,25},{2,10},{10,18},{18,26},{... | collective-permute-start | bytes 6152 | tf_op jit(solution)/shard_map/ppermute | solution.py:25
  247.8 12.3 %collective-permute-start.40 = (f32[1,512]{0,1:T(8,128)S(1)}, f32[1,512]{0,1:T(8,128)S(1)}, u32[]{:S(2)}, u32[]{:S(2)}) collective-permute-start(f32[1,512]{0,1:T(8,128)S(1)} %get-tuple-element.132), channel_id=1, source_target_pairs={{8,0},{16,8},{24,16},{9,1},{17,9},{25,17},{10,2},{18,10},{26,18},{... | collective-permute-start | bytes 6152 | tf_op jit(solution)/shard_map/ppermute | solution.py:26
  311.0 8.2 %collective-permute-start.45 = (f32[1,512]{0,1:T(8,128)S(1)}, f32[1,512]{0,1:T(8,128)S(1)}, u32[]{:S(2)}, u32[]{:S(2)}) collective-permute-start(f32[1,512]{0,1:T(8,128)S(1)} %get-tuple-element.129), channel_id=1, source_target_pairs={{0,8},{8,16},{16,24},{1,9},{9,17},{17,25},{2,10},{10,18},{18,26},{... | collective-permute-start | bytes 6152 | tf_op jit(solution)/shard_map/ppermute | solution.py:25
  315.3 11.2 %collective-permute-start.44 = (f32[1,512]{0,1:T(8,128)S(1)}, f32[1,512]{0,1:T(8,128)S(1)}, u32[]{:S(2)}, u32[]{:S(2)}) collective-permute-start(f32[1,512]{0,1:T(8,128)S(1)} %get-tuple-element.130), channel_id=1, source_target_pairs={{8,0},{16,8},{24,16},{9,1},{17,9},{25,17},{10,2},{18,10},{26,18},{... | collective-permute-start | bytes 6152 | tf_op jit(solution)/shard_map/ppermute | solution.py:26
  380.0 9.7 %collective-permute-start.49 = (f32[1,512]{0,1:T(8,128)S(1)}, f32[1,512]{0,1:T(8,128)S(1)}, u32[]{:S(2)}, u32[]{:S(2)}) collective-permute-start(f32[1,512]{0,1:T(8,128)S(1)} %get-tuple-element.127), channel_id=1, source_target_pairs={{0,8},{8,16},{16,24},{1,9},{9,17},{17,25},{2,10},{10,18},{18,26},{... | collective-permute-start | bytes 6152 | tf_op jit(solution)/shard_map/ppermute | solution.py:25
  384.3 12.9 %collective-permute-start.48 = (f32[1,512]{0,1:T(8,128)S(1)}, f32[1,512]{0,1:T(8,128)S(1)}, u32[]{:S(2)}, u32[]{:S(2)}) collective-permute-start(f32[1,512]{0,1:T(8,128)S(1)} %get-tuple-element.128), channel_id=1, source_target_pairs={{8,0},{16,8},{24,16},{9,1},{17,9},{25,17},{10,2},{18,10},{26,18},{... | collective-permute-start | bytes 6152 | tf_op jit(solution)/shard_map/ppermute | solution.py:26
  397.4 5.2 %collective-permute-start.50 = (f32[258,1]{0,1:T(1,128)S(1)}, f32[258,1]{0,1:T(1,128)S(1)}, u32[]{:S(2)}, u32[]{:S(2)}) collective-permute-start(f32[258,1]{0,1:T(1,128)S(1)} %get-tuple-element.101), channel_id=1, source_target_pairs={{1,0},{2,1},{3,2},{4,3},{5,4},{6,5},{7,6},{9,8},{10,9},{11,10},{12... | collective-permute-start | bytes 3104 | tf_op jit(solution)/shard_map/ppermute | solution.py:26
  (34 other events, 477.7 us)
where the time goes:
time: 452 us; the launch traced here: 449 us
  starting transfers between devices  164 us (36%)
  blocking collectives  123 us (27%)
  waiting for transfers between devices  97.7 us (22%)
  other arithmetic  36.8 us (8%)
  local copies, waits for them, and re-layouts  15.4 us (3%)
  between operations  12.4 us (3%)
    psum x3, blocking collectives, pair_sums(): lax.psum((jnp.sum(residual * precond), jnp.sum(precond * applied)), ('grp...  123 us
    ppermute x32, starting transfers between devices, passed_along(): return lax.ppermute(array, axis, pairs)  99.9 us
    ppermute x32, waiting for transfers between devices, passed_along(): return lax.ppermute(array, axis, pairs)  47.3 us
    ppermute x10, starting transfers between devices, extended(): before = lax.ppermute(last, axis, up)  40.1 us
    ppermute x10, waiting for transfers between devices, extended(): after = lax.ppermute(first, axis, down)  21.2 us
    all_to_all x1, waiting for transfers between devices, shards(): lax.all_to_all(parcel, 'grp', split_axis=1, concat_axis=1, tiled=True)  14.2 us
    ppermute x10, waiting for transfers between devices, extended(): before = lax.ppermute(last, axis, up)  13.3 us
    ppermute x10, starting transfers between devices, extended(): after = lax.ppermute(first, axis, down)  13.1 us
  transfers between devices with their start and end apart: 54, of which 26 were waited for; matrix products, arithmetic and copies ran while one was open for 4% of the time, Pallas kernels for 0%

commit v1 on v0

v1 whole, which is shorter than its diff:
```python
import functools

import jax
import jax.numpy as jnp
from jax import lax
from jax.experimental import pallas as pl
from jax.experimental.pallas import tpu as pltpu
from jax.sharding import PartitionSpec as P

BS = 8
NSUB = 8
ITERS = 3

DAMP = 0.05
RELAX = 0.2
STRENGTH = 0.5
DRAG = 1.0
STEP = 0.5

F32 = jnp.float32
SUB = 8
LANES = 128
EDGE = 16
SLOTS = LANES // EDGE
NICE = 8
NEXT = NICE + 2
NOC = 3


def vmem():
    return pl.BlockSpec(memory_space=pltpu.VMEM)


def smem():
    return pl.BlockSpec(memory_space=pltpu.SMEM)


def call(body, name, outs, ins, scratch=(), mib=24, flops=1000000):
    shapes = tuple(jax.ShapeDtypeStruct(s, F32) for s in outs)
    specs = [smem() if i == 0 else vmem() for i in range(len(ins))]
    return pl.pallas_call(
        body,
        name=name,
        out_shape=shapes,
        in_specs=specs,
        out_specs=tuple(vmem() for _ in outs),
        scratch_shapes=[pltpu.VMEM(s, F32) for s in scratch],
        cost_estimate=pl.CostEstimate(flops=flops, bytes_accessed=4000000, transcendentals=0),
        compiler_params=pltpu.CompilerParams(vmem_limit_bytes=mib * 1024 * 1024),
    )(*ins)


def tile(k):
    return slice(k * SUB, k * SUB + SUB)


def expanded_cols(blocks):
    count = blocks.shape[-1]
    row = lax.broadcasted_iota(jnp.int32, (count, count * BS), 0) * BS
    col = lax.broadcasted_iota(jnp.int32, (count, count * BS), 1)
    spread = ((col >= row) & (col < row + BS)).astype(F32)
    return jnp.dot(blocks.astype(F32), spread, preferred_element_type=F32)


def row_iota(cols):
    return lax.broadcasted_iota(jnp.int32, (SUB, cols), 0)


def lane_iota():
    return lax.broadcasted_iota(jnp.int32, (SUB, LANES), 1)


def from_next_row(here, after, row):
    return pltpu.roll(jnp.where(row == 0, after, here), SUB - 1, 0)


def from_prev_row(here, before, row):
    return pltpu.roll(jnp.where(row == SUB - 1, before, here), 1, 0)


def from_next_col(here):
    return pltpu.roll(here, here.shape[1] - 1, 1)


def from_prev_col(here):
    return pltpu.roll(here, 1, 1)


def own_tile(cur, comp, first, j):
    last = cur.shape[1] // SUB - 1
    t = jnp.clip(first + j, 0, last)
    return cur[comp, pl.ds(pl.multiple_of(t * SUB, SUB), SUB), :]


def pack_rows(groups, g_ref, base, depth, x0, cur, land, thick, iceb, vel, stress, wind,
              gf, h, a, b, c, d):
    g = g_ref[0]
    rows, ice_rows = base.shape[0], thick.shape[1]
    slab_tiles = ice_rows // SUB
    wet = expanded_cols(land[...])
    for k in range(rows // SUB):
        gf[tile(k), :] = depth[tile(k), :] * wet[k : k + 1, :]
    for cap in range(2):
        cover = expanded_cols(iceb[cap])
        for k in range(slab_tiles):
            h[cap, tile(k), :] = thick[cap, tile(k), :] * cover[k : k + 1, :]

    def halo(out, last):
        r = slice(ice_rows - SUB, ice_rows) if last else slice(0, SUB)
        ro = slice(rows - SUB, rows) if last else slice(0, SUB)
        n = 0
        for cap in range(2):
            pieces = [h[cap, r, :], vel[0, cap, r, :], vel[1, cap, r, :]]
            pieces += [stress[i, cap, r, :] for i in range(3)]
            pieces += [wind[i, cap, r, :] for i in range(2)]
            for piece in pieces:
                out[tile(n), :] = piece
                n += 1
        for field in (base, gf, x0):
            out[tile(n), :] = field[ro, :]
            n += 1
        for k in range(n, out.shape[0] // SUB):
            out[tile(k), :] = jnp.zeros((SUB, out.shape[1]), F32)

    def slab(out, dest):
        for comp in range(2):
            for j in range(slab_tiles + 2):
                out[tile(comp * (slab_tiles + 2) + j), :] = own_tile(cur, comp, slab_tiles * dest - 1, j)

    @pl.when((g == 0) | (g == 3))
    def _():
        slab(a, g ^ 1)
        slab(b, g ^ 2)
        slab(c, g ^ 3)

    @pl.when(g == 0)
    def _():
        halo(d, True)

    @pl.when(g == 3)
    def _():
        halo(d, False)

    @pl.when(g == 1)
    def _():
        halo(a, False)
        halo(c, True)

    @pl.when(g == 2)
    def _():
        halo(a, True)
        halo(c, False)


def pack_cols(g_ref, ra, rb, rc, rd, cur, h, vel, stress, wind, base, gf, x0, ice, ocean, left, right):
    g = g_ref[0]
    cols = base.shape[1]
    slab_tiles = h.shape[1] // SUB
    ext = slab_tiles + 2
    rows = base.shape[0] // SUB
    lane = lane_iota()
    zero = jnp.zeros((SUB, cols), F32)
    state = {"n": 0, "l": None, "r": None}

    def emit(value):
        n = state["n"]
        s = n % SLOTS
        first, last = value[:, :LANES], value[:, cols - LANES :]
        first = pltpu.roll(first, EDGE * s, 1) if s else first
        shift = EDGE * (s + 1) % LANES
        last = pltpu.roll(last, shift, 1) if shift else last
        if s == 0:
            state["l"], state["r"] = first, last
        else:
            state["l"] = jnp.where(lane >= EDGE * s, first, state["l"])
            state["r"] = jnp.where(lane >= EDGE * s, last, state["r"])
        if s == SLOTS - 1:
            k = n // SLOTS
            left[tile(k), :] = state["l"]
            right[tile(k), :] = state["r"]
        state["n"] = n + 1

    def low(k):
        r = tile(k)
        return jnp.where(g == 1, rd[r, :], jnp.where(g == 2, rc[r, :], jnp.where(g == 3, ra[r, :], zero)))

    def high(k):
        r = tile(k)
        return jnp.where(g == 0, ra[r, :], jnp.where(g == 1, rc[r, :], jnp.where(g == 2, rd[r, :], zero)))

    for cap in range(2):
        own = [h.at[cap], vel.at[0, cap], vel.at[1, cap], stress.at[0, cap], stress.at[1, cap],
               stress.at[2, cap], wind.at[0, cap], wind.at[1, cap]]
        for f in range(NICE):
            for j in range(ext):
                if j == 0:
                    value = low(cap * NICE + f)
                elif j == ext - 1:
                    value = high(cap * NICE + f)
                else:
                    value = own[f][tile(j - 1), :]
                ice[cap, f, tile(j), :] = value
                emit(value)
        for comp in range(2):
            for j in range(ext):
                r = tile(comp * ext + j)
                mine = own_tile(cur, comp, slab_tiles * g - 1, j)
                if cap == 0:
                    value = jnp.where(g == 0, mine, jnp.where(g == 1, ra[r, :], jnp.where(g == 2, rb[r, :], rc[r, :])))
                else:
                    value = jnp.where(g == 3, mine, jnp.where(g == 2, ra[r, :], jnp.where(g == 1, rb[r, :], rc[r, :])))
                ice[cap, NICE + comp, tile(j), :] = value
                emit(value)
    for i, field in enumerate((base, gf, x0)):
        for j in range(rows + 2):
            if j == 0:
                value = low(2 * NICE + i)
            elif j == rows + 1:
                value = high(2 * NICE + i)
            else:
                value = field[tile(j - 1), :]
            ocean[i, tile(j), :] = value
            emit(value)
    while state["n"] % SLOTS:
        emit(zero)


def widened(value, from_left, from_right, n, lane):
    s = n % SLOTS
    k = n // SLOTS
    after, before = from_right[tile(k), :], from_left[tile(k), :]
    after = pltpu.roll(after, LANES - EDGE * s, 1) if s else after
    shift = (LANES - EDGE * (s + 1)) % LANES
    before = pltpu.roll(before, shift, 1) if shift else before
    outer = jnp.where(lane < EDGE, after, jnp.where(lane >= LANES - EDGE, before, 0.0))
    return jnp.concatenate([value, outer], axis=1)


def ice_steps(g_ref, ice, from_left, from_right, vel_out, stress_out, p1, p2, p3, mine,
              u_s, v_s, s0_s, s1_s, s2_s, a_s, m_s, q_s, fx_s, fy_s, f0_s, f1_s):
    g = g_ref[0]
    cols = ice.shape[3]
    wide = cols + LANES
    ext = ice.shape[2] // SUB
    lane = lane_iota()
    row = row_iota(wide)
    zero = jnp.zeros((SUB, wide), F32)
    keep = 1.0 / (1.0 + RELAX)
    for cap in range(2):
        for j in range(ext):
            t = tile(j)

            def field(f):
                return widened(ice[cap, f, t, :], from_left, from_right, (cap * NEXT + f) * ext + j, lane)

            hh = field(0)
            u_s[cap, t, :] = field(1)
            v_s[cap, t, :] = field(2)
            s0_s[cap, t, :] = field(3)
            s1_s[cap, t, :] = field(4)
            s2_s[cap, t, :] = field(5)
            w0, w1, f0, f1 = field(6), field(7), field(8), field(9)
            inv = jnp.where(hh > 0.0, 1.0 / (hh + (1.0 + STEP * DRAG)), 0.0)
            quick = STEP * inv
            a_s[cap, t, :] = hh * (RELAX * STRENGTH * keep)
            m_s[cap, t, :] = (hh + 1.0) * inv
            q_s[cap, t, :] = quick
            fx_s[cap, t, :] = quick * (w0 + DRAG * f0)
            fy_s[cap, t, :] = quick * (w1 + DRAG * f1)
            f0_s[cap, t, :] = f0
            f1_s[cap, t, :] = f1

    def subcycle(_, carry):
        for cap in range(2):
            p_prev, s2_prev = zero, zero
            u, v = u_s[cap, tile(0), :], v_s[cap, tile(0), :]
            for j in range(ext):
                t = tile(j)
                if j + 1 < ext:
                    u_next, v_next = u_s[cap, tile(j + 1), :], v_s[cap, tile(j + 1), :]
                else:
                    u_next, v_next = zero, zero
                ux = from_next_row(u, u_next, row) - u
                vx = from_next_row(v, v_next, row) - v
                uy = from_next_col(u) - u
                vy = from_next_col(v) - v
                ed, et, es = ux + vy, ux - vy, uy + vx
                a = a_s[cap, t, :]
                ratio = a * lax.rsqrt(ed * ed + et * et + es * es + 1.0)
                s0 = s0_s[cap, t, :] * keep + (ratio * ed - a)
                s1 = s1_s[cap, t, :] * keep + ratio * et
                s2 = s2_s[cap, t, :] * keep + ratio * es
                s0_s[cap, t, :] = s0
                s1_s[cap, t, :] = s1
                s2_s[cap, t, :] = s2
                p = 0.5 * (s0 + s1)
                q = 0.5 * (s0 - s1)
                force_x = (p - from_prev_row(p, p_prev, row)) + (s2 - from_prev_col(s2))
                force_y = (q - from_prev_col(q)) + (s2 - from_prev_row(s2, s2_prev, row))
                m, quick = m_s[cap, t, :], q_s[cap, t, :]
                u_s[cap, t, :] = m * u + (quick * force_x + fx_s[cap, t, :])
                v_s[cap, t, :] = m * v + (quick * force_y + fy_s[cap, t, :])
                p_prev, s2_prev = p, s2
                u, v = u_next, v_next
        return carry

    lax.fori_loop(0, NSUB, subcycle, 0)
    spreads = []
    for cap in range(2):
        parts = []
        d0_prev = zero
        for j in range(1, ext):
            t = tile(j)
            if j < ext - 1:
                out = tile(j - 1)
                u, v = u_s[cap, t, :], v_s[cap, t, :]
                vel_out[0, cap, out, :] = u[:, :cols]
                vel_out[1, cap, out, :] = v[:, :cols]
                stress_out[0, cap, out, :] = s0_s[cap, t, :][:, :cols]
                stress_out[1, cap, out, :] = s1_s[cap, t, :][:, :cols]
                stress_out[2, cap, out, :] = s2_s[cap, t, :][:, :cols]
                iced = m_s[cap, t, :] > 0.0
                d0 = jnp.where(iced, DRAG * (u - f0_s[cap, t, :]), 0.0)
                d1 = jnp.where(iced, DRAG * (v - f1_s[cap, t, :]), 0.0)
            else:
                d0 = d1 = zero
            parts.append((d0 - from_prev_row(d0, d0_prev, row)) + (d1 - from_prev_col(d1)))
            d0_prev = d0
        spreads.append(parts)
    for k, (north, south) in enumerate(zip(*spreads)):
        t = tile(k)
        p1[t, :] = jnp.where((g == 1) | (g == 3), north, south)
        p2[t, :] = jnp.where(g == 2, north, south)
        p3[t, :] = jnp.where(g == 3, north, south)
        mine[t, :] = jnp.where(g == 0, north, south)


def neighbour_sum(ref, k, row):
    here, before, after = ref[tile(k), :], ref[tile(k - 1), :], ref[tile(k + 1), :]
    along = from_prev_row(here, before, row) + from_next_row(here, after, row)
    return along + (from_prev_col(here) + from_next_col(here))


def ocean_before(first, g_ref, ocean, from_left, from_right, gw, invd, ra, g_s, gx_s, x_s, b_s):
    cols = ocean.shape[2]
    wide = cols + LANES
    ext = ocean.shape[1] // SUB
    lane = lane_iota()
    row = row_iota(wide)
    zero = jnp.zeros((SUB, wide), F32)
    for ref in (g_s, gx_s):
        ref[tile(0), :] = zero
        ref[tile(ext + 1), :] = zero
    for j in range(ext):
        t = tile(j + 1)

        def field(i):
            return widened(ocean[i, tile(j), :], from_left, from_right, first + i * ext + j, lane)

        b_s[tile(j), :] = field(0)
        depth = field(1)
        x = field(2)
        g_s[t, :] = depth
        gx_s[t, :] = depth * x
        x_s[tile(j), :] = x
        gw[tile(j), :] = depth
    for j in range(ext):
        t = tile(j)
        depth = g_s[tile(j + 1), :]
        diag = DAMP + depth * neighbour_sum(g_s, j + 1, row)
        invd[t, :] = 1.0 / diag
        around = depth * neighbour_sum(gx_s, j + 1, row)
        ra[t, :] = jnp.where(depth > 0.0, b_s[t, :], 0.0) - (diag * x_s[t, :] - around)


def ocean_basis(g_ref, gw, invd, ra, r1, r2, r3, mine, y0_out, y1_out, y2_out, sums,
                sp, u0_s, u1_s, u2_s):
    g = g_ref[0]
    wide = gw.shape[1]
    ext = gw.shape[0] // SUB
    cols = y0_out.shape[1]
    slab = r1.shape[0] // SUB - 1
    row = row_iota(wide)
    zero = jnp.zeros((SUB, wide), F32)
    for ref in (u0_s, u1_s, u2_s):
        ref[tile(0), :] = zero
        ref[tile(ext + 1), :] = zero

    def clear(which):
        for j in which:
            sp[tile(j), :] = zero

    def whole(slabs):
        clear([0])
        for k, ref in enumerate(slabs):
            for t in range(slab):
                value = ref[tile(t), :]
                if t == 0 and k > 0:
                    value = value + slabs[k - 1][tile(slab), :]
                sp[tile(1 + slab * k + t), :] = value
        sp[tile(1 + slab * len(slabs)), :] = slabs[-1][tile(slab), :]

    @pl.when(g == 0)
    def _():
        whole([mine, r1, r2, r3])

    @pl.when(g == 3)
    def _():
        whole([r3, r2, r1, mine])

    @pl.when(g == 1)
    def _():
        clear(range(2, ext))
        sp[tile(0), :] = r1[tile(slab - 1), :]
        sp[tile(1), :] = r1[tile(slab), :]

    @pl.when(g == 2)
    def _():
        clear(range(ext - 1))
        sp[tile(ext - 1), :] = r1[tile(0), :]

    acc = [jnp.zeros((SUB, cols), F32) for _ in range(6)]

    def add(k, left, right, j):
        if 0 < j < ext - 1:
            acc[k] = acc[k] + left[:, :cols] * right[:, :cols]

    for j in range(ext):
        t = tile(j)
        depth = gw[t, :]
        r0 = ra[t, :] + jnp.where(depth > 0.0, sp[t, :], 0.0)
        y0 = r0 * invd[t, :]
        u0_s[tile(j + 1), :] = depth * y0
        if 0 < j < ext - 1:
            y0_out[tile(j - 1), :] = y0[:, :cols]
        add(0, r0, y0, j)
    for j in range(ext):
        t = tile(j)
        depth = gw[t, :]
        w = depth * neighbour_sum(u0_s, j + 1, row)
        y1 = w * invd[t, :]
        u1_s[tile(j + 1), :] = depth * y1
        if 0 < j < ext - 1:
            y1_out[tile(j - 1), :] = y1[:, :cols]
            acc[1] = acc[1] + y0_out[tile(j - 1), :] * w[:, :cols]
        add(2, w, y1, j)
    for j in range(ext):
        t = tile(j)
        depth = gw[t, :]
        w = depth * neighbour_sum(u1_s, j + 1, row)
        y2 = w * invd[t, :]
        u2_s[tile(j + 1), :] = depth * y2
        if 0 < j < ext - 1:
            y2_out[tile(j - 1), :] = y2[:, :cols]
            acc[3] = acc[3] + y1_out[tile(j - 1), :] * w[:, :cols]
        add(4, w, y2, j)
    for j in range(1, ext - 1):
        w = neighbour_sum(u2_s, j + 1, row)[:, :cols] * u2_s[tile(j + 1), :][:, :cols]
        acc[5] = acc[5] + w
    for k in range(6):
        total = acc[k][:, :LANES]
        for c in range(1, cols // LANES):
            total = total + acc[k][:, c * LANES : (c + 1) * LANES]
        sums[k : k + 1, :] = jnp.sum(total, axis=0, keepdims=True)
    sums[6:8, :] = jnp.zeros((2, LANES), F32)


def combine(g_ref, parts, x0, y0, y1, y2, out):
    total = jnp.sum(jnp.sum(parts[...], axis=0), axis=1, keepdims=True)
    total = jnp.broadcast_to(total, (SUB, LANES))
    m = [jnp.broadcast_to(total[k : k + 1, :], (SUB, LANES)) for k in range(6)]

    def dot(left, right, image):
        value = None
        for i, a in enumerate(left):
            for j, b in enumerate(right):
                moment = m[i + j] - m[i + j + 1] if image else m[i + j]
                term = a * b * moment
                value = term if value is None else value + term
        return value

    z = [jnp.ones((SUB, LANES), F32)]
    p = z
    rz = m[0]
    coef = [0.0, 0.0, 0.0]
    for step in range(ITERS):
        alpha = rz / dot(p, p, True)
        for i, a in enumerate(p):
            coef[i] = coef[i] + alpha * a
        if step + 1 < ITERS:
            image = [a for a in p] + [jnp.zeros((SUB, LANES), F32)]
            for i, a in enumerate(p):
                image[i + 1] = image[i + 1] - a
            z = [(z[i] if i < len(z) else 0.0) - alpha * image[i] for i in range(len(image))]
            fresh = dot(z, z, False)
            beta = fresh / rz
            p = [z[i] + beta * p[i] if i < len(p) else z[i] for i in range(len(z))]
            rz = fresh
    reps = x0.shape[1] // LANES
    wide = [jnp.concatenate([c] * reps, axis=1) for c in coef]
    for k in range(x0.shape[0] // SUB):
        t = tile(k)
        out[t, :] = x0[t, :] + (wide[0] * y0[t, :] + wide[1] * y1[t, :] + wide[2] * y2[t, :])


def shards(
    base_rhs,
    depth,
    ssh_prev,
    currents,
    land_blocks,
    ice_thick,
    ice_blocks,
    ice_vel,
    ice_stress,
    wind,
):
    groups = lax.axis_size("grp")
    tiles = lax.axis_size("tile")
    assert groups == 4
    g = lax.axis_index("grp").astype(jnp.int32).reshape(1)
    rows, cols = base_rhs.shape
    ice_rows = ice_thick.shape[1]
    assert rows == groups * ice_rows
    slab = ice_rows + 2 * SUB
    wide = cols + LANES

    strip = (2 * slab, cols)
    gf, h, a, b, c, d = call(
        functools.partial(pack_rows, groups), "pack_rows",
        [(rows, cols), (2, ice_rows, cols), strip, strip, strip, strip],
        [g, base_rhs, depth, ssh_prev, currents, land_blocks, ice_thick, ice_blocks, ice_vel, ice_stress, wind],
    )
    ra = lax.ppermute(a, "grp", [(0, 1), (1, 0), (2, 3), (3, 2)])
    rc = lax.ppermute(c, "grp", [(0, 3), (3, 0), (1, 2), (2, 1)])
    rb = lax.ppermute(b, "grp", [(0, 2), (3, 1)])
    rd = lax.ppermute(d, "grp", [(0, 1), (3, 2)])

    ice_tiles = 2 * NEXT * (slab // SUB)
    ocean_rows = rows + 2 * SUB
    count = ice_tiles + NOC * (ocean_rows // SUB)
    packed = (-(-count // SLOTS) * SUB, LANES)
    ice, ocean, left, right = call(
        pack_cols, "pack_cols",
        [(2, NEXT, slab, cols), (NOC, ocean_rows, cols), packed, packed],
        [g, ra, rb, rc, rd, currents, h, ice_vel, ice_stress, wind, base_rhs, gf, ssh_prev],
    )
    from_left = lax.ppermute(right, "tile", [(i, i + 1) for i in range(tiles - 1)])
    from_right = lax.ppermute(left, "tile", [(i + 1, i) for i in range(tiles - 1)])

    back = (ice_rows + SUB, wide)
    velocity, stress, p1, p2, p3, mine = call(
        ice_steps, "ice_steps",
        [ice_vel.shape, ice_stress.shape, back, back, back, back],
        [g, ice, from_left, from_right],
        scratch=[(2, slab, wide)] * 12,
        mib=32,
    )
    r1 = lax.ppermute(p1, "grp", [(1, 0), (2, 3), (3, 1), (0, 2)])
    r2 = lax.ppermute(p2, "grp", [(2, 0), (1, 3)])
    r3 = lax.ppermute(p3, "grp", [(3, 0), (0, 3)])

    field = (ocean_rows, wide)
    padded = (ocean_rows + 2 * SUB, wide)
    gw, invd, known = call(
        functools.partial(ocean_before, ice_tiles), "ocean_before",
        [field] * 3,
        [g, ocean, from_left, from_right],
        scratch=[padded, padded, field, field],
        flops=20000000,
    )
    y0, y1, y2, sums = call(
        ocean_basis, "ocean_basis",
        [(rows, cols)] * 3 + [(SUB, LANES)],
        [g, gw, invd, known, r1, r2, r3, mine],
        scratch=[field, padded, padded, padded],
    )
    devices = groups * tiles
    shared = lax.all_to_all(
        jnp.broadcast_to(sums[None], (devices, SUB, LANES)), ("grp", "tile"), 0, 0, tiled=True
    )
    (ssh,) = call(combine, "combine", [(rows, cols)], [g, shared, ssh_prev, y0, y1, y2])
    return ssh, velocity, stress


def solution(mesh):
    return jax.shard_map(
        shards,
        mesh=mesh,
        in_specs=(
            P("grp", "tile"),
            P("grp", "tile"),
            P("grp", "tile"),
            P(None, "grp", "tile"),
            P("grp", "tile"),
            P(None, "grp", "tile"),
            P(None, "grp", "tile"),
            P(None, None, "grp", "tile"),
            P(None, None, "grp", "tile"),
            P(None, None, "grp", "tile"),
        ),
        out_specs=(P("grp", "tile"), P(None, None, "grp", "tile"), P(None, None, "grp", "tile")),
        check_vma=False,
    )
```

time: 452 us -> 89 us (0.20)
  starting transfers between devices: 164 us -> 19 us
  blocking collectives: 123 us -> 16.8 us
  waiting for transfers between devices: 97.7 us -> 22.5 us
  other arithmetic: 36.8 us -> 0 us
  Pallas kernels: 0 us -> 19.3 us
  between operations: 12.4 us -> 0.78 us
  local copies, waits for them, and re-layouts: 15.4 us -> 9.95 us
    ppermute x52 -> x9, starting transfers between devices: 153 us -> 19 us  [the longest x1 3.49 us: shards(): rb = lax.ppermute(b, 'grp', [(0, 2), (3, 1)])]
    psum x3 -> x0, blocking collectives: 123 us -> none  [pair_sums(): lax.psum((jnp.sum(residual * precond), jnp.sum(precond * applied)), ('grp...]
    ppermute x52 -> x9, waiting for transfers between devices: 81.8 us -> 22.5 us  [the longest x1 8.61 us: shards(): rb = lax.ppermute(b, 'grp', [(0, 2), (3, 1)])]
    pallas_call x0 -> x6, Pallas kernels: none -> 19.3 us  [call(): pl.pallas_call(body, name=name, out_shape=shapes, in_specs=specs, out_spe...]
    all_to_all x0 -> x1, blocking collectives: none -> 16.8 us  [shards(): lax.all_to_all(jnp.broadcast_to(sums[None], (devices, SUB, LANES)), ('grp...]
    all_to_all x2 -> x0, waiting for transfers between devices: 16 us -> none  [the longest x1 14.2 us: shards(): lax.all_to_all(parcel, 'grp', split_axis=1, concat_axis=1, tiled=True)]
    all_to_all x2 -> x0, starting transfers between devices: 10.8 us -> none  [the longest x1 6.47 us: shards(): lax.all_to_all(outgoing, 'grp', split_axis=2, concat_axis=2, tiled=True)]
    div x10 -> x0, other arithmetic: 7.94 us -> none  [the longest x3 4.79 us: shards(): precond = residual / diagonal]
  transfers between devices with their start and end apart: 54 -> 9, of which waited for: 26 -> 6; matrix products, arithmetic and copies ran while one was open for 4% -> 0% of each run, Pallas kernels for 0% -> 1%
where the time goes in v1:
time: 89 us; the launch traced here: 88.3 us
  waiting for transfers between devices  22.5 us (25%)
  Pallas kernels  19.3 us (22%)
  starting transfers between devices  19 us (21%)
  blocking collectives  16.8 us (19%)
  local copies, waits for them, and re-layouts  9.95 us (11%)
    pallas_call x6, Pallas kernels, call(): pl.pallas_call(body, name=name, out_shape=shapes, in_specs=specs, out_spe...  19.3 us
    all_to_all x1, blocking collectives, shards(): lax.all_to_all(jnp.broadcast_to(sums[None], (devices, SUB, LANES)), ('grp...  16.8 us
    unnamed x30, local copies, waits for them, and re-layouts  9.94 us
    ppermute x1, waiting for transfers between devices, shards(): rb = lax.ppermute(b, 'grp', [(0, 2), (3, 1)])  8.61 us
    ppermute x1, waiting for transfers between devices, shards(): rd = lax.ppermute(d, 'grp', [(0, 1), (3, 2)])  3.84 us
    ppermute x1, waiting for transfers between devices, shards(): lax.ppermute(left, 'tile', [(i + 1, i) for i in range(tiles - 1)])  3.77 us
    ppermute x1, starting transfers between devices, shards(): rb = lax.ppermute(b, 'grp', [(0, 2), (3, 1)])  3.49 us
    ppermute x1, starting transfers between devices, shards(): r3 = lax.ppermute(p3, 'grp', [(3, 0), (0, 3)])  3.34 us
  transfers between devices with their start and end apart: 9, of which 6 were waited for; matrix products, arithmetic and copies ran while one was open for 0% of the time, Pallas kernels for 1%

profile of v1, /device:TPU:0, one launch (start us, length us, event | category | flops | bytes accessed | tf_op | source)
XLA Modules:
  0.0 88.3 jit_solution(6205869174441021566)
XLA Ops:
  0.6 0.0 copy-start
  0.6 1.0 %copy-done = f32[256,512]{1,0:T(8,128)S(1)} copy-done((f32[256,512]{1,0:T(8,128)S(1)}, f32[256,512]{1,0:T(8,128)}, u32[]{:S(2)}) %copy-start) | copy-done | bytes 524312
  1.7 0.0 copy-start.2
  1.7 1.2 %copy-done.2 = f32[2,256,512]{2,1,0:T(8,128)S(1)} copy-done((f32[2,256,512]{2,1,0:T(8,128)S(1)}, f32[2,256,512]{2,1,0:T(8,128)}, u32[]{:S(2)}) %copy-start.2) | copy-done | bytes 1048600
  2.9 0.0 copy-start.4
  2.9 1.1 %copy-done.4 = f32[3,2,64,512]{3,2,1,0:T(8,128)S(1)} copy-done((f32[3,2,64,512]{3,2,1,0:T(8,128)S(1)}, f32[3,2,64,512]{3,2,1,0:T(8,128)}, u32[]{:S(2)}) %copy-start.4) | copy-done | bytes 786456
  4.0 0.0 copy-start.6
  4.0 1.0 %copy-done.6 = f32[256,512]{1,0:T(8,128)S(1)} copy-done((f32[256,512]{1,0:T(8,128)S(1)}, f32[256,512]{1,0:T(8,128)}, u32[]{:S(2)}) %copy-start.6) | copy-done | bytes 524312
  5.1 0.0 copy-start.7
  5.1 1.0 %copy-done.7 = f32[2,2,64,512]{3,2,1,0:T(8,128)S(1)} copy-done((f32[2,2,64,512]{3,2,1,0:T(8,128)S(1)}, f32[2,2,64,512]{3,2,1,0:T(8,128)}, u32[]{:S(2)}) %copy-start.7) | copy-done | bytes 524312
  6.1 0.0 copy-start.9
  6.1 1.0 %copy-done.9 = f32[2,2,64,512]{3,2,1,0:T(8,128)S(1)} copy-done((f32[2,2,64,512]{3,2,1,0:T(8,128)S(1)}, f32[2,2,64,512]{3,2,1,0:T(8,128)}, u32[]{:S(2)}) %copy-start.9) | copy-done | bytes 524312
  7.2 0.0 copy-start.11
  7.2 1.0 %copy-done.11 = f32[256,512]{1,0:T(8,128)S(1)} copy-done((f32[256,512]{1,0:T(8,128)S(1)}, f32[256,512]{1,0:T(8,128)}, u32[]{:S(2)}) %copy-start.11) | copy-done | bytes 524312
  8.2 0.9 %copy-done.12 = f32[2,64,512]{2,1,0:T(8,128)S(1)} copy-done((f32[2,64,512]{2,1,0:T(8,128)S(1)}, f32[2,64,512]{2,1,0:T(8,128)}, u32[]{:S(2)}) %copy-start.12) | copy-done | bytes 262168
  9.2 0.7 copy-done.13
  9.9 0.7 copy-done.14
  10.6 0.0 copy-start.10
  10.6 0.3 pack_rows.1
  10.9 3.0 %collective-permute-start = (f32[160,512]{1,0:T(8,128)S(1)}, f32[160,512]{1,0:T(8,128)S(1)}, u32[]{:S(2)}, u32[]{:S(2)}) collective-permute-start(f32[160,512]{1,0:T(8,128)S(1)} %get-tuple-element.26), channel_id=1, source_target_pairs={{0,8},{8,0},{16,24},{24,16},{1,9},{9,1},{17,25},{25,17},{2,10},{10... | collective-permute-start | bytes 983048 | tf_op jit(solution)/shard_map/ppermute | solution.py:534
  13.9 3.5 %collective-permute-start.1 = (f32[160,512]{1,0:T(8,128)S(1)}, f32[160,512]{1,0:T(8,128)S(1)}, u32[]{:S(2)}, u32[]{:S(2)}) collective-permute-start(f32[160,512]{1,0:T(8,128)S(1)} %get-tuple-element.27), channel_id=1, source_target_pairs={{0,16},{24,8},{1,17},{25,9},{2,18},{26,10},{3,19},{27,11},{4,20},{... | collective-permute-start | bytes 983048 | tf_op jit(solution)/shard_map/ppermute | solution.py:536
  17.4 0.1 collective-permute-start.2
  17.5 2.7 %collective-permute-start.3 = (f32[160,512]{1,0:T(8,128)S(1)}, f32[160,512]{1,0:T(8,128)S(1)}, u32[]{:S(2)}, u32[]{:S(2)}) collective-permute-start(f32[160,512]{1,0:T(8,128)S(1)} %get-tuple-element.29), channel_id=1, source_target_pairs={{0,8},{24,16},{1,9},{25,17},{2,10},{26,18},{3,11},{27,19},{4,12},{... | collective-permute-start | bytes 983048 | tf_op jit(solution)/shard_map/ppermute | solution.py:537
  20.2 2.2 %collective-permute-done.ra = f32[160,512]{1,0:T(8,128)S(1)} collective-permute-done((f32[160,512]{1,0:T(8,128)S(1)}, f32[160,512]{1,0:T(8,128)S(1)}, u32[]{:S(2)}, u32[]{:S(2)}) %collective-permute-start) | collective-permute-done | bytes 327712 | tf_op jit(solution)/shard_map/ppermute | solution.py:534
  22.5 8.6 %collective-permute-done.1.rb = f32[160,512]{1,0:T(8,128)S(1)} collective-permute-done((f32[160,512]{1,0:T(8,128)S(1)}, f32[160,512]{1,0:T(8,128)S(1)}, u32[]{:S(2)}, u32[]{:S(2)}) %collective-permute-start.1) | collective-permute-done | bytes 327712 | tf_op jit(solution)/shard_map/ppermute | solution.py:536
  31.1 0.0 collective-permute-done.2.rc
  31.1 3.8 %collective-permute-done.3.rd = f32[160,512]{1,0:T(8,128)S(1)} collective-permute-done((f32[160,512]{1,0:T(8,128)S(1)}, f32[160,512]{1,0:T(8,128)S(1)}, u32[]{:S(2)}, u32[]{:S(2)}) %collective-permute-start.3) | collective-permute-done | bytes 327712 | tf_op jit(solution)/shard_map/ppermute | solution.py:537
  34.9 0.0 copy-done.1
  34.9 0.0 copy-done.3
  34.9 0.0 copy-done.5
  34.9 0.0 copy-done.8
  34.9 0.0 copy-done.10
  34.9 0.8 pack_cols.1
  35.7 1.3 %collective-permute-start.4 = (f32[304,128]{1,0:T(8,128)S(1)}, f32[304,128]{1,0:T(8,128)S(1)}, u32[]{:S(2)}, u32[]{:S(2)}) collective-permute-start(f32[304,128]{1,0:T(8,128)S(1)} %get-tuple-element.33), channel_id=1, source_target_pairs={{0,1},{1,2},{2,3},{3,4},{4,5},{5,6},{6,7},{8,9},{9,10},{10,11},{11... | collective-permute-start | bytes 466952 | tf_op jit(solution)/shard_map/ppermute | solution.py:548
  37.0 1.3 %collective-permute-start.5 = (f32[304,128]{1,0:T(8,128)S(1)}, f32[304,128]{1,0:T(8,128)S(1)}, u32[]{:S(2)}, u32[]{:S(2)}) collective-permute-start(f32[304,128]{1,0:T(8,128)S(1)} %get-tuple-element.34), channel_id=1, source_target_pairs={{1,0},{2,1},{3,2},{4,3},{5,4},{6,5},{7,6},{9,8},{10,9},{11,10},{12... | collective-permute-start | bytes 466952 | tf_op jit(solution)/shard_map/ppermute | solution.py:549
  38.3 0.0 collective-permute-done.4.from_left
  38.4 3.8 %collective-permute-done.5.from_right = f32[304,128]{1,0:T(8,128)S(1)} collective-permute-done((f32[304,128]{1,0:T(8,128)S(1)}, f32[304,128]{1,0:T(8,128)S(1)}, u32[]{:S(2)}, u32[]{:S(2)}) %collective-permute-start.5) | collective-permute-done | bytes 155680 | tf_op jit(solution)/shard_map/ppermute | solution.py:549
  42.1 14.6 %ice_steps.1 = (f32[2,2,64,512]{3,2,1,0:T(8,128)}, f32[3,2,64,512]{3,2,1,0:T(8,128)}, f32[72,640]{1,0:T(8,128)S(1)}, f32[72,640]{1,0:T(8,128)S(1)}, f32[72,640]{1,0:T(8,128)S(1)}, /*index=5*/f32[72,640]{1,0:T(8,128)S(1)}) custom-call(s32[1]{0:T(128)} %bitcast.g_ref, f32[2,10,80,512]{3,2,1,0:T(8,128)S(1)} %get-tuple-element.38.ice, ...), custom_call_target="tpu_custom_call" | custom-call | flops 1000000 | bytes 4000000 | tf_op jit(solution)/shard_map/ice_steps/pallas_call | solution.py:41
  56.7 2.5 %collective-permute-start.6 = (f32[72,640]{1,0:T(8,128)S(1)}, f32[72,640]{1,0:T(8,128)S(1)}, u32[]{:S(2)}, u32[]{:S(2)}) collective-permute-start(f32[72,640]{1,0:T(8,128)S(1)} %get-tuple-element.39), channel_id=1, source_target_pairs={{8,0},{16,24},{24,8},{0,16},{9,1},{17,25},{25,9},{1,17},{10,2},{18... | collective-permute-start | bytes 552968 | tf_op jit(solution)/shard_map/ppermute | solution.py:559
  59.2 1.3 %collective-permute-start.7 = (f32[72,640]{1,0:T(8,128)S(1)}, f32[72,640]{1,0:T(8,128)S(1)}, u32[]{:S(2)}, u32[]{:S(2)}) collective-permute-start(f32[72,640]{1,0:T(8,128)S(1)} %get-tuple-element.40), channel_id=1, source_target_pairs={{16,0},{8,24},{17,1},{9,25},{18,2},{10,26},{19,3},{11,27},{20,4},{... | collective-permute-start | bytes 552968 | tf_op jit(solution)/shard_map/ppermute | solution.py:560
  60.5 3.3 %collective-permute-start.8 = (f32[72,640]{1,0:T(8,128)S(1)}, f32[72,640]{1,0:T(8,128)S(1)}, u32[]{:S(2)}, u32[]{:S(2)}) collective-permute-start(f32[72,640]{1,0:T(8,128)S(1)} %get-tuple-element.41), channel_id=1, source_target_pairs={{24,0},{0,24},{25,1},{1,25},{26,2},{2,26},{27,3},{3,27},{28,4},{4,... | collective-permute-start | bytes 552968 | tf_op jit(solution)/shard_map/ppermute | solution.py:561
  63.8 1.0 %ocean_before.1 = (f32[272,640]{1,0:T(8,128)S(1)}, f32[272,640]{1,0:T(8,128)S(1)}, f32[272,640]{1,0:T(8,128)S(1)}) custom-call(s32[1]{0:T(128)} %bitcast.g_ref, f32[3,272,512]{2,1,0:T(8,128)S(1)} %get-tuple-element.32.ocean, f32[304,128]{1,0:T(8,128)S(1)} %collective-permute-done.4.from_left, f32[304,128]{1,0:T(8,128)S(1)} %collective-permute-done.5.from_right), custom_call_target="tpu_custom_call" | custom-call | flops 20000000 | bytes 4000000 | tf_op jit(solution)/shard_map/ocean_before/pallas_call | solution.py:41
  64.9 0.0 collective-permute-done.6.r1
  64.9 1.7 %collective-permute-done.7.r2 = f32[72,640]{1,0:T(8,128)S(1)} collective-permute-done((f32[72,640]{1,0:T(8,128)S(1)}, f32[72,640]{1,0:T(8,128)S(1)}, u32[]{:S(2)}, u32[]{:S(2)}) %collective-permute-start.7) | collective-permute-done | bytes 184352 | tf_op jit(solution)/shard_map/ppermute | solution.py:560
  66.6 2.3 %collective-permute-done.8.r3 = f32[72,640]{1,0:T(8,128)S(1)} collective-permute-done((f32[72,640]{1,0:T(8,128)S(1)}, f32[72,640]{1,0:T(8,128)S(1)}, u32[]{:S(2)}, u32[]{:S(2)}) %collective-permute-start.8) | collective-permute-done | bytes 184352 | tf_op jit(solution)/shard_map/ppermute | solution.py:561
  68.9 1.4 %ocean_basis.1 = (f32[256,512]{1,0:T(8,128)S(1)}, f32[256,512]{1,0:T(8,128)S(1)}, f32[256,512]{1,0:T(8,128)S(1)}, f32[8,128]{1,0:T(8,128)S(1)}) custom-call(s32[1]{0:T(128)} %bitcast.g_ref, f32[272,640]{1,0:T(8,128)S(1)} %get-tuple-element.35.gw, f32[272,640]{1,0:T(8,128)S(1)} %get-tuple-element.36.invd, f32[272,640]{1,0:T(8,128)S(1)} %get-tuple-element.37.ra, ...), custom_call_target="tpu_custom_call" | custom-call | flops 1000000 | bytes 4000000 | tf_op jit(solution)/shard_map/ocean_basis/pallas_call | solution.py:41
  70.4 16.8 %all_to_all.5.parts = f32[32,8,128]{2,1,0:T(8,128)S(1)} all-to-all(f32[32,8,128]{2,1,0:T(8,128)S(1)} %broadcast_in_dim.2), channel_id=1, replica_groups=mesh['grp'=4,'tile'=8] {'grp','tile'}, dimensions={0} | all-to-all | bytes 262144 | tf_op jit(solution)/shard_map/all_to_all | solution.py:579
  87.2 1.1 %combine.1 = f32[256,512]{1,0:T(8,128)} custom-call(s32[1]{0:T(128)} %bitcast.g_ref, f32[32,8,128]{2,1,0:T(8,128)S(1)} %all_to_all.5.parts, f32[256,512]{1,0:T(8,128)S(1)} %copy-done.1, f32[256,512]{1,0:T(8,128)S(1)} %get-tuple-element.44.y0, f32[256,512]{1,0:T(8,128)S(1)} %get-tuple-element.45.y1, f32[256,512]{1,0:T(8,128)S(1)} %get-tuple-element.46.y2), custom_call_target="tpu_custom_call" | custom-call | flops 1000000 | bytes 4000000 | tf_op jit(solution)/shard_map/combine/pallas_call | solution.py:41
  (8 shorter events, 0.0 us)
Async XLA Ops:
  0.6 1.0 %copy-start = (f32[256,512]{1,0:T(8,128)S(1)}, f32[256,512]{1,0:T(8,128)}, u32[]{:S(2)}) copy-start(f32[256,512]{1,0:T(8,128)} %x0.5) | copy-start | bytes 1572868
  1.7 1.2 %copy-start.2 = (f32[2,256,512]{2,1,0:T(8,128)S(1)}, f32[2,256,512]{2,1,0:T(8,128)}, u32[]{:S(2)}) copy-start(f32[2,256,512]{2,1,0:T(8,128)} %cur.3) | copy-start | bytes 3145732
  2.9 1.1 %copy-start.4 = (f32[3,2,64,512]{3,2,1,0:T(8,128)S(1)}, f32[3,2,64,512]{3,2,1,0:T(8,128)}, u32[]{:S(2)}) copy-start(f32[3,2,64,512]{3,2,1,0:T(8,128)} %stress.3) | copy-start | bytes 2359300
  4.0 1.0 %copy-start.6 = (f32[256,512]{1,0:T(8,128)S(1)}, f32[256,512]{1,0:T(8,128)}, u32[]{:S(2)}) copy-start(f32[256,512]{1,0:T(8,128)} %base.3) | copy-start | bytes 1572868
  5.1 1.0 %copy-start.7 = (f32[2,2,64,512]{3,2,1,0:T(8,128)S(1)}, f32[2,2,64,512]{3,2,1,0:T(8,128)}, u32[]{:S(2)}) copy-start(f32[2,2,64,512]{3,2,1,0:T(8,128)} %vel.3) | copy-start | bytes 1572868
  6.1 1.0 %copy-start.9 = (f32[2,2,64,512]{3,2,1,0:T(8,128)S(1)}, f32[2,2,64,512]{3,2,1,0:T(8,128)}, u32[]{:S(2)}) copy-start(f32[2,2,64,512]{3,2,1,0:T(8,128)} %wind.3) | copy-start | bytes 1572868
  7.2 1.0 %copy-start.11 = (f32[256,512]{1,0:T(8,128)S(1)}, f32[256,512]{1,0:T(8,128)}, u32[]{:S(2)}) copy-start(f32[256,512]{1,0:T(8,128)} %depth.1) | copy-start | bytes 1572868
  8.2 0.9 %copy-start.12 = (f32[2,64,512]{2,1,0:T(8,128)S(1)}, f32[2,64,512]{2,1,0:T(8,128)}, u32[]{:S(2)}) copy-start(f32[2,64,512]{2,1,0:T(8,128)} %thick.1) | copy-start | bytes 786436
  9.2 0.7 copy-start.13
  9.9 0.7 copy-start.14
  10.6 24.3 %copy-start.1 = (f32[256,512]{1,0:T(8,128)S(1)}, f32[256,512]{1,0:T(8,128)}, u32[]{:S(2)}) copy-start(f32[256,512]{1,0:T(8,128)} %x0.5) | copy-start | bytes 1572868
  10.6 24.4 %copy-start.3 = (f32[2,256,512]{2,1,0:T(8,128)S(1)}, f32[2,256,512]{2,1,0:T(8,128)}, u32[]{:S(2)}) copy-start(f32[2,256,512]{2,1,0:T(8,128)} %cur.3) | copy-start | bytes 3145732
  10.6 24.4 %copy-start.5 = (f32[3,2,64,512]{3,2,1,0:T(8,128)S(1)}, f32[3,2,64,512]{3,2,1,0:T(8,128)}, u32[]{:S(2)}) copy-start(f32[3,2,64,512]{3,2,1,0:T(8,128)} %stress.3) | copy-start | bytes 2359300
  10.6 24.4 %copy-start.8 = (f32[2,2,64,512]{3,2,1,0:T(8,128)S(1)}, f32[2,2,64,512]{3,2,1,0:T(8,128)}, u32[]{:S(2)}) copy-start(f32[2,2,64,512]{3,2,1,0:T(8,128)} %vel.3) | copy-start | bytes 1572868
  10.6 24.4 %copy-start.10 = (f32[2,2,64,512]{3,2,1,0:T(8,128)S(1)}, f32[2,2,64,512]{3,2,1,0:T(8,128)}, u32[]{:S(2)}) copy-start(f32[2,2,64,512]{3,2,1,0:T(8,128)} %wind.3) | copy-start | bytes 1572868
  10.9 11.5 %collective-permute-start = (f32[160,512]{1,0:T(8,128)S(1)}, f32[160,512]{1,0:T(8,128)S(1)}, u32[]{:S(2)}, u32[]{:S(2)}) collective-permute-start(f32[160,512]{1,0:T(8,128)S(1)} %get-tuple-element.26), channel_id=1, source_target_pairs={{0,8},{8,0},{16,24},{24,16},{1,9},{9,1},{17,25},{25,17},{2,10},{10... | collective-permute-start | bytes 983048 | tf_op jit(solution)/shard_map/ppermute | solution.py:534
  13.9 17.2 %collective-permute-start.1 = (f32[160,512]{1,0:T(8,128)S(1)}, f32[160,512]{1,0:T(8,128)S(1)}, u32[]{:S(2)}, u32[]{:S(2)}) collective-permute-start(f32[160,512]{1,0:T(8,128)S(1)} %get-tuple-element.27), channel_id=1, source_target_pairs={{0,16},{24,8},{1,17},{25,9},{2,18},{26,10},{3,19},{27,11},{4,20},{... | collective-permute-start | bytes 983048 | tf_op jit(solution)/shard_map/ppermute | solution.py:536
  17.4 13.7 %collective-permute-start.2 = (f32[160,512]{1,0:T(8,128)S(1)}, f32[160,512]{1,0:T(8,128)S(1)}, u32[]{:S(2)}, u32[]{:S(2)}) collective-permute-start(f32[160,512]{1,0:T(8,128)S(1)} %get-tuple-element.28), channel_id=1, source_target_pairs={{0,24},{24,0},{8,16},{16,8},{1,25},{25,1},{9,17},{17,9},{2,26},{26... | collective-permute-start | bytes 983048 | tf_op jit(solution)/shard_map/ppermute | solution.py:535
  17.5 17.4 %collective-permute-start.3 = (f32[160,512]{1,0:T(8,128)S(1)}, f32[160,512]{1,0:T(8,128)S(1)}, u32[]{:S(2)}, u32[]{:S(2)}) collective-permute-start(f32[160,512]{1,0:T(8,128)S(1)} %get-tuple-element.29), channel_id=1, source_target_pairs={{0,8},{24,16},{1,9},{25,17},{2,10},{26,18},{3,11},{27,19},{4,12},{... | collective-permute-start | bytes 983048 | tf_op jit(solution)/shard_map/ppermute | solution.py:537
  35.7 2.6 %collective-permute-start.4 = (f32[304,128]{1,0:T(8,128)S(1)}, f32[304,128]{1,0:T(8,128)S(1)}, u32[]{:S(2)}, u32[]{:S(2)}) collective-permute-start(f32[304,128]{1,0:T(8,128)S(1)} %get-tuple-element.33), channel_id=1, source_target_pairs={{0,1},{1,2},{2,3},{3,4},{4,5},{5,6},{6,7},{8,9},{9,10},{10,11},{11... | collective-permute-start | bytes 466952 | tf_op jit(solution)/shard_map/ppermute | solution.py:548
  37.0 5.1 %collective-permute-start.5 = (f32[304,128]{1,0:T(8,128)S(1)}, f32[304,128]{1,0:T(8,128)S(1)}, u32[]{:S(2)}, u32[]{:S(2)}) collective-permute-start(f32[304,128]{1,0:T(8,128)S(1)} %get-tuple-element.34), channel_id=1, source_target_pairs={{1,0},{2,1},{3,2},{4,3},{5,4},{6,5},{7,6},{9,8},{10,9},{11,10},{12... | collective-permute-start | bytes 466952 | tf_op jit(solution)/shard_map/ppermute | solution.py:549
  56.7 8.2 %collective-permute-start.6 = (f32[72,640]{1,0:T(8,128)S(1)}, f32[72,640]{1,0:T(8,128)S(1)}, u32[]{:S(2)}, u32[]{:S(2)}) collective-permute-start(f32[72,640]{1,0:T(8,128)S(1)} %get-tuple-element.39), channel_id=1, source_target_pairs={{8,0},{16,24},{24,8},{0,16},{9,1},{17,25},{25,9},{1,17},{10,2},{18... | collective-permute-start | bytes 552968 | tf_op jit(solution)/shard_map/ppermute | solution.py:559
  59.2 7.4 %collective-permute-start.7 = (f32[72,640]{1,0:T(8,128)S(1)}, f32[72,640]{1,0:T(8,128)S(1)}, u32[]{:S(2)}, u32[]{:S(2)}) collective-permute-start(f32[72,640]{1,0:T(8,128)S(1)} %get-tuple-element.40), channel_id=1, source_target_pairs={{16,0},{8,24},{17,1},{9,25},{18,2},{10,26},{19,3},{11,27},{20,4},{... | collective-permute-start | bytes 552968 | tf_op jit(solution)/shard_map/ppermute | solution.py:560
  60.5 8.4 %collective-permute-start.8 = (f32[72,640]{1,0:T(8,128)S(1)}, f32[72,640]{1,0:T(8,128)S(1)}, u32[]{:S(2)}, u32[]{:S(2)}) collective-permute-start(f32[72,640]{1,0:T(8,128)S(1)} %get-tuple-element.41), channel_id=1, source_target_pairs={{24,0},{0,24},{25,1},{1,25},{26,2},{2,26},{27,3},{3,27},{28,4},{4,... | collective-permute-start | bytes 552968 | tf_op jit(solution)/shard_map/ppermute | solution.py:561

commit v2 on v1

--- a/solution.py
+++ b/solution.py
@@ -22,6 +22,8 @@
 LANES = 128
 EDGE = 16
 SLOTS = LANES // EDGE
+GROUP = 4
+SKEW = 2
 NICE = 8
 NEXT = NICE + 2
 NOC = 3
@@ -35,16 +37,20 @@
     return pl.BlockSpec(memory_space=pltpu.SMEM)
 
 
-def call(body, name, outs, ins, scratch=(), mib=24, flops=1000000):
+def call(body, name, outs, ins, scratch=(), sems=0, hbm=False, mib=24, flops=1000000):
     shapes = tuple(jax.ShapeDtypeStruct(s, F32) for s in outs)
-    specs = [smem() if i == 0 else vmem() for i in range(len(ins))]
+    other = pl.BlockSpec(memory_space=pltpu.HBM) if hbm else vmem()
+    specs = [smem() if i == 0 else other for i in range(len(ins))]
+    held = [pltpu.VMEM(*s) if isinstance(s[0], tuple) else pltpu.VMEM(s, F32) for s in scratch]
+    if sems:
+        held.append(pltpu.SemaphoreType.DMA((sems,)))
     return pl.pallas_call(
         body,
         name=name,
         out_shape=shapes,
         in_specs=specs,
         out_specs=tuple(vmem() for _ in outs),
-        scratch_shapes=[pltpu.VMEM(s, F32) for s in scratch],
+        scratch_shapes=held,
         cost_estimate=pl.CostEstimate(flops=flops, bytes_accessed=4000000, transcendentals=0),
         compiler_params=pltpu.CompilerParams(vmem_limit_bytes=mib * 1024 * 1024),
     )(*ins)
@@ -92,64 +98,87 @@
     return cur[comp, pl.ds(pl.multiple_of(t * SUB, SUB), SUB), :]
 
 
-def pack_rows(groups, g_ref, base, depth, x0, cur, land, thick, iceb, vel, stress, wind,
-              gf, h, a, b, c, d):
+def pack_rows(g_ref, base, depth, x0, cur, land, thick, iceb, vel, stress, wind,
+              a, b, c, d, thick_s, depth_s, land_s, iceb_s, sems):
     g = g_ref[0]
-    rows, ice_rows = base.shape[0], thick.shape[1]
-    slab_tiles = ice_rows // SUB
+    rows, cols = base.shape
+    ice_rows = thick.shape[1]
+    slab = ice_rows + 2 * SUB
+
+    def run(slabs, halos):
+        copies = []
+
+        def copy(src, dst):
+            made = pltpu.make_async_copy(src, dst, sems.at[len(copies)])
+            made.start()
+            copies.append(made)
+
+        for out, dest in slabs:
+            start = ice_rows * dest - SUB
+            first, last = max(start, 0), min(start + slab, rows)
+            for comp in range(2):
+                at = comp * slab + first - start
+                copy(cur.at[comp, first:last, :], out.at[at : at + last - first, :])
+                if first > start:
+                    out[comp * slab : at, :] = jnp.zeros((first - start, cols), F32)
+                if last < start + slab:
+                    out[at + last - first : (comp + 1) * slab, :] = jnp.zeros((start + slab - last, cols), F32)
+        if halos:
+            copy(land, land_s)
+            copy(iceb, iceb_s)
+        for i, (out, last) in enumerate(halos):
+            r = slice(ice_rows - SUB, ice_rows) if last else slice(0, SUB)
+            ro = slice(rows - SUB, rows) if last else slice(0, SUB)
+            for cap in range(2):
+                copy(thick.at[cap, r, :], thick_s.at[i, cap])
+                n = cap * NICE + 1
+                pieces = [vel.at[0, cap, r, :], vel.at[1, cap, r, :]]
+                pieces += [stress.at[k, cap, r, :] for k in range(3)]
+                pieces += [wind.at[k, cap, r, :] for k in range(2)]
+                for piece in pieces:
+                    copy(piece, out.at[tile(n), :])
+                    n += 1
+            copy(depth.at[ro, :], depth_s.at[i])
+            copy(base.at[ro, :], out.at[tile(2 * NICE), :])
+            copy(x0.at[ro, :], out.at[tile(2 * NICE + 2), :])
+            out[tile(2 * NICE + 3), :] = jnp.zeros((SUB, cols), F32)
+        for made in copies:
+            made.wait()
+        if halos:
+            wet = expanded_cols(land_s[...])
+            covers = [expanded_cols(iceb_s[cap]) for cap in range(2)]
+        for i, (out, last) in enumerate(halos):
+            for cap in range(2):
+                k = covers[cap].shape[0] - 1 if last else 0
+                out[tile(cap * NICE), :] = thick_s[i, cap] * covers[cap][k : k + 1, :]
+            k = wet.shape[0] - 1 if last else 0
+            out[tile(2 * NICE + 1), :] = depth_s[i] * wet[k : k + 1, :]
+
+    @pl.when(g == 0)
+    def _():
+        run([(c, 3), (a, 1), (b, 2)], [(d, True)])
+
+    @pl.when(g == 3)
+    def _():
+        run([(c, 0), (a, 2), (b, 1)], [(d, False)])
+
+    @pl.when(g == 1)
+    def _():
+        run([], [(a, False), (c, True)])
+
+    @pl.when(g == 2)
+    def _():
+        run([], [(a, True), (c, False)])
+
+
+def masks(g_ref, depth, land, thick, iceb, gf, h):
     wet = expanded_cols(land[...])
-    for k in range(rows // SUB):
+    for k in range(depth.shape[0] // SUB):
         gf[tile(k), :] = depth[tile(k), :] * wet[k : k + 1, :]
     for cap in range(2):
         cover = expanded_cols(iceb[cap])
-        for k in range(slab_tiles):
+        for k in range(thick.shape[1] // SUB):
             h[cap, tile(k), :] = thick[cap, tile(k), :] * cover[k : k + 1, :]
-
-    def halo(out, last):
-        r = slice(ice_rows - SUB, ice_rows) if last else slice(0, SUB)
-        ro = slice(rows - SUB, rows) if last else slice(0, SUB)
-        n = 0
-        for cap in range(2):
-            pieces = [h[cap, r, :], vel[0, cap, r, :], vel[1, cap, r, :]]
-            pieces += [stress[i, cap, r, :] for i in range(3)]
-            pieces += [wind[i, cap, r, :] for i in range(2)]
-            for piece in pieces:
-                out[tile(n), :] = piece
-                n += 1
-        for field in (base, gf, x0):
-            out[tile(n), :] = field[ro, :]
-            n += 1
-        for k in range(n, out.shape[0] // SUB):
-            out[tile(k), :] = jnp.zeros((SUB, out.shape[1]), F32)
-
-    def slab(out, dest):
-        for comp in range(2):
-            for j in range(slab_tiles + 2):
-                out[tile(comp * (slab_tiles + 2) + j), :] = own_tile(cur, comp, slab_tiles * dest - 1, j)
-
-    @pl.when((g == 0) | (g == 3))
-    def _():
-        slab(a, g ^ 1)
-        slab(b, g ^ 2)
-        slab(c, g ^ 3)
-
-    @pl.when(g == 0)
-    def _():
-        halo(d, True)
-
-    @pl.when(g == 3)
-    def _():
-        halo(d, False)
-
-    @pl.when(g == 1)
-    def _():
-        halo(a, False)
-        halo(c, True)
-
-    @pl.when(g == 2)
-    def _():
-        halo(a, True)
-        halo(c, False)
 
 
 def pack_cols(g_ref, ra, rb, rc, rd, cur, h, vel, stress, wind, base, gf, x0, ice, ocean, left, right):
@@ -159,21 +188,21 @@
     ext = slab_tiles + 2
     rows = base.shape[0] // SUB
     lane = lane_iota()
+    slot = lane // EDGE
     zero = jnp.zeros((SUB, cols), F32)
     state = {"n": 0, "l": None, "r": None}
 
     def emit(value):
         n = state["n"]
         s = n % SLOTS
-        first, last = value[:, :LANES], value[:, cols - LANES :]
-        first = pltpu.roll(first, EDGE * s, 1) if s else first
-        shift = EDGE * (s + 1) % LANES
-        last = pltpu.roll(last, shift, 1) if shift else last
+        both = jnp.where(lane < EDGE, value[:, :LANES], value[:, cols - LANES :])
+        both = pltpu.roll(both, EDGE * s, 1) if s else both
+        before = (s - 1) % SLOTS
         if s == 0:
-            state["l"], state["r"] = first, last
+            state["l"] = state["r"] = both
         else:
-            state["l"] = jnp.where(lane >= EDGE * s, first, state["l"])
-            state["r"] = jnp.where(lane >= EDGE * s, last, state["r"])
+            state["l"] = jnp.where(slot == s, both, state["l"])
+            state["r"] = jnp.where(slot == before, both, state["r"])
         if s == SLOTS - 1:
             k = n // SLOTS
             left[tile(k), :] = state["l"]
@@ -225,114 +254,165 @@
         emit(zero)
 
 
-def widened(value, from_left, from_right, n, lane):
-    s = n % SLOTS
-    k = n // SLOTS
-    after, before = from_right[tile(k), :], from_left[tile(k), :]
-    after = pltpu.roll(after, LANES - EDGE * s, 1) if s else after
-    shift = (LANES - EDGE * (s + 1)) % LANES
-    before = pltpu.roll(before, shift, 1) if shift else before
-    outer = jnp.where(lane < EDGE, after, jnp.where(lane >= LANES - EDGE, before, 0.0))
-    return jnp.concatenate([value, outer], axis=1)
+def outer_columns(from_left, from_right, n, lane):
+    s, k = n % SLOTS, n // SLOTS
+    both = jnp.where(lane // EDGE == s, from_right[tile(k), :], from_left[tile(k), :])
+    both = pltpu.roll(both, LANES - EDGE * s, 1) if s else both
+    return jnp.where((lane < EDGE) | (lane >= LANES - EDGE), both, 0.0)
+
+
+def split(value):
+    return [value[:, c * LANES : (c + 1) * LANES] for c in range(value.shape[1] // LANES)]
+
+
+def turned_next(regs, lane):
+    n = len(regs)
+    return [pltpu.roll(jnp.where(lane == 0, regs[(c + 1) % n], regs[c]), LANES - 1, 1) for c in range(n)]
+
+
+def turned_prev(regs, lane):
+    n = len(regs)
+    return [pltpu.roll(jnp.where(lane == LANES - 1, regs[c - 1], regs[c]), 1, 1) for c in range(n)]
 
 
 def ice_steps(g_ref, ice, from_left, from_right, vel_out, stress_out, p1, p2, p3, mine,
-              u_s, v_s, s0_s, s1_s, s2_s, a_s, m_s, q_s, fx_s, fy_s, f0_s, f1_s):
+              u_s, v_s, p_s, q_s, s_s, un_s, vn_s, qp_s, sp_s, a_s, m_s, w_s, fx_s, fy_s, f0_s, f1_s):
     g = g_ref[0]
     cols = ice.shape[3]
-    wide = cols + LANES
+    regs = cols // LANES + 1
     ext = ice.shape[2] // SUB
     lane = lane_iota()
-    row = row_iota(wide)
-    zero = jnp.zeros((SUB, wide), F32)
+    zero = jnp.zeros((SUB, LANES), F32)
     keep = 1.0 / (1.0 + RELAX)
+
+    def at(j, shift=0):
+        return slice(SUB * (j + 1) + shift, SUB * (j + 2) + shift)
+
     for cap in range(2):
+        for c in range(regs):
+            for ref in (p_s, s_s):
+                ref[cap, c, at(-1), :] = zero
+            for ref in (u_s, v_s):
+                ref[cap, c, at(ext), :] = zero
+        outers = []
         for j in range(ext):
-            t = tile(j)
-
-            def field(f):
-                return widened(ice[cap, f, t, :], from_left, from_right, (cap * NEXT + f) * ext + j, lane)
-
-            hh = field(0)
-            u_s[cap, t, :] = field(1)
-            v_s[cap, t, :] = field(2)
-            s0_s[cap, t, :] = field(3)
-            s1_s[cap, t, :] = field(4)
-            s2_s[cap, t, :] = field(5)
-            w0, w1, f0, f1 = field(6), field(7), field(8), field(9)
-            inv = jnp.where(hh > 0.0, 1.0 / (hh + (1.0 + STEP * DRAG)), 0.0)
-            quick = STEP * inv
-            a_s[cap, t, :] = hh * (RELAX * STRENGTH * keep)
-            m_s[cap, t, :] = (hh + 1.0) * inv
-            q_s[cap, t, :] = quick
-            fx_s[cap, t, :] = quick * (w0 + DRAG * f0)
-            fy_s[cap, t, :] = quick * (w1 + DRAG * f1)
-            f0_s[cap, t, :] = f0
-            f1_s[cap, t, :] = f1
+            if j % GROUP == 0:
+                outers = [
+                    [outer_columns(from_left, from_right, (cap * NEXT + f) * ext + i, lane) for f in range(NEXT)]
+                    for i in range(j, min(j + GROUP, ext))
+                ]
+            fields = [split(ice[cap, f, tile(j), :]) + [outers[j % GROUP][f]] for f in range(NEXT)]
+            for c in range(regs):
+                hh, u, v, s0, s1, s2, w0, w1, f0, f1 = (f[c] for f in fields)
+                u_s[cap, c, at(j), :] = u
+                v_s[cap, c, at(j), :] = v
+                p_s[cap, c, at(j), :] = 0.5 * (s0 + s1)
+                q_s[cap, c, at(j), :] = 0.5 * (s0 - s1)
+                s_s[cap, c, at(j), :] = s2
+                inv = jnp.where(hh > 0.0, 1.0 / (hh + (1.0 + STEP * DRAG)), 0.0)
+                quick = STEP * inv
+                a_s[cap, c, at(j), :] = hh * (RELAX * STRENGTH * keep)
+                m_s[cap, c, at(j), :] = (hh + 1.0) * inv
+                w_s[cap, c, at(j), :] = quick
+                fx_s[cap, c, at(j), :] = quick * (w0 + DRAG * f0)
+                fy_s[cap, c, at(j), :] = quick * (w1 + DRAG * f1)
+                f0_s[cap, c, at(j), :] = f0
+                f1_s[cap, c, at(j), :] = f1
+    for j in range(ext):
+        for cap in range(2):
+            for ref, source in ((un_s, u_s), (vn_s, v_s)):
+                turned = turned_next([source[cap, c, at(j), :] for c in range(regs)], lane)
+                for c in range(regs):
+                    ref[cap, c, at(j), :] = turned[c]
+
+    def stress_tile(cap, j):
+        qs, ss = [], []
+        for c in range(regs):
+            u, v = u_s[cap, c, at(j), :], v_s[cap, c, at(j), :]
+            ux = u_s[cap, c, at(j, 1), :] - u
+            vx = v_s[cap, c, at(j, 1), :] - v
+            uy = un_s[cap, c, at(j), :] - u
+            vy = vn_s[cap, c, at(j), :] - v
+            es = uy + vx
+            half = ux * ux + vy * vy
+            a = a_s[cap, c, at(j), :]
+            ratio = a * lax.rsqrt((half + half) + (es * es + 1.0))
+            low = 0.5 * a
+            q = q_s[cap, c, at(j), :] * keep + (ratio * vy - low)
+            s = s_s[cap, c, at(j), :] * keep + ratio * es
+            p_s[cap, c, at(j), :] = p_s[cap, c, at(j), :] * keep + (ratio * ux - low)
+            q_s[cap, c, at(j), :] = q
+            s_s[cap, c, at(j), :] = s
+            qs.append(q)
+            ss.append(s)
+        for ref, turned in ((qp_s, turned_prev(qs, lane)), (sp_s, turned_prev(ss, lane))):
+            for c in range(regs):
+                ref[cap, c, at(j), :] = turned[c]
+
+    def velocity_tile(cap, j):
+        us, vs = [], []
+        for c in range(regs):
+            s = s_s[cap, c, at(j), :]
+            force_x = (p_s[cap, c, at(j), :] - p_s[cap, c, at(j, -1), :]) + (s - sp_s[cap, c, at(j), :])
+            force_y = (q_s[cap, c, at(j), :] - qp_s[cap, c, at(j), :]) + (s - s_s[cap, c, at(j, -1), :])
+            m, quick = m_s[cap, c, at(j), :], w_s[cap, c, at(j), :]
+            u = m * u_s[cap, c, at(j), :] + (quick * force_x + fx_s[cap, c, at(j), :])
+            v = m * v_s[cap, c, at(j), :] + (quick * force_y + fy_s[cap, c, at(j), :])
+            u_s[cap, c, at(j), :] = u
+            v_s[cap, c, at(j), :] = v
+            us.append(u)
+            vs.append(v)
+        for ref, turned in ((un_s, turned_next(us, lane)), (vn_s, turned_next(vs, lane))):
+            for c in range(regs):
+                ref[cap, c, at(j), :] = turned[c]
 
     def subcycle(_, carry):
-        for cap in range(2):
-            p_prev, s2_prev = zero, zero
-            u, v = u_s[cap, tile(0), :], v_s[cap, tile(0), :]
-            for j in range(ext):
-                t = tile(j)
-                if j + 1 < ext:
-                    u_next, v_next = u_s[cap, tile(j + 1), :], v_s[cap, tile(j + 1), :]
-                else:
-                    u_next, v_next = zero, zero
-                ux = from_next_row(u, u_next, row) - u
-                vx = from_next_row(v, v_next, row) - v
-                uy = from_next_col(u) - u
-                vy = from_next_col(v) - v
-                ed, et, es = ux + vy, ux - vy, uy + vx
-                a = a_s[cap, t, :]
-                ratio = a * lax.rsqrt(ed * ed + et * et + es * es + 1.0)
-                s0 = s0_s[cap, t, :] * keep + (ratio * ed - a)
-                s1 = s1_s[cap, t, :] * keep + ratio * et
-                s2 = s2_s[cap, t, :] * keep + ratio * es
-                s0_s[cap, t, :] = s0
-                s1_s[cap, t, :] = s1
-                s2_s[cap, t, :] = s2
-                p = 0.5 * (s0 + s1)
-                q = 0.5 * (s0 - s1)
-                force_x = (p - from_prev_row(p, p_prev, row)) + (s2 - from_prev_col(s2))
-                force_y = (q - from_prev_col(q)) + (s2 - from_prev_row(s2, s2_prev, row))
-                m, quick = m_s[cap, t, :], q_s[cap, t, :]
-                u_s[cap, t, :] = m * u + (quick * force_x + fx_s[cap, t, :])
-                v_s[cap, t, :] = m * v + (quick * force_y + fy_s[cap, t, :])
-                p_prev, s2_prev = p, s2
-                u, v = u_next, v_next
+        for j in range(ext + SKEW):
+            for cap in range(2):
+                if j < ext:
+                    stress_tile(cap, j)
+                if j >= SKEW:
+                    velocity_tile(cap, j - SKEW)
         return carry
 
     lax.fori_loop(0, NSUB, subcycle, 0)
     spreads = []
     for cap in range(2):
+        for c in range(regs):
+            q_s[cap, c, at(0), :] = zero
+            q_s[cap, c, at(ext - 1), :] = zero
         parts = []
-        d0_prev = zero
+        across = [[zero] * regs]
+        for j in range(1, ext - 1):
+            d1s = []
+            for c in range(regs):
+                u, v = u_s[cap, c, at(j), :], v_s[cap, c, at(j), :]
+                p, q = p_s[cap, c, at(j), :], q_s[cap, c, at(j), :]
+                if c + 1 < regs:
+                    block = (tile(j - 1), slice(c * LANES, (c + 1) * LANES))
+                    vel_out[(0, cap) + block] = u
+                    vel_out[(1, cap) + block] = v
+                    stress_out[(0, cap) + block] = p + q
+                    stress_out[(1, cap) + block] = p - q
+                    stress_out[(2, cap) + block] = s_s[cap, c, at(j), :]
+                iced = m_s[cap, c, at(j), :] > 0.0
+                q_s[cap, c, at(j), :] = jnp.where(iced, DRAG * (u - f0_s[cap, c, at(j), :]), 0.0)
+                d1s.append(jnp.where(iced, DRAG * (v - f1_s[cap, c, at(j), :]), 0.0))
+            turned = turned_prev(d1s, lane)
+            across.append([d1s[c] - turned[c] for c in range(regs)])
+        across.append([zero] * regs)
         for j in range(1, ext):
-            t = tile(j)
-            if j < ext - 1:
-                out = tile(j - 1)
-                u, v = u_s[cap, t, :], v_s[cap, t, :]
-                vel_out[0, cap, out, :] = u[:, :cols]
-                vel_out[1, cap, out, :] = v[:, :cols]
-                stress_out[0, cap, out, :] = s0_s[cap, t, :][:, :cols]
-                stress_out[1, cap, out, :] = s1_s[cap, t, :][:, :cols]
-                stress_out[2, cap, out, :] = s2_s[cap, t, :][:, :cols]
-                iced = m_s[cap, t, :] > 0.0
-                d0 = jnp.where(iced, DRAG * (u - f0_s[cap, t, :]), 0.0)
-                d1 = jnp.where(iced, DRAG * (v - f1_s[cap, t, :]), 0.0)
-            else:
-                d0 = d1 = zero
-            parts.append((d0 - from_prev_row(d0, d0_prev, row)) + (d1 - from_prev_col(d1)))
-            d0_prev = d0
+            parts.append([
+                (q_s[cap, c, at(j), :] - q_s[cap, c, at(j, -1), :]) + across[j][c] for c in range(regs)
+            ])
         spreads.append(parts)
-    for k, (north, south) in enumerate(zip(*spreads)):
-        t = tile(k)
-        p1[t, :] = jnp.where((g == 1) | (g == 3), north, south)
-        p2[t, :] = jnp.where(g == 2, north, south)
-        p3[t, :] = jnp.where(g == 3, north, south)
-        mine[t, :] = jnp.where(g == 0, north, south)
+    for k, (norths, souths) in enumerate(zip(*spreads)):
+        for c, (north, south) in enumerate(zip(norths, souths)):
+            block = (tile(k), slice(c * LANES, (c + 1) * LANES))
+            p1[block] = jnp.where((g == 1) | (g == 3), north, south)
+            p2[block] = jnp.where(g == 2, north, south)
+            p3[block] = jnp.where(g == 3, north, south)
+            mine[block] = jnp.where(g == 0, north, south)
 
 
 def neighbour_sum(ref, k, row):
@@ -355,7 +435,8 @@
         t = tile(j + 1)
 
         def field(i):
-            return widened(ocean[i, tile(j), :], from_left, from_right, first + i * ext + j, lane)
+            outer = outer_columns(from_left, from_right, first + i * ext + j, lane)
+            return jnp.concatenate([ocean[i, tile(j), :], outer], axis=1)
 
         b_s[tile(j), :] = field(0)
         depth = field(1)
@@ -526,13 +607,25 @@
     wide = cols + LANES
 
     strip = (2 * slab, cols)
-    gf, h, a, b, c, d = call(
-        functools.partial(pack_rows, groups), "pack_rows",
-        [(rows, cols), (2, ice_rows, cols), strip, strip, strip, strip],
+    a, b, c, d = call(
+        pack_rows, "pack_rows",
+        [strip] * 4,
         [g, base_rhs, depth, ssh_prev, currents, land_blocks, ice_thick, ice_blocks, ice_vel, ice_stress, wind],
-    )
+        scratch=[
+            (2, 2, SUB, cols), (2, SUB, cols),
+            (land_blocks.shape, jnp.int32), (ice_blocks.shape, jnp.int32),
+        ],
+        sems=48,
+        hbm=True,
+    )
+    gf, h = call(
+        masks, "masks",
+        [(rows, cols), (2, ice_rows, cols)],
+        [g, depth, land_blocks, ice_thick, ice_blocks],
+        flops=10000000,
+    )
+    rc = lax.ppermute(c, "grp", [(0, 3), (3, 0), (1, 2), (2, 1)])
     ra = lax.ppermute(a, "grp", [(0, 1), (1, 0), (2, 3), (3, 2)])
-    rc = lax.ppermute(c, "grp", [(0, 3), (3, 0), (1, 2), (2, 1)])
     rb = lax.ppermute(b, "grp", [(0, 2), (3, 1)])
     rd = lax.ppermute(d, "grp", [(0, 1), (3, 2)])
 
@@ -553,7 +646,7 @@
         ice_steps, "ice_steps",
         [ice_vel.shape, ice_stress.shape, back, back, back, back],
         [g, ice, from_left, from_right],
-        scratch=[(2, slab, wide)] * 12,
+        scratch=[(2, cols // LANES + 1, slab + 2 * SUB, LANES)] * 16,
         mib=32,
     )
     r1 = lax.ppermute(p1, "grp", [(1, 0), (2, 3), (3, 1), (0, 2)])

time: 89 us -> 85 us (0.955)
  Pallas kernels: 19.3 us -> 16.1 us
    pallas_call x6 -> x7, Pallas kernels: 19.3 us -> 16.1 us  [call(): pl.pallas_call(body, name=name, out_shape=shapes, in_specs=specs, out_spe...]
    ppermute x1, waiting for transfers between devices: 2.24 us -> 1.29 us  [shards(): ra = lax.ppermute(a, 'grp', [(0, 1), (1, 0), (2, 3), (3, 2)])]
    unnamed x30 -> x34, local copies, waits for them, and re-layouts: 9.94 us -> 9.95 us
where the time goes in v2:
time: 85 us; the launch traced here: 84.3 us
  waiting for transfers between devices  22.2 us (26%)
  starting transfers between devices  19 us (22%)
  blocking collectives  16.2 us (19%)
  Pallas kernels  16.1 us (19%)
  local copies, waits for them, and re-layouts  9.96 us (12%)
    all_to_all x1, blocking collectives, shards(): lax.all_to_all(jnp.broadcast_to(sums[None], (devices, SUB, LANES)), ('grp...  16.2 us
    pallas_call x7, Pallas kernels, call(): pl.pallas_call(body, name=name, out_shape=shapes, in_specs=specs, out_spe...  16.1 us
    unnamed x34, local copies, waits for them, and re-layouts  9.95 us
    ppermute x1, waiting for transfers between devices, shards(): rb = lax.ppermute(b, 'grp', [(0, 2), (3, 1)])  9.34 us
    ppermute x1, starting transfers between devices, shards(): rb = lax.ppermute(b, 'grp', [(0, 2), (3, 1)])  4.22 us
    ppermute x1, waiting for transfers between devices, shards(): lax.ppermute(left, 'tile', [(i + 1, i) for i in range(tiles - 1)])  3.77 us
    ppermute x1, waiting for transfers between devices, shards(): rd = lax.ppermute(d, 'grp', [(0, 1), (3, 2)])  3.11 us
    ppermute x1, starting transfers between devices, shards(): r1 = lax.ppermute(p1, 'grp', [(1, 0), (2, 3), (3, 1), (0, 2)])  3.06 us
  transfers between devices with their start and end apart: 9, of which 6 were waited for; matrix products, arithmetic and copies ran while one was open for 0% of the time, Pallas kernels for 1%

profile of v2, /device:TPU:0, one launch (start us, length us, event | category | flops | bytes accessed | tf_op | source)
XLA Modules:
  0.0 84.3 jit_solution(7263266678121084062)
XLA Ops:
  0.6 0.0 copy-start
  0.6 1.0 %copy-done = f32[256,512]{1,0:T(8,128)S(1)} copy-done((f32[256,512]{1,0:T(8,128)S(1)}, f32[256,512]{1,0:T(8,128)}, u32[]{:S(2)}) %copy-start) | copy-done | bytes 524312
  1.7 0.0 copy-start.2
  1.7 1.2 %copy-done.2 = f32[2,256,512]{2,1,0:T(8,128)S(1)} copy-done((f32[2,256,512]{2,1,0:T(8,128)S(1)}, f32[2,256,512]{2,1,0:T(8,128)}, u32[]{:S(2)}) %copy-start.2) | copy-done | bytes 1048600
  2.9 1.1 %copy-done.4 = f32[3,2,64,512]{3,2,1,0:T(8,128)S(1)} copy-done((f32[3,2,64,512]{3,2,1,0:T(8,128)S(1)}, f32[3,2,64,512]{3,2,1,0:T(8,128)}, u32[]{:S(2)}) %copy-start.4) | copy-done | bytes 786456
  4.0 1.0 %copy-done.6 = f32[256,512]{1,0:T(8,128)S(1)} copy-done((f32[256,512]{1,0:T(8,128)S(1)}, f32[256,512]{1,0:T(8,128)}, u32[]{:S(2)}) %copy-start.6) | copy-done | bytes 524312
  5.1 1.0 %copy-done.8 = f32[2,2,64,512]{3,2,1,0:T(8,128)S(1)} copy-done((f32[2,2,64,512]{3,2,1,0:T(8,128)S(1)}, f32[2,2,64,512]{3,2,1,0:T(8,128)}, u32[]{:S(2)}) %copy-start.8) | copy-done | bytes 524312
  6.1 1.0 %copy-done.10 = f32[2,2,64,512]{3,2,1,0:T(8,128)S(1)} copy-done((f32[2,2,64,512]{3,2,1,0:T(8,128)S(1)}, f32[2,2,64,512]{3,2,1,0:T(8,128)}, u32[]{:S(2)}) %copy-start.10) | copy-done | bytes 524312
  7.2 1.0 %copy-done.12 = f32[256,512]{1,0:T(8,128)S(1)} copy-done((f32[256,512]{1,0:T(8,128)S(1)}, f32[256,512]{1,0:T(8,128)}, u32[]{:S(2)}) %copy-start.12) | copy-done | bytes 524312
  8.2 0.9 %copy-done.14 = f32[2,64,512]{2,1,0:T(8,128)S(1)} copy-done((f32[2,64,512]{2,1,0:T(8,128)S(1)}, f32[2,64,512]{2,1,0:T(8,128)}, u32[]{:S(2)}) %copy-start.14) | copy-done | bytes 262168
  9.2 0.7 copy-done.15
  9.9 0.7 copy-done.16
  10.6 0.0 copy-start.7
  10.6 0.0 copy-start.9
  10.6 0.0 copy-start.11
  10.6 2.3 %pack_rows.1 = (f32[160,512]{1,0:T(8,128)S(1)}, f32[160,512]{1,0:T(8,128)S(1)}, f32[160,512]{1,0:T(8,128)S(1)}, f32[160,512]{1,0:T(8,128)S(1)}) custom-call(s32[1]{0:T(128)} %bitcast.g_ref, f32[256,512]{1,0:T(8,128)S(1)} %copy-done.6, f32[256,512]{1,0:T(8,128)S(1)} %copy-done.12, f32[256,512]{1,0:T(8,128)S(1)} %copy-done, f32[2,256,512]{2,1,0:T(8,128)S(1)} %copy-done.2, ...), custom_call_target="tpu_custom_call" | custom-call | flops 1000000 | bytes 4000000 | tf_op jit(solution)/shard_map/pack_rows/pallas_call | solution.py:47
  12.9 2.2 %collective-permute-start = (f32[160,512]{1,0:T(8,128)S(1)}, f32[160,512]{1,0:T(8,128)S(1)}, u32[]{:S(2)}, u32[]{:S(2)}) collective-permute-start(f32[160,512]{1,0:T(8,128)S(1)} %get-tuple-element.26), channel_id=1, source_target_pairs={{0,8},{8,0},{16,24},{24,16},{1,9},{9,1},{17,25},{25,17},{2,10},{10... | collective-permute-start | bytes 983048 | tf_op jit(solution)/shard_map/ppermute | solution.py:628
  15.2 4.2 %collective-permute-start.1 = (f32[160,512]{1,0:T(8,128)S(1)}, f32[160,512]{1,0:T(8,128)S(1)}, u32[]{:S(2)}, u32[]{:S(2)}) collective-permute-start(f32[160,512]{1,0:T(8,128)S(1)} %get-tuple-element.27), channel_id=1, source_target_pairs={{0,16},{24,8},{1,17},{25,9},{2,18},{26,10},{3,19},{27,11},{4,20},{... | collective-permute-start | bytes 983048 | tf_op jit(solution)/shard_map/ppermute | solution.py:629
  19.4 0.1 collective-permute-start.2
  19.5 2.7 %collective-permute-start.3 = (f32[160,512]{1,0:T(8,128)S(1)}, f32[160,512]{1,0:T(8,128)S(1)}, u32[]{:S(2)}, u32[]{:S(2)}) collective-permute-start(f32[160,512]{1,0:T(8,128)S(1)} %get-tuple-element.29), channel_id=1, source_target_pairs={{0,8},{24,16},{1,9},{25,17},{2,10},{26,18},{3,11},{27,19},{4,12},{... | collective-permute-start | bytes 983048 | tf_op jit(solution)/shard_map/ppermute | solution.py:630
  22.2 0.0 copy-done.13
  22.2 0.2 masks.1
  22.5 1.3 %collective-permute-done.ra = f32[160,512]{1,0:T(8,128)S(1)} collective-permute-done((f32[160,512]{1,0:T(8,128)S(1)}, f32[160,512]{1,0:T(8,128)S(1)}, u32[]{:S(2)}, u32[]{:S(2)}) %collective-permute-start) | collective-permute-done | bytes 327712 | tf_op jit(solution)/shard_map/ppermute | solution.py:628
  23.7 9.3 %collective-permute-done.1.rb = f32[160,512]{1,0:T(8,128)S(1)} collective-permute-done((f32[160,512]{1,0:T(8,128)S(1)}, f32[160,512]{1,0:T(8,128)S(1)}, u32[]{:S(2)}, u32[]{:S(2)}) %collective-permute-start.1) | collective-permute-done | bytes 327712 | tf_op jit(solution)/shard_map/ppermute | solution.py:629
  33.1 0.0 collective-permute-done.2.rc
  33.1 3.1 %collective-permute-done.3.rd = f32[160,512]{1,0:T(8,128)S(1)} collective-permute-done((f32[160,512]{1,0:T(8,128)S(1)}, f32[160,512]{1,0:T(8,128)S(1)}, u32[]{:S(2)}, u32[]{:S(2)}) %collective-permute-start.3) | collective-permute-done | bytes 327712 | tf_op jit(solution)/shard_map/ppermute | solution.py:630
  36.2 0.0 copy-done.1
  36.2 0.0 copy-done.3
  36.2 0.0 copy-done.5
  36.2 0.0 copy-done.7
  36.2 0.0 copy-done.9
  36.2 0.0 copy-done.11
  36.2 0.5 pack_cols.1
  36.8 1.3 %collective-permute-start.4 = (f32[304,128]{1,0:T(8,128)S(1)}, f32[304,128]{1,0:T(8,128)S(1)}, u32[]{:S(2)}, u32[]{:S(2)}) collective-permute-start(f32[304,128]{1,0:T(8,128)S(1)} %get-tuple-element.33), channel_id=1, source_target_pairs={{0,1},{1,2},{2,3},{3,4},{4,5},{5,6},{6,7},{8,9},{9,10},{10,11},{11... | collective-permute-start | bytes 466952 | tf_op jit(solution)/shard_map/ppermute | solution.py:641
  38.1 1.3 %collective-permute-start.5 = (f32[304,128]{1,0:T(8,128)S(1)}, f32[304,128]{1,0:T(8,128)S(1)}, u32[]{:S(2)}, u32[]{:S(2)}) collective-permute-start(f32[304,128]{1,0:T(8,128)S(1)} %get-tuple-element.34), channel_id=1, source_target_pairs={{1,0},{2,1},{3,2},{4,3},{5,4},{6,5},{7,6},{9,8},{10,9},{11,10},{12... | collective-permute-start | bytes 466952 | tf_op jit(solution)/shard_map/ppermute | solution.py:642
  39.4 0.0 collective-permute-done.4.from_left
  39.4 3.8 %collective-permute-done.5.from_right = f32[304,128]{1,0:T(8,128)S(1)} collective-permute-done((f32[304,128]{1,0:T(8,128)S(1)}, f32[304,128]{1,0:T(8,128)S(1)}, u32[]{:S(2)}, u32[]{:S(2)}) %collective-permute-start.5) | collective-permute-done | bytes 155680 | tf_op jit(solution)/shard_map/ppermute | solution.py:642
  43.2 9.6 %ice_steps.1 = (f32[2,2,64,512]{3,2,1,0:T(8,128)}, f32[3,2,64,512]{3,2,1,0:T(8,128)}, f32[72,640]{1,0:T(8,128)S(1)}, f32[72,640]{1,0:T(8,128)S(1)}, f32[72,640]{1,0:T(8,128)S(1)}, /*index=5*/f32[72,640]{1,0:T(8,128)S(1)}) custom-call(s32[1]{0:T(128)} %bitcast.g_ref, f32[2,10,80,512]{3,2,1,0:T(8,128)S(1)} %get-tuple-element.38.ice, ...), custom_call_target="tpu_custom_call" | custom-call | flops 1000000 | bytes 4000000 | tf_op jit(solution)/shard_map/ice_steps/pallas_call | solution.py:47
  52.8 3.1 %collective-permute-start.6 = (f32[72,640]{1,0:T(8,128)S(1)}, f32[72,640]{1,0:T(8,128)S(1)}, u32[]{:S(2)}, u32[]{:S(2)}) collective-permute-start(f32[72,640]{1,0:T(8,128)S(1)} %get-tuple-element.39), channel_id=1, source_target_pairs={{8,0},{16,24},{24,8},{0,16},{9,1},{17,25},{25,9},{1,17},{10,2},{18... | collective-permute-start | bytes 552968 | tf_op jit(solution)/shard_map/ppermute | solution.py:652
  55.8 1.3 %collective-permute-start.7 = (f32[72,640]{1,0:T(8,128)S(1)}, f32[72,640]{1,0:T(8,128)S(1)}, u32[]{:S(2)}, u32[]{:S(2)}) collective-permute-start(f32[72,640]{1,0:T(8,128)S(1)} %get-tuple-element.40), channel_id=1, source_target_pairs={{16,0},{8,24},{17,1},{9,25},{18,2},{10,26},{19,3},{11,27},{20,4},{... | collective-permute-start | bytes 552968 | tf_op jit(solution)/shard_map/ppermute | solution.py:653
  57.1 2.8 %collective-permute-start.8 = (f32[72,640]{1,0:T(8,128)S(1)}, f32[72,640]{1,0:T(8,128)S(1)}, u32[]{:S(2)}, u32[]{:S(2)}) collective-permute-start(f32[72,640]{1,0:T(8,128)S(1)} %get-tuple-element.41), channel_id=1, source_target_pairs={{24,0},{0,24},{25,1},{1,25},{26,2},{2,26},{27,3},{3,27},{28,4},{4,... | collective-permute-start | bytes 552968 | tf_op jit(solution)/shard_map/ppermute | solution.py:654
  59.9 0.9 %ocean_before.1 = (f32[272,640]{1,0:T(8,128)S(1)}, f32[272,640]{1,0:T(8,128)S(1)}, f32[272,640]{1,0:T(8,128)S(1)}) custom-call(s32[1]{0:T(128)} %bitcast.g_ref, f32[3,272,512]{2,1,0:T(8,128)S(1)} %get-tuple-element.32.ocean, f32[304,128]{1,0:T(8,128)S(1)} %collective-permute-done.4.from_left, f32[304,128]{1,0:T(8,128)S(1)} %collective-permute-done.5.from_right), custom_call_target="tpu_custom_call" | custom-call | flops 20000000 | bytes 4000000 | tf_op jit(solution)/shard_map/ocean_before/pallas_call | solution.py:47
  60.9 0.0 collective-permute-done.6.r1
  60.9 2.4 %collective-permute-done.7.r2 = f32[72,640]{1,0:T(8,128)S(1)} collective-permute-done((f32[72,640]{1,0:T(8,128)S(1)}, f32[72,640]{1,0:T(8,128)S(1)}, u32[]{:S(2)}, u32[]{:S(2)}) %collective-permute-start.7) | collective-permute-done | bytes 184352 | tf_op jit(solution)/shard_map/ppermute | solution.py:653
  63.2 2.3 %collective-permute-done.8.r3 = f32[72,640]{1,0:T(8,128)S(1)} collective-permute-done((f32[72,640]{1,0:T(8,128)S(1)}, f32[72,640]{1,0:T(8,128)S(1)}, u32[]{:S(2)}, u32[]{:S(2)}) %collective-permute-start.8) | collective-permute-done | bytes 184352 | tf_op jit(solution)/shard_map/ppermute | solution.py:654
  65.5 1.4 %ocean_basis.1 = (f32[256,512]{1,0:T(8,128)S(1)}, f32[256,512]{1,0:T(8,128)S(1)}, f32[256,512]{1,0:T(8,128)S(1)}, f32[8,128]{1,0:T(8,128)S(1)}) custom-call(s32[1]{0:T(128)} %bitcast.g_ref, f32[272,640]{1,0:T(8,128)S(1)} %get-tuple-element.35.gw, f32[272,640]{1,0:T(8,128)S(1)} %get-tuple-element.36.invd, f32[272,640]{1,0:T(8,128)S(1)} %get-tuple-element.37.ra, ...), custom_call_target="tpu_custom_call" | custom-call | flops 1000000 | bytes 4000000 | tf_op jit(solution)/shard_map/ocean_basis/pallas_call | solution.py:47
  67.0 16.2 %all_to_all.5.parts = f32[32,8,128]{2,1,0:T(8,128)S(1)} all-to-all(f32[32,8,128]{2,1,0:T(8,128)S(1)} %broadcast_in_dim.2), channel_id=1, replica_groups=mesh['grp'=4,'tile'=8] {'grp','tile'}, dimensions={0} | all-to-all | bytes 262144 | tf_op jit(solution)/shard_map/all_to_all | solution.py:672
  83.2 1.1 %combine.1 = f32[256,512]{1,0:T(8,128)} custom-call(s32[1]{0:T(128)} %bitcast.g_ref, f32[32,8,128]{2,1,0:T(8,128)S(1)} %all_to_all.5.parts, f32[256,512]{1,0:T(8,128)S(1)} %copy-done.1, f32[256,512]{1,0:T(8,128)S(1)} %get-tuple-element.44.y0, f32[256,512]{1,0:T(8,128)S(1)} %get-tuple-element.45.y1, f32[256,512]{1,0:T(8,128)S(1)} %get-tuple-element.46.y2), custom_call_target="tpu_custom_call" | custom-call | flops 1000000 | bytes 4000000 | tf_op jit(solution)/shard_map/combine/pallas_call | solution.py:47
  (13 shorter events, 0.0 us)
Async XLA Ops:
  0.6 1.0 %copy-start = (f32[256,512]{1,0:T(8,128)S(1)}, f32[256,512]{1,0:T(8,128)}, u32[]{:S(2)}) copy-start(f32[256,512]{1,0:T(8,128)} %x0.5) | copy-start | bytes 1572868
  1.7 1.2 %copy-start.2 = (f32[2,256,512]{2,1,0:T(8,128)S(1)}, f32[2,256,512]{2,1,0:T(8,128)}, u32[]{:S(2)}) copy-start(f32[2,256,512]{2,1,0:T(8,128)} %cur.3) | copy-start | bytes 3145732
  2.9 1.1 %copy-start.4 = (f32[3,2,64,512]{3,2,1,0:T(8,128)S(1)}, f32[3,2,64,512]{3,2,1,0:T(8,128)}, u32[]{:S(2)}) copy-start(f32[3,2,64,512]{3,2,1,0:T(8,128)} %stress.3) | copy-start | bytes 2359300
  4.0 1.0 %copy-start.6 = (f32[256,512]{1,0:T(8,128)S(1)}, f32[256,512]{1,0:T(8,128)}, u32[]{:S(2)}) copy-start(f32[256,512]{1,0:T(8,128)} %base.3) | copy-start | bytes 1572868
  5.1 1.0 %copy-start.8 = (f32[2,2,64,512]{3,2,1,0:T(8,128)S(1)}, f32[2,2,64,512]{3,2,1,0:T(8,128)}, u32[]{:S(2)}) copy-start(f32[2,2,64,512]{3,2,1,0:T(8,128)} %vel.3) | copy-start | bytes 1572868
  6.1 1.0 %copy-start.10 = (f32[2,2,64,512]{3,2,1,0:T(8,128)S(1)}, f32[2,2,64,512]{3,2,1,0:T(8,128)}, u32[]{:S(2)}) copy-start(f32[2,2,64,512]{3,2,1,0:T(8,128)} %wind.3) | copy-start | bytes 1572868
  7.2 1.0 %copy-start.12 = (f32[256,512]{1,0:T(8,128)S(1)}, f32[256,512]{1,0:T(8,128)}, u32[]{:S(2)}) copy-start(f32[256,512]{1,0:T(8,128)} %depth.3) | copy-start | bytes 1572868
  8.2 0.9 %copy-start.14 = (f32[2,64,512]{2,1,0:T(8,128)S(1)}, f32[2,64,512]{2,1,0:T(8,128)}, u32[]{:S(2)}) copy-start(f32[2,64,512]{2,1,0:T(8,128)} %thick.3) | copy-start | bytes 786436
  9.2 0.7 copy-start.15
  9.9 0.7 copy-start.16
  10.6 11.7 %copy-start.13 = (f32[256,512]{1,0:T(8,128)S(1)}, f32[256,512]{1,0:T(8,128)}, u32[]{:S(2)}) copy-start(f32[256,512]{1,0:T(8,128)} %depth.3) | copy-start | bytes 1572868
  10.6 25.6 %copy-start.1 = (f32[256,512]{1,0:T(8,128)S(1)}, f32[256,512]{1,0:T(8,128)}, u32[]{:S(2)}) copy-start(f32[256,512]{1,0:T(8,128)} %x0.5) | copy-start | bytes 1572868
  10.6 25.6 %copy-start.3 = (f32[2,256,512]{2,1,0:T(8,128)S(1)}, f32[2,256,512]{2,1,0:T(8,128)}, u32[]{:S(2)}) copy-start(f32[2,256,512]{2,1,0:T(8,128)} %cur.3) | copy-start | bytes 3145732
  10.6 25.6 %copy-start.5 = (f32[3,2,64,512]{3,2,1,0:T(8,128)S(1)}, f32[3,2,64,512]{3,2,1,0:T(8,128)}, u32[]{:S(2)}) copy-start(f32[3,2,64,512]{3,2,1,0:T(8,128)} %stress.3) | copy-start | bytes 2359300
  10.6 25.6 %copy-start.7 = (f32[256,512]{1,0:T(8,128)S(1)}, f32[256,512]{1,0:T(8,128)}, u32[]{:S(2)}) copy-start(f32[256,512]{1,0:T(8,128)} %base.3) | copy-start | bytes 1572868
  10.6 25.6 %copy-start.9 = (f32[2,2,64,512]{3,2,1,0:T(8,128)S(1)}, f32[2,2,64,512]{3,2,1,0:T(8,128)}, u32[]{:S(2)}) copy-start(f32[2,2,64,512]{3,2,1,0:T(8,128)} %vel.3) | copy-start | bytes 1572868
  10.6 25.6 %copy-start.11 = (f32[2,2,64,512]{3,2,1,0:T(8,128)S(1)}, f32[2,2,64,512]{3,2,1,0:T(8,128)}, u32[]{:S(2)}) copy-start(f32[2,2,64,512]{3,2,1,0:T(8,128)} %wind.3) | copy-start | bytes 1572868
  12.9 10.8 %collective-permute-start = (f32[160,512]{1,0:T(8,128)S(1)}, f32[160,512]{1,0:T(8,128)S(1)}, u32[]{:S(2)}, u32[]{:S(2)}) collective-permute-start(f32[160,512]{1,0:T(8,128)S(1)} %get-tuple-element.26), channel_id=1, source_target_pairs={{0,8},{8,0},{16,24},{24,16},{1,9},{9,1},{17,25},{25,17},{2,10},{10... | collective-permute-start | bytes 983048 | tf_op jit(solution)/shard_map/ppermute | solution.py:628
  15.2 17.9 %collective-permute-start.1 = (f32[160,512]{1,0:T(8,128)S(1)}, f32[160,512]{1,0:T(8,128)S(1)}, u32[]{:S(2)}, u32[]{:S(2)}) collective-permute-start(f32[160,512]{1,0:T(8,128)S(1)} %get-tuple-element.27), channel_id=1, source_target_pairs={{0,16},{24,8},{1,17},{25,9},{2,18},{26,10},{3,19},{27,11},{4,20},{... | collective-permute-start | bytes 983048 | tf_op jit(solution)/shard_map/ppermute | solution.py:629
  19.4 13.7 %collective-permute-start.2 = (f32[160,512]{1,0:T(8,128)S(1)}, f32[160,512]{1,0:T(8,128)S(1)}, u32[]{:S(2)}, u32[]{:S(2)}) collective-permute-start(f32[160,512]{1,0:T(8,128)S(1)} %get-tuple-element.28), channel_id=1, source_target_pairs={{0,24},{24,0},{8,16},{16,8},{1,25},{25,1},{9,17},{17,9},{2,26},{26... | collective-permute-start | bytes 983048 | tf_op jit(solution)/shard_map/ppermute | solution.py:627
  19.5 16.7 %collective-permute-start.3 = (f32[160,512]{1,0:T(8,128)S(1)}, f32[160,512]{1,0:T(8,128)S(1)}, u32[]{:S(2)}, u32[]{:S(2)}) collective-permute-start(f32[160,512]{1,0:T(8,128)S(1)} %get-tuple-element.29), channel_id=1, source_target_pairs={{0,8},{24,16},{1,9},{25,17},{2,10},{26,18},{3,11},{27,19},{4,12},{... | collective-permute-start | bytes 983048 | tf_op jit(solution)/shard_map/ppermute | solution.py:630
  36.8 2.6 %collective-permute-start.4 = (f32[304,128]{1,0:T(8,128)S(1)}, f32[304,128]{1,0:T(8,128)S(1)}, u32[]{:S(2)}, u32[]{:S(2)}) collective-permute-start(f32[304,128]{1,0:T(8,128)S(1)} %get-tuple-element.33), channel_id=1, source_target_pairs={{0,1},{1,2},{2,3},{3,4},{4,5},{5,6},{6,7},{8,9},{9,10},{10,11},{11... | collective-permute-start | bytes 466952 | tf_op jit(solution)/shard_map/ppermute | solution.py:641
  38.1 5.1 %collective-permute-start.5 = (f32[304,128]{1,0:T(8,128)S(1)}, f32[304,128]{1,0:T(8,128)S(1)}, u32[]{:S(2)}, u32[]{:S(2)}) collective-permute-start(f32[304,128]{1,0:T(8,128)S(1)} %get-tuple-element.34), channel_id=1, source_target_pairs={{1,0},{2,1},{3,2},{4,3},{5,4},{6,5},{7,6},{9,8},{10,9},{11,10},{12... | collective-permute-start | bytes 466952 | tf_op jit(solution)/shard_map/ppermute | solution.py:642
  52.8 8.1 %collective-permute-start.6 = (f32[72,640]{1,0:T(8,128)S(1)}, f32[72,640]{1,0:T(8,128)S(1)}, u32[]{:S(2)}, u32[]{:S(2)}) collective-permute-start(f32[72,640]{1,0:T(8,128)S(1)} %get-tuple-element.39), channel_id=1, source_target_pairs={{8,0},{16,24},{24,8},{0,16},{9,1},{17,25},{25,9},{1,17},{10,2},{18... | collective-permute-start | bytes 552968 | tf_op jit(solution)/shard_map/ppermute | solution.py:652
  55.8 7.4 %collective-permute-start.7 = (f32[72,640]{1,0:T(8,128)S(1)}, f32[72,640]{1,0:T(8,128)S(1)}, u32[]{:S(2)}, u32[]{:S(2)}) collective-permute-start(f32[72,640]{1,0:T(8,128)S(1)} %get-tuple-element.40), channel_id=1, source_target_pairs={{16,0},{8,24},{17,1},{9,25},{18,2},{10,26},{19,3},{11,27},{20,4},{... | collective-permute-start | bytes 552968 | tf_op jit(solution)/shard_map/ppermute | solution.py:653
  57.1 8.4 %collective-permute-start.8 = (f32[72,640]{1,0:T(8,128)S(1)}, f32[72,640]{1,0:T(8,128)S(1)}, u32[]{:S(2)}, u32[]{:S(2)}) collective-permute-start(f32[72,640]{1,0:T(8,128)S(1)} %get-tuple-element.41), channel_id=1, source_target_pairs={{24,0},{0,24},{25,1},{1,25},{26,2},{2,26},{27,3},{3,27},{28,4},{4,... | collective-permute-start | bytes 552968 | tf_op jit(solution)/shard_map/ppermute | solution.py:654

commit v3 on v2

--- a/solution.py
+++ b/solution.py
@@ -23,7 +23,7 @@
 EDGE = 16
 SLOTS = LANES // EDGE
 GROUP = 4
-SKEW = 2
+SKEW = 1
 NICE = 8
 NEXT = NICE + 2
 NOC = 3
@@ -53,7 +53,7 @@
         scratch_shapes=held,
         cost_estimate=pl.CostEstimate(flops=flops, bytes_accessed=4000000, transcendentals=0),
         compiler_params=pltpu.CompilerParams(vmem_limit_bytes=mib * 1024 * 1024),
-    )(*ins)
+    )(*([ins[0]] + [pltpu.with_memory_space_constraint(x, pltpu.HBM) for x in ins[1:]] if hbm else ins))
 
 
 def tile(k):

time: 85 us -> 74.7 us (0.88)
  local copies, waits for them, and re-layouts: 9.96 us -> 0.05 us
    unnamed x34 -> x20, local copies, waits for them, and re-layouts: 9.95 us -> 0.04 us
  transfers between devices with their start and end apart: 9 -> 9, of which waited for: 6 -> 6; matrix products, arithmetic and copies ran while one was open for 0% -> 0% of each run, Pallas kernels for 1% -> 2%
where the time goes in v3:
time: 74.7 us; the launch traced here: 74.4 us
  waiting for transfers between devices  22.2 us (30%)
  starting transfers between devices  19 us (25%)
  blocking collectives  16.7 us (22%)
  Pallas kernels  15.6 us (21%)
  between operations  0.89 us (1%)
    all_to_all x1, blocking collectives, shards(): lax.all_to_all(jnp.broadcast_to(sums[None], (devices, SUB, LANES)), ('grp...  16.7 us
    pallas_call x7, Pallas kernels, call(): pl.pallas_call(body, name=name, out_shape=shapes, in_specs=specs, out_spe...  15.6 us
    ppermute x1, waiting for transfers between devices, shards(): rb = lax.ppermute(b, 'grp', [(0, 2), (3, 1)])  8.92 us
    ppermute x1, starting transfers between devices, shards(): rb = lax.ppermute(b, 'grp', [(0, 2), (3, 1)])  3.8 us
    ppermute x1, waiting for transfers between devices, shards(): lax.ppermute(left, 'tile', [(i + 1, i) for i in range(tiles - 1)])  3.77 us
    ppermute x1, waiting for transfers between devices, shards(): rd = lax.ppermute(d, 'grp', [(0, 1), (3, 2)])  3.53 us
    ppermute x1, starting transfers between devices, shards(): r3 = lax.ppermute(p3, 'grp', [(3, 0), (0, 3)])  3.22 us
    ppermute x1, starting transfers between devices, shards(): rd = lax.ppermute(d, 'grp', [(0, 1), (3, 2)])  2.73 us
  transfers between devices with their start and end apart: 9, of which 6 were waited for; matrix products, arithmetic and copies ran while one was open for 0% of the time, Pallas kernels for 2%

profile of v3, /device:TPU:0, one launch (start us, length us, event | category | flops | bytes accessed | tf_op | source)
XLA Modules:
  0.0 74.4 jit_solution(6576816906922130620)
XLA Ops:
  0.6 0.0 copy-start
  0.6 0.0 copy-start.2
  0.7 0.0 copy-start.4
  0.7 0.0 copy-start.9
  0.7 0.0 copy-start.8
  0.7 0.0 copy-start.1
  0.7 0.0 copy-start.3
  0.7 0.0 copy-start.6
  0.7 0.0 copy-start.7
  0.7 0.0 copy-start.5
  0.7 2.0 %pack_rows.1 = (f32[160,512]{1,0:T(8,128)S(1)}, f32[160,512]{1,0:T(8,128)S(1)}, f32[160,512]{1,0:T(8,128)S(1)}, f32[160,512]{1,0:T(8,128)S(1)}) custom-call(s32[1]{0:T(128)} %bitcast.g_ref, f32[256,512]{1,0:T(8,128)} %base.3, f32[256,512]{1,0:T(8,128)} %depth.3, f32[256,512]{1,0:T(8,128)} %x0.5, f32[2,256,512]{2,1,0:T(8,128)} %cur.3, s32[32,64]{1,0:T(8,128)} %land.3, ...), custom_call_target="tpu_custom_call" | custom-call | flops 1000000 | bytes 4000000 | tf_op jit(solution)/shard_map/pack_rows/pallas_call | solution.py:47
  2.8 2.7 %collective-permute-start = (f32[160,512]{1,0:T(8,128)S(1)}, f32[160,512]{1,0:T(8,128)S(1)}, u32[]{:S(2)}, u32[]{:S(2)}) collective-permute-start(f32[160,512]{1,0:T(8,128)S(1)} %get-tuple-element.26), channel_id=1, source_target_pairs={{0,8},{8,0},{16,24},{24,16},{1,9},{9,1},{17,25},{25,17},{2,10},{10... | collective-permute-start | bytes 983048 | tf_op jit(solution)/shard_map/ppermute | solution.py:628
  5.5 3.8 %collective-permute-start.1 = (f32[160,512]{1,0:T(8,128)S(1)}, f32[160,512]{1,0:T(8,128)S(1)}, u32[]{:S(2)}, u32[]{:S(2)}) collective-permute-start(f32[160,512]{1,0:T(8,128)S(1)} %get-tuple-element.27), channel_id=1, source_target_pairs={{0,16},{24,8},{1,17},{25,9},{2,18},{26,10},{3,19},{27,11},{4,20},{... | collective-permute-start | bytes 983048 | tf_op jit(solution)/shard_map/ppermute | solution.py:629
  9.3 0.1 collective-permute-start.2
  9.3 2.7 %collective-permute-start.3 = (f32[160,512]{1,0:T(8,128)S(1)}, f32[160,512]{1,0:T(8,128)S(1)}, u32[]{:S(2)}, u32[]{:S(2)}) collective-permute-start(f32[160,512]{1,0:T(8,128)S(1)} %get-tuple-element.29), channel_id=1, source_target_pairs={{0,8},{24,16},{1,9},{25,17},{2,10},{26,18},{3,11},{27,19},{4,12},{... | collective-permute-start | bytes 983048 | tf_op jit(solution)/shard_map/ppermute | solution.py:630
  12.1 0.0 copy-done.9
  12.1 0.0 copy-done.8
  12.1 0.0 copy-done.6
  12.1 0.0 copy-done.7
  12.1 0.2 masks.1
  12.3 1.7 %collective-permute-done.ra = f32[160,512]{1,0:T(8,128)S(1)} collective-permute-done((f32[160,512]{1,0:T(8,128)S(1)}, f32[160,512]{1,0:T(8,128)S(1)}, u32[]{:S(2)}, u32[]{:S(2)}) %collective-permute-start) | collective-permute-done | bytes 327712 | tf_op jit(solution)/shard_map/ppermute | solution.py:628
  14.0 8.9 %collective-permute-done.1.rb = f32[160,512]{1,0:T(8,128)S(1)} collective-permute-done((f32[160,512]{1,0:T(8,128)S(1)}, f32[160,512]{1,0:T(8,128)S(1)}, u32[]{:S(2)}, u32[]{:S(2)}) %collective-permute-start.1) | collective-permute-done | bytes 327712 | tf_op jit(solution)/shard_map/ppermute | solution.py:629
  22.9 0.0 collective-permute-done.2.rc
  22.9 3.5 %collective-permute-done.3.rd = f32[160,512]{1,0:T(8,128)S(1)} collective-permute-done((f32[160,512]{1,0:T(8,128)S(1)}, f32[160,512]{1,0:T(8,128)S(1)}, u32[]{:S(2)}, u32[]{:S(2)}) %collective-permute-start.3) | collective-permute-done | bytes 327712 | tf_op jit(solution)/shard_map/ppermute | solution.py:630
  26.5 0.0 copy-done
  26.5 0.0 copy-done.2
  26.5 0.0 copy-done.4
  26.5 0.0 copy-done.1
  26.5 0.0 copy-done.3
  26.5 0.0 copy-done.5
  26.5 0.6 pack_cols.1
  27.1 1.3 %collective-permute-start.4 = (f32[304,128]{1,0:T(8,128)S(1)}, f32[304,128]{1,0:T(8,128)S(1)}, u32[]{:S(2)}, u32[]{:S(2)}) collective-permute-start(f32[304,128]{1,0:T(8,128)S(1)} %get-tuple-element.33), channel_id=1, source_target_pairs={{0,1},{1,2},{2,3},{3,4},{4,5},{5,6},{6,7},{8,9},{9,10},{10,11},{11... | collective-permute-start | bytes 466952 | tf_op jit(solution)/shard_map/ppermute | solution.py:641
  28.4 1.3 %collective-permute-start.5 = (f32[304,128]{1,0:T(8,128)S(1)}, f32[304,128]{1,0:T(8,128)S(1)}, u32[]{:S(2)}, u32[]{:S(2)}) collective-permute-start(f32[304,128]{1,0:T(8,128)S(1)} %get-tuple-element.34), channel_id=1, source_target_pairs={{1,0},{2,1},{3,2},{4,3},{5,4},{6,5},{7,6},{9,8},{10,9},{11,10},{12... | collective-permute-start | bytes 466952 | tf_op jit(solution)/shard_map/ppermute | solution.py:642
  29.7 0.0 collective-permute-done.4.from_left
  29.7 3.8 %collective-permute-done.5.from_right = f32[304,128]{1,0:T(8,128)S(1)} collective-permute-done((f32[304,128]{1,0:T(8,128)S(1)}, f32[304,128]{1,0:T(8,128)S(1)}, u32[]{:S(2)}, u32[]{:S(2)}) %collective-permute-start.5) | collective-permute-done | bytes 155680 | tf_op jit(solution)/shard_map/ppermute | solution.py:642
  33.5 9.3 %ice_steps.1 = (f32[2,2,64,512]{3,2,1,0:T(8,128)}, f32[3,2,64,512]{3,2,1,0:T(8,128)}, f32[72,640]{1,0:T(8,128)S(1)}, f32[72,640]{1,0:T(8,128)S(1)}, f32[72,640]{1,0:T(8,128)S(1)}, /*index=5*/f32[72,640]{1,0:T(8,128)S(1)}) custom-call(s32[1]{0:T(128)} %bitcast.g_ref, f32[2,10,80,512]{3,2,1,0:T(8,128)S(1)} %get-tuple-element.38.ice, ...), custom_call_target="tpu_custom_call" | custom-call | flops 1000000 | bytes 4000000 | tf_op jit(solution)/shard_map/ice_steps/pallas_call | solution.py:47
  42.8 2.6 %collective-permute-start.6 = (f32[72,640]{1,0:T(8,128)S(1)}, f32[72,640]{1,0:T(8,128)S(1)}, u32[]{:S(2)}, u32[]{:S(2)}) collective-permute-start(f32[72,640]{1,0:T(8,128)S(1)} %get-tuple-element.39), channel_id=1, source_target_pairs={{8,0},{16,24},{24,8},{0,16},{9,1},{17,25},{25,9},{1,17},{10,2},{18... | collective-permute-start | bytes 552968 | tf_op jit(solution)/shard_map/ppermute | solution.py:652
  45.4 1.3 %collective-permute-start.7 = (f32[72,640]{1,0:T(8,128)S(1)}, f32[72,640]{1,0:T(8,128)S(1)}, u32[]{:S(2)}, u32[]{:S(2)}) collective-permute-start(f32[72,640]{1,0:T(8,128)S(1)} %get-tuple-element.40), channel_id=1, source_target_pairs={{16,0},{8,24},{17,1},{9,25},{18,2},{10,26},{19,3},{11,27},{20,4},{... | collective-permute-start | bytes 552968 | tf_op jit(solution)/shard_map/ppermute | solution.py:653
  46.7 3.2 %collective-permute-start.8 = (f32[72,640]{1,0:T(8,128)S(1)}, f32[72,640]{1,0:T(8,128)S(1)}, u32[]{:S(2)}, u32[]{:S(2)}) collective-permute-start(f32[72,640]{1,0:T(8,128)S(1)} %get-tuple-element.41), channel_id=1, source_target_pairs={{24,0},{0,24},{25,1},{1,25},{26,2},{2,26},{27,3},{3,27},{28,4},{4,... | collective-permute-start | bytes 552968 | tf_op jit(solution)/shard_map/ppermute | solution.py:654
  50.0 0.9 %ocean_before.1 = (f32[272,640]{1,0:T(8,128)S(1)}, f32[272,640]{1,0:T(8,128)S(1)}, f32[272,640]{1,0:T(8,128)S(1)}) custom-call(s32[1]{0:T(128)} %bitcast.g_ref, f32[3,272,512]{2,1,0:T(8,128)S(1)} %get-tuple-element.32.ocean, f32[304,128]{1,0:T(8,128)S(1)} %collective-permute-done.4.from_left, f32[304,128]{1,0:T(8,128)S(1)} %collective-permute-done.5.from_right), custom_call_target="tpu_custom_call" | custom-call | flops 20000000 | bytes 4000000 | tf_op jit(solution)/shard_map/ocean_before/pallas_call | solution.py:47
  50.9 0.0 collective-permute-done.6.r1
  50.9 2.0 %collective-permute-done.7.r2 = f32[72,640]{1,0:T(8,128)S(1)} collective-permute-done((f32[72,640]{1,0:T(8,128)S(1)}, f32[72,640]{1,0:T(8,128)S(1)}, u32[]{:S(2)}, u32[]{:S(2)}) %collective-permute-start.7) | collective-permute-done | bytes 184352 | tf_op jit(solution)/shard_map/ppermute | solution.py:653
  52.9 2.3 %collective-permute-done.8.r3 = f32[72,640]{1,0:T(8,128)S(1)} collective-permute-done((f32[72,640]{1,0:T(8,128)S(1)}, f32[72,640]{1,0:T(8,128)S(1)}, u32[]{:S(2)}, u32[]{:S(2)}) %collective-permute-start.8) | collective-permute-done | bytes 184352 | tf_op jit(solution)/shard_map/ppermute | solution.py:654
  55.2 1.4 %ocean_basis.1 = (f32[256,512]{1,0:T(8,128)S(1)}, f32[256,512]{1,0:T(8,128)S(1)}, f32[256,512]{1,0:T(8,128)S(1)}, f32[8,128]{1,0:T(8,128)S(1)}) custom-call(s32[1]{0:T(128)} %bitcast.g_ref, f32[272,640]{1,0:T(8,128)S(1)} %get-tuple-element.35.gw, f32[272,640]{1,0:T(8,128)S(1)} %get-tuple-element.36.invd, f32[272,640]{1,0:T(8,128)S(1)} %get-tuple-element.37.ra, ...), custom_call_target="tpu_custom_call" | custom-call | flops 1000000 | bytes 4000000 | tf_op jit(solution)/shard_map/ocean_basis/pallas_call | solution.py:47
  56.6 16.7 %all_to_all.5.parts = f32[32,8,128]{2,1,0:T(8,128)S(1)} all-to-all(f32[32,8,128]{2,1,0:T(8,128)S(1)} %broadcast_in_dim.2), channel_id=1, replica_groups=mesh['grp'=4,'tile'=8] {'grp','tile'}, dimensions={0} | all-to-all | bytes 262144 | tf_op jit(solution)/shard_map/all_to_all | solution.py:672
  73.3 1.1 %combine.1 = f32[256,512]{1,0:T(8,128)} custom-call(s32[1]{0:T(128)} %bitcast.g_ref, f32[32,8,128]{2,1,0:T(8,128)S(1)} %all_to_all.5.parts, f32[256,512]{1,0:T(8,128)S(1)} %copy-done, f32[256,512]{1,0:T(8,128)S(1)} %get-tuple-element.44.y0, f32[256,512]{1,0:T(8,128)S(1)} %get-tuple-element.45.y1, f32[256,512]{1,0:T(8,128)S(1)} %get-tuple-element.46.y2), custom_call_target="tpu_custom_call" | custom-call | flops 1000000 | bytes 4000000 | tf_op jit(solution)/shard_map/combine/pallas_call | solution.py:47
  (1 shorter events, 0.0 us)
Async XLA Ops:
  0.6 25.8 %copy-start = (f32[256,512]{1,0:T(8,128)S(1)}, f32[256,512]{1,0:T(8,128)}, u32[]{:S(2)}) copy-start(f32[256,512]{1,0:T(8,128)} %x0.5) | copy-start | bytes 1572868
  0.6 25.8 %copy-start.2 = (f32[3,2,64,512]{3,2,1,0:T(8,128)S(1)}, f32[3,2,64,512]{3,2,1,0:T(8,128)}, u32[]{:S(2)}) copy-start(f32[3,2,64,512]{3,2,1,0:T(8,128)} %stress.3) | copy-start | bytes 2359300
  0.7 25.8 %copy-start.4 = (f32[2,2,64,512]{3,2,1,0:T(8,128)S(1)}, f32[2,2,64,512]{3,2,1,0:T(8,128)}, u32[]{:S(2)}) copy-start(f32[2,2,64,512]{3,2,1,0:T(8,128)} %vel.3) | copy-start | bytes 1572868
  0.7 11.4 %copy-start.9 = (s32[2,8,64]{2,1,0:T(8,128)S(1)}, s32[2,8,64]{2,1,0:T(8,128)}, u32[]{:S(2)}) copy-start(s32[2,8,64]{2,1,0:T(8,128)} %iceb.3) | copy-start | bytes 12292
  0.7 11.4 %copy-start.8 = (s32[32,64]{1,0:T(8,128)S(1)}, s32[32,64]{1,0:T(8,128)}, u32[]{:S(2)}) copy-start(s32[32,64]{1,0:T(8,128)} %land.3) | copy-start | bytes 24580
  0.7 25.8 %copy-start.1 = (f32[2,256,512]{2,1,0:T(8,128)S(1)}, f32[2,256,512]{2,1,0:T(8,128)}, u32[]{:S(2)}) copy-start(f32[2,256,512]{2,1,0:T(8,128)} %cur.3) | copy-start | bytes 3145732
  0.7 25.8 %copy-start.3 = (f32[256,512]{1,0:T(8,128)S(1)}, f32[256,512]{1,0:T(8,128)}, u32[]{:S(2)}) copy-start(f32[256,512]{1,0:T(8,128)} %base.3) | copy-start | bytes 1572868
  0.7 11.4 %copy-start.6 = (f32[256,512]{1,0:T(8,128)S(1)}, f32[256,512]{1,0:T(8,128)}, u32[]{:S(2)}) copy-start(f32[256,512]{1,0:T(8,128)} %depth.3) | copy-start | bytes 1572868
  0.7 11.4 %copy-start.7 = (f32[2,64,512]{2,1,0:T(8,128)S(1)}, f32[2,64,512]{2,1,0:T(8,128)}, u32[]{:S(2)}) copy-start(f32[2,64,512]{2,1,0:T(8,128)} %thick.3) | copy-start | bytes 786436
  0.7 25.8 %copy-start.5 = (f32[2,2,64,512]{3,2,1,0:T(8,128)S(1)}, f32[2,2,64,512]{3,2,1,0:T(8,128)}, u32[]{:S(2)}) copy-start(f32[2,2,64,512]{3,2,1,0:T(8,128)} %wind.3) | copy-start | bytes 1572868
  2.8 11.2 %collective-permute-start = (f32[160,512]{1,0:T(8,128)S(1)}, f32[160,512]{1,0:T(8,128)S(1)}, u32[]{:S(2)}, u32[]{:S(2)}) collective-permute-start(f32[160,512]{1,0:T(8,128)S(1)} %get-tuple-element.26), channel_id=1, source_target_pairs={{0,8},{8,0},{16,24},{24,16},{1,9},{9,1},{17,25},{25,17},{2,10},{10... | collective-permute-start | bytes 983048 | tf_op jit(solution)/shard_map/ppermute | solution.py:628
  5.5 17.5 %collective-permute-start.1 = (f32[160,512]{1,0:T(8,128)S(1)}, f32[160,512]{1,0:T(8,128)S(1)}, u32[]{:S(2)}, u32[]{:S(2)}) collective-permute-start(f32[160,512]{1,0:T(8,128)S(1)} %get-tuple-element.27), channel_id=1, source_target_pairs={{0,16},{24,8},{1,17},{25,9},{2,18},{26,10},{3,19},{27,11},{4,20},{... | collective-permute-start | bytes 983048 | tf_op jit(solution)/shard_map/ppermute | solution.py:629
  9.3 13.7 %collective-permute-start.2 = (f32[160,512]{1,0:T(8,128)S(1)}, f32[160,512]{1,0:T(8,128)S(1)}, u32[]{:S(2)}, u32[]{:S(2)}) collective-permute-start(f32[160,512]{1,0:T(8,128)S(1)} %get-tuple-element.28), channel_id=1, source_target_pairs={{0,24},{24,0},{8,16},{16,8},{1,25},{25,1},{9,17},{17,9},{2,26},{26... | collective-permute-start | bytes 983048 | tf_op jit(solution)/shard_map/ppermute | solution.py:627
  9.3 17.1 %collective-permute-start.3 = (f32[160,512]{1,0:T(8,128)S(1)}, f32[160,512]{1,0:T(8,128)S(1)}, u32[]{:S(2)}, u32[]{:S(2)}) collective-permute-start(f32[160,512]{1,0:T(8,128)S(1)} %get-tuple-element.29), channel_id=1, source_target_pairs={{0,8},{24,16},{1,9},{25,17},{2,10},{26,18},{3,11},{27,19},{4,12},{... | collective-permute-start | bytes 983048 | tf_op jit(solution)/shard_map/ppermute | solution.py:630
  27.1 2.6 %collective-permute-start.4 = (f32[304,128]{1,0:T(8,128)S(1)}, f32[304,128]{1,0:T(8,128)S(1)}, u32[]{:S(2)}, u32[]{:S(2)}) collective-permute-start(f32[304,128]{1,0:T(8,128)S(1)} %get-tuple-element.33), channel_id=1, source_target_pairs={{0,1},{1,2},{2,3},{3,4},{4,5},{5,6},{6,7},{8,9},{9,10},{10,11},{11... | collective-permute-start | bytes 466952 | tf_op jit(solution)/shard_map/ppermute | solution.py:641
  28.4 5.1 %collective-permute-start.5 = (f32[304,128]{1,0:T(8,128)S(1)}, f32[304,128]{1,0:T(8,128)S(1)}, u32[]{:S(2)}, u32[]{:S(2)}) collective-permute-start(f32[304,128]{1,0:T(8,128)S(1)} %get-tuple-element.34), channel_id=1, source_target_pairs={{1,0},{2,1},{3,2},{4,3},{5,4},{6,5},{7,6},{9,8},{10,9},{11,10},{12... | collective-permute-start | bytes 466952 | tf_op jit(solution)/shard_map/ppermute | solution.py:642
  42.8 8.1 %collective-permute-start.6 = (f32[72,640]{1,0:T(8,128)S(1)}, f32[72,640]{1,0:T(8,128)S(1)}, u32[]{:S(2)}, u32[]{:S(2)}) collective-permute-start(f32[72,640]{1,0:T(8,128)S(1)} %get-tuple-element.39), channel_id=1, source_target_pairs={{8,0},{16,24},{24,8},{0,16},{9,1},{17,25},{25,9},{1,17},{10,2},{18... | collective-permute-start | bytes 552968 | tf_op jit(solution)/shard_map/ppermute | solution.py:652
  45.4 7.4 %collective-permute-start.7 = (f32[72,640]{1,0:T(8,128)S(1)}, f32[72,640]{1,0:T(8,128)S(1)}, u32[]{:S(2)}, u32[]{:S(2)}) collective-permute-start(f32[72,640]{1,0:T(8,128)S(1)} %get-tuple-element.40), channel_id=1, source_target_pairs={{16,0},{8,24},{17,1},{9,25},{18,2},{10,26},{19,3},{11,27},{20,4},{... | collective-permute-start | bytes 552968 | tf_op jit(solution)/shard_map/ppermute | solution.py:653
  46.7 8.4 %collective-permute-start.8 = (f32[72,640]{1,0:T(8,128)S(1)}, f32[72,640]{1,0:T(8,128)S(1)}, u32[]{:S(2)}, u32[]{:S(2)}) collective-permute-start(f32[72,640]{1,0:T(8,128)S(1)} %get-tuple-element.41), channel_id=1, source_target_pairs={{24,0},{0,24},{25,1},{1,25},{26,2},{2,26},{27,3},{3,27},{28,4},{4,... | collective-permute-start | bytes 552968 | tf_op jit(solution)/shard_map/ppermute | solution.py:654

commit v4 on v3

--- a/solution.py
+++ b/solution.py
@@ -1,5 +1,3 @@
-import functools
-
 import jax
 import jax.numpy as jnp
 from jax import lax
@@ -7,6 +5,7 @@
 from jax.experimental.pallas import tpu as pltpu
 from jax.sharding import PartitionSpec as P
 
+
 BS = 8
 NSUB = 8
 ITERS = 3
@@ -22,10 +21,10 @@
 LANES = 128
 EDGE = 16
 SLOTS = LANES // EDGE
+WIDE_SLOTS = LANES // (2 * EDGE)
 GROUP = 4
 SKEW = 1
 NICE = 8
-NEXT = NICE + 2
 NOC = 3
 
 
@@ -37,7 +36,7 @@
     return pl.BlockSpec(memory_space=pltpu.SMEM)
 
 
-def call(body, name, outs, ins, scratch=(), sems=0, hbm=False, mib=24, flops=1000000):
+def call(body, outs, ins, scratch=(), sems=0, hbm=False, mib=24, flops=1000000):
     shapes = tuple(jax.ShapeDtypeStruct(s, F32) for s in outs)
     other = pl.BlockSpec(memory_space=pltpu.HBM) if hbm else vmem()
     specs = [smem() if i == 0 else other for i in range(len(ins))]
@@ -46,7 +45,6 @@
         held.append(pltpu.SemaphoreType.DMA((sems,)))
     return pl.pallas_call(
         body,
-        name=name,
         out_shape=shapes,
         in_specs=specs,
         out_specs=tuple(vmem() for _ in outs),
@@ -99,11 +97,12 @@
 
 
 def pack_rows(g_ref, base, depth, x0, cur, land, thick, iceb, vel, stress, wind,
-              a, b, c, d, thick_s, depth_s, land_s, iceb_s, sems):
+              c, a, b, token, thick_s, depth_s, land_s, iceb_s, sems):
     g = g_ref[0]
     rows, cols = base.shape
     ice_rows = thick.shape[1]
     slab = ice_rows + 2 * SUB
+    token[...] = jnp.zeros((SUB, LANES), F32)
 
     def run(slabs, halos):
         copies = []
@@ -156,11 +155,11 @@
 
     @pl.when(g == 0)
     def _():
-        run([(c, 3), (a, 1), (b, 2)], [(d, True)])
+        run([(c, 3), (a, 1), (b, 2)], [])
 
     @pl.when(g == 3)
     def _():
-        run([(c, 0), (a, 2), (b, 1)], [(d, False)])
+        run([(c, 0), (a, 2), (b, 1)], [])
 
     @pl.when(g == 1)
     def _():
@@ -171,7 +170,32 @@
         run([], [(a, True), (c, False)])
 
 
-def masks(g_ref, depth, land, thick, iceb, gf, h):
+def pack_own(g_ref, token, base, depth, x0, cur, land, thick, iceb, vel, stress, wind, gf, h, left, right):
+    cols = base.shape[1]
+    lane = lane_iota()
+    slot = lane // EDGE
+    state = {"n": 0, "l": None, "r": None}
+
+    def emit(first, last):
+        n = state["n"]
+        s = n % SLOTS
+        both = jnp.where(lane < EDGE, first, last)
+        both = pltpu.roll(both, EDGE * s, 1) if s else both
+        if s == 0:
+            state["l"] = state["r"] = both
+        else:
+            state["l"] = jnp.where(slot == s, both, state["l"])
+            state["r"] = jnp.where(slot == s - 1, both, state["r"])
+        if s == SLOTS - 1:
+            k = n // SLOTS
+            left[tile(k), :] = state["l"]
+            right[tile(k), :] = state["r"]
+        state["n"] = n + 1
+
+    def emit_all(ref):
+        for k in range(ref.shape[0] // SUB):
+            emit(ref[tile(k), :LANES], ref[tile(k), cols - LANES :])
+
     wet = expanded_cols(land[...])
     for k in range(depth.shape[0] // SUB):
         gf[tile(k), :] = depth[tile(k), :] * wet[k : k + 1, :]
@@ -179,79 +203,151 @@
         cover = expanded_cols(iceb[cap])
         for k in range(thick.shape[1] // SUB):
             h[cap, tile(k), :] = thick[cap, tile(k), :] * cover[k : k + 1, :]
-
-
-def pack_cols(g_ref, ra, rb, rc, rd, cur, h, vel, stress, wind, base, gf, x0, ice, ocean, left, right):
+    for cap in range(2):
+        for ref in own_ice(h, vel, stress, wind, cap):
+            emit_all(ref)
+    for ref in (base, gf, x0):
+        emit_all(ref)
+    for comp in range(2):
+        emit_all(cur.at[comp])
+    while state["n"] % SLOTS:
+        emit(jnp.zeros((SUB, LANES), F32), jnp.zeros((SUB, LANES), F32))
+
+
+def own_ice(h, vel, stress, wind, cap):
+    fields = [h.at[cap], vel.at[0, cap], vel.at[1, cap]]
+    fields += [stress.at[i, cap] for i in range(3)]
+    return fields + [wind.at[i, cap] for i in range(2)]
+
+
+def own_count(rows, ice_rows):
+    return 2 * NICE * (ice_rows // SUB), NOC * (rows // SUB), 2 * (rows // SUB)
+
+
+def halo_tiles(rows, ice_rows, last):
+    ice_tiles, ocean_tiles = ice_rows // SUB, rows // SUB
+    picked = [n * ice_tiles + (ice_tiles - 1 if last else 0) for n in range(2 * NICE)]
+    start = 2 * NICE * ice_tiles
+    return picked + [start + i * ocean_tiles + (ocean_tiles - 1 if last else 0) for i in range(NOC)]
+
+
+def pack_narrow(g_ref, from_left, from_right, h, gf, base, x0, vel, stress, wind, outer, narrow, d):
     g = g_ref[0]
-    cols = base.shape[1]
-    slab_tiles = h.shape[1] // SUB
-    ext = slab_tiles + 2
-    rows = base.shape[0] // SUB
+    rows, cols = base.shape
+    ice_rows = h.shape[1]
     lane = lane_iota()
-    slot = lane // EDGE
-    zero = jnp.zeros((SUB, cols), F32)
-    state = {"n": 0, "l": None, "r": None}
-
-    def emit(value):
-        n = state["n"]
-        s = n % SLOTS
-        both = jnp.where(lane < EDGE, value[:, :LANES], value[:, cols - LANES :])
-        both = pltpu.roll(both, EDGE * s, 1) if s else both
-        before = (s - 1) % SLOTS
-        if s == 0:
-            state["l"] = state["r"] = both
-        else:
-            state["l"] = jnp.where(slot == s, both, state["l"])
-            state["r"] = jnp.where(slot == before, both, state["r"])
-        if s == SLOTS - 1:
-            k = n // SLOTS
-            left[tile(k), :] = state["l"]
-            right[tile(k), :] = state["r"]
-        state["n"] = n + 1
-
-    def low(k):
-        r = tile(k)
-        return jnp.where(g == 1, rd[r, :], jnp.where(g == 2, rc[r, :], jnp.where(g == 3, ra[r, :], zero)))
-
-    def high(k):
-        r = tile(k)
-        return jnp.where(g == 0, ra[r, :], jnp.where(g == 1, rc[r, :], jnp.where(g == 2, rd[r, :], zero)))
-
-    for cap in range(2):
-        own = [h.at[cap], vel.at[0, cap], vel.at[1, cap], stress.at[0, cap], stress.at[1, cap],
-               stress.at[2, cap], wind.at[0, cap], wind.at[1, cap]]
-        for f in range(NICE):
-            for j in range(ext):
-                if j == 0:
-                    value = low(cap * NICE + f)
-                elif j == ext - 1:
-                    value = high(cap * NICE + f)
-                else:
-                    value = own[f][tile(j - 1), :]
-                ice[cap, f, tile(j), :] = value
-                emit(value)
+    count = sum(own_count(rows, ice_rows))
+    batch = 32
+    for n in range(0, count, batch):
+        made = [outer_columns(from_left, from_right, i, lane) for i in range(n, min(n + batch, count))]
+        for i, value in enumerate(made):
+            outer[tile(n + i), :] = value
+    packed = narrow.shape[1] // SUB
+
+    def pack(put, tiles):
+        for k in range(packed):
+            value = None
+            for i in range(WIDE_SLOTS):
+                n = k * WIDE_SLOTS + i
+                if n < len(tiles):
+                    one = tiles[n]()
+                    one = pltpu.roll(one, i * 2 * EDGE, 1) if i else one
+                    value = one if value is None else value + one
+            put(k, jnp.zeros((SUB, LANES), F32) if value is None else value)
+
+    def picked(n):
+        return lambda: outer[tile(n), :]
+
+    def slab(dest):
+        start = sum(own_count(rows, ice_rows)[:2])
+        per = rows // SUB
+        tiles = []
         for comp in range(2):
-            for j in range(ext):
-                r = tile(comp * ext + j)
-                mine = own_tile(cur, comp, slab_tiles * g - 1, j)
-                if cap == 0:
-                    value = jnp.where(g == 0, mine, jnp.where(g == 1, ra[r, :], jnp.where(g == 2, rb[r, :], rc[r, :])))
-                else:
-                    value = jnp.where(g == 3, mine, jnp.where(g == 2, ra[r, :], jnp.where(g == 1, rb[r, :], rc[r, :])))
-                ice[cap, NICE + comp, tile(j), :] = value
-                emit(value)
-    for i, field in enumerate((base, gf, x0)):
-        for j in range(rows + 2):
-            if j == 0:
-                value = low(2 * NICE + i)
-            elif j == rows + 1:
-                value = high(2 * NICE + i)
-            else:
-                value = field[tile(j - 1), :]
-            ocean[i, tile(j), :] = value
-            emit(value)
-    while state["n"] % SLOTS:
-        emit(zero)
+            for j in range(ice_rows // SUB + 2):
+                t = ice_rows // SUB * dest - 1 + j
+                inside = 0 <= t < per
+                tiles.append(picked(start + comp * per + t) if inside else lambda: jnp.zeros((SUB, LANES), F32))
+        return tiles
+
+    def halo(last):
+        return [picked(n) for n in halo_tiles(rows, ice_rows, last)]
+
+    def send(dest, tiles):
+        def put(k, value):
+            narrow[dest, tile(k), :] = value
+
+        pack(put, tiles)
+
+    def strip(last):
+        r = slice(ice_rows - SUB, ice_rows) if last else slice(0, SUB)
+        ro = slice(rows - SUB, rows) if last else slice(0, SUB)
+        n = 0
+        for cap in range(2):
+            for ref in own_ice(h, vel, stress, wind, cap):
+                d[tile(n), :] = ref[r, :]
+                n += 1
+        for ref in (base, gf, x0):
+            d[tile(n), :] = ref[ro, :]
+            n += 1
+        per = cols // LANES
+
+        def put(k, value):
+            c = k % per
+            d[tile(n + k // per), c * LANES : (c + 1) * LANES] = value
+
+        pack(put, halo(last))
+
+    @pl.when(g == 0)
+    def _():
+        send(0, [])
+        send(1, slab(1))
+        send(2, slab(2))
+        send(3, slab(3))
+        strip(True)
+
+    @pl.when(g == 1)
+    def _():
+        send(0, halo(False))
+        send(1, [])
+        send(2, halo(True))
+        send(3, [])
+
+    @pl.when(g == 2)
+    def _():
+        send(0, [])
+        send(1, halo(False))
+        send(2, [])
+        send(3, halo(True))
+
+    @pl.when(g == 3)
+    def _():
+        send(0, slab(0))
+        send(1, slab(1))
+        send(2, slab(2))
+        send(3, [])
+        strip(False)
+
+
+def wide_outer(value, i, lane):
+    value = pltpu.roll(value, LANES - 2 * EDGE * i, 1) if i else value
+    return jnp.where((lane < EDGE) | (lane >= LANES - EDGE), value, 0.0)
+
+
+def low_high(g, ra, rc, rd, nx, n, lane, low):
+    cols = ra.shape[1]
+    inner_zero = jnp.zeros((SUB, cols), F32)
+    k, i = n // WIDE_SLOTS, n % WIDE_SLOTS
+    per = cols // LANES
+    first = 2 * NICE + NOC
+    tail = rd[tile(first + k // per), (k % per) * LANES : (k % per + 1) * LANES]
+    t = tile(n)
+    if low:
+        inner = jnp.where(g == 1, rd[t, :], jnp.where(g == 2, rc[t, :], jnp.where(g == 3, ra[t, :], inner_zero)))
+        packed = jnp.where(g == 1, tail, jnp.where(g == 2, nx[1, tile(k), :], jnp.where(g == 3, nx[2, tile(k), :], 0.0)))
+    else:
+        inner = jnp.where(g == 2, rd[t, :], jnp.where(g == 1, rc[t, :], jnp.where(g == 0, ra[t, :], inner_zero)))
+        packed = jnp.where(g == 2, tail, jnp.where(g == 1, nx[2, tile(k), :], jnp.where(g == 0, nx[1, tile(k), :], 0.0)))
+    return split(inner) + [wide_outer(packed, i, lane)]
 
 
 def outer_columns(from_left, from_right, n, lane):
@@ -275,33 +371,58 @@
     return [pltpu.roll(jnp.where(lane == LANES - 1, regs[c - 1], regs[c]), 1, 1) for c in range(n)]
 
 
-def ice_steps(g_ref, ice, from_left, from_right, vel_out, stress_out, p1, p2, p3, mine,
+def ice_steps(g_ref, ra, rb, rc, rd, nx, outer, h, vel, stress, wind, cur,
+              vel_out, stress_out, p3, p2, p1, mine,
               u_s, v_s, p_s, q_s, s_s, un_s, vn_s, qp_s, sp_s, a_s, m_s, w_s, fx_s, fy_s, f0_s, f1_s):
     g = g_ref[0]
-    cols = ice.shape[3]
+    ice_rows, cols = h.shape[1:]
+    rows = cur.shape[1]
     regs = cols // LANES + 1
-    ext = ice.shape[2] // SUB
+    per = ice_rows // SUB
+    ext = per + 2
     lane = lane_iota()
     zero = jnp.zeros((SUB, LANES), F32)
     keep = 1.0 / (1.0 + RELAX)
+    flow_first = sum(own_count(rows, ice_rows)[:2])
 
     def at(j, shift=0):
         return slice(SUB * (j + 1) + shift, SUB * (j + 2) + shift)
 
+    def flow(cap, comp, j):
+        n = comp * ext + j
+        t = tile(n)
+        k, i = n // WIDE_SLOTS, n % WIDE_SLOTS
+        here = jnp.clip(per * g - 1 + j, 0, rows // SUB - 1)
+        own = own_tile(cur, comp, per * g - 1, j)
+        spot = pl.multiple_of((flow_first + comp * (rows // SUB) + here) * SUB, SUB)
+        own_outer = outer[pl.ds(spot, SUB), :]
+        if cap == 0:
+            inner = jnp.where(g == 0, own, jnp.where(g == 1, ra[t, :], jnp.where(g == 2, rb[t, :], rc[t, :])))
+            edge = jnp.where(g == 0, own_outer, wide_outer(nx[0, tile(k), :], i, lane))
+        else:
+            inner = jnp.where(g == 3, own, jnp.where(g == 2, ra[t, :], jnp.where(g == 1, rb[t, :], rc[t, :])))
+            edge = jnp.where(g == 3, own_outer, wide_outer(nx[3, tile(k), :], i, lane))
+        return split(inner) + [edge]
+
     for cap in range(2):
+        own = own_ice(h, vel, stress, wind, cap)
         for c in range(regs):
             for ref in (p_s, s_s):
                 ref[cap, c, at(-1), :] = zero
             for ref in (u_s, v_s):
                 ref[cap, c, at(ext), :] = zero
-        outers = []
+        flows = []
         for j in range(ext):
             if j % GROUP == 0:
-                outers = [
-                    [outer_columns(from_left, from_right, (cap * NEXT + f) * ext + i, lane) for f in range(NEXT)]
-                    for i in range(j, min(j + GROUP, ext))
+                flows = [[flow(cap, comp, i) for comp in range(2)] for i in range(j, min(j + GROUP, ext))]
+            if j == 0 or j == ext - 1:
+                fields = [low_high(g, ra, rc, rd, nx, cap * NICE + f, lane, j == 0) for f in range(NICE)]
+            else:
+                fields = [
+                    split(own[f][tile(j - 1), :]) + [outer[tile((cap * NICE + f) * per + j - 1), :]]
+                    for f in range(NICE)
                 ]
-            fields = [split(ice[cap, f, tile(j), :]) + [outers[j % GROUP][f]] for f in range(NEXT)]
+            fields = fields + flows[j % GROUP]
             for c in range(regs):
                 hh, u, v, s0, s1, s2, w0, w1, f0, f1 = (f[c] for f in fields)
                 u_s[cap, c, at(j), :] = u
@@ -406,13 +527,28 @@
                 (q_s[cap, c, at(j), :] - q_s[cap, c, at(j, -1), :]) + across[j][c] for c in range(regs)
             ])
         spreads.append(parts)
-    for k, (norths, souths) in enumerate(zip(*spreads)):
-        for c, (north, south) in enumerate(zip(norths, souths)):
-            block = (tile(k), slice(c * LANES, (c + 1) * LANES))
-            p1[block] = jnp.where((g == 1) | (g == 3), north, south)
-            p2[block] = jnp.where(g == 2, north, south)
-            p3[block] = jnp.where(g == 3, north, south)
-            mine[block] = jnp.where(g == 0, north, south)
+    bands = per + 1
+    packs = [[None] * -(-bands // WIDE_SLOTS) for _ in range(2)]
+    for cap in range(2):
+        for k in range(bands):
+            i = k % WIDE_SLOTS
+            edge = jnp.where((lane < EDGE) | (lane >= LANES - EDGE), spreads[cap][k][regs - 1], 0.0)
+            edge = pltpu.roll(edge, 2 * EDGE * i, 1) if i else edge
+            held = packs[cap][k // WIDE_SLOTS]
+            packs[cap][k // WIDE_SLOTS] = edge if held is None else held + edge
+
+    def put(block, north, south):
+        p3[block] = jnp.where(g == 3, north, south)
+        p2[block] = jnp.where(g == 2, north, south)
+        p1[block] = jnp.where((g == 1) | (g == 3), north, south)
+        mine[block] = jnp.where(g == 0, north, south)
+
+    for k in range(bands):
+        for c in range(regs - 1):
+            put((tile(k), slice(c * LANES, (c + 1) * LANES)), spreads[0][k][c], spreads[1][k][c])
+    for c in range(regs - 1):
+        pair = [pack[c] if c < len(pack) else zero for pack in packs]
+        put((tile(bands), slice(c * LANES, (c + 1) * LANES)), *pair)
 
 
 def neighbour_sum(ref, k, row):
@@ -421,26 +557,32 @@
     return along + (from_prev_col(here) + from_next_col(here))
 
 
-def ocean_before(first, g_ref, ocean, from_left, from_right, gw, invd, ra, g_s, gx_s, x_s, b_s):
-    cols = ocean.shape[2]
+def ocean_before(g_ref, ra, rc, rd, nx, outer, base, gf, x0, gw, invd, ra_out, g_s, gx_s, x_s, b_s):
+    g = g_ref[0]
+    rows, cols = base.shape
     wide = cols + LANES
-    ext = ocean.shape[1] // SUB
+    per = rows // SUB
+    ext = per + 2
     lane = lane_iota()
     row = row_iota(wide)
     zero = jnp.zeros((SUB, wide), F32)
+    ocean_first = (outer.shape[0] // SUB - 2 * per) - NOC * per
     for ref in (g_s, gx_s):
         ref[tile(0), :] = zero
         ref[tile(ext + 1), :] = zero
     for j in range(ext):
         t = tile(j + 1)
 
-        def field(i):
-            outer = outer_columns(from_left, from_right, first + i * ext + j, lane)
-            return jnp.concatenate([ocean[i, tile(j), :], outer], axis=1)
-
-        b_s[tile(j), :] = field(0)
-        depth = field(1)
-        x = field(2)
+        def field(i, ref):
+            if j == 0 or j == ext - 1:
+                parts = low_high(g, ra, rc, rd, nx, 2 * NICE + i, lane, j == 0)
+            else:
+                parts = [ref[tile(j - 1), :], outer[tile(ocean_first + i * per + j - 1), :]]
+            return jnp.concatenate(parts, axis=1)
+
+        b_s[tile(j), :] = field(0, base)
+        depth = field(1, gf)
+        x = field(2, x0)
         g_s[t, :] = depth
         gx_s[t, :] = depth * x
         x_s[tile(j), :] = x
@@ -451,7 +593,7 @@
         diag = DAMP + depth * neighbour_sum(g_s, j + 1, row)
         invd[t, :] = 1.0 / diag
         around = depth * neighbour_sum(gx_s, j + 1, row)
-        ra[t, :] = jnp.where(depth > 0.0, b_s[t, :], 0.0) - (diag * x_s[t, :] - around)
+        ra_out[t, :] = jnp.where(depth > 0.0, b_s[t, :], 0.0) - (diag * x_s[t, :] - around)
 
 
 def ocean_basis(g_ref, gw, invd, ra, r1, r2, r3, mine, y0_out, y1_out, y2_out, sums,
@@ -460,9 +602,16 @@
     wide = gw.shape[1]
     ext = gw.shape[0] // SUB
     cols = y0_out.shape[1]
-    slab = r1.shape[0] // SUB - 1
+    slab = r1.shape[0] // SUB - 2
+    lane = lane_iota()
     row = row_iota(wide)
     zero = jnp.zeros((SUB, wide), F32)
+
+    def strip(ref, k):
+        n, i = k // WIDE_SLOTS, k % WIDE_SLOTS
+        edge = wide_outer(ref[tile(slab + 1), n * LANES : (n + 1) * LANES], i, lane)
+        return jnp.concatenate([ref[tile(k), :], edge], axis=1)
+
     for ref in (u0_s, u1_s, u2_s):
         ref[tile(0), :] = zero
         ref[tile(ext + 1), :] = zero
@@ -473,13 +622,14 @@
 
     def whole(slabs):
         clear([0])
+        over = None
         for k, ref in enumerate(slabs):
+            values = [strip(ref, t) for t in range(slab + 1)]
             for t in range(slab):
-                value = ref[tile(t), :]
-                if t == 0 and k > 0:
-                    value = value + slabs[k - 1][tile(slab), :]
+                value = values[t] if t or over is None else values[t] + over
                 sp[tile(1 + slab * k + t), :] = value
-        sp[tile(1 + slab * len(slabs)), :] = slabs[-1][tile(slab), :]
+            over = values[slab]
+        sp[tile(1 + slab * len(slabs)), :] = over
 
     @pl.when(g == 0)
     def _():
@@ -492,13 +642,13 @@
     @pl.when(g == 1)
     def _():
         clear(range(2, ext))
-        sp[tile(0), :] = r1[tile(slab - 1), :]
-        sp[tile(1), :] = r1[tile(slab), :]
+        sp[tile(0), :] = strip(r1, slab - 1)
+        sp[tile(1), :] = strip(r1, slab)
 
     @pl.when(g == 2)
     def _():
         clear(range(ext - 1))
-        sp[tile(ext - 1), :] = r1[tile(0), :]
+        sp[tile(ext - 1), :] = strip(r1, 0)
 
     acc = [jnp.zeros((SUB, cols), F32) for _ in range(6)]
 
@@ -607,9 +757,9 @@
     wide = cols + LANES
 
     strip = (2 * slab, cols)
-    a, b, c, d = call(
-        pack_rows, "pack_rows",
-        [strip] * 4,
+    c, a, b, token = call(
+        pack_rows,
+        [strip] * 3 + [(SUB, LANES)],
         [g, base_rhs, depth, ssh_prev, currents, land_blocks, ice_thick, ice_blocks, ice_vel, ice_stress, wind],
         scratch=[
             (2, 2, SUB, cols), (2, SUB, cols),
@@ -618,52 +768,55 @@
         sems=48,
         hbm=True,
     )
-    gf, h = call(
-        masks, "masks",
-        [(rows, cols), (2, ice_rows, cols)],
-        [g, depth, land_blocks, ice_thick, ice_blocks],
-        flops=10000000,
-    )
     rc = lax.ppermute(c, "grp", [(0, 3), (3, 0), (1, 2), (2, 1)])
     ra = lax.ppermute(a, "grp", [(0, 1), (1, 0), (2, 3), (3, 2)])
     rb = lax.ppermute(b, "grp", [(0, 2), (3, 1)])
-    rd = lax.ppermute(d, "grp", [(0, 1), (3, 2)])
-
-    ice_tiles = 2 * NEXT * (slab // SUB)
-    ocean_rows = rows + 2 * SUB
-    count = ice_tiles + NOC * (ocean_rows // SUB)
-    packed = (-(-count // SLOTS) * SUB, LANES)
-    ice, ocean, left, right = call(
-        pack_cols, "pack_cols",
-        [(2, NEXT, slab, cols), (NOC, ocean_rows, cols), packed, packed],
-        [g, ra, rb, rc, rd, currents, h, ice_vel, ice_stress, wind, base_rhs, gf, ssh_prev],
+
+    own = sum(own_count(rows, ice_rows))
+    packed = (-(-own // SLOTS) * SUB, LANES)
+    gf, h, left, right = call(
+        pack_own,
+        [(rows, cols), (2, ice_rows, cols), packed, packed],
+        [g, token, base_rhs, depth, ssh_prev, currents, land_blocks, ice_thick, ice_blocks, ice_vel, ice_stress,
+         wind],
     )
     from_left = lax.ppermute(right, "tile", [(i, i + 1) for i in range(tiles - 1)])
     from_right = lax.ppermute(left, "tile", [(i + 1, i) for i in range(tiles - 1)])
-
-    back = (ice_rows + SUB, wide)
-    velocity, stress, p1, p2, p3, mine = call(
-        ice_steps, "ice_steps",
+    strip_tiles = 2 * (slab // SUB)
+    narrow_rows = -(-strip_tiles // WIDE_SLOTS) * SUB
+    tail = -(-narrow_rows * LANES // (SUB * cols)) * SUB
+    outer, narrow, d = call(
+        pack_narrow,
+        [(own * SUB, LANES), (groups, narrow_rows, LANES), ((2 * NICE + NOC) * SUB + tail, cols)],
+        [g, from_left, from_right, h, gf, base_rhs, ssh_prev, ice_vel, ice_stress, wind],
+    )
+    rd = lax.ppermute(d, "grp", [(0, 1), (3, 2)])
+    nx = lax.all_to_all(narrow, "grp", 0, 0, tiled=True)
+
+    back = (ice_rows + 2 * SUB, cols)
+    velocity, stress, p3, p2, p1, mine = call(
+        ice_steps,
         [ice_vel.shape, ice_stress.shape, back, back, back, back],
-        [g, ice, from_left, from_right],
+        [g, ra, rb, rc, rd, nx, outer, h, ice_vel, ice_stress, wind, currents],
         scratch=[(2, cols // LANES + 1, slab + 2 * SUB, LANES)] * 16,
         mib=32,
     )
+    r3 = lax.ppermute(p3, "grp", [(3, 0), (0, 3)])
+    r2 = lax.ppermute(p2, "grp", [(2, 0), (1, 3)])
     r1 = lax.ppermute(p1, "grp", [(1, 0), (2, 3), (3, 1), (0, 2)])
-    r2 = lax.ppermute(p2, "grp", [(2, 0), (1, 3)])
-    r3 = lax.ppermute(p3, "grp", [(3, 0), (0, 3)])
-
+
+    ocean_rows = rows + 2 * SUB
     field = (ocean_rows, wide)
     padded = (ocean_rows + 2 * SUB, wide)
     gw, invd, known = call(
-        functools.partial(ocean_before, ice_tiles), "ocean_before",
+        ocean_before,
         [field] * 3,
-        [g, ocean, from_left, from_right],
+        [g, ra, rc, rd, nx, outer, base_rhs, gf, ssh_prev],
         scratch=[padded, padded, field, field],
         flops=20000000,
     )
     y0, y1, y2, sums = call(
-        ocean_basis, "ocean_basis",
+        ocean_basis,
         [(rows, cols)] * 3 + [(SUB, LANES)],
         [g, gw, invd, known, r1, r2, r3, mine],
         scratch=[field, padded, padded, padded],
@@ -672,7 +825,7 @@
     shared = lax.all_to_all(
         jnp.broadcast_to(sums[None], (devices, SUB, LANES)), ("grp", "tile"), 0, 0, tiled=True
     )
-    (ssh,) = call(combine, "combine", [(rows, cols)], [g, shared, ssh_prev, y0, y1, y2])
+    (ssh,) = call(combine, [(rows, cols)], [g, shared, ssh_prev, y0, y1, y2])
     return ssh, velocity, stress
 
 

time: 74.7 us -> 77.9 us (1.043)
  blocking collectives: 16.7 us -> 33.8 us
  waiting for transfers between devices: 22.2 us -> 9.08 us
  starting transfers between devices: 19 us -> 17.5 us
    all_to_all x0 -> x1, blocking collectives: none -> 16.6 us  [shards(): nx = lax.all_to_all(narrow, 'grp', 0, 0, tiled=True)]
    ppermute x1, waiting for transfers between devices: 8.92 us -> 0.01 us  [shards(): rb = lax.ppermute(b, 'grp', [(0, 2), (3, 1)])]
    ppermute x1, waiting for transfers between devices: 3.53 us -> 0.01 us  [shards(): rd = lax.ppermute(d, 'grp', [(0, 1), (3, 2)])]
    ppermute x1, starting transfers between devices: 2.67 us -> 0.07 us  [shards(): ra = lax.ppermute(a, 'grp', [(0, 1), (1, 0), (2, 3), (3, 2)])]
    ppermute x1, waiting for transfers between devices: 1.68 us -> 0.01 us  [shards(): ra = lax.ppermute(a, 'grp', [(0, 1), (1, 0), (2, 3), (3, 2)])]
    ppermute x1, starting transfers between devices: 2.64 us -> 1 us  [shards(): r1 = lax.ppermute(p1, 'grp', [(1, 0), (2, 3), (3, 1), (0, 2)])]
    ppermute x1, starting transfers between devices: 0.07 us -> 1.55 us  [shards(): rc = lax.ppermute(c, 'grp', [(0, 3), (3, 0), (1, 2), (2, 1)])]
    ppermute x1, starting transfers between devices: 1.3 us -> 2.41 us  [shards(): lax.ppermute(right, 'tile', [(i, i + 1) for i in range(tiles - 1)])]
  transfers between devices with their start and end apart: 9 -> 9, of which waited for: 6 -> 3; matrix products, arithmetic and copies ran while one was open for 0% -> 0% of each run, Pallas kernels for 2% -> 1%
where the time goes in v4:
time: 77.9 us; the launch traced here: 77.6 us
  blocking collectives  33.8 us (43%)
  starting transfers between devices  17.5 us (22%)
  Pallas kernels  15.5 us (20%)
  waiting for transfers between devices  9.08 us (12%)
  between operations  0.87 us (1%)
    all_to_all x1, blocking collectives, shards(): lax.all_to_all(jnp.broadcast_to(sums[None], (devices, SUB, LANES)), ('grp...  17.2 us
    all_to_all x1, blocking collectives, shards(): nx = lax.all_to_all(narrow, 'grp', 0, 0, tiled=True)  16.6 us
    pallas_call x7, Pallas kernels, call(): pl.pallas_call(body, out_shape=shapes, in_specs=specs, out_specs=tuple((v...  15.5 us
    ppermute x1, waiting for transfers between devices, shards(): lax.ppermute(left, 'tile', [(i + 1, i) for i in range(tiles - 1)])  4.13 us
    ppermute x1, starting transfers between devices, shards(): rb = lax.ppermute(b, 'grp', [(0, 2), (3, 1)])  3.84 us
    ppermute x1, starting transfers between devices, shards(): rd = lax.ppermute(d, 'grp', [(0, 1), (3, 2)])  3.19 us
    ppermute x1, starting transfers between devices, shards(): r3 = lax.ppermute(p3, 'grp', [(3, 0), (0, 3)])  2.92 us
    ppermute x1, waiting for transfers between devices, shards(): r2 = lax.ppermute(p2, 'grp', [(2, 0), (1, 3)])  2.61 us
  transfers between devices with their start and end apart: 9, of which 3 were waited for; matrix products, arithmetic and copies ran while one was open for 0% of the time, Pallas kernels for 1%

profile of v4, /device:TPU:0, one launch (start us, length us, event | category | flops | bytes accessed | tf_op | source)
XLA Modules:
  0.0 77.6 jit_solution(2177039110456086254)
XLA Ops:
  0.6 0.0 copy-start
  0.6 0.0 copy-start.1
  0.7 0.0 copy-start.2
  0.7 0.0 copy-start.3
  0.7 0.0 copy-start.4
  0.7 0.0 copy-start.5
  0.7 0.0 copy-start.6
  0.7 0.0 copy-start.7
  0.7 0.0 copy-start.8
  0.7 0.0 copy-start.9
  0.7 1.8 %shard_map.121 = (f32[160,512]{1,0:T(8,128)S(1)}, f32[160,512]{1,0:T(8,128)S(1)}, f32[160,512]{1,0:T(8,128)S(1)}, f32[8,128]{1,0:T(8,128)S(1)}) custom-call(s32[1]{0:T(128)} %bitcast.g_ref, f32[256,512]{1,0:T(8,128)} %base.7, f32[256,512]{1,0:T(8,128)} %depth.3, f32[256,512]{1,0:T(8,128)} %x0.9, f32[2,256,512]{2,1,0:T(8,128)} %cur.5, s32[32,64]{1,0:T(8,128)} %land.3, ...), custom_call_target="tpu_custom_call" | custom-call | flops 1000000 | bytes 4000000 | tf_op jit(solution)/shard_map/pallas_call | solution.py:46
  2.6 0.0 copy-done
  2.6 0.0 copy-done.1
  2.6 0.1 copy-done.2
  2.7 0.1 copy-done.3
  2.8 0.2 copy-done.4
  3.0 0.2 copy-done.5
  3.1 0.2 copy-done.6
  3.3 0.1 copy-done.7
  3.3 0.0 copy-done.8
  3.3 0.0 copy-done.9
  3.3 0.4 shard_map.122
  3.8 2.4 %collective-permute-start.2 = (f32[288,128]{1,0:T(8,128)S(1)}, f32[288,128]{1,0:T(8,128)S(1)}, u32[]{:S(2)}, u32[]{:S(2)}) collective-permute-start(f32[288,128]{1,0:T(8,128)S(1)} %get-tuple-element.30), channel_id=1, source_target_pairs={{0,1},{1,2},{2,3},{3,4},{4,5},{5,6},{6,7},{8,9},{9,10},{10,11},{11... | collective-permute-start | bytes 442376 | tf_op jit(solution)/shard_map/ppermute | solution.py:783
  6.2 1.3 %collective-permute-start.3 = (f32[288,128]{1,0:T(8,128)S(1)}, f32[288,128]{1,0:T(8,128)S(1)}, u32[]{:S(2)}, u32[]{:S(2)}) collective-permute-start(f32[288,128]{1,0:T(8,128)S(1)} %get-tuple-element.31), channel_id=1, source_target_pairs={{1,0},{2,1},{3,2},{4,3},{5,4},{6,5},{7,6},{9,8},{10,9},{11,10},{12... | collective-permute-start | bytes 442376 | tf_op jit(solution)/shard_map/ppermute | solution.py:784
  7.5 0.0 collective-permute-done.2.from_left
  7.5 4.1 %collective-permute-done.3.from_right = f32[288,128]{1,0:T(8,128)S(1)} collective-permute-done((f32[288,128]{1,0:T(8,128)S(1)}, f32[288,128]{1,0:T(8,128)S(1)}, u32[]{:S(2)}, u32[]{:S(2)}) %collective-permute-start.3) | collective-permute-done | bytes 147488 | tf_op jit(solution)/shard_map/ppermute | solution.py:784
  11.6 0.5 shard_map.123
  12.1 3.2 %collective-permute-start.4 = (f32[168,512]{1,0:T(8,128)S(1)}, f32[168,512]{1,0:T(8,128)S(1)}, u32[]{:S(2)}, u32[]{:S(2)}) collective-permute-start(f32[168,512]{1,0:T(8,128)S(1)} %get-tuple-element.34), channel_id=1, source_target_pairs={{0,8},{24,16},{1,9},{25,17},{2,10},{26,18},{3,11},{27,19},{4,12},{... | collective-permute-start | bytes 1032200 | tf_op jit(solution)/shard_map/ppermute | solution.py:793
  15.3 0.1 collective-permute-start
  15.4 1.6 %collective-permute-start.1 = (f32[160,512]{1,0:T(8,128)S(1)}, f32[160,512]{1,0:T(8,128)S(1)}, u32[]{:S(2)}, u32[]{:S(2)}) collective-permute-start(f32[160,512]{1,0:T(8,128)S(1)} %get-tuple-element.28), channel_id=1, source_target_pairs={{0,24},{24,0},{8,16},{16,8},{1,25},{25,1},{9,17},{17,9},{2,26},{26... | collective-permute-start | bytes 983048 | tf_op jit(solution)/shard_map/ppermute | solution.py:771
  16.9 3.8 %collective-permute-start.5 = (f32[160,512]{1,0:T(8,128)S(1)}, f32[160,512]{1,0:T(8,128)S(1)}, u32[]{:S(2)}, u32[]{:S(2)}) collective-permute-start(f32[160,512]{1,0:T(8,128)S(1)} %get-tuple-element.40), channel_id=1, source_target_pairs={{0,16},{24,8},{1,17},{25,9},{2,18},{26,10},{3,19},{27,11},{4,20},{... | collective-permute-start | bytes 983048 | tf_op jit(solution)/shard_map/ppermute | solution.py:773
  20.8 16.6 %all_to_all.10.nx = f32[4,40,128]{2,1,0:T(8,128)S(1)} all-to-all(f32[4,40,128]{2,1,0:T(8,128)S(1)} %get-tuple-element.35), channel_id=1, replica_groups=mesh['grp'=4,'tile'=8] {'grp'}, dimensions={0} | all-to-all | bytes 163840 | tf_op jit(solution)/shard_map/all_to_all | solution.py:794
  37.4 0.0 collective-permute-done.ra
  37.4 0.0 collective-permute-done.1.rc
  37.4 0.0 collective-permute-done.5.rb
  37.4 0.0 collective-permute-done.4.rd
  37.4 9.4 %shard_map.125 = (f32[2,2,64,512]{3,2,1,0:T(8,128)}, f32[3,2,64,512]{3,2,1,0:T(8,128)}, f32[80,512]{1,0:T(8,128)S(1)}, f32[80,512]{1,0:T(8,128)S(1)}, f32[80,512]{1,0:T(8,128)S(1)}, /*index=5*/f32[80,512]{1,0:T(8,128)S(1)}) custom-call(s32[1]{0:T(128)} %bitcast.g_ref, f32[160,512]{1,0:T(8,128)S(1)} %collective-permute-done.ra, ...), custom_call_target="tpu_custom_call" | custom-call | flops 1000000 | bytes 4000000 | tf_op jit(solution)/shard_map/pallas_call | solution.py:46
  46.8 1.0 %collective-permute-start.6 = (f32[80,512]{1,0:T(8,128)S(1)}, f32[80,512]{1,0:T(8,128)S(1)}, u32[]{:S(2)}, u32[]{:S(2)}) collective-permute-start(f32[80,512]{1,0:T(8,128)S(1)} %get-tuple-element.41), channel_id=1, source_target_pairs={{8,0},{16,24},{24,8},{0,16},{9,1},{17,25},{25,9},{1,17},{10,2},{18... | collective-permute-start | bytes 491528 | tf_op jit(solution)/shard_map/ppermute | solution.py:806
  47.8 1.3 %collective-permute-start.7 = (f32[80,512]{1,0:T(8,128)S(1)}, f32[80,512]{1,0:T(8,128)S(1)}, u32[]{:S(2)}, u32[]{:S(2)}) collective-permute-start(f32[80,512]{1,0:T(8,128)S(1)} %get-tuple-element.42), channel_id=1, source_target_pairs={{16,0},{8,24},{17,1},{9,25},{18,2},{10,26},{19,3},{11,27},{20,4},{... | collective-permute-start | bytes 491528 | tf_op jit(solution)/shard_map/ppermute | solution.py:805
  49.1 2.9 %collective-permute-start.8 = (f32[80,512]{1,0:T(8,128)S(1)}, f32[80,512]{1,0:T(8,128)S(1)}, u32[]{:S(2)}, u32[]{:S(2)}) collective-permute-start(f32[80,512]{1,0:T(8,128)S(1)} %get-tuple-element.43), channel_id=1, source_target_pairs={{24,0},{0,24},{25,1},{1,25},{26,2},{2,26},{27,3},{3,27},{28,4},{4,... | collective-permute-start | bytes 491528 | tf_op jit(solution)/shard_map/ppermute | solution.py:804
  52.1 0.8 %shard_map.124 = (f32[272,640]{1,0:T(8,128)S(1)}, f32[272,640]{1,0:T(8,128)S(1)}, f32[272,640]{1,0:T(8,128)S(1)}) custom-call(s32[1]{0:T(128)} %bitcast.g_ref, f32[160,512]{1,0:T(8,128)S(1)} %collective-permute-done.ra, f32[160,512]{1,0:T(8,128)S(1)} %collective-permute-done.1.rc, f32[168,512]{1,0:T(8,128)S(1)} %collective-permute-done.4.rd, ...), custom_call_target="tpu_custom_call" | custom-call | flops 20000000 | bytes 4000000 | tf_op jit(solution)/shard_map/pallas_call | solution.py:46
  52.9 0.0 collective-permute-done.6.r1
  52.9 2.6 %collective-permute-done.7.r2 = f32[80,512]{1,0:T(8,128)S(1)} collective-permute-done((f32[80,512]{1,0:T(8,128)S(1)}, f32[80,512]{1,0:T(8,128)S(1)}, u32[]{:S(2)}, u32[]{:S(2)}) %collective-permute-start.7) | collective-permute-done | bytes 163872 | tf_op jit(solution)/shard_map/ppermute | solution.py:805
  55.5 2.3 %collective-permute-done.8.r3 = f32[80,512]{1,0:T(8,128)S(1)} collective-permute-done((f32[80,512]{1,0:T(8,128)S(1)}, f32[80,512]{1,0:T(8,128)S(1)}, u32[]{:S(2)}, u32[]{:S(2)}) %collective-permute-start.8) | collective-permute-done | bytes 163872 | tf_op jit(solution)/shard_map/ppermute | solution.py:804
  57.8 1.5 %shard_map.126 = (f32[256,512]{1,0:T(8,128)S(1)}, f32[256,512]{1,0:T(8,128)S(1)}, f32[256,512]{1,0:T(8,128)S(1)}, f32[8,128]{1,0:T(8,128)S(1)}) custom-call(s32[1]{0:T(128)} %bitcast.g_ref, f32[272,640]{1,0:T(8,128)S(1)} %get-tuple-element.37.gw, f32[272,640]{1,0:T(8,128)S(1)} %get-tuple-element.38.invd, f32[272,640]{1,0:T(8,128)S(1)} %get-tuple-element.39.ra, ...), custom_call_target="tpu_custom_call" | custom-call | flops 1000000 | bytes 4000000 | tf_op jit(solution)/shard_map/pallas_call | solution.py:46
  59.3 17.2 %all_to_all.11.parts = f32[32,8,128]{2,1,0:T(8,128)S(1)} all-to-all(f32[32,8,128]{2,1,0:T(8,128)S(1)} %broadcast_in_dim.2), channel_id=1, replica_groups=mesh['grp'=4,'tile'=8] {'grp','tile'}, dimensions={0} | all-to-all | bytes 262144 | tf_op jit(solution)/shard_map/all_to_all | solution.py:825
  76.5 1.1 %shard_map.127 = f32[256,512]{1,0:T(8,128)} custom-call(s32[1]{0:T(128)} %bitcast.g_ref, f32[32,8,128]{2,1,0:T(8,128)S(1)} %all_to_all.11.parts, f32[256,512]{1,0:T(8,128)S(1)} %copy-done, f32[256,512]{1,0:T(8,128)S(1)} %get-tuple-element.46.y0, f32[256,512]{1,0:T(8,128)S(1)} %get-tuple-element.47.y1, f32[256,512]{1,0:T(8,128)S(1)} %get-tuple-element.48.y2), custom_call_target="tpu_custom_call" | custom-call | flops 1000000 | bytes 4000000 | tf_op jit(solution)/shard_map/pallas_call | solution.py:46
  (1 shorter events, 0.0 us)
Async XLA Ops:
  0.6 2.0 %copy-start = (f32[256,512]{1,0:T(8,128)S(1)}, f32[256,512]{1,0:T(8,128)}, u32[]{:S(2)}) copy-start(f32[256,512]{1,0:T(8,128)} %x0.9) | copy-start | bytes 1572868
  0.6 2.0 %copy-start.1 = (f32[3,2,64,512]{3,2,1,0:T(8,128)S(1)}, f32[3,2,64,512]{3,2,1,0:T(8,128)}, u32[]{:S(2)}) copy-start(f32[3,2,64,512]{3,2,1,0:T(8,128)} %stress.7) | copy-start | bytes 2359300
  0.7 2.0 %copy-start.2 = (f32[2,256,512]{2,1,0:T(8,128)S(1)}, f32[2,256,512]{2,1,0:T(8,128)}, u32[]{:S(2)}) copy-start(f32[2,256,512]{2,1,0:T(8,128)} %cur.5) | copy-start | bytes 3145732
  0.7 2.1 %copy-start.3 = (f32[2,2,64,512]{3,2,1,0:T(8,128)S(1)}, f32[2,2,64,512]{3,2,1,0:T(8,128)}, u32[]{:S(2)}) copy-start(f32[2,2,64,512]{3,2,1,0:T(8,128)} %vel.7) | copy-start | bytes 1572868
  0.7 2.3 %copy-start.4 = (f32[2,2,64,512]{3,2,1,0:T(8,128)S(1)}, f32[2,2,64,512]{3,2,1,0:T(8,128)}, u32[]{:S(2)}) copy-start(f32[2,2,64,512]{3,2,1,0:T(8,128)} %wind.7) | copy-start | bytes 1572868
  0.7 2.4 %copy-start.5 = (f32[256,512]{1,0:T(8,128)S(1)}, f32[256,512]{1,0:T(8,128)}, u32[]{:S(2)}) copy-start(f32[256,512]{1,0:T(8,128)} %base.7) | copy-start | bytes 1572868
  0.7 2.6 %copy-start.6 = (f32[256,512]{1,0:T(8,128)S(1)}, f32[256,512]{1,0:T(8,128)}, u32[]{:S(2)}) copy-start(f32[256,512]{1,0:T(8,128)} %depth.3) | copy-start | bytes 1572868
  0.7 2.6 %copy-start.7 = (f32[2,64,512]{2,1,0:T(8,128)S(1)}, f32[2,64,512]{2,1,0:T(8,128)}, u32[]{:S(2)}) copy-start(f32[2,64,512]{2,1,0:T(8,128)} %thick.3) | copy-start | bytes 786436
  0.7 2.6 %copy-start.8 = (s32[32,64]{1,0:T(8,128)S(1)}, s32[32,64]{1,0:T(8,128)}, u32[]{:S(2)}) copy-start(s32[32,64]{1,0:T(8,128)} %land.3) | copy-start | bytes 24580
  0.7 2.6 %copy-start.9 = (s32[2,8,64]{2,1,0:T(8,128)S(1)}, s32[2,8,64]{2,1,0:T(8,128)}, u32[]{:S(2)}) copy-start(s32[2,8,64]{2,1,0:T(8,128)} %iceb.3) | copy-start | bytes 12292
  3.8 3.7 %collective-permute-start.2 = (f32[288,128]{1,0:T(8,128)S(1)}, f32[288,128]{1,0:T(8,128)S(1)}, u32[]{:S(2)}, u32[]{:S(2)}) collective-permute-start(f32[288,128]{1,0:T(8,128)S(1)} %get-tuple-element.30), channel_id=1, source_target_pairs={{0,1},{1,2},{2,3},{3,4},{4,5},{5,6},{6,7},{8,9},{9,10},{10,11},{11... | collective-permute-start | bytes 442376 | tf_op jit(solution)/shard_map/ppermute | solution.py:783
  6.2 5.4 %collective-permute-start.3 = (f32[288,128]{1,0:T(8,128)S(1)}, f32[288,128]{1,0:T(8,128)S(1)}, u32[]{:S(2)}, u32[]{:S(2)}) collective-permute-start(f32[288,128]{1,0:T(8,128)S(1)} %get-tuple-element.31), channel_id=1, source_target_pairs={{1,0},{2,1},{3,2},{4,3},{5,4},{6,5},{7,6},{9,8},{10,9},{11,10},{12... | collective-permute-start | bytes 442376 | tf_op jit(solution)/shard_map/ppermute | solution.py:784
  12.1 25.3 %collective-permute-start.4 = (f32[168,512]{1,0:T(8,128)S(1)}, f32[168,512]{1,0:T(8,128)S(1)}, u32[]{:S(2)}, u32[]{:S(2)}) collective-permute-start(f32[168,512]{1,0:T(8,128)S(1)} %get-tuple-element.34), channel_id=1, source_target_pairs={{0,8},{24,16},{1,9},{25,17},{2,10},{26,18},{3,11},{27,19},{4,12},{... | collective-permute-start | bytes 1032200 | tf_op jit(solution)/shard_map/ppermute | solution.py:793
  15.3 22.1 %collective-permute-start = (f32[160,512]{1,0:T(8,128)S(1)}, f32[160,512]{1,0:T(8,128)S(1)}, u32[]{:S(2)}, u32[]{:S(2)}) collective-permute-start(f32[160,512]{1,0:T(8,128)S(1)} %get-tuple-element.27), channel_id=1, source_target_pairs={{0,8},{8,0},{16,24},{24,16},{1,9},{9,1},{17,25},{25,17},{2,10},{10... | collective-permute-start | bytes 983048 | tf_op jit(solution)/shard_map/ppermute | solution.py:772
  15.4 22.0 %collective-permute-start.1 = (f32[160,512]{1,0:T(8,128)S(1)}, f32[160,512]{1,0:T(8,128)S(1)}, u32[]{:S(2)}, u32[]{:S(2)}) collective-permute-start(f32[160,512]{1,0:T(8,128)S(1)} %get-tuple-element.28), channel_id=1, source_target_pairs={{0,24},{24,0},{8,16},{16,8},{1,25},{25,1},{9,17},{17,9},{2,26},{26... | collective-permute-start | bytes 983048 | tf_op jit(solution)/shard_map/ppermute | solution.py:771
  16.9 20.5 %collective-permute-start.5 = (f32[160,512]{1,0:T(8,128)S(1)}, f32[160,512]{1,0:T(8,128)S(1)}, u32[]{:S(2)}, u32[]{:S(2)}) collective-permute-start(f32[160,512]{1,0:T(8,128)S(1)} %get-tuple-element.40), channel_id=1, source_target_pairs={{0,16},{24,8},{1,17},{25,9},{2,18},{26,10},{3,19},{27,11},{4,20},{... | collective-permute-start | bytes 983048 | tf_op jit(solution)/shard_map/ppermute | solution.py:773
  46.8 6.1 %collective-permute-start.6 = (f32[80,512]{1,0:T(8,128)S(1)}, f32[80,512]{1,0:T(8,128)S(1)}, u32[]{:S(2)}, u32[]{:S(2)}) collective-permute-start(f32[80,512]{1,0:T(8,128)S(1)} %get-tuple-element.41), channel_id=1, source_target_pairs={{8,0},{16,24},{24,8},{0,16},{9,1},{17,25},{25,9},{1,17},{10,2},{18... | collective-permute-start | bytes 491528 | tf_op jit(solution)/shard_map/ppermute | solution.py:806
  47.8 7.7 %collective-permute-start.7 = (f32[80,512]{1,0:T(8,128)S(1)}, f32[80,512]{1,0:T(8,128)S(1)}, u32[]{:S(2)}, u32[]{:S(2)}) collective-permute-start(f32[80,512]{1,0:T(8,128)S(1)} %get-tuple-element.42), channel_id=1, source_target_pairs={{16,0},{8,24},{17,1},{9,25},{18,2},{10,26},{19,3},{11,27},{20,4},{... | collective-permute-start | bytes 491528 | tf_op jit(solution)/shard_map/ppermute | solution.py:805
  49.1 8.7 %collective-permute-start.8 = (f32[80,512]{1,0:T(8,128)S(1)}, f32[80,512]{1,0:T(8,128)S(1)}, u32[]{:S(2)}, u32[]{:S(2)}) collective-permute-start(f32[80,512]{1,0:T(8,128)S(1)} %get-tuple-element.43), channel_id=1, source_target_pairs={{24,0},{0,24},{25,1},{1,25},{26,2},{2,26},{27,3},{3,27},{28,4},{4,... | collective-permute-start | bytes 491528 | tf_op jit(solution)/shard_map/ppermute | solution.py:804

commit v5 on v4

--- a/solution.py
+++ b/solution.py
@@ -688,18 +688,24 @@
     for j in range(1, ext - 1):
         w = neighbour_sum(u2_s, j + 1, row)[:, :cols] * u2_s[tile(j + 1), :][:, :cols]
         acc[5] = acc[5] + w
+    lane_sums = []
     for k in range(6):
         total = acc[k][:, :LANES]
         for c in range(1, cols // LANES):
             total = total + acc[k][:, c * LANES : (c + 1) * LANES]
-        sums[k : k + 1, :] = jnp.sum(total, axis=0, keepdims=True)
-    sums[6:8, :] = jnp.zeros((2, LANES), F32)
+        lane_sums.append(jnp.sum(total, axis=0, keepdims=True))
+    stacked = jnp.concatenate(lane_sums + [jnp.zeros((2, LANES), F32)], axis=0)
+    each = jnp.broadcast_to(jnp.sum(stacked, axis=1, keepdims=True), (SUB, LANES))
+    sums[...] = jnp.sum(jnp.where(lane == row_iota(LANES), each, 0.0), axis=0, keepdims=True)
 
 
 def combine(g_ref, parts, x0, y0, y1, y2, out):
-    total = jnp.sum(jnp.sum(parts[...], axis=0), axis=1, keepdims=True)
-    total = jnp.broadcast_to(total, (SUB, LANES))
-    m = [jnp.broadcast_to(total[k : k + 1, :], (SUB, LANES)) for k in range(6)]
+    total = jnp.broadcast_to(jnp.sum(parts[...], axis=0), (SUB, LANES))
+    lane = lane_iota()
+    m = [
+        jnp.broadcast_to(jnp.sum(jnp.where(lane == k, total, 0.0), axis=1, keepdims=True), (SUB, LANES))
+        for k in range(6)
+    ]
 
     def dot(left, right, image):
         value = None
@@ -817,13 +823,13 @@
     )
     y0, y1, y2, sums = call(
         ocean_basis,
-        [(rows, cols)] * 3 + [(SUB, LANES)],
+        [(rows, cols)] * 3 + [(1, LANES)],
         [g, gw, invd, known, r1, r2, r3, mine],
         scratch=[field, padded, padded, padded],
     )
     devices = groups * tiles
     shared = lax.all_to_all(
-        jnp.broadcast_to(sums[None], (devices, SUB, LANES)), ("grp", "tile"), 0, 0, tiled=True
+        jnp.broadcast_to(sums[None], (devices, 1, LANES)), ("grp", "tile"), 0, 0, tiled=True
     )
     (ssh,) = call(combine, [(rows, cols)], [g, shared, ssh_prev, y0, y1, y2])
     return ssh, velocity, stress

time: 77.9 us -> 77.1 us (0.990)
  blocking collectives: 33.8 us -> 32.9 us
    all_to_all x1, blocking collectives: 17.2 us -> 16.2 us  [shards(): lax.all_to_all(jnp.broadcast_to(sums[None], (devices, 1, LANES)), ('grp',...]
where the time goes in v5:
time: 77.1 us; the launch traced here: 76.7 us
  blocking collectives  32.9 us (43%)
  starting transfers between devices  17.5 us (23%)
  Pallas kernels  15.6 us (20%)
  waiting for transfers between devices  9.08 us (12%)
  between operations  0.86 us (1%)
    all_to_all x1, blocking collectives, shards(): nx = lax.all_to_all(narrow, 'grp', 0, 0, tiled=True)  16.6 us
    all_to_all x1, blocking collectives, shards(): lax.all_to_all(jnp.broadcast_to(sums[None], (devices, 1, LANES)), ('grp',...  16.2 us
    pallas_call x7, Pallas kernels, call(): pl.pallas_call(body, out_shape=shapes, in_specs=specs, out_specs=tuple((v...  15.6 us
    ppermute x1, waiting for transfers between devices, shards(): lax.ppermute(left, 'tile', [(i + 1, i) for i in range(tiles - 1)])  4.13 us
    ppermute x1, starting transfers between devices, shards(): rb = lax.ppermute(b, 'grp', [(0, 2), (3, 1)])  3.84 us
    ppermute x1, starting transfers between devices, shards(): rd = lax.ppermute(d, 'grp', [(0, 1), (3, 2)])  3.19 us
    ppermute x1, starting transfers between devices, shards(): r3 = lax.ppermute(p3, 'grp', [(3, 0), (0, 3)])  2.92 us
    ppermute x1, waiting for transfers between devices, shards(): r2 = lax.ppermute(p2, 'grp', [(2, 0), (1, 3)])  2.61 us
  transfers between devices with their start and end apart: 9, of which 3 were waited for; matrix products, arithmetic and copies ran while one was open for 0% of the time, Pallas kernels for 1%

profile of v5, /device:TPU:0, one launch (start us, length us, event | category | flops | bytes accessed | tf_op | source)
XLA Modules:
  0.0 76.7 jit_solution(16951737814056423532)
XLA Ops:
  0.6 0.0 copy-start
  0.6 0.0 copy-start.1
  0.7 0.0 copy-start.2
  0.7 0.0 copy-start.3
  0.7 0.0 copy-start.4
  0.7 0.0 copy-start.5
  0.7 0.0 copy-start.6
  0.7 0.0 copy-start.7
  0.7 0.0 copy-start.8
  0.7 0.0 copy-start.9
  0.7 1.8 %shard_map.121 = (f32[160,512]{1,0:T(8,128)S(1)}, f32[160,512]{1,0:T(8,128)S(1)}, f32[160,512]{1,0:T(8,128)S(1)}, f32[8,128]{1,0:T(8,128)S(1)}) custom-call(s32[1]{0:T(128)} %bitcast.g_ref, f32[256,512]{1,0:T(8,128)} %base.7, f32[256,512]{1,0:T(8,128)} %depth.3, f32[256,512]{1,0:T(8,128)} %x0.9, f32[2,256,512]{2,1,0:T(8,128)} %cur.5, s32[32,64]{1,0:T(8,128)} %land.3, ...), custom_call_target="tpu_custom_call" | custom-call | flops 1000000 | bytes 4000000 | tf_op jit(solution)/shard_map/pallas_call | solution.py:46
  2.6 0.0 copy-done
  2.6 0.0 copy-done.1
  2.6 0.1 copy-done.2
  2.7 0.1 copy-done.3
  2.8 0.2 copy-done.4
  3.0 0.2 copy-done.5
  3.1 0.2 copy-done.6
  3.3 0.1 copy-done.7
  3.3 0.0 copy-done.8
  3.3 0.0 copy-done.9
  3.3 0.4 shard_map.122
  3.8 2.4 %collective-permute-start.2 = (f32[288,128]{1,0:T(8,128)S(1)}, f32[288,128]{1,0:T(8,128)S(1)}, u32[]{:S(2)}, u32[]{:S(2)}) collective-permute-start(f32[288,128]{1,0:T(8,128)S(1)} %get-tuple-element.30), channel_id=1, source_target_pairs={{0,1},{1,2},{2,3},{3,4},{4,5},{5,6},{6,7},{8,9},{9,10},{10,11},{11... | collective-permute-start | bytes 442376 | tf_op jit(solution)/shard_map/ppermute | solution.py:789
  6.2 1.3 %collective-permute-start.3 = (f32[288,128]{1,0:T(8,128)S(1)}, f32[288,128]{1,0:T(8,128)S(1)}, u32[]{:S(2)}, u32[]{:S(2)}) collective-permute-start(f32[288,128]{1,0:T(8,128)S(1)} %get-tuple-element.31), channel_id=1, source_target_pairs={{1,0},{2,1},{3,2},{4,3},{5,4},{6,5},{7,6},{9,8},{10,9},{11,10},{12... | collective-permute-start | bytes 442376 | tf_op jit(solution)/shard_map/ppermute | solution.py:790
  7.5 0.0 collective-permute-done.2.from_left
  7.5 4.1 %collective-permute-done.3.from_right = f32[288,128]{1,0:T(8,128)S(1)} collective-permute-done((f32[288,128]{1,0:T(8,128)S(1)}, f32[288,128]{1,0:T(8,128)S(1)}, u32[]{:S(2)}, u32[]{:S(2)}) %collective-permute-start.3) | collective-permute-done | bytes 147488 | tf_op jit(solution)/shard_map/ppermute | solution.py:790
  11.6 0.5 shard_map.123
  12.1 3.2 %collective-permute-start.4 = (f32[168,512]{1,0:T(8,128)S(1)}, f32[168,512]{1,0:T(8,128)S(1)}, u32[]{:S(2)}, u32[]{:S(2)}) collective-permute-start(f32[168,512]{1,0:T(8,128)S(1)} %get-tuple-element.34), channel_id=1, source_target_pairs={{0,8},{24,16},{1,9},{25,17},{2,10},{26,18},{3,11},{27,19},{4,12},{... | collective-permute-start | bytes 1032200 | tf_op jit(solution)/shard_map/ppermute | solution.py:799
  15.3 0.1 collective-permute-start
  15.4 1.6 %collective-permute-start.1 = (f32[160,512]{1,0:T(8,128)S(1)}, f32[160,512]{1,0:T(8,128)S(1)}, u32[]{:S(2)}, u32[]{:S(2)}) collective-permute-start(f32[160,512]{1,0:T(8,128)S(1)} %get-tuple-element.28), channel_id=1, source_target_pairs={{0,24},{24,0},{8,16},{16,8},{1,25},{25,1},{9,17},{17,9},{2,26},{26... | collective-permute-start | bytes 983048 | tf_op jit(solution)/shard_map/ppermute | solution.py:777
  16.9 3.8 %collective-permute-start.5 = (f32[160,512]{1,0:T(8,128)S(1)}, f32[160,512]{1,0:T(8,128)S(1)}, u32[]{:S(2)}, u32[]{:S(2)}) collective-permute-start(f32[160,512]{1,0:T(8,128)S(1)} %get-tuple-element.40), channel_id=1, source_target_pairs={{0,16},{24,8},{1,17},{25,9},{2,18},{26,10},{3,19},{27,11},{4,20},{... | collective-permute-start | bytes 983048 | tf_op jit(solution)/shard_map/ppermute | solution.py:779
  20.8 16.6 %all_to_all.10.nx = f32[4,40,128]{2,1,0:T(8,128)S(1)} all-to-all(f32[4,40,128]{2,1,0:T(8,128)S(1)} %get-tuple-element.35), channel_id=1, replica_groups=mesh['grp'=4,'tile'=8] {'grp'}, dimensions={0} | all-to-all | bytes 163840 | tf_op jit(solution)/shard_map/all_to_all | solution.py:800
  37.4 0.0 collective-permute-done.ra
  37.4 0.0 collective-permute-done.1.rc
  37.4 0.0 collective-permute-done.5.rb
  37.4 0.0 collective-permute-done.4.rd
  37.4 9.4 %shard_map.125 = (f32[2,2,64,512]{3,2,1,0:T(8,128)}, f32[3,2,64,512]{3,2,1,0:T(8,128)}, f32[80,512]{1,0:T(8,128)S(1)}, f32[80,512]{1,0:T(8,128)S(1)}, f32[80,512]{1,0:T(8,128)S(1)}, /*index=5*/f32[80,512]{1,0:T(8,128)S(1)}) custom-call(s32[1]{0:T(128)} %bitcast.g_ref, f32[160,512]{1,0:T(8,128)S(1)} %collective-permute-done.ra, ...), custom_call_target="tpu_custom_call" | custom-call | flops 1000000 | bytes 4000000 | tf_op jit(solution)/shard_map/pallas_call | solution.py:46
  46.8 1.0 %collective-permute-start.6 = (f32[80,512]{1,0:T(8,128)S(1)}, f32[80,512]{1,0:T(8,128)S(1)}, u32[]{:S(2)}, u32[]{:S(2)}) collective-permute-start(f32[80,512]{1,0:T(8,128)S(1)} %get-tuple-element.41), channel_id=1, source_target_pairs={{8,0},{16,24},{24,8},{0,16},{9,1},{17,25},{25,9},{1,17},{10,2},{18... | collective-permute-start | bytes 491528 | tf_op jit(solution)/shard_map/ppermute | solution.py:812
  47.8 1.3 %collective-permute-start.7 = (f32[80,512]{1,0:T(8,128)S(1)}, f32[80,512]{1,0:T(8,128)S(1)}, u32[]{:S(2)}, u32[]{:S(2)}) collective-permute-start(f32[80,512]{1,0:T(8,128)S(1)} %get-tuple-element.42), channel_id=1, source_target_pairs={{16,0},{8,24},{17,1},{9,25},{18,2},{10,26},{19,3},{11,27},{20,4},{... | collective-permute-start | bytes 491528 | tf_op jit(solution)/shard_map/ppermute | solution.py:811
  49.1 2.9 %collective-permute-start.8 = (f32[80,512]{1,0:T(8,128)S(1)}, f32[80,512]{1,0:T(8,128)S(1)}, u32[]{:S(2)}, u32[]{:S(2)}) collective-permute-start(f32[80,512]{1,0:T(8,128)S(1)} %get-tuple-element.43), channel_id=1, source_target_pairs={{24,0},{0,24},{25,1},{1,25},{26,2},{2,26},{27,3},{3,27},{28,4},{4,... | collective-permute-start | bytes 491528 | tf_op jit(solution)/shard_map/ppermute | solution.py:810
  52.1 0.8 %shard_map.124 = (f32[272,640]{1,0:T(8,128)S(1)}, f32[272,640]{1,0:T(8,128)S(1)}, f32[272,640]{1,0:T(8,128)S(1)}) custom-call(s32[1]{0:T(128)} %bitcast.g_ref, f32[160,512]{1,0:T(8,128)S(1)} %collective-permute-done.ra, f32[160,512]{1,0:T(8,128)S(1)} %collective-permute-done.1.rc, f32[168,512]{1,0:T(8,128)S(1)} %collective-permute-done.4.rd, ...), custom_call_target="tpu_custom_call" | custom-call | flops 20000000 | bytes 4000000 | tf_op jit(solution)/shard_map/pallas_call | solution.py:46
  52.9 0.0 collective-permute-done.6.r1
  52.9 2.6 %collective-permute-done.7.r2 = f32[80,512]{1,0:T(8,128)S(1)} collective-permute-done((f32[80,512]{1,0:T(8,128)S(1)}, f32[80,512]{1,0:T(8,128)S(1)}, u32[]{:S(2)}, u32[]{:S(2)}) %collective-permute-start.7) | collective-permute-done | bytes 163872 | tf_op jit(solution)/shard_map/ppermute | solution.py:811
  55.5 2.3 %collective-permute-done.8.r3 = f32[80,512]{1,0:T(8,128)S(1)} collective-permute-done((f32[80,512]{1,0:T(8,128)S(1)}, f32[80,512]{1,0:T(8,128)S(1)}, u32[]{:S(2)}, u32[]{:S(2)}) %collective-permute-start.8) | collective-permute-done | bytes 163872 | tf_op jit(solution)/shard_map/ppermute | solution.py:810
  57.8 1.6 %shard_map.126 = (f32[256,512]{1,0:T(8,128)S(1)}, f32[256,512]{1,0:T(8,128)S(1)}, f32[256,512]{1,0:T(8,128)S(1)}, f32[1,128]{1,0:T(1,128)S(1)}) custom-call(s32[1]{0:T(128)} %bitcast.g_ref, f32[272,640]{1,0:T(8,128)S(1)} %get-tuple-element.37.gw, f32[272,640]{1,0:T(8,128)S(1)} %get-tuple-element.38.invd, f32[272,640]{1,0:T(8,128)S(1)} %get-tuple-element.39.ra, ...), custom_call_target="tpu_custom_call" | custom-call | flops 1000000 | bytes 4000000 | tf_op jit(solution)/shard_map/pallas_call | solution.py:46
  59.4 16.2 %all_to_all.11.parts = f32[32,1,128]{2,1,0:T(1,128)S(1)} all-to-all(f32[32,1,128]{2,1,0:T(1,128)S(1)} %broadcast_in_dim.9), channel_id=1, replica_groups=mesh['grp'=4,'tile'=8] {'grp','tile'}, dimensions={0} | all-to-all | bytes 32768 | tf_op jit(solution)/shard_map/all_to_all | solution.py:831
  75.6 1.1 %shard_map.127 = f32[256,512]{1,0:T(8,128)} custom-call(s32[1]{0:T(128)} %bitcast.g_ref, f32[32,1,128]{2,1,0:T(1,128)S(1)} %all_to_all.11.parts, f32[256,512]{1,0:T(8,128)S(1)} %copy-done, f32[256,512]{1,0:T(8,128)S(1)} %get-tuple-element.46.y0, f32[256,512]{1,0:T(8,128)S(1)} %get-tuple-element.47.y1, f32[256,512]{1,0:T(8,128)S(1)} %get-tuple-element.48.y2), custom_call_target="tpu_custom_call" | custom-call | flops 1000000 | bytes 4000000 | tf_op jit(solution)/shard_map/pallas_call | solution.py:46
  (1 shorter events, 0.0 us)
Async XLA Ops:
  0.6 2.0 %copy-start = (f32[256,512]{1,0:T(8,128)S(1)}, f32[256,512]{1,0:T(8,128)}, u32[]{:S(2)}) copy-start(f32[256,512]{1,0:T(8,128)} %x0.9) | copy-start | bytes 1572868
  0.6 2.0 %copy-start.1 = (f32[3,2,64,512]{3,2,1,0:T(8,128)S(1)}, f32[3,2,64,512]{3,2,1,0:T(8,128)}, u32[]{:S(2)}) copy-start(f32[3,2,64,512]{3,2,1,0:T(8,128)} %stress.7) | copy-start | bytes 2359300
  0.7 2.0 %copy-start.2 = (f32[2,256,512]{2,1,0:T(8,128)S(1)}, f32[2,256,512]{2,1,0:T(8,128)}, u32[]{:S(2)}) copy-start(f32[2,256,512]{2,1,0:T(8,128)} %cur.5) | copy-start | bytes 3145732
  0.7 2.1 %copy-start.3 = (f32[2,2,64,512]{3,2,1,0:T(8,128)S(1)}, f32[2,2,64,512]{3,2,1,0:T(8,128)}, u32[]{:S(2)}) copy-start(f32[2,2,64,512]{3,2,1,0:T(8,128)} %vel.7) | copy-start | bytes 1572868
  0.7 2.3 %copy-start.4 = (f32[2,2,64,512]{3,2,1,0:T(8,128)S(1)}, f32[2,2,64,512]{3,2,1,0:T(8,128)}, u32[]{:S(2)}) copy-start(f32[2,2,64,512]{3,2,1,0:T(8,128)} %wind.7) | copy-start | bytes 1572868
  0.7 2.4 %copy-start.5 = (f32[256,512]{1,0:T(8,128)S(1)}, f32[256,512]{1,0:T(8,128)}, u32[]{:S(2)}) copy-start(f32[256,512]{1,0:T(8,128)} %base.7) | copy-start | bytes 1572868
  0.7 2.6 %copy-start.6 = (f32[256,512]{1,0:T(8,128)S(1)}, f32[256,512]{1,0:T(8,128)}, u32[]{:S(2)}) copy-start(f32[256,512]{1,0:T(8,128)} %depth.3) | copy-start | bytes 1572868
  0.7 2.6 %copy-start.7 = (f32[2,64,512]{2,1,0:T(8,128)S(1)}, f32[2,64,512]{2,1,0:T(8,128)}, u32[]{:S(2)}) copy-start(f32[2,64,512]{2,1,0:T(8,128)} %thick.3) | copy-start | bytes 786436
  0.7 2.6 %copy-start.8 = (s32[32,64]{1,0:T(8,128)S(1)}, s32[32,64]{1,0:T(8,128)}, u32[]{:S(2)}) copy-start(s32[32,64]{1,0:T(8,128)} %land.3) | copy-start | bytes 24580
  0.7 2.6 %copy-start.9 = (s32[2,8,64]{2,1,0:T(8,128)S(1)}, s32[2,8,64]{2,1,0:T(8,128)}, u32[]{:S(2)}) copy-start(s32[2,8,64]{2,1,0:T(8,128)} %iceb.3) | copy-start | bytes 12292
  3.8 3.7 %collective-permute-start.2 = (f32[288,128]{1,0:T(8,128)S(1)}, f32[288,128]{1,0:T(8,128)S(1)}, u32[]{:S(2)}, u32[]{:S(2)}) collective-permute-start(f32[288,128]{1,0:T(8,128)S(1)} %get-tuple-element.30), channel_id=1, source_target_pairs={{0,1},{1,2},{2,3},{3,4},{4,5},{5,6},{6,7},{8,9},{9,10},{10,11},{11... | collective-permute-start | bytes 442376 | tf_op jit(solution)/shard_map/ppermute | solution.py:789
  6.2 5.4 %collective-permute-start.3 = (f32[288,128]{1,0:T(8,128)S(1)}, f32[288,128]{1,0:T(8,128)S(1)}, u32[]{:S(2)}, u32[]{:S(2)}) collective-permute-start(f32[288,128]{1,0:T(8,128)S(1)} %get-tuple-element.31), channel_id=1, source_target_pairs={{1,0},{2,1},{3,2},{4,3},{5,4},{6,5},{7,6},{9,8},{10,9},{11,10},{12... | collective-permute-start | bytes 442376 | tf_op jit(solution)/shard_map/ppermute | solution.py:790
  12.1 25.3 %collective-permute-start.4 = (f32[168,512]{1,0:T(8,128)S(1)}, f32[168,512]{1,0:T(8,128)S(1)}, u32[]{:S(2)}, u32[]{:S(2)}) collective-permute-start(f32[168,512]{1,0:T(8,128)S(1)} %get-tuple-element.34), channel_id=1, source_target_pairs={{0,8},{24,16},{1,9},{25,17},{2,10},{26,18},{3,11},{27,19},{4,12},{... | collective-permute-start | bytes 1032200 | tf_op jit(solution)/shard_map/ppermute | solution.py:799
  15.3 22.1 %collective-permute-start = (f32[160,512]{1,0:T(8,128)S(1)}, f32[160,512]{1,0:T(8,128)S(1)}, u32[]{:S(2)}, u32[]{:S(2)}) collective-permute-start(f32[160,512]{1,0:T(8,128)S(1)} %get-tuple-element.27), channel_id=1, source_target_pairs={{0,8},{8,0},{16,24},{24,16},{1,9},{9,1},{17,25},{25,17},{2,10},{10... | collective-permute-start | bytes 983048 | tf_op jit(solution)/shard_map/ppermute | solution.py:778
  15.4 22.0 %collective-permute-start.1 = (f32[160,512]{1,0:T(8,128)S(1)}, f32[160,512]{1,0:T(8,128)S(1)}, u32[]{:S(2)}, u32[]{:S(2)}) collective-permute-start(f32[160,512]{1,0:T(8,128)S(1)} %get-tuple-element.28), channel_id=1, source_target_pairs={{0,24},{24,0},{8,16},{16,8},{1,25},{25,1},{9,17},{17,9},{2,26},{26... | collective-permute-start | bytes 983048 | tf_op jit(solution)/shard_map/ppermute | solution.py:777
  16.9 20.5 %collective-permute-start.5 = (f32[160,512]{1,0:T(8,128)S(1)}, f32[160,512]{1,0:T(8,128)S(1)}, u32[]{:S(2)}, u32[]{:S(2)}) collective-permute-start(f32[160,512]{1,0:T(8,128)S(1)} %get-tuple-element.40), channel_id=1, source_target_pairs={{0,16},{24,8},{1,17},{25,9},{2,18},{26,10},{3,19},{27,11},{4,20},{... | collective-permute-start | bytes 983048 | tf_op jit(solution)/shard_map/ppermute | solution.py:779
  46.8 6.1 %collective-permute-start.6 = (f32[80,512]{1,0:T(8,128)S(1)}, f32[80,512]{1,0:T(8,128)S(1)}, u32[]{:S(2)}, u32[]{:S(2)}) collective-permute-start(f32[80,512]{1,0:T(8,128)S(1)} %get-tuple-element.41), channel_id=1, source_target_pairs={{8,0},{16,24},{24,8},{0,16},{9,1},{17,25},{25,9},{1,17},{10,2},{18... | collective-permute-start | bytes 491528 | tf_op jit(solution)/shard_map/ppermute | solution.py:812
  47.8 7.7 %collective-permute-start.7 = (f32[80,512]{1,0:T(8,128)S(1)}, f32[80,512]{1,0:T(8,128)S(1)}, u32[]{:S(2)}, u32[]{:S(2)}) collective-permute-start(f32[80,512]{1,0:T(8,128)S(1)} %get-tuple-element.42), channel_id=1, source_target_pairs={{16,0},{8,24},{17,1},{9,25},{18,2},{10,26},{19,3},{11,27},{20,4},{... | collective-permute-start | bytes 491528 | tf_op jit(solution)/shard_map/ppermute | solution.py:811
  49.1 8.7 %collective-permute-start.8 = (f32[80,512]{1,0:T(8,128)S(1)}, f32[80,512]{1,0:T(8,128)S(1)}, u32[]{:S(2)}, u32[]{:S(2)}) collective-permute-start(f32[80,512]{1,0:T(8,128)S(1)} %get-tuple-element.43), channel_id=1, source_target_pairs={{24,0},{0,24},{25,1},{1,25},{26,2},{2,26},{27,3},{3,27},{28,4},{4,... | collective-permute-start | bytes 491528 | tf_op jit(solution)/shard_map/ppermute | solution.py:810

commit v6 on v5

--- a/solution.py
+++ b/solution.py
@@ -333,20 +333,22 @@
     return jnp.where((lane < EDGE) | (lane >= LANES - EDGE), value, 0.0)
 
 
-def low_high(g, ra, rc, rd, nx, n, lane, low):
-    cols = ra.shape[1]
-    inner_zero = jnp.zeros((SUB, cols), F32)
+def late_tile(rd, n, lane):
+    per = rd.shape[1] // LANES
     k, i = n // WIDE_SLOTS, n % WIDE_SLOTS
-    per = cols // LANES
-    first = 2 * NICE + NOC
-    tail = rd[tile(first + k // per), (k % per) * LANES : (k % per + 1) * LANES]
+    tail = rd[tile(2 * NICE + NOC + k // per), (k % per) * LANES : (k % per + 1) * LANES]
+    return split(rd[tile(n), :]) + [wide_outer(tail, i, lane)]
+
+
+def low_high(g, ra, rc, nx, n, lane, low):
+    k, i = n // WIDE_SLOTS, n % WIDE_SLOTS
     t = tile(n)
-    if low:
-        inner = jnp.where(g == 1, rd[t, :], jnp.where(g == 2, rc[t, :], jnp.where(g == 3, ra[t, :], inner_zero)))
-        packed = jnp.where(g == 1, tail, jnp.where(g == 2, nx[1, tile(k), :], jnp.where(g == 3, nx[2, tile(k), :], 0.0)))
-    else:
-        inner = jnp.where(g == 2, rd[t, :], jnp.where(g == 1, rc[t, :], jnp.where(g == 0, ra[t, :], inner_zero)))
-        packed = jnp.where(g == 2, tail, jnp.where(g == 1, nx[2, tile(k), :], jnp.where(g == 0, nx[1, tile(k), :], 0.0)))
+    pieces = [(2, rc, 1), (3, ra, 2)] if low else [(0, ra, 1), (1, rc, 2)]
+    inner = jnp.zeros((SUB, ra.shape[1]), F32)
+    packed = jnp.zeros((SUB, LANES), F32)
+    for group, ref, source in pieces:
+        inner = jnp.where(g == group, ref[t, :], inner)
+        packed = jnp.where(g == group, nx[source, tile(k), :], packed)
     return split(inner) + [wide_outer(packed, i, lane)]
 
 
@@ -371,58 +373,26 @@
     return [pltpu.roll(jnp.where(lane == LANES - 1, regs[c - 1], regs[c]), 1, 1) for c in range(n)]
 
 
-def ice_steps(g_ref, ra, rb, rc, rd, nx, outer, h, vel, stress, wind, cur,
-              vel_out, stress_out, p3, p2, p1, mine,
-              u_s, v_s, p_s, q_s, s_s, un_s, vn_s, qp_s, sp_s, a_s, m_s, w_s, fx_s, fy_s, f0_s, f1_s):
-    g = g_ref[0]
-    ice_rows, cols = h.shape[1:]
-    rows = cur.shape[1]
-    regs = cols // LANES + 1
-    per = ice_rows // SUB
-    ext = per + 2
-    lane = lane_iota()
+KEEP = 1.0 / (1.0 + RELAX)
+
+
+def at(j, shift=0):
+    return slice(SUB * (j + 1) + shift, SUB * (j + 2) + shift)
+
+
+def ice_core(count, load, state, rest, lane):
+    u_s, v_s, p_s, q_s, s_s = state
+    un_s, vn_s, qp_s, sp_s, a_s, m_s, w_s, fx_s, fy_s, f0_s, f1_s = rest
+    regs = u_s.shape[1]
     zero = jnp.zeros((SUB, LANES), F32)
-    keep = 1.0 / (1.0 + RELAX)
-    flow_first = sum(own_count(rows, ice_rows)[:2])
-
-    def at(j, shift=0):
-        return slice(SUB * (j + 1) + shift, SUB * (j + 2) + shift)
-
-    def flow(cap, comp, j):
-        n = comp * ext + j
-        t = tile(n)
-        k, i = n // WIDE_SLOTS, n % WIDE_SLOTS
-        here = jnp.clip(per * g - 1 + j, 0, rows // SUB - 1)
-        own = own_tile(cur, comp, per * g - 1, j)
-        spot = pl.multiple_of((flow_first + comp * (rows // SUB) + here) * SUB, SUB)
-        own_outer = outer[pl.ds(spot, SUB), :]
-        if cap == 0:
-            inner = jnp.where(g == 0, own, jnp.where(g == 1, ra[t, :], jnp.where(g == 2, rb[t, :], rc[t, :])))
-            edge = jnp.where(g == 0, own_outer, wide_outer(nx[0, tile(k), :], i, lane))
-        else:
-            inner = jnp.where(g == 3, own, jnp.where(g == 2, ra[t, :], jnp.where(g == 1, rb[t, :], rc[t, :])))
-            edge = jnp.where(g == 3, own_outer, wide_outer(nx[3, tile(k), :], i, lane))
-        return split(inner) + [edge]
-
     for cap in range(2):
-        own = own_ice(h, vel, stress, wind, cap)
         for c in range(regs):
             for ref in (p_s, s_s):
                 ref[cap, c, at(-1), :] = zero
             for ref in (u_s, v_s):
-                ref[cap, c, at(ext), :] = zero
-        flows = []
-        for j in range(ext):
-            if j % GROUP == 0:
-                flows = [[flow(cap, comp, i) for comp in range(2)] for i in range(j, min(j + GROUP, ext))]
-            if j == 0 or j == ext - 1:
-                fields = [low_high(g, ra, rc, rd, nx, cap * NICE + f, lane, j == 0) for f in range(NICE)]
-            else:
-                fields = [
-                    split(own[f][tile(j - 1), :]) + [outer[tile((cap * NICE + f) * per + j - 1), :]]
-                    for f in range(NICE)
-                ]
-            fields = fields + flows[j % GROUP]
+                ref[cap, c, at(count), :] = zero
+        for j in range(count):
+            fields = load(cap, j)
             for c in range(regs):
                 hh, u, v, s0, s1, s2, w0, w1, f0, f1 = (f[c] for f in fields)
                 u_s[cap, c, at(j), :] = u
@@ -432,14 +402,14 @@
                 s_s[cap, c, at(j), :] = s2
                 inv = jnp.where(hh > 0.0, 1.0 / (hh + (1.0 + STEP * DRAG)), 0.0)
                 quick = STEP * inv
-                a_s[cap, c, at(j), :] = hh * (RELAX * STRENGTH * keep)
+                a_s[cap, c, at(j), :] = hh * (RELAX * STRENGTH * KEEP)
                 m_s[cap, c, at(j), :] = (hh + 1.0) * inv
                 w_s[cap, c, at(j), :] = quick
                 fx_s[cap, c, at(j), :] = quick * (w0 + DRAG * f0)
                 fy_s[cap, c, at(j), :] = quick * (w1 + DRAG * f1)
                 f0_s[cap, c, at(j), :] = f0
                 f1_s[cap, c, at(j), :] = f1
-    for j in range(ext):
+    for j in range(count):
         for cap in range(2):
             for ref, source in ((un_s, u_s), (vn_s, v_s)):
                 turned = turned_next([source[cap, c, at(j), :] for c in range(regs)], lane)
@@ -459,9 +429,9 @@
             a = a_s[cap, c, at(j), :]
             ratio = a * lax.rsqrt((half + half) + (es * es + 1.0))
             low = 0.5 * a
-            q = q_s[cap, c, at(j), :] * keep + (ratio * vy - low)
-            s = s_s[cap, c, at(j), :] * keep + ratio * es
-            p_s[cap, c, at(j), :] = p_s[cap, c, at(j), :] * keep + (ratio * ux - low)
+            q = q_s[cap, c, at(j), :] * KEEP + (ratio * vy - low)
+            s = s_s[cap, c, at(j), :] * KEEP + ratio * es
+            p_s[cap, c, at(j), :] = p_s[cap, c, at(j), :] * KEEP + (ratio * ux - low)
             q_s[cap, c, at(j), :] = q
             s_s[cap, c, at(j), :] = s
             qs.append(q)
@@ -488,54 +458,111 @@
                 ref[cap, c, at(j), :] = turned[c]
 
     def subcycle(_, carry):
-        for j in range(ext + SKEW):
+        for j in range(count + SKEW):
             for cap in range(2):
-                if j < ext:
+                if j < count:
                     stress_tile(cap, j)
                 if j >= SKEW:
                     velocity_tile(cap, j - SKEW)
         return carry
 
     lax.fori_loop(0, NSUB, subcycle, 0)
+
+
+def drag_tile(state, rest, cap, j):
+    u_s, v_s = state[:2]
+    m_s, f0_s, f1_s = rest[5], rest[9], rest[10]
+    d0, d1 = [], []
+    for c in range(u_s.shape[1]):
+        iced = m_s[cap, c, at(j), :] > 0.0
+        d0.append(jnp.where(iced, DRAG * (u_s[cap, c, at(j), :] - f0_s[cap, c, at(j), :]), 0.0))
+        d1.append(jnp.where(iced, DRAG * (v_s[cap, c, at(j), :] - f1_s[cap, c, at(j), :]), 0.0))
+    return d0, d1
+
+
+def packed_edge(edge, k, lane):
+    edge = jnp.where((lane < EDGE) | (lane >= LANES - EDGE), edge, 0.0)
+    i = k % WIDE_SLOTS
+    return pltpu.roll(edge, 2 * EDGE * i, 1) if i else edge
+
+
+def ice_steps(g_ref, ra, rb, rc, nx, outer, h, vel, stress, wind, cur,
+              u_s, v_s, p_s, q_s, s_s, p3, p2, p1, mine, kept, *rest):
+    g = g_ref[0]
+    state = (u_s, v_s, p_s, q_s, s_s)
+    ice_rows, cols = h.shape[1:]
+    rows = cur.shape[1]
+    regs = cols // LANES + 1
+    per = ice_rows // SUB
+    ext = per + 2
+    lane = lane_iota()
+    zero = jnp.zeros((SUB, LANES), F32)
+    flow_first = sum(own_count(rows, ice_rows)[:2])
+
+    def flow(cap, comp, j):
+        n = comp * ext + j
+        t = tile(n)
+        k, i = n // WIDE_SLOTS, n % WIDE_SLOTS
+        here = jnp.clip(per * g - 1 + j, 0, rows // SUB - 1)
+        own = own_tile(cur, comp, per * g - 1, j)
+        spot = pl.multiple_of((flow_first + comp * (rows // SUB) + here) * SUB, SUB)
+        own_outer = outer[pl.ds(spot, SUB), :]
+        if cap == 0:
+            inner = jnp.where(g == 0, own, jnp.where(g == 1, ra[t, :], jnp.where(g == 2, rb[t, :], rc[t, :])))
+            edge = jnp.where(g == 0, own_outer, wide_outer(nx[0, tile(k), :], i, lane))
+        else:
+            inner = jnp.where(g == 3, own, jnp.where(g == 2, ra[t, :], jnp.where(g == 1, rb[t, :], rc[t, :])))
+            edge = jnp.where(g == 3, own_outer, wide_outer(nx[3, tile(k), :], i, lane))
+        return split(inner) + [edge]
+
+    flows = {}
+
+    def load(cap, j):
+        own = own_ice(h, vel, stress, wind, cap)
+        if j % GROUP == 0:
+            flows.clear()
+            for i in range(j, min(j + GROUP, ext)):
+                flows[i] = [flow(cap, comp, i) for comp in range(2)]
+        if j == 0 or j == ext - 1:
+            fields = [low_high(g, ra, rc, nx, cap * NICE + f, lane, j == 0) for f in range(NICE)]
+        else:
+            fields = [
+                split(own[f][tile(j - 1), :]) + [outer[tile((cap * NICE + f) * per + j - 1), :]]
+                for f in range(NICE)
+            ]
+        return fields + flows[j]
+
+    ice_core(ext, load, state, rest, lane)
+    drag_s = rest[0]
+    bands = per + 1
+    packs = [[None] * -(-bands // WIDE_SLOTS) for _ in range(2)]
     spreads = []
     for cap in range(2):
+        across = [[zero] * regs]
         for c in range(regs):
-            q_s[cap, c, at(0), :] = zero
-            q_s[cap, c, at(ext - 1), :] = zero
+            drag_s[cap, c, at(0), :] = zero
+            drag_s[cap, c, at(ext - 1), :] = zero
+        for j in range(1, ext - 1):
+            d0, d1 = drag_tile(state, rest, cap, j)
+            turned = turned_prev(d1, lane)
+            across.append([d1[c] - turned[c] for c in range(regs)])
+            for c in range(regs):
+                drag_s[cap, c, at(j), :] = d0[c]
+                if j == 1:
+                    kept[0, cap, c] = d0[c]
+                if j == ext - 3:
+                    kept[1, cap, c] = d0[c]
+        across.append([zero] * regs)
         parts = []
-        across = [[zero] * regs]
-        for j in range(1, ext - 1):
-            d1s = []
-            for c in range(regs):
-                u, v = u_s[cap, c, at(j), :], v_s[cap, c, at(j), :]
-                p, q = p_s[cap, c, at(j), :], q_s[cap, c, at(j), :]
-                if c + 1 < regs:
-                    block = (tile(j - 1), slice(c * LANES, (c + 1) * LANES))
-                    vel_out[(0, cap) + block] = u
-                    vel_out[(1, cap) + block] = v
-                    stress_out[(0, cap) + block] = p + q
-                    stress_out[(1, cap) + block] = p - q
-                    stress_out[(2, cap) + block] = s_s[cap, c, at(j), :]
-                iced = m_s[cap, c, at(j), :] > 0.0
-                q_s[cap, c, at(j), :] = jnp.where(iced, DRAG * (u - f0_s[cap, c, at(j), :]), 0.0)
-                d1s.append(jnp.where(iced, DRAG * (v - f1_s[cap, c, at(j), :]), 0.0))
-            turned = turned_prev(d1s, lane)
-            across.append([d1s[c] - turned[c] for c in range(regs)])
-        across.append([zero] * regs)
         for j in range(1, ext):
             parts.append([
-                (q_s[cap, c, at(j), :] - q_s[cap, c, at(j, -1), :]) + across[j][c] for c in range(regs)
+                (drag_s[cap, c, at(j), :] - drag_s[cap, c, at(j, -1), :]) + across[j][c] for c in range(regs)
             ])
-        spreads.append(parts)
-    bands = per + 1
-    packs = [[None] * -(-bands // WIDE_SLOTS) for _ in range(2)]
-    for cap in range(2):
         for k in range(bands):
-            i = k % WIDE_SLOTS
-            edge = jnp.where((lane < EDGE) | (lane >= LANES - EDGE), spreads[cap][k][regs - 1], 0.0)
-            edge = pltpu.roll(edge, 2 * EDGE * i, 1) if i else edge
+            edge = packed_edge(parts[k][regs - 1], k, lane)
             held = packs[cap][k // WIDE_SLOTS]
             packs[cap][k // WIDE_SLOTS] = edge if held is None else held + edge
+        spreads.append(parts)
 
     def put(block, north, south):
         p3[block] = jnp.where(g == 3, north, south)
@@ -549,6 +576,110 @@
     for c in range(regs - 1):
         pair = [pack[c] if c < len(pack) else zero for pack in packs]
         put((tile(bands), slice(c * LANES, (c + 1) * LANES)), *pair)
+
+
+def ice_late(g_ref, rd, ra, rb, nx, outer, h, vel, stress, wind, kept, p2_in, p1_in, p2, p1, fixed, *scratch):
+    g = g_ref[0]
+    state, rest = scratch[:5], scratch[5:]
+    ice_rows, cols = h.shape[1:]
+    regs = cols // LANES + 1
+    per = ice_rows // SUB
+    ext = per + 2
+    bands = per + 1
+    lane = lane_iota()
+    row = row_iota(LANES)
+    zero = jnp.zeros((SUB, LANES), F32)
+    count = 3
+    for k in range(p2.shape[0] // SUB):
+        p2[tile(k), :] = p2_in[tile(k), :]
+        p1[tile(k), :] = p1_in[tile(k), :]
+
+    def run(group):
+        first = 0 if group == 1 else ext - count
+        edge_tile = 0 if group == 1 else ext - 1
+        flow_of = (ra, rb) if group == 1 else (rb, ra)
+        outs = (p1, p2) if group == 1 else (p2, p1)
+
+        def load(cap, jj):
+            j = first + jj
+            own = own_ice(h, vel, stress, wind, cap)
+            if j == edge_tile:
+                fields = [late_tile(rd, cap * NICE + f, lane) for f in range(NICE)]
+            else:
+                fields = [
+                    split(own[f][tile(j - 1), :]) + [outer[tile((cap * NICE + f) * per + j - 1), :]]
+                    for f in range(NICE)
+                ]
+            for comp in range(2):
+                n = comp * ext + j
+                edge = wide_outer(nx[3 * cap, tile(n // WIDE_SLOTS), :], n % WIDE_SLOTS, lane)
+                fields.append(split(flow_of[cap][tile(n), :]) + [edge])
+            return fields
+
+        ice_core(count, load, state, rest, lane)
+        for cap in range(2):
+            d0, d1 = drag_tile(state, rest, cap, 1)
+            turned = turned_prev(d1, lane)
+            bits = []
+            for c in range(regs):
+                across = d1[c] - turned[c]
+                if group == 1:
+                    here = (d0[c] - from_prev_row(d0[c], zero, row)) + across
+                    change = jnp.where(row == 0, pltpu.roll(kept[0, cap, c] - d0[c], 1, 0), 0.0)
+                    bits.append((here, change))
+                else:
+                    here = (d0[c] - from_prev_row(d0[c], kept[1, cap, c], row)) + across
+                    bits.append((here, jnp.where(row == 0, -pltpu.roll(d0[c], 1, 0), 0.0)))
+                if c + 1 < regs:
+                    cut = slice(c * LANES, (c + 1) * LANES)
+                    p, q = state[2][cap, c, at(1), :], state[3][cap, c, at(1), :]
+                    fixed[cap, 0, :, cut] = state[0][cap, c, at(1), :]
+                    fixed[cap, 1, :, cut] = state[1][cap, c, at(1), :]
+                    fixed[cap, 2, :, cut] = p + q
+                    fixed[cap, 3, :, cut] = p - q
+                    fixed[cap, 4, :, cut] = state[4][cap, c, at(1), :]
+            out = outs[cap]
+            k = 0 if group == 1 else per - 1
+            for c in range(regs - 1):
+                cut = slice(c * LANES, (c + 1) * LANES)
+                out[tile(k), cut] = bits[c][0]
+                out[tile(k + 1), cut] = out[tile(k + 1), cut] + bits[c][1] if group == 1 else bits[c][1]
+            for n, add in ((k, False), (k + 1, group == 1)):
+                c = n // WIDE_SLOTS
+                cut = slice(c * LANES, (c + 1) * LANES)
+                edge = packed_edge(bits[regs - 1][n - k], n, lane)
+                start = (2 * EDGE * (n % WIDE_SLOTS) - EDGE) % LANES
+                inside = (lane - start) % LANES < 2 * EDGE if start else lane < 2 * EDGE
+                old = out[tile(bands), cut]
+                out[tile(bands), cut] = old + edge if add else jnp.where(inside, edge, old)
+
+    @pl.when(g == 1)
+    def _():
+        run(1)
+
+    @pl.when(g == 2)
+    def _():
+        run(2)
+
+
+def ice_results(g_ref, u_s, v_s, p_s, q_s, s_s, fixed, vel_out, stress_out):
+    g = g_ref[0]
+    per = vel_out.shape[2] // SUB
+    regs = u_s.shape[1]
+    for cap in range(2):
+        for j in range(per):
+            for c in range(regs - 1):
+                cut = slice(c * LANES, (c + 1) * LANES)
+                p, q = p_s[cap, c, at(j + 1), :], q_s[cap, c, at(j + 1), :]
+                values = [u_s[cap, c, at(j + 1), :], v_s[cap, c, at(j + 1), :], p + q, p - q, s_s[cap, c, at(j + 1), :]]
+                if j == 0 or j == per - 1:
+                    late = g == (1 if j == 0 else 2)
+                    values = [jnp.where(late, fixed[cap, f, :, cut], value) for f, value in enumerate(values)]
+                for f, value in enumerate(values):
+                    if f < 2:
+                        vel_out[f, cap, tile(j), cut] = value
+                    else:
+                        stress_out[f - 2, cap, tile(j), cut] = value
 
 
 def neighbour_sum(ref, k, row):
@@ -575,7 +706,10 @@
 
         def field(i, ref):
             if j == 0 or j == ext - 1:
-                parts = low_high(g, ra, rc, rd, nx, 2 * NICE + i, lane, j == 0)
+                n = 2 * NICE + i
+                late = g == (1 if j == 0 else 2)
+                pairs = zip(late_tile(rd, n, lane), low_high(g, ra, rc, nx, n, lane, j == 0))
+                parts = [jnp.where(late, x, y) for x, y in pairs]
             else:
                 parts = [ref[tile(j - 1), :], outer[tile(ocean_first + i * per + j - 1), :]]
             return jnp.concatenate(parts, axis=1)
@@ -796,20 +930,32 @@
         [(own * SUB, LANES), (groups, narrow_rows, LANES), ((2 * NICE + NOC) * SUB + tail, cols)],
         [g, from_left, from_right, h, gf, base_rhs, ssh_prev, ice_vel, ice_stress, wind],
     )
+    nx = lax.all_to_all(narrow, "grp", 0, 0, tiled=True)
+    d, nx = lax.optimization_barrier((d, nx))
     rd = lax.ppermute(d, "grp", [(0, 1), (3, 2)])
-    nx = lax.all_to_all(narrow, "grp", 0, 0, tiled=True)
 
     back = (ice_rows + 2 * SUB, cols)
-    velocity, stress, p3, p2, p1, mine = call(
+    regs = cols // LANES + 1
+    held = (2, regs, slab + 2 * SUB, LANES)
+    *state, p3, p2, p1, mine, kept = call(
         ice_steps,
-        [ice_vel.shape, ice_stress.shape, back, back, back, back],
-        [g, ra, rb, rc, rd, nx, outer, h, ice_vel, ice_stress, wind, currents],
-        scratch=[(2, cols // LANES + 1, slab + 2 * SUB, LANES)] * 16,
+        [held] * 5 + [back] * 4 + [(2, 2, regs, SUB, LANES)],
+        [g, ra, rb, rc, nx, outer, h, ice_vel, ice_stress, wind, currents],
+        scratch=[held] * 11,
         mib=32,
+        flops=20000000,
+    )
+    p2, p1, fixed = call(
+        ice_late,
+        [back, back, (2, 5, SUB, cols)],
+        [g, rd, ra, rb, nx, outer, h, ice_vel, ice_stress, wind, kept, p2, p1],
+        scratch=[(2, regs, 5 * SUB, LANES)] * 16,
+        flops=20000000,
     )
     r3 = lax.ppermute(p3, "grp", [(3, 0), (0, 3)])
     r2 = lax.ppermute(p2, "grp", [(2, 0), (1, 3)])
     r1 = lax.ppermute(p1, "grp", [(1, 0), (2, 3), (3, 1), (0, 2)])
+    velocity, stress = call(ice_results, [ice_vel.shape, ice_stress.shape], [g, *state, fixed], flops=10000000)
 
     ocean_rows = rows + 2 * SUB
     field = (ocean_rows, wide)

time: 77.1 us -> 84.6 us (1.097)
  blocking collectives: 32.9 us -> 8.41 us
  waiting for transfers between devices: 9.08 us -> 32.3 us
  starting transfers between devices: 17.5 us -> 21.6 us
  local copies, waits for them, and re-layouts: 0.76 us -> 4.46 us
    all_to_all x1 -> x0, blocking collectives: 16.2 us -> none  [shards(): lax.all_to_all(jnp.broadcast_to(sums[None], (devices, 1, LANES)), ('grp',...]
    ppermute x1, waiting for transfers between devices: 0.01 us -> 8.94 us  [shards(): rc = lax.ppermute(c, 'grp', [(0, 3), (3, 0), (1, 2), (2, 1)])]
    ppermute x1, waiting for transfers between devices: 0.01 us -> 8.66 us  [shards(): ra = lax.ppermute(a, 'grp', [(0, 1), (1, 0), (2, 3), (3, 2)])]
    all_to_all x1, blocking collectives: 16.6 us -> 8.41 us  [shards(): nx = lax.all_to_all(narrow, 'grp', 0, 0, tiled=True)]
    all_to_all x0 -> x1, starting transfers between devices: none -> 5.03 us  [shards(): lax.all_to_all(jnp.broadcast_to(sums[None], (devices, 1, LANES)), ('grp',...]
    unnamed x20 -> x32, local copies, waits for them, and re-layouts: 0.75 us -> 3.84 us
    all_to_all x0 -> x1, waiting for transfers between devices: none -> 2.9 us  [shards(): lax.all_to_all(jnp.broadcast_to(sums[None], (devices, 1, LANES)), ('grp',...]
    ppermute x1, waiting for transfers between devices: 2.33 us -> 4.14 us  [shards(): r3 = lax.ppermute(p3, 'grp', [(3, 0), (0, 3)])]
  transfers between devices with their start and end apart: 9 -> 10, of which waited for: 3 -> 7; matrix products, arithmetic and copies ran while one was open for 0% -> 0% of each run, Pallas kernels for 1% -> 13%
where the time goes in v6:
time: 84.6 us; the launch traced here: 84.2 us
  waiting for transfers between devices  32.3 us (38%)
  starting transfers between devices  21.6 us (26%)
  Pallas kernels  16.4 us (19%)
  blocking collectives  8.41 us (10%)
  local copies, waits for them, and re-layouts  4.46 us (5%)
  between operations  0.95 us (1%)
    pallas_call x9, Pallas kernels, call(): pl.pallas_call(body, out_shape=shapes, in_specs=specs, out_specs=tuple((v...  16.4 us
    ppermute x1, waiting for transfers between devices, shards(): rc = lax.ppermute(c, 'grp', [(0, 3), (3, 0), (1, 2), (2, 1)])  8.94 us
    ppermute x1, waiting for transfers between devices, shards(): ra = lax.ppermute(a, 'grp', [(0, 1), (1, 0), (2, 3), (3, 2)])  8.66 us
    all_to_all x1, blocking collectives, shards(): nx = lax.all_to_all(narrow, 'grp', 0, 0, tiled=True)  8.41 us
    all_to_all x1, starting transfers between devices, shards(): lax.all_to_all(jnp.broadcast_to(sums[None], (devices, 1, LANES)), ('grp',...  5.03 us
    ppermute x1, waiting for transfers between devices, shards(): r3 = lax.ppermute(p3, 'grp', [(3, 0), (0, 3)])  4.14 us
    ppermute x1, waiting for transfers between devices, shards(): lax.ppermute(left, 'tile', [(i + 1, i) for i in range(tiles - 1)])  4.13 us
    ppermute x1, starting transfers between devices, shards(): rb = lax.ppermute(b, 'grp', [(0, 2), (3, 1)])  3.86 us
  transfers between devices with their start and end apart: 10, of which 7 were waited for; matrix products, arithmetic and copies ran while one was open for 0% of the time, Pallas kernels for 13%

profile of v6, /device:TPU:0, one launch (start us, length us, event | category | flops | bytes accessed | tf_op | source)
XLA Modules:
  0.0 84.2 jit_solution(17572540917243366718)
XLA Ops:
  0.6 0.0 copy-start
  0.6 0.0 copy-start.1
  0.7 0.0 copy-start.2
  0.7 0.0 copy-start.3
  0.7 0.0 copy-start.4
  0.7 1.8 %shard_map.121 = (f32[160,512]{1,0:T(8,128)S(1)}, f32[160,512]{1,0:T(8,128)S(1)}, f32[160,512]{1,0:T(8,128)S(1)}, f32[8,128]{1,0:T(8,128)S(1)}) custom-call(s32[1]{0:T(128)} %bitcast.g_ref, f32[256,512]{1,0:T(8,128)} %base.7, f32[256,512]{1,0:T(8,128)} %depth.3, f32[256,512]{1,0:T(8,128)} %x0.9, f32[2,256,512]{2,1,0:T(8,128)} %cur.5, s32[32,64]{1,0:T(8,128)} %land.3, ...), custom_call_target="tpu_custom_call" | custom-call | flops 1000000 | bytes 4000000 | tf_op jit(solution)/shard_map/pallas_call | solution.py:46
  2.6 0.0 copy-done.3
  2.6 0.3 copy-done.4
  3.0 0.1 copy-done.5
  3.1 0.2 copy-done.6
  3.3 0.1 copy-done.7
  3.3 0.0 copy-done.15
  3.3 0.4 shard_map.122
  3.8 2.4 %collective-permute-start.2 = (f32[288,128]{1,0:T(8,128)S(1)}, f32[288,128]{1,0:T(8,128)S(1)}, u32[]{:S(2)}, u32[]{:S(2)}) collective-permute-start(f32[288,128]{1,0:T(8,128)S(1)} %get-tuple-element.41), channel_id=1, source_target_pairs={{0,1},{1,2},{2,3},{3,4},{4,5},{5,6},{6,7},{8,9},{9,10},{10,11},{11... | collective-permute-start | bytes 442376 | tf_op jit(solution)/shard_map/ppermute | solution.py:923
  6.2 1.3 %collective-permute-start.3 = (f32[288,128]{1,0:T(8,128)S(1)}, f32[288,128]{1,0:T(8,128)S(1)}, u32[]{:S(2)}, u32[]{:S(2)}) collective-permute-start(f32[288,128]{1,0:T(8,128)S(1)} %get-tuple-element.42), channel_id=1, source_target_pairs={{1,0},{2,1},{3,2},{4,3},{5,4},{6,5},{7,6},{9,8},{10,9},{11,10},{12... | collective-permute-start | bytes 442376 | tf_op jit(solution)/shard_map/ppermute | solution.py:924
  7.5 0.0 collective-permute-done.2.from_left
  7.5 4.1 %collective-permute-done.3.from_right = f32[288,128]{1,0:T(8,128)S(1)} collective-permute-done((f32[288,128]{1,0:T(8,128)S(1)}, f32[288,128]{1,0:T(8,128)S(1)}, u32[]{:S(2)}, u32[]{:S(2)}) %collective-permute-start.3) | collective-permute-done | bytes 147488 | tf_op jit(solution)/shard_map/ppermute | solution.py:924
  11.6 0.5 shard_map.123
  12.1 8.4 %all_to_all.10.nx = f32[4,40,128]{2,1,0:T(8,128)S(1)} all-to-all(f32[4,40,128]{2,1,0:T(8,128)S(1)} %get-tuple-element.46), channel_id=1, replica_groups=mesh['grp'=4,'tile'=8] {'grp'}, dimensions={0} | all-to-all | bytes 163840 | tf_op jit(solution)/shard_map/all_to_all | solution.py:933
  20.5 2.7 %collective-permute-start.4 = (f32[168,512]{1,0:T(8,128)S(1)}, f32[168,512]{1,0:T(8,128)S(1)}, u32[]{:S(2)}, u32[]{:S(2)}) collective-permute-start(f32[168,512]{1,0:T(8,128)S(1)} %get-tuple-element.47), channel_id=1, source_target_pairs={{0,8},{24,16},{1,9},{25,17},{2,10},{26,18},{3,11},{27,19},{4,12},{... | collective-permute-start | bytes 1032200 | tf_op jit(solution)/shard_map/ppermute | solution.py:935
  23.2 0.1 collective-permute-start
  23.3 1.5 %collective-permute-start.1 = (f32[160,512]{1,0:T(8,128)S(1)}, f32[160,512]{1,0:T(8,128)S(1)}, u32[]{:S(2)}, u32[]{:S(2)}) collective-permute-start(f32[160,512]{1,0:T(8,128)S(1)} %get-tuple-element.39), channel_id=1, source_target_pairs={{0,24},{24,0},{8,16},{16,8},{1,25},{25,1},{9,17},{17,9},{2,26},{26... | collective-permute-start | bytes 983048 | tf_op jit(solution)/shard_map/ppermute | solution.py:911
  24.8 3.9 %collective-permute-start.5 = (f32[160,512]{1,0:T(8,128)S(1)}, f32[160,512]{1,0:T(8,128)S(1)}, u32[]{:S(2)}, u32[]{:S(2)}) collective-permute-start(f32[160,512]{1,0:T(8,128)S(1)} %get-tuple-element.53), channel_id=1, source_target_pairs={{0,16},{24,8},{1,17},{25,9},{2,18},{26,10},{3,19},{27,11},{4,20},{... | collective-permute-start | bytes 983048 | tf_op jit(solution)/shard_map/ppermute | solution.py:913
  28.7 8.7 %collective-permute-done.ra = f32[160,512]{1,0:T(8,128)S(1)} collective-permute-done((f32[160,512]{1,0:T(8,128)S(1)}, f32[160,512]{1,0:T(8,128)S(1)}, u32[]{:S(2)}, u32[]{:S(2)}) %collective-permute-start) | collective-permute-done | bytes 327712 | tf_op jit(solution)/shard_map/ppermute | solution.py:912
  37.3 8.9 %collective-permute-done.1.rc = f32[160,512]{1,0:T(8,128)S(1)} collective-permute-done((f32[160,512]{1,0:T(8,128)S(1)}, f32[160,512]{1,0:T(8,128)S(1)}, u32[]{:S(2)}, u32[]{:S(2)}) %collective-permute-start.1) | collective-permute-done | bytes 327712 | tf_op jit(solution)/shard_map/ppermute | solution.py:911
  46.3 0.0 collective-permute-done.5.rb
  46.3 9.0 %shard_map.125 = (f32[2,5,96,128]{3,2,1,0:T(8,128)S(1)}, f32[2,5,96,128]{3,2,1,0:T(8,128)S(1)}, f32[2,5,96,128]{3,2,1,0:T(8,128)S(1)}, f32[2,5,96,128]{3,2,1,0:T...) custom-call(s32[1]{0:T(128)} %bitcast.g_ref, ...), custom_call_target="tpu_custom_call" | custom-call | flops 20000000 | bytes 4000000 | tf_op jit(solution)/shard_map/pallas_call | solution.py:46
  55.3 0.0 copy-start.8
  55.3 0.0 copy-start.10
  55.3 0.0 copy-start.12
  55.3 3.4 %collective-permute-start.8 = (f32[80,512]{1,0:T(8,128)S(1)}, f32[80,512]{1,0:T(8,128)S(1)}, u32[]{:S(2)}, u32[]{:S(2)}) collective-permute-start(f32[80,512]{1,0:T(8,128)S(1)} %get-tuple-element.59), channel_id=1, source_target_pairs={{24,0},{0,24},{25,1},{1,25},{26,2},{2,26},{27,3},{3,27},{28,4},{4,... | collective-permute-start | bytes 491528 | tf_op jit(solution)/shard_map/ppermute | solution.py:955
  58.7 0.0 collective-permute-done.4.rd
  58.8 0.1 collective-permute-start.6
  58.9 1.3 %collective-permute-start.7 = (f32[80,512]{1,0:T(8,128)S(1)}, f32[80,512]{1,0:T(8,128)S(1)}, u32[]{:S(2)}, u32[]{:S(2)}) collective-permute-start(f32[80,512]{1,0:T(8,128)S(1)} %get-tuple-element.58), channel_id=1, source_target_pairs={{16,0},{8,24},{17,1},{9,25},{18,2},{10,26},{19,3},{11,27},{20,4},{... | collective-permute-start | bytes 491528 | tf_op jit(solution)/shard_map/ppermute | solution.py:956
  60.2 0.8 shard_map.124
  61.0 4.1 %collective-permute-done.8.r3 = f32[80,512]{1,0:T(8,128)S(1)} collective-permute-done((f32[80,512]{1,0:T(8,128)S(1)}, f32[80,512]{1,0:T(8,128)S(1)}, u32[]{:S(2)}, u32[]{:S(2)}) %collective-permute-start.8) | collective-permute-done | bytes 163872 | tf_op jit(solution)/shard_map/ppermute | solution.py:955
  65.1 0.7 collective-permute-done.6.r1
  65.8 2.9 %collective-permute-done.7.r2 = f32[80,512]{1,0:T(8,128)S(1)} collective-permute-done((f32[80,512]{1,0:T(8,128)S(1)}, f32[80,512]{1,0:T(8,128)S(1)}, u32[]{:S(2)}, u32[]{:S(2)}) %collective-permute-start.7) | collective-permute-done | bytes 163872 | tf_op jit(solution)/shard_map/ppermute | solution.py:956
  68.7 1.6 %shard_map.127 = (f32[256,512]{1,0:T(8,128)S(1)}, f32[256,512]{1,0:T(8,128)S(1)}, f32[256,512]{1,0:T(8,128)S(1)}, f32[1,128]{1,0:T(1,128)S(1)}) custom-call(s32[1]{0:T(128)} %bitcast.g_ref, f32[272,640]{1,0:T(8,128)S(1)} %get-tuple-element.50.gw, f32[272,640]{1,0:T(8,128)S(1)} %get-tuple-element.51.invd, f32[272,640]{1,0:T(8,128)S(1)} %get-tuple-element.52.ra, ...), custom_call_target="tpu_custom_call" | custom-call | flops 1000000 | bytes 4000000 | tf_op jit(solution)/shard_map/pallas_call | solution.py:46
  70.3 0.6 broadcast_in_dim.9
  70.9 5.0 %all-to-all-start.1 = ((f32[32,1,128]{2,1,0:T(1,128)}), f32[32,1,128]{2,1,0:T(1,128)S(1)}, u32[]{:S(2)}, u32[]{:S(2)}) async-start(f32[32,1,128]{2,1,0:T(1,128)} %broadcast_in_dim.9), calls=%async_computation.1 | async-start | bytes 32768 | tf_op jit(solution)/shard_map/all_to_all | solution.py:977
  75.9 0.0 copy-start.9
  75.9 1.0 %copy-done.9 = f32[2,5,96,128]{3,2,1,0:T(8,128)S(1)} copy-done((f32[2,5,96,128]{3,2,1,0:T(8,128)S(1)}, f32[2,5,96,128]{3,2,1,0:T(8,128)}, u32[]{:S(2)}) %copy-start.9) | copy-done | bytes 491544
  77.0 1.0 %copy-done.11 = f32[2,5,96,128]{3,2,1,0:T(8,128)S(1)} copy-done((f32[2,5,96,128]{3,2,1,0:T(8,128)S(1)}, f32[2,5,96,128]{3,2,1,0:T(8,128)}, u32[]{:S(2)}) %copy-start.11) | copy-done | bytes 491544
  78.0 1.0 %copy-done.13 = f32[2,5,96,128]{3,2,1,0:T(8,128)S(1)} copy-done((f32[2,5,96,128]{3,2,1,0:T(8,128)S(1)}, f32[2,5,96,128]{3,2,1,0:T(8,128)}, u32[]{:S(2)}) %copy-start.13) | copy-done | bytes 491544
  79.0 1.2 %shard_map.129 = (f32[2,2,64,512]{3,2,1,0:T(8,128)}, f32[3,2,64,512]{3,2,1,0:T(8,128)}) custom-call(s32[1]{0:T(128)} %bitcast.g_ref, f32[2,5,96,128]{3,2,1,0:T(8,128)S(1)} %get-tuple-element.65.u_s, f32[2,5,96,128]{3,2,1,0:T(8,128)S(1)} %get-tuple-element.66.v_s, f32[2,5,96,128]{3,2,1,0:T(8,128)S(1)} %copy-done.9, f32[2,5,96,128]{3,2,1,0:T(8,128)S(1)} %copy-done.11, ...), custom_call_target="tpu_custom_call" | custom-call | flops 10000000 | bytes 4000000 | tf_op jit(solution)/shard_map/pallas_call | solution.py:46
  80.2 2.9 %all-to-all-done.1.parts = f32[32,1,128]{2,1,0:T(1,128)S(1)} async-done(((f32[32,1,128]{2,1,0:T(1,128)}), f32[32,1,128]{2,1,0:T(1,128)S(1)}, u32[]{:S(2)}, u32[]{:S(2)}) %all-to-all-start.1) | async-done | bytes 16416 | tf_op jit(solution)/shard_map/all_to_all | solution.py:977
  83.1 1.1 %shard_map.128 = f32[256,512]{1,0:T(8,128)} custom-call(s32[1]{0:T(128)} %bitcast.g_ref, f32[32,1,128]{2,1,0:T(1,128)S(1)} %all-to-all-done.1.parts, f32[256,512]{1,0:T(8,128)S(1)} %copy-done.3, f32[256,512]{1,0:T(8,128)S(1)} %get-tuple-element.62.y0, f32[256,512]{1,0:T(8,128)S(1)} %get-tuple-element.63.y1, f32[256,512]{1,0:T(8,128)S(1)} %get-tuple-element.64.y2), custom_call_target="tpu_custom_call" | custom-call | flops 1000000 | bytes 4000000 | tf_op jit(solution)/shard_map/pallas_call | solution.py:46
  (15 shorter events, 0.1 us)
Async XLA Ops:
  0.6 2.0 %copy-start = (f32[3,2,64,512]{3,2,1,0:T(8,128)S(1)}, f32[3,2,64,512]{3,2,1,0:T(8,128)}, u32[]{:S(2)}) copy-start(f32[3,2,64,512]{3,2,1,0:T(8,128)} %stress.9) | copy-start | bytes 2359300
  0.6 2.0 %copy-start.1 = (f32[2,2,64,512]{3,2,1,0:T(8,128)S(1)}, f32[2,2,64,512]{3,2,1,0:T(8,128)}, u32[]{:S(2)}) copy-start(f32[2,2,64,512]{3,2,1,0:T(8,128)} %vel.9) | copy-start | bytes 1572868
  0.7 2.0 %copy-start.2 = (f32[2,2,64,512]{3,2,1,0:T(8,128)S(1)}, f32[2,2,64,512]{3,2,1,0:T(8,128)}, u32[]{:S(2)}) copy-start(f32[2,2,64,512]{3,2,1,0:T(8,128)} %wind.9) | copy-start | bytes 1572868
  0.7 2.0 %copy-start.3 = (f32[256,512]{1,0:T(8,128)S(1)}, f32[256,512]{1,0:T(8,128)}, u32[]{:S(2)}) copy-start(f32[256,512]{1,0:T(8,128)} %x0.9) | copy-start | bytes 1572868
  0.7 2.3 %copy-start.4 = (f32[2,256,512]{2,1,0:T(8,128)S(1)}, f32[2,256,512]{2,1,0:T(8,128)}, u32[]{:S(2)}) copy-start(f32[2,256,512]{2,1,0:T(8,128)} %cur.5) | copy-start | bytes 3145732
  0.7 2.4 %copy-start.5 = (f32[256,512]{1,0:T(8,128)S(1)}, f32[256,512]{1,0:T(8,128)}, u32[]{:S(2)}) copy-start(f32[256,512]{1,0:T(8,128)} %base.7) | copy-start | bytes 1572868
  0.7 2.6 %copy-start.6 = (f32[256,512]{1,0:T(8,128)S(1)}, f32[256,512]{1,0:T(8,128)}, u32[]{:S(2)}) copy-start(f32[256,512]{1,0:T(8,128)} %depth.3) | copy-start | bytes 1572868
  0.7 2.6 %copy-start.7 = (f32[2,64,512]{2,1,0:T(8,128)S(1)}, f32[2,64,512]{2,1,0:T(8,128)}, u32[]{:S(2)}) copy-start(f32[2,64,512]{2,1,0:T(8,128)} %thick.3) | copy-start | bytes 786436
  0.7 2.6 %copy-start.14 = (s32[32,64]{1,0:T(8,128)S(1)}, s32[32,64]{1,0:T(8,128)}, u32[]{:S(2)}) copy-start(s32[32,64]{1,0:T(8,128)} %land.3) | copy-start | bytes 24580
  0.7 2.6 %copy-start.15 = (s32[2,8,64]{2,1,0:T(8,128)S(1)}, s32[2,8,64]{2,1,0:T(8,128)}, u32[]{:S(2)}) copy-start(s32[2,8,64]{2,1,0:T(8,128)} %iceb.3) | copy-start | bytes 12292
  3.8 3.7 %collective-permute-start.2 = (f32[288,128]{1,0:T(8,128)S(1)}, f32[288,128]{1,0:T(8,128)S(1)}, u32[]{:S(2)}, u32[]{:S(2)}) collective-permute-start(f32[288,128]{1,0:T(8,128)S(1)} %get-tuple-element.41), channel_id=1, source_target_pairs={{0,1},{1,2},{2,3},{3,4},{4,5},{5,6},{6,7},{8,9},{9,10},{10,11},{11... | collective-permute-start | bytes 442376 | tf_op jit(solution)/shard_map/ppermute | solution.py:923
  6.2 5.4 %collective-permute-start.3 = (f32[288,128]{1,0:T(8,128)S(1)}, f32[288,128]{1,0:T(8,128)S(1)}, u32[]{:S(2)}, u32[]{:S(2)}) collective-permute-start(f32[288,128]{1,0:T(8,128)S(1)} %get-tuple-element.42), channel_id=1, source_target_pairs={{1,0},{2,1},{3,2},{4,3},{5,4},{6,5},{7,6},{9,8},{10,9},{11,10},{12... | collective-permute-start | bytes 442376 | tf_op jit(solution)/shard_map/ppermute | solution.py:924
  20.5 38.2 %collective-permute-start.4 = (f32[168,512]{1,0:T(8,128)S(1)}, f32[168,512]{1,0:T(8,128)S(1)}, u32[]{:S(2)}, u32[]{:S(2)}) collective-permute-start(f32[168,512]{1,0:T(8,128)S(1)} %get-tuple-element.47), channel_id=1, source_target_pairs={{0,8},{24,16},{1,9},{25,17},{2,10},{26,18},{3,11},{27,19},{4,12},{... | collective-permute-start | bytes 1032200 | tf_op jit(solution)/shard_map/ppermute | solution.py:935
  23.2 14.1 %collective-permute-start = (f32[160,512]{1,0:T(8,128)S(1)}, f32[160,512]{1,0:T(8,128)S(1)}, u32[]{:S(2)}, u32[]{:S(2)}) collective-permute-start(f32[160,512]{1,0:T(8,128)S(1)} %get-tuple-element.38), channel_id=1, source_target_pairs={{0,8},{8,0},{16,24},{24,16},{1,9},{9,1},{17,25},{25,17},{2,10},{10... | collective-permute-start | bytes 983048 | tf_op jit(solution)/shard_map/ppermute | solution.py:912
  23.3 23.0 %collective-permute-start.1 = (f32[160,512]{1,0:T(8,128)S(1)}, f32[160,512]{1,0:T(8,128)S(1)}, u32[]{:S(2)}, u32[]{:S(2)}) collective-permute-start(f32[160,512]{1,0:T(8,128)S(1)} %get-tuple-element.39), channel_id=1, source_target_pairs={{0,24},{24,0},{8,16},{16,8},{1,25},{25,1},{9,17},{17,9},{2,26},{26... | collective-permute-start | bytes 983048 | tf_op jit(solution)/shard_map/ppermute | solution.py:911
  24.8 21.5 %collective-permute-start.5 = (f32[160,512]{1,0:T(8,128)S(1)}, f32[160,512]{1,0:T(8,128)S(1)}, u32[]{:S(2)}, u32[]{:S(2)}) collective-permute-start(f32[160,512]{1,0:T(8,128)S(1)} %get-tuple-element.53), channel_id=1, source_target_pairs={{0,16},{24,8},{1,17},{25,9},{2,18},{26,10},{3,19},{27,11},{4,20},{... | collective-permute-start | bytes 983048 | tf_op jit(solution)/shard_map/ppermute | solution.py:913
  55.3 3.5 %copy-start.8 = (f32[2,5,96,128]{3,2,1,0:T(8,128)}, f32[2,5,96,128]{3,2,1,0:T(8,128)S(1)}, u32[]{:S(2)}) copy-start(f32[2,5,96,128]{3,2,1,0:T(8,128)S(1)} %get-tuple-element.67.p_s) | copy-start | bytes 1474564
  55.3 3.5 %copy-start.10 = (f32[2,5,96,128]{3,2,1,0:T(8,128)}, f32[2,5,96,128]{3,2,1,0:T(8,128)S(1)}, u32[]{:S(2)}) copy-start(f32[2,5,96,128]{3,2,1,0:T(8,128)S(1)} %get-tuple-element.68.q_s) | copy-start | bytes 1474564
  55.3 3.5 %copy-start.12 = (f32[2,5,96,128]{3,2,1,0:T(8,128)}, f32[2,5,96,128]{3,2,1,0:T(8,128)S(1)}, u32[]{:S(2)}) copy-start(f32[2,5,96,128]{3,2,1,0:T(8,128)S(1)} %get-tuple-element.69.s_s) | copy-start | bytes 1474564
  55.3 9.8 %collective-permute-start.8 = (f32[80,512]{1,0:T(8,128)S(1)}, f32[80,512]{1,0:T(8,128)S(1)}, u32[]{:S(2)}, u32[]{:S(2)}) collective-permute-start(f32[80,512]{1,0:T(8,128)S(1)} %get-tuple-element.59), channel_id=1, source_target_pairs={{24,0},{0,24},{25,1},{1,25},{26,2},{2,26},{27,3},{3,27},{28,4},{4,... | collective-permute-start | bytes 491528 | tf_op jit(solution)/shard_map/ppermute | solution.py:955
  58.8 7.0 %collective-permute-start.6 = (f32[80,512]{1,0:T(8,128)S(1)}, f32[80,512]{1,0:T(8,128)S(1)}, u32[]{:S(2)}, u32[]{:S(2)}) collective-permute-start(f32[80,512]{1,0:T(8,128)S(1)} %get-tuple-element.57), channel_id=1, source_target_pairs={{8,0},{16,24},{24,8},{0,16},{9,1},{17,25},{25,9},{1,17},{10,2},{18... | collective-permute-start | bytes 491528 | tf_op jit(solution)/shard_map/ppermute | solution.py:957
  58.9 9.9 %collective-permute-start.7 = (f32[80,512]{1,0:T(8,128)S(1)}, f32[80,512]{1,0:T(8,128)S(1)}, u32[]{:S(2)}, u32[]{:S(2)}) collective-permute-start(f32[80,512]{1,0:T(8,128)S(1)} %get-tuple-element.58), channel_id=1, source_target_pairs={{16,0},{8,24},{17,1},{9,25},{18,2},{10,26},{19,3},{11,27},{20,4},{... | collective-permute-start | bytes 491528 | tf_op jit(solution)/shard_map/ppermute | solution.py:956
  70.9 12.2 %all-to-all-start.1 = ((f32[32,1,128]{2,1,0:T(1,128)}), f32[32,1,128]{2,1,0:T(1,128)S(1)}, u32[]{:S(2)}, u32[]{:S(2)}) async-start(f32[32,1,128]{2,1,0:T(1,128)} %broadcast_in_dim.9), calls=%async_computation.1 | async-start | bytes 32768 | tf_op jit(solution)/shard_map/all_to_all | solution.py:977
  75.9 1.0 %copy-start.9 = (f32[2,5,96,128]{3,2,1,0:T(8,128)S(1)}, f32[2,5,96,128]{3,2,1,0:T(8,128)}, u32[]{:S(2)}) copy-start(f32[2,5,96,128]{3,2,1,0:T(8,128)} %copy-done.8) | copy-start | bytes 1474564
  77.0 1.0 %copy-start.11 = (f32[2,5,96,128]{3,2,1,0:T(8,128)S(1)}, f32[2,5,96,128]{3,2,1,0:T(8,128)}, u32[]{:S(2)}) copy-start(f32[2,5,96,128]{3,2,1,0:T(8,128)} %copy-done.10) | copy-start | bytes 1474564
  78.0 1.0 %copy-start.13 = (f32[2,5,96,128]{3,2,1,0:T(8,128)S(1)}, f32[2,5,96,128]{3,2,1,0:T(8,128)}, u32[]{:S(2)}) copy-start(f32[2,5,96,128]{3,2,1,0:T(8,128)} %copy-done.12) | copy-start | bytes 1474564

commit v7 on v6

--- a/solution.py
+++ b/solution.py
@@ -74,26 +74,33 @@
     return lax.broadcasted_iota(jnp.int32, (SUB, LANES), 1)
 
 
-def from_next_row(here, after, row):
-    return pltpu.roll(jnp.where(row == 0, after, here), SUB - 1, 0)
-
-
 def from_prev_row(here, before, row):
     return pltpu.roll(jnp.where(row == SUB - 1, before, here), 1, 0)
-
-
-def from_next_col(here):
-    return pltpu.roll(here, here.shape[1] - 1, 1)
-
-
-def from_prev_col(here):
-    return pltpu.roll(here, 1, 1)
 
 
 def own_tile(cur, comp, first, j):
     last = cur.shape[1] // SUB - 1
     t = jnp.clip(first + j, 0, last)
     return cur[comp, pl.ds(pl.multiple_of(t * SUB, SUB), SUB), :]
+
+
+def half_and_half(base, depth, last):
+    row = row_iota(base.shape[1])
+    return jnp.where(row >= SUB // 2 if last else row < SUB // 2, base, pltpu.roll(depth, SUB // 2, 0))
+
+
+def halved(value, which, last):
+    row = row_iota(value.shape[1])
+    value = pltpu.roll(value, SUB // 2, 0) if which else value
+    return jnp.where(row >= SUB // 2 if last else row < SUB // 2, value, 0.0)
+
+
+def strip_tile(ref, n, low):
+    if n < 2 * NICE:
+        return ref[tile(n), :]
+    if n == 2 * NICE + 2:
+        return ref[tile(2 * NICE + 1), :]
+    return halved(ref[tile(2 * NICE), :], n - 2 * NICE, low)
 
 
 def pack_rows(g_ref, base, depth, x0, cur, land, thick, iceb, vel, stress, wind,
@@ -116,12 +123,8 @@
             start = ice_rows * dest - SUB
             first, last = max(start, 0), min(start + slab, rows)
             for comp in range(2):
-                at = comp * slab + first - start
-                copy(cur.at[comp, first:last, :], out.at[at : at + last - first, :])
-                if first > start:
-                    out[comp * slab : at, :] = jnp.zeros((first - start, cols), F32)
-                if last < start + slab:
-                    out[at + last - first : (comp + 1) * slab, :] = jnp.zeros((start + slab - last, cols), F32)
+                begin = comp * (last - first)
+                copy(cur.at[comp, first:last, :], out.at[begin : begin + last - first, :])
         if halos:
             copy(land, land_s)
             copy(iceb, iceb_s)
@@ -137,10 +140,11 @@
                 for piece in pieces:
                     copy(piece, out.at[tile(n), :])
                     n += 1
-            copy(depth.at[ro, :], depth_s.at[i])
-            copy(base.at[ro, :], out.at[tile(2 * NICE), :])
-            copy(x0.at[ro, :], out.at[tile(2 * NICE + 2), :])
-            out[tile(2 * NICE + 3), :] = jnp.zeros((SUB, cols), F32)
+            copy(depth.at[ro, :], depth_s.at[i, 0])
+            copy(base.at[ro, :], depth_s.at[i, 1])
+            copy(x0.at[ro, :], out.at[tile(2 * NICE + 1), :])
+            for k in range(2 * NICE + 2, out.shape[0] // SUB):
+                out[tile(k), :] = jnp.zeros((SUB, cols), F32)
         for made in copies:
             made.wait()
         if halos:
@@ -151,7 +155,7 @@
                 k = covers[cap].shape[0] - 1 if last else 0
                 out[tile(cap * NICE), :] = thick_s[i, cap] * covers[cap][k : k + 1, :]
             k = wet.shape[0] - 1 if last else 0
-            out[tile(2 * NICE + 1), :] = depth_s[i] * wet[k : k + 1, :]
+            out[tile(2 * NICE), :] = half_and_half(depth_s[i, 1], depth_s[i, 0] * wet[k : k + 1, :], last)
 
     @pl.when(g == 0)
     def _():
@@ -286,9 +290,9 @@
             for ref in own_ice(h, vel, stress, wind, cap):
                 d[tile(n), :] = ref[r, :]
                 n += 1
-        for ref in (base, gf, x0):
-            d[tile(n), :] = ref[ro, :]
-            n += 1
+        d[tile(n), :] = half_and_half(base[ro, :], gf[ro, :], last)
+        d[tile(n + 1), :] = x0[ro, :]
+        n += 2
         per = cols // LANES
 
         def put(k, value):
@@ -333,21 +337,20 @@
     return jnp.where((lane < EDGE) | (lane >= LANES - EDGE), value, 0.0)
 
 
-def late_tile(rd, n, lane):
+def late_tile(rd, n, lane, low):
     per = rd.shape[1] // LANES
     k, i = n // WIDE_SLOTS, n % WIDE_SLOTS
-    tail = rd[tile(2 * NICE + NOC + k // per), (k % per) * LANES : (k % per + 1) * LANES]
-    return split(rd[tile(n), :]) + [wide_outer(tail, i, lane)]
+    tail = rd[tile(2 * NICE + 2 + k // per), (k % per) * LANES : (k % per + 1) * LANES]
+    return split(strip_tile(rd, n, low)) + [wide_outer(tail, i, lane)]
 
 
 def low_high(g, ra, rc, nx, n, lane, low):
     k, i = n // WIDE_SLOTS, n % WIDE_SLOTS
-    t = tile(n)
     pieces = [(2, rc, 1), (3, ra, 2)] if low else [(0, ra, 1), (1, rc, 2)]
     inner = jnp.zeros((SUB, ra.shape[1]), F32)
     packed = jnp.zeros((SUB, LANES), F32)
     for group, ref, source in pieces:
-        inner = jnp.where(g == group, ref[t, :], inner)
+        inner = jnp.where(g == group, strip_tile(ref, n, low), inner)
         packed = jnp.where(g == group, nx[source, tile(k), :], packed)
     return split(inner) + [wide_outer(packed, i, lane)]
 
@@ -503,15 +506,17 @@
         n = comp * ext + j
         t = tile(n)
         k, i = n // WIDE_SLOTS, n % WIDE_SLOTS
+        far = j - cap
+        diag = rc[tile(comp * (per + 1) + far), :] if 0 <= far <= per else jnp.zeros((SUB, cols), F32)
         here = jnp.clip(per * g - 1 + j, 0, rows // SUB - 1)
         own = own_tile(cur, comp, per * g - 1, j)
         spot = pl.multiple_of((flow_first + comp * (rows // SUB) + here) * SUB, SUB)
         own_outer = outer[pl.ds(spot, SUB), :]
         if cap == 0:
-            inner = jnp.where(g == 0, own, jnp.where(g == 1, ra[t, :], jnp.where(g == 2, rb[t, :], rc[t, :])))
+            inner = jnp.where(g == 0, own, jnp.where(g == 1, ra[t, :], jnp.where(g == 2, rb[t, :], diag)))
             edge = jnp.where(g == 0, own_outer, wide_outer(nx[0, tile(k), :], i, lane))
         else:
-            inner = jnp.where(g == 3, own, jnp.where(g == 2, ra[t, :], jnp.where(g == 1, rb[t, :], rc[t, :])))
+            inner = jnp.where(g == 3, own, jnp.where(g == 2, ra[t, :], jnp.where(g == 1, rb[t, :], diag)))
             edge = jnp.where(g == 3, own_outer, wide_outer(nx[3, tile(k), :], i, lane))
         return split(inner) + [edge]
 
@@ -604,7 +609,7 @@
             j = first + jj
             own = own_ice(h, vel, stress, wind, cap)
             if j == edge_tile:
-                fields = [late_tile(rd, cap * NICE + f, lane) for f in range(NICE)]
+                fields = [late_tile(rd, cap * NICE + f, lane, group == 1) for f in range(NICE)]
             else:
                 fields = [
                     split(own[f][tile(j - 1), :]) + [outer[tile((cap * NICE + f) * per + j - 1), :]]
@@ -682,77 +687,78 @@
                         stress_out[f - 2, cap, tile(j), cut] = value
 
 
-def neighbour_sum(ref, k, row):
-    here, before, after = ref[tile(k), :], ref[tile(k - 1), :], ref[tile(k + 1), :]
-    along = from_prev_row(here, before, row) + from_next_row(here, after, row)
-    return along + (from_prev_col(here) + from_next_col(here))
-
-
-def ocean_before(g_ref, ra, rc, rd, nx, outer, base, gf, x0, gw, invd, ra_out, g_s, gx_s, x_s, b_s):
+def neighbour_sums(ref, j, lane):
+    regs = ref.shape[0]
+    here = [ref[c, at(j), :] for c in range(regs)]
+    after, before = turned_next(here, lane), turned_prev(here, lane)
+    return [
+        (ref[c, at(j, -1), :] + ref[c, at(j, 1), :]) + (before[c] + after[c]) for c in range(regs)
+    ]
+
+
+def clear_ends(refs, count):
+    zero = jnp.zeros((SUB, LANES), F32)
+    for ref in refs:
+        for c in range(ref.shape[0]):
+            ref[c, at(-1), :] = zero
+            ref[c, at(count), :] = zero
+
+
+def ocean_before(g_ref, ra, rc, rd, nx, outer, base, gf, x0, g_s, invd, ra_out, gx_s, x_s, b_s):
     g = g_ref[0]
     rows, cols = base.shape
-    wide = cols + LANES
+    regs = cols // LANES + 1
     per = rows // SUB
     ext = per + 2
     lane = lane_iota()
-    row = row_iota(wide)
-    zero = jnp.zeros((SUB, wide), F32)
     ocean_first = (outer.shape[0] // SUB - 2 * per) - NOC * per
-    for ref in (g_s, gx_s):
-        ref[tile(0), :] = zero
-        ref[tile(ext + 1), :] = zero
+    clear_ends((g_s, gx_s), ext)
     for j in range(ext):
-        t = tile(j + 1)
 
         def field(i, ref):
             if j == 0 or j == ext - 1:
                 n = 2 * NICE + i
                 late = g == (1 if j == 0 else 2)
-                pairs = zip(late_tile(rd, n, lane), low_high(g, ra, rc, nx, n, lane, j == 0))
-                parts = [jnp.where(late, x, y) for x, y in pairs]
-            else:
-                parts = [ref[tile(j - 1), :], outer[tile(ocean_first + i * per + j - 1), :]]
-            return jnp.concatenate(parts, axis=1)
-
-        b_s[tile(j), :] = field(0, base)
-        depth = field(1, gf)
-        x = field(2, x0)
-        g_s[t, :] = depth
-        gx_s[t, :] = depth * x
-        x_s[tile(j), :] = x
-        gw[tile(j), :] = depth
+                pairs = zip(late_tile(rd, n, lane, j == 0), low_high(g, ra, rc, nx, n, lane, j == 0))
+                return [jnp.where(late, x, y) for x, y in pairs]
+            return split(ref[tile(j - 1), :]) + [outer[tile(ocean_first + i * per + j - 1), :]]
+
+        for c, (b, depth, x) in enumerate(zip(field(0, base), field(1, gf), field(2, x0))):
+            b_s[c, at(j), :] = b
+            g_s[c, at(j), :] = depth
+            gx_s[c, at(j), :] = depth * x
+            x_s[c, at(j), :] = x
     for j in range(ext):
-        t = tile(j)
-        depth = g_s[tile(j + 1), :]
-        diag = DAMP + depth * neighbour_sum(g_s, j + 1, row)
-        invd[t, :] = 1.0 / diag
-        around = depth * neighbour_sum(gx_s, j + 1, row)
-        ra_out[t, :] = jnp.where(depth > 0.0, b_s[t, :], 0.0) - (diag * x_s[t, :] - around)
+        around, products = neighbour_sums(g_s, j, lane), neighbour_sums(gx_s, j, lane)
+        for c in range(regs):
+            depth = g_s[c, at(j), :]
+            diag = DAMP + depth * around[c]
+            invd[c, at(j), :] = 1.0 / diag
+            known = jnp.where(depth > 0.0, b_s[c, at(j), :], 0.0)
+            ra_out[c, at(j), :] = known - (diag * x_s[c, at(j), :] - depth * products[c])
 
 
 def ocean_basis(g_ref, gw, invd, ra, r1, r2, r3, mine, y0_out, y1_out, y2_out, sums,
                 sp, u0_s, u1_s, u2_s):
     g = g_ref[0]
-    wide = gw.shape[1]
-    ext = gw.shape[0] // SUB
-    cols = y0_out.shape[1]
+    regs = gw.shape[0]
+    ext = gw.shape[1] // SUB - 2
     slab = r1.shape[0] // SUB - 2
     lane = lane_iota()
-    row = row_iota(wide)
-    zero = jnp.zeros((SUB, wide), F32)
+    zero = jnp.zeros((SUB, LANES), F32)
+    clear_ends((u0_s, u1_s, u2_s), ext)
 
     def strip(ref, k):
         n, i = k // WIDE_SLOTS, k % WIDE_SLOTS
-        edge = wide_outer(ref[tile(slab + 1), n * LANES : (n + 1) * LANES], i, lane)
-        return jnp.concatenate([ref[tile(k), :], edge], axis=1)
-
-    for ref in (u0_s, u1_s, u2_s):
-        ref[tile(0), :] = zero
-        ref[tile(ext + 1), :] = zero
+        return split(ref[tile(k), :]) + [wide_outer(ref[tile(slab + 1), n * LANES : (n + 1) * LANES], i, lane)]
+
+    def put(j, values):
+        for c in range(regs):
+            sp[c, at(j), :] = values[c]
 
     def clear(which):
         for j in which:
-            sp[tile(j), :] = zero
+            put(j, [zero] * regs)
 
     def whole(slabs):
         clear([0])
@@ -760,10 +766,12 @@
         for k, ref in enumerate(slabs):
             values = [strip(ref, t) for t in range(slab + 1)]
             for t in range(slab):
-                value = values[t] if t or over is None else values[t] + over
-                sp[tile(1 + slab * k + t), :] = value
+                value = values[t]
+                if t == 0 and over is not None:
+                    value = [x + y for x, y in zip(value, over)]
+                put(1 + slab * k + t, value)
             over = values[slab]
-        sp[tile(1 + slab * len(slabs)), :] = over
+        put(1 + slab * len(slabs), over)
 
     @pl.when(g == 0)
     def _():
@@ -776,57 +784,53 @@
     @pl.when(g == 1)
     def _():
         clear(range(2, ext))
-        sp[tile(0), :] = strip(r1, slab - 1)
-        sp[tile(1), :] = strip(r1, slab)
+        put(0, strip(r1, slab - 1))
+        put(1, strip(r1, slab))
 
     @pl.when(g == 2)
     def _():
         clear(range(ext - 1))
-        sp[tile(ext - 1), :] = strip(r1, 0)
-
-    acc = [jnp.zeros((SUB, cols), F32) for _ in range(6)]
-
-    def add(k, left, right, j):
-        if 0 < j < ext - 1:
-            acc[k] = acc[k] + left[:, :cols] * right[:, :cols]
+        put(ext - 1, strip(r1, 0))
+
+    acc = [[zero] * (regs - 1) for _ in range(6)]
+
+    def add(k, c, left, right):
+        acc[k][c] = acc[k][c] + left * right
 
     for j in range(ext):
-        t = tile(j)
-        depth = gw[t, :]
-        r0 = ra[t, :] + jnp.where(depth > 0.0, sp[t, :], 0.0)
-        y0 = r0 * invd[t, :]
-        u0_s[tile(j + 1), :] = depth * y0
-        if 0 < j < ext - 1:
-            y0_out[tile(j - 1), :] = y0[:, :cols]
-        add(0, r0, y0, j)
-    for j in range(ext):
-        t = tile(j)
-        depth = gw[t, :]
-        w = depth * neighbour_sum(u0_s, j + 1, row)
-        y1 = w * invd[t, :]
-        u1_s[tile(j + 1), :] = depth * y1
-        if 0 < j < ext - 1:
-            y1_out[tile(j - 1), :] = y1[:, :cols]
-            acc[1] = acc[1] + y0_out[tile(j - 1), :] * w[:, :cols]
-        add(2, w, y1, j)
-    for j in range(ext):
-        t = tile(j)
-        depth = gw[t, :]
-        w = depth * neighbour_sum(u1_s, j + 1, row)
-        y2 = w * invd[t, :]
-        u2_s[tile(j + 1), :] = depth * y2
-        if 0 < j < ext - 1:
-            y2_out[tile(j - 1), :] = y2[:, :cols]
-            acc[3] = acc[3] + y1_out[tile(j - 1), :] * w[:, :cols]
-        add(4, w, y2, j)
+        inside = 0 < j < ext - 1
+        for c in range(regs):
+            depth = gw[c, at(j), :]
+            r0 = ra[c, at(j), :] + jnp.where(depth > 0.0, sp[c, at(j), :], 0.0)
+            y0 = r0 * invd[c, at(j), :]
+            u0_s[c, at(j), :] = depth * y0
+            if inside and c + 1 < regs:
+                y0_out[c, tile(j - 1), :] = y0
+                add(0, c, r0, y0)
+    for level, (source, target, before, here) in enumerate(
+        ((u0_s, u1_s, y0_out, y1_out), (u1_s, u2_s, y1_out, y2_out))
+    ):
+        for j in range(ext):
+            inside = 0 < j < ext - 1
+            around = neighbour_sums(source, j, lane)
+            for c in range(regs):
+                depth = gw[c, at(j), :]
+                w = depth * around[c]
+                y = w * invd[c, at(j), :]
+                target[c, at(j), :] = depth * y
+                if inside and c + 1 < regs:
+                    here[c, tile(j - 1), :] = y
+                    add(2 * level + 1, c, before[c, tile(j - 1), :], w)
+                    add(2 * level + 2, c, w, y)
     for j in range(1, ext - 1):
-        w = neighbour_sum(u2_s, j + 1, row)[:, :cols] * u2_s[tile(j + 1), :][:, :cols]
-        acc[5] = acc[5] + w
+        around = neighbour_sums(u2_s, j, lane)
+        for c in range(regs - 1):
+            add(5, c, u2_s[c, at(j), :], around[c])
     lane_sums = []
     for k in range(6):
-        total = acc[k][:, :LANES]
-        for c in range(1, cols // LANES):
-            total = total + acc[k][:, c * LANES : (c + 1) * LANES]
+        total = acc[k][0]
+        for c in range(1, regs - 1):
+            total = total + acc[k][c]
         lane_sums.append(jnp.sum(total, axis=0, keepdims=True))
     stacked = jnp.concatenate(lane_sums + [jnp.zeros((2, LANES), F32)], axis=0)
     each = jnp.broadcast_to(jnp.sum(stacked, axis=1, keepdims=True), (SUB, LANES))
@@ -867,11 +871,12 @@
             beta = fresh / rz
             p = [z[i] + beta * p[i] if i < len(p) else z[i] for i in range(len(z))]
             rz = fresh
-    reps = x0.shape[1] // LANES
-    wide = [jnp.concatenate([c] * reps, axis=1) for c in coef]
     for k in range(x0.shape[0] // SUB):
         t = tile(k)
-        out[t, :] = x0[t, :] + (wide[0] * y0[t, :] + wide[1] * y1[t, :] + wide[2] * y2[t, :])
+        for c in range(y0.shape[0]):
+            cut = slice(c * LANES, (c + 1) * LANES)
+            move = coef[0] * y0[c, t, :] + coef[1] * y1[c, t, :] + coef[2] * y2[c, t, :]
+            out[t, cut] = x0[t, cut] + move
 
 
 def shards(
@@ -894,15 +899,13 @@
     ice_rows = ice_thick.shape[1]
     assert rows == groups * ice_rows
     slab = ice_rows + 2 * SUB
-    wide = cols + LANES
-
     strip = (2 * slab, cols)
     c, a, b, token = call(
         pack_rows,
-        [strip] * 3 + [(SUB, LANES)],
+        [(2 * (ice_rows + SUB), cols), strip, strip, (SUB, LANES)],
         [g, base_rhs, depth, ssh_prev, currents, land_blocks, ice_thick, ice_blocks, ice_vel, ice_stress, wind],
         scratch=[
-            (2, 2, SUB, cols), (2, SUB, cols),
+            (2, 2, SUB, cols), (2, 2, SUB, cols),
             (land_blocks.shape, jnp.int32), (ice_blocks.shape, jnp.int32),
         ],
         sems=48,
@@ -927,7 +930,7 @@
     tail = -(-narrow_rows * LANES // (SUB * cols)) * SUB
     outer, narrow, d = call(
         pack_narrow,
-        [(own * SUB, LANES), (groups, narrow_rows, LANES), ((2 * NICE + NOC) * SUB + tail, cols)],
+        [(own * SUB, LANES), (groups, narrow_rows, LANES), ((2 * NICE + 2) * SUB + tail, cols)],
         [g, from_left, from_right, h, gf, base_rhs, ssh_prev, ice_vel, ice_stress, wind],
     )
     nx = lax.all_to_all(narrow, "grp", 0, 0, tiled=True)
@@ -957,21 +960,19 @@
     r1 = lax.ppermute(p1, "grp", [(1, 0), (2, 3), (3, 1), (0, 2)])
     velocity, stress = call(ice_results, [ice_vel.shape, ice_stress.shape], [g, *state, fixed], flops=10000000)
 
-    ocean_rows = rows + 2 * SUB
-    field = (ocean_rows, wide)
-    padded = (ocean_rows + 2 * SUB, wide)
+    field = (regs, rows + 4 * SUB, LANES)
     gw, invd, known = call(
         ocean_before,
         [field] * 3,
         [g, ra, rc, rd, nx, outer, base_rhs, gf, ssh_prev],
-        scratch=[padded, padded, field, field],
+        scratch=[field] * 3,
         flops=20000000,
     )
     y0, y1, y2, sums = call(
         ocean_basis,
-        [(rows, cols)] * 3 + [(1, LANES)],
+        [(regs - 1, rows, LANES)] * 3 + [(1, LANES)],
         [g, gw, invd, known, r1, r2, r3, mine],
-        scratch=[field, padded, padded, padded],
+        scratch=[field] * 4,
     )
     devices = groups * tiles
     shared = lax.all_to_all(

time: 84.6 us -> 86 us (1.017)
  blocking collectives: 8.41 us -> 0 us
  starting transfers between devices: 21.6 us -> 27.9 us
  local copies, waits for them, and re-layouts: 4.46 us -> 10.1 us
  waiting for transfers between devices: 32.3 us -> 27.5 us
  Pallas kernels: 16.4 us -> 18.8 us
    ppermute x1, waiting for transfers between devices: 8.66 us -> 0.01 us  [shards(): ra = lax.ppermute(a, 'grp', [(0, 1), (1, 0), (2, 3), (3, 2)])]
    all_to_all x1 -> x0, blocking collectives: 8.41 us -> none  [shards(): nx = lax.all_to_all(narrow, 'grp', 0, 0, tiled=True)]
    ppermute x1, waiting for transfers between devices: 8.94 us -> 15 us  [shards(): rc = lax.ppermute(c, 'grp', [(0, 3), (3, 0), (1, 2), (2, 1)])]
    unnamed x32 -> x66, local copies, waits for them, and re-layouts: 3.84 us -> 9.51 us
    all_to_all x0 -> x1, starting transfers between devices: none -> 3.9 us  [shards(): nx = lax.all_to_all(narrow, 'grp', 0, 0, tiled=True)]
    ppermute x1, waiting for transfers between devices: 4.14 us -> 0.74 us  [shards(): r3 = lax.ppermute(p3, 'grp', [(3, 0), (0, 3)])]
    pallas_call x9, Pallas kernels: 16.4 us -> 18.8 us  [call(): pl.pallas_call(body, out_shape=shapes, in_specs=specs, out_specs=tuple((v...]
    ppermute x1, waiting for transfers between devices: 0.65 us -> 2.83 us  [shards(): r1 = lax.ppermute(p1, 'grp', [(1, 0), (2, 3), (3, 1), (0, 2)])]
  transfers between devices with their start and end apart: 10 -> 11, of which waited for: 7 -> 6; matrix products, arithmetic and copies ran while one was open for 0% -> 0% of each run, Pallas kernels for 13% -> 16%
where the time goes in v7:
time: 86 us; the launch traced here: 85.4 us
  starting transfers between devices  27.9 us (32%)
  waiting for transfers between devices  27.5 us (32%)
  Pallas kernels  18.8 us (22%)
  local copies, waits for them, and re-layouts  10.1 us (12%)
  between operations  1.1 us (1%)
    pallas_call x9, Pallas kernels, call(): pl.pallas_call(body, out_shape=shapes, in_specs=specs, out_specs=tuple((v...  18.8 us
    ppermute x1, waiting for transfers between devices, shards(): rc = lax.ppermute(c, 'grp', [(0, 3), (3, 0), (1, 2), (2, 1)])  15 us
    unnamed x66, local copies, waits for them, and re-layouts  9.51 us
    all_to_all x1, starting transfers between devices, shards(): lax.all_to_all(jnp.broadcast_to(sums[None], (devices, 1, LANES)), ('grp',...  6.49 us
    ppermute x1, waiting for transfers between devices, shards(): lax.ppermute(left, 'tile', [(i + 1, i) for i in range(tiles - 1)])  4.13 us
    ppermute x1, starting transfers between devices, shards(): rb = lax.ppermute(b, 'grp', [(0, 2), (3, 1)])  4.11 us
    all_to_all x1, starting transfers between devices, shards(): nx = lax.all_to_all(narrow, 'grp', 0, 0, tiled=True)  3.9 us
    ppermute x1, starting transfers between devices, shards(): r3 = lax.ppermute(p3, 'grp', [(3, 0), (0, 3)])  3.37 us
  transfers between devices with their start and end apart: 11, of which 6 were waited for; matrix products, arithmetic and copies ran while one was open for 0% of the time, Pallas kernels for 16%

profile of v7, /device:TPU:0, one launch (start us, length us, event | category | flops | bytes accessed | tf_op | source)
XLA Modules:
  0.0 85.4 jit_solution(3988914749242617008)
XLA Ops:
  0.7 0.0 copy-start.4
  0.7 0.0 copy-start.6
  0.7 1.8 %shard_map.121 = (f32[144,512]{1,0:T(8,128)S(1)}, f32[160,512]{1,0:T(8,128)S(1)}, f32[160,512]{1,0:T(8,128)S(1)}, f32[8,128]{1,0:T(8,128)S(1)}) custom-call(s32[1]{0:T(128)} %bitcast.g_ref, f32[256,512]{1,0:T(8,128)} %base.7, f32[256,512]{1,0:T(8,128)} %depth.3, f32[256,512]{1,0:T(8,128)} %x0.9, f32[2,256,512]{2,1,0:T(8,128)} %cur.5, s32[32,64]{1,0:T(8,128)} %land.3, ...), custom_call_target="tpu_custom_call" | custom-call | flops 1000000 | bytes 4000000 | tf_op jit(solution)/shard_map/pallas_call | solution.py:46
  2.6 0.0 copy-start.29
  2.6 0.7 copy-done.29
  3.3 0.7 copy-done.30
  4.0 0.7 copy-done.32
  4.8 0.4 shard_map.122
  5.3 0.0 copy-start.10
  5.3 2.4 %collective-permute-start.2 = (f32[288,128]{1,0:T(8,128)S(1)}, f32[288,128]{1,0:T(8,128)S(1)}, u32[]{:S(2)}, u32[]{:S(2)}) collective-permute-start(f32[288,128]{1,0:T(8,128)S(1)} %get-tuple-element.41), channel_id=1, source_target_pairs={{0,1},{1,2},{2,3},{3,4},{4,5},{5,6},{6,7},{8,9},{9,10},{10,11},{11... | collective-permute-start | bytes 442376 | tf_op jit(solution)/shard_map/ppermute | solution.py:926
  7.7 1.3 %collective-permute-start.3 = (f32[288,128]{1,0:T(8,128)S(1)}, f32[288,128]{1,0:T(8,128)S(1)}, u32[]{:S(2)}, u32[]{:S(2)}) collective-permute-start(f32[288,128]{1,0:T(8,128)S(1)} %get-tuple-element.42), channel_id=1, source_target_pairs={{1,0},{2,1},{3,2},{4,3},{5,4},{6,5},{7,6},{9,8},{10,9},{11,10},{12... | collective-permute-start | bytes 442376 | tf_op jit(solution)/shard_map/ppermute | solution.py:927
  9.0 4.1 %collective-permute-done.3.from_right = f32[288,128]{1,0:T(8,128)S(1)} collective-permute-done((f32[288,128]{1,0:T(8,128)S(1)}, f32[288,128]{1,0:T(8,128)S(1)}, u32[]{:S(2)}, u32[]{:S(2)}) %collective-permute-start.3) | collective-permute-done | bytes 147488 | tf_op jit(solution)/shard_map/ppermute | solution.py:927
  13.1 0.5 shard_map.123
  13.6 0.6 copy-done.26
  14.3 0.7 copy-done.31
  15.0 3.9 %all-to-all-start = ((f32[4,40,128]{2,1,0:T(8,128)}), f32[4,40,128]{2,1,0:T(8,128)}, u32[]{:S(2)}, u32[]{:S(2)}) async-start(f32[4,40,128]{2,1,0:T(8,128)} %copy-done.26), calls=%async_computation | async-start | bytes 163840 | tf_op jit(solution)/shard_map/all_to_all | solution.py:936
  18.9 2.0 %collective-permute-start = (f32[160,512]{1,0:T(8,128)}, f32[160,512]{1,0:T(8,128)}, u32[]{:S(2)}, u32[]{:S(2)}) collective-permute-start(f32[160,512]{1,0:T(8,128)} %copy-done.30), channel_id=1, source_target_pairs={{0,8},{8,0},{16,24},{24,16},{1,9},{9,1},{17,25},{25,17},{2,10},{10... | collective-permute-start | bytes 983048 | tf_op jit(solution)/shard_map/ppermute | solution.py:915
  20.9 4.1 %collective-permute-start.5 = (f32[160,512]{1,0:T(8,128)}, f32[160,512]{1,0:T(8,128)}, u32[]{:S(2)}, u32[]{:S(2)}) collective-permute-start(f32[160,512]{1,0:T(8,128)} %copy-done.29), channel_id=1, source_target_pairs={{0,16},{24,8},{1,17},{25,9},{2,18},{26,10},{3,19},{27,11},{4,20},{... | collective-permute-start | bytes 983048 | tf_op jit(solution)/shard_map/ppermute | solution.py:916
  25.0 0.0 all-to-all-done.nx
  25.0 1.6 %collective-permute-start.4 = (f32[160,512]{1,0:T(8,128)}, f32[160,512]{1,0:T(8,128)S(1)}, u32[]{:S(2)}, u32[]{:S(2)}) collective-permute-start(f32[160,512]{1,0:T(8,128)} %copy-done.31), channel_id=1, source_target_pairs={{0,8},{24,16},{1,9},{25,17},{2,10},{26,18},{3,11},{27,19},{4,12},{... | collective-permute-start | bytes 983048 | tf_op jit(solution)/shard_map/ppermute | solution.py:938
  26.5 1.5 %collective-permute-start.1 = (f32[144,512]{1,0:T(8,128)}, f32[144,512]{1,0:T(8,128)S(1)}, u32[]{:S(2)}, u32[]{:S(2)}) collective-permute-start(f32[144,512]{1,0:T(8,128)} %copy-done.32), channel_id=1, source_target_pairs={{0,24},{24,0},{8,16},{16,8},{1,25},{25,1},{9,17},{17,9},{2,26},{26... | collective-permute-start | bytes 884744 | tf_op jit(solution)/shard_map/ppermute | solution.py:914
  28.1 15.0 %collective-permute-done.1.rc = f32[144,512]{1,0:T(8,128)S(1)} collective-permute-done((f32[144,512]{1,0:T(8,128)}, f32[144,512]{1,0:T(8,128)S(1)}, u32[]{:S(2)}, u32[]{:S(2)}) %collective-permute-start.1) | collective-permute-done | bytes 294944 | tf_op jit(solution)/shard_map/ppermute | solution.py:914
  43.1 0.0 collective-permute-done.ra
  43.1 0.0 collective-permute-done.5.rb
  43.1 1.2 %copy-done.5 = f32[2,256,512]{2,1,0:T(8,128)S(1)} copy-done((f32[2,256,512]{2,1,0:T(8,128)S(1)}, f32[2,256,512]{2,1,0:T(8,128)}, u32[]{:S(2)}) %copy-start.5) | copy-done | bytes 1048600
  44.3 0.9 %copy-done.9 = f32[2,64,512]{2,1,0:T(8,128)S(1)} copy-done((f32[2,64,512]{2,1,0:T(8,128)S(1)}, f32[2,64,512]{2,1,0:T(8,128)}, u32[]{:S(2)}) %copy-start.9) | copy-done | bytes 262168
  45.2 9.4 %shard_map.125 = (f32[2,5,96,128]{3,2,1,0:T(8,128)S(1)}, f32[2,5,96,128]{3,2,1,0:T(8,128)S(1)}, f32[2,5,96,128]{3,2,1,0:T(8,128)S(1)}, f32[2,5,96,128]{3,2,1,0:T...) custom-call(s32[1]{0:T(128)} %bitcast.g_ref, ...), custom_call_target="tpu_custom_call" | custom-call | flops 20000000 | bytes 4000000 | tf_op jit(solution)/shard_map/pallas_call | solution.py:46
  54.7 0.0 copy-start.14
  54.7 0.0 copy-start.16
  54.7 3.4 %collective-permute-start.8 = (f32[80,512]{1,0:T(8,128)S(1)}, f32[80,512]{1,0:T(8,128)S(1)}, u32[]{:S(2)}, u32[]{:S(2)}) collective-permute-start(f32[80,512]{1,0:T(8,128)S(1)} %get-tuple-element.59), channel_id=1, source_target_pairs={{24,0},{0,24},{25,1},{1,25},{26,2},{2,26},{27,3},{3,27},{28,4},{4,... | collective-permute-start | bytes 491528 | tf_op jit(solution)/shard_map/ppermute | solution.py:958
  58.1 0.0 copy-start.7
  58.2 0.0 copy-start.11
  58.2 1.2 %shard_map.126 = (f32[80,512]{1,0:T(8,128)S(1)}, f32[80,512]{1,0:T(8,128)S(1)}, f32[2,5,8,512]{3,2,1,0:T(8,128)S(1)}) custom-call(s32[1]{0:T(128)} %bitcast.g_ref, f32[160,512]{1,0:T(8,128)S(1)} %collective-permute-done.4.rd, f32[160,512]{1,0:T(8,128)} %collective-permute-done.ra, f32[160,512]{1,0:T(8,128)} %collective-permute-done.5.rb, ...), custom_call_target="tpu_custom_call" | custom-call | flops 20000000 | bytes 4000000 | tf_op jit(solution)/shard_map/pallas_call | solution.py:46
  59.4 0.7 copy-done.24
  60.1 1.3 %collective-permute-start.7 = (f32[80,512]{1,0:T(8,128)S(1)}, f32[80,512]{1,0:T(8,128)S(1)}, u32[]{:S(2)}, u32[]{:S(2)}) collective-permute-start(f32[80,512]{1,0:T(8,128)S(1)} %get-tuple-element.58), channel_id=1, source_target_pairs={{16,0},{8,24},{17,1},{9,25},{18,2},{10,26},{19,3},{11,27},{20,4},{... | collective-permute-start | bytes 491528 | tf_op jit(solution)/shard_map/ppermute | solution.py:959
  61.4 1.8 %shard_map.124 = (f32[5,288,128]{2,1,0:T(8,128)S(1)}, f32[5,288,128]{2,1,0:T(8,128)S(1)}, f32[5,288,128]{2,1,0:T(8,128)S(1)}) custom-call(s32[1]{0:T(128)} %bitcast.g_ref, f32[160,512]{1,0:T(8,128)} %collective-permute-done.ra, f32[144,512]{1,0:T(8,128)S(1)} %collective-permute-done.1.rc, f32[160,512]{1,0:T(8,128)S(1)} %collective-permute-done.4.rd, ...), custom_call_target="tpu_custom_call" | custom-call | flops 20000000 | bytes 4000000 | tf_op jit(solution)/shard_map/pallas_call | solution.py:46
  63.2 0.7 collective-permute-done.8.r3
  63.9 2.8 %collective-permute-done.6.r1 = f32[80,512]{1,0:T(8,128)S(1)} collective-permute-done((f32[80,512]{1,0:T(8,128)S(1)}, f32[80,512]{1,0:T(8,128)S(1)}, u32[]{:S(2)}, u32[]{:S(2)}) %collective-permute-start.6) | collective-permute-done | bytes 163872 | tf_op jit(solution)/shard_map/ppermute | solution.py:960
  66.8 1.9 %collective-permute-done.7.r2 = f32[80,512]{1,0:T(8,128)S(1)} collective-permute-done((f32[80,512]{1,0:T(8,128)S(1)}, f32[80,512]{1,0:T(8,128)S(1)}, u32[]{:S(2)}, u32[]{:S(2)}) %collective-permute-start.7) | collective-permute-done | bytes 163872 | tf_op jit(solution)/shard_map/ppermute | solution.py:959
  68.7 1.4 %shard_map.127 = (f32[4,256,128]{2,1,0:T(8,128)S(1)}, f32[4,256,128]{2,1,0:T(8,128)S(1)}, f32[4,256,128]{2,1,0:T(8,128)S(1)}, f32[1,128]{1,0:T(1,128)S(1)}) custom-call(s32[1]{0:T(128)} %bitcast.g_ref, f32[5,288,128]{2,1,0:T(8,128)S(1)} %get-tuple-element.50.gw, f32[5,288,128]{2,1,0:T(8,128)S(1)} %get-tuple-element.51.invd, ...), custom_call_target="tpu_custom_call" | custom-call | flops 1000000 | bytes 4000000 | tf_op jit(solution)/shard_map/pallas_call | solution.py:46
  70.0 0.6 broadcast_in_dim.9
  70.6 6.5 %all-to-all-start.1 = ((f32[32,1,128]{2,1,0:T(1,128)}), f32[32,1,128]{2,1,0:T(1,128)S(1)}, u32[]{:S(2)}, u32[]{:S(2)}) async-start(f32[32,1,128]{2,1,0:T(1,128)} %broadcast_in_dim.9), calls=%async_computation.1 | async-start | bytes 32768 | tf_op jit(solution)/shard_map/all_to_all | solution.py:978
  77.2 1.0 %copy-done.19 = f32[2,5,96,128]{3,2,1,0:T(8,128)S(1)} copy-done((f32[2,5,96,128]{3,2,1,0:T(8,128)S(1)}, f32[2,5,96,128]{3,2,1,0:T(8,128)}, u32[]{:S(2)}) %copy-start.19) | copy-done | bytes 491544
  78.2 1.0 %copy-done.21 = f32[2,5,96,128]{3,2,1,0:T(8,128)S(1)} copy-done((f32[2,5,96,128]{3,2,1,0:T(8,128)S(1)}, f32[2,5,96,128]{3,2,1,0:T(8,128)}, u32[]{:S(2)}) %copy-start.21) | copy-done | bytes 491544
  79.2 1.0 %copy-done.23 = f32[2,5,96,128]{3,2,1,0:T(8,128)S(1)} copy-done((f32[2,5,96,128]{3,2,1,0:T(8,128)S(1)}, f32[2,5,96,128]{3,2,1,0:T(8,128)}, u32[]{:S(2)}) %copy-start.23) | copy-done | bytes 491544
  80.3 1.1 %shard_map.129 = (f32[2,2,64,512]{3,2,1,0:T(8,128)}, f32[3,2,64,512]{3,2,1,0:T(8,128)}) custom-call(s32[1]{0:T(128)} %bitcast.g_ref, f32[2,5,96,128]{3,2,1,0:T(8,128)S(1)} %copy-done.15, f32[2,5,96,128]{3,2,1,0:T(8,128)S(1)} %copy-done.17, f32[2,5,96,128]{3,2,1,0:T(8,128)S(1)} %copy-done.19, f32[2,5,96,128]{3,2,1,0:T(8,128)S(1)} %copy-done.21, ...), custom_call_target="tpu_custom_call" | custom-call | flops 10000000 | bytes 4000000 | tf_op jit(solution)/shard_map/pallas_call | solution.py:46
  81.4 2.9 %all-to-all-done.1.parts = f32[32,1,128]{2,1,0:T(1,128)S(1)} async-done(((f32[32,1,128]{2,1,0:T(1,128)}), f32[32,1,128]{2,1,0:T(1,128)S(1)}, u32[]{:S(2)}, u32[]{:S(2)}) %all-to-all-start.1) | async-done | bytes 16416 | tf_op jit(solution)/shard_map/all_to_all | solution.py:978
  84.3 1.1 %shard_map.128 = f32[256,512]{1,0:T(8,128)} custom-call(s32[1]{0:T(128)} %bitcast.g_ref, f32[32,1,128]{2,1,0:T(1,128)S(1)} %all-to-all-done.1.parts, f32[256,512]{1,0:T(8,128)S(1)} %copy-done.3, f32[4,256,128]{2,1,0:T(8,128)S(1)} %get-tuple-element.62.y0, f32[4,256,128]{2,1,0:T(8,128)S(1)} %get-tuple-element.63.y1, f32[4,256,128]{2,1,0:T(8,128)S(1)} %get-tuple-element.64.y2), custom_call_target="tpu_custom_call" | custom-call | flops 1000000 | bytes 4000000 | tf_op jit(solution)/shard_map/pallas_call | solution.py:46
  (50 shorter events, 0.1 us)
Async XLA Ops:
  0.6 4.1 %copy-start = (f32[3,2,64,512]{3,2,1,0:T(8,128)S(1)}, f32[3,2,64,512]{3,2,1,0:T(8,128)}, u32[]{:S(2)}) copy-start(f32[3,2,64,512]{3,2,1,0:T(8,128)} %stress.9) | copy-start | bytes 2359300
  0.6 4.1 %copy-start.1 = (f32[2,2,64,512]{3,2,1,0:T(8,128)S(1)}, f32[2,2,64,512]{3,2,1,0:T(8,128)}, u32[]{:S(2)}) copy-start(f32[2,2,64,512]{3,2,1,0:T(8,128)} %vel.9) | copy-start | bytes 1572868
  0.7 4.1 %copy-start.2 = (f32[2,2,64,512]{3,2,1,0:T(8,128)S(1)}, f32[2,2,64,512]{3,2,1,0:T(8,128)}, u32[]{:S(2)}) copy-start(f32[2,2,64,512]{3,2,1,0:T(8,128)} %wind.9) | copy-start | bytes 1572868
  0.7 4.1 %copy-start.3 = (f32[256,512]{1,0:T(8,128)S(1)}, f32[256,512]{1,0:T(8,128)}, u32[]{:S(2)}) copy-start(f32[256,512]{1,0:T(8,128)} %x0.9) | copy-start | bytes 1572868
  0.7 4.1 %copy-start.4 = (f32[2,256,512]{2,1,0:T(8,128)S(1)}, f32[2,256,512]{2,1,0:T(8,128)}, u32[]{:S(2)}) copy-start(f32[2,256,512]{2,1,0:T(8,128)} %cur.5) | copy-start | bytes 3145732
  0.7 4.1 %copy-start.6 = (f32[256,512]{1,0:T(8,128)S(1)}, f32[256,512]{1,0:T(8,128)}, u32[]{:S(2)}) copy-start(f32[256,512]{1,0:T(8,128)} %base.7) | copy-start | bytes 1572868
  0.7 4.1 %copy-start.12 = (f32[256,512]{1,0:T(8,128)S(1)}, f32[256,512]{1,0:T(8,128)}, u32[]{:S(2)}) copy-start(f32[256,512]{1,0:T(8,128)} %depth.3) | copy-start | bytes 1572868
  0.7 4.1 %copy-start.13 = (f32[2,64,512]{2,1,0:T(8,128)S(1)}, f32[2,64,512]{2,1,0:T(8,128)}, u32[]{:S(2)}) copy-start(f32[2,64,512]{2,1,0:T(8,128)} %thick.3) | copy-start | bytes 786436
  0.7 4.1 %copy-start.27 = (s32[32,64]{1,0:T(8,128)S(1)}, s32[32,64]{1,0:T(8,128)}, u32[]{:S(2)}) copy-start(s32[32,64]{1,0:T(8,128)} %land.3) | copy-start | bytes 24580
  0.7 4.1 %copy-start.28 = (s32[2,8,64]{2,1,0:T(8,128)S(1)}, s32[2,8,64]{2,1,0:T(8,128)}, u32[]{:S(2)}) copy-start(s32[2,8,64]{2,1,0:T(8,128)} %iceb.3) | copy-start | bytes 12292
  2.6 0.7 copy-start.29
  3.3 0.7 copy-start.30
  4.0 0.7 copy-start.32
  5.3 8.3 %copy-start.8 = (f32[2,64,512]{2,1,0:T(8,128)}, f32[2,64,512]{2,1,0:T(8,128)S(1)}, u32[]{:S(2)}) copy-start(f32[2,64,512]{2,1,0:T(8,128)S(1)} %get-tuple-element.43.h) | copy-start | bytes 786436
  5.3 8.3 %copy-start.10 = (f32[256,512]{1,0:T(8,128)}, f32[256,512]{1,0:T(8,128)S(1)}, u32[]{:S(2)}) copy-start(f32[256,512]{1,0:T(8,128)S(1)} %get-tuple-element.44.gf) | copy-start | bytes 1572868
  5.3 3.7 %collective-permute-start.2 = (f32[288,128]{1,0:T(8,128)S(1)}, f32[288,128]{1,0:T(8,128)S(1)}, u32[]{:S(2)}, u32[]{:S(2)}) collective-permute-start(f32[288,128]{1,0:T(8,128)S(1)} %get-tuple-element.41), channel_id=1, source_target_pairs={{0,1},{1,2},{2,3},{3,4},{4,5},{5,6},{6,7},{8,9},{9,10},{10,11},{11... | collective-permute-start | bytes 442376 | tf_op jit(solution)/shard_map/ppermute | solution.py:926
  7.7 5.4 %collective-permute-start.3 = (f32[288,128]{1,0:T(8,128)S(1)}, f32[288,128]{1,0:T(8,128)S(1)}, u32[]{:S(2)}, u32[]{:S(2)}) collective-permute-start(f32[288,128]{1,0:T(8,128)S(1)} %get-tuple-element.42), channel_id=1, source_target_pairs={{1,0},{2,1},{3,2},{4,3},{5,4},{6,5},{7,6},{9,8},{10,9},{11,10},{12... | collective-permute-start | bytes 442376 | tf_op jit(solution)/shard_map/ppermute | solution.py:927
  13.6 0.6 copy-start.26
  14.3 0.7 copy-start.31
  15.0 10.0 %all-to-all-start = ((f32[4,40,128]{2,1,0:T(8,128)}), f32[4,40,128]{2,1,0:T(8,128)}, u32[]{:S(2)}, u32[]{:S(2)}) async-start(f32[4,40,128]{2,1,0:T(8,128)} %copy-done.26), calls=%async_computation | async-start | bytes 163840 | tf_op jit(solution)/shard_map/all_to_all | solution.py:936
  18.9 24.2 %collective-permute-start = (f32[160,512]{1,0:T(8,128)}, f32[160,512]{1,0:T(8,128)}, u32[]{:S(2)}, u32[]{:S(2)}) collective-permute-start(f32[160,512]{1,0:T(8,128)} %copy-done.30), channel_id=1, source_target_pairs={{0,8},{8,0},{16,24},{24,16},{1,9},{9,1},{17,25},{25,17},{2,10},{10... | collective-permute-start | bytes 983048 | tf_op jit(solution)/shard_map/ppermute | solution.py:915
  20.9 22.2 %collective-permute-start.5 = (f32[160,512]{1,0:T(8,128)}, f32[160,512]{1,0:T(8,128)}, u32[]{:S(2)}, u32[]{:S(2)}) collective-permute-start(f32[160,512]{1,0:T(8,128)} %copy-done.29), channel_id=1, source_target_pairs={{0,16},{24,8},{1,17},{25,9},{2,18},{26,10},{3,19},{27,11},{4,20},{... | collective-permute-start | bytes 983048 | tf_op jit(solution)/shard_map/ppermute | solution.py:916
  25.0 33.2 %collective-permute-start.4 = (f32[160,512]{1,0:T(8,128)}, f32[160,512]{1,0:T(8,128)S(1)}, u32[]{:S(2)}, u32[]{:S(2)}) collective-permute-start(f32[160,512]{1,0:T(8,128)} %copy-done.31), channel_id=1, source_target_pairs={{0,8},{24,16},{1,9},{25,17},{2,10},{26,18},{3,11},{27,19},{4,12},{... | collective-permute-start | bytes 983048 | tf_op jit(solution)/shard_map/ppermute | solution.py:938
  26.5 16.5 %collective-permute-start.1 = (f32[144,512]{1,0:T(8,128)}, f32[144,512]{1,0:T(8,128)S(1)}, u32[]{:S(2)}, u32[]{:S(2)}) collective-permute-start(f32[144,512]{1,0:T(8,128)} %copy-done.32), channel_id=1, source_target_pairs={{0,24},{24,0},{8,16},{16,8},{1,25},{25,1},{9,17},{17,9},{2,26},{26... | collective-permute-start | bytes 884744 | tf_op jit(solution)/shard_map/ppermute | solution.py:914
  43.1 1.2 %copy-start.5 = (f32[2,256,512]{2,1,0:T(8,128)S(1)}, f32[2,256,512]{2,1,0:T(8,128)}, u32[]{:S(2)}) copy-start(f32[2,256,512]{2,1,0:T(8,128)} %cur.5) | copy-start | bytes 3145732
  44.3 0.9 %copy-start.9 = (f32[2,64,512]{2,1,0:T(8,128)S(1)}, f32[2,64,512]{2,1,0:T(8,128)}, u32[]{:S(2)}) copy-start(f32[2,64,512]{2,1,0:T(8,128)} %copy-done.8) | copy-start | bytes 786436
  54.7 4.7 %copy-start.14 = (f32[2,5,96,128]{3,2,1,0:T(8,128)}, f32[2,5,96,128]{3,2,1,0:T(8,128)S(1)}, u32[]{:S(2)}) copy-start(f32[2,5,96,128]{3,2,1,0:T(8,128)S(1)} %get-tuple-element.65.u_s) | copy-start | bytes 1474564
  54.7 4.7 %copy-start.16 = (f32[2,5,96,128]{3,2,1,0:T(8,128)}, f32[2,5,96,128]{3,2,1,0:T(8,128)S(1)}, u32[]{:S(2)}) copy-start(f32[2,5,96,128]{3,2,1,0:T(8,128)S(1)} %get-tuple-element.66.v_s) | copy-start | bytes 1474564
  54.7 4.7 %copy-start.18 = (f32[2,5,96,128]{3,2,1,0:T(8,128)}, f32[2,5,96,128]{3,2,1,0:T(8,128)S(1)}, u32[]{:S(2)}) copy-start(f32[2,5,96,128]{3,2,1,0:T(8,128)S(1)} %get-tuple-element.67.p_s) | copy-start | bytes 1474564
  54.7 4.7 %copy-start.20 = (f32[2,5,96,128]{3,2,1,0:T(8,128)}, f32[2,5,96,128]{3,2,1,0:T(8,128)S(1)}, u32[]{:S(2)}) copy-start(f32[2,5,96,128]{3,2,1,0:T(8,128)S(1)} %get-tuple-element.68.q_s) | copy-start | bytes 1474564
  54.7 4.7 %copy-start.22 = (f32[2,5,96,128]{3,2,1,0:T(8,128)}, f32[2,5,96,128]{3,2,1,0:T(8,128)S(1)}, u32[]{:S(2)}) copy-start(f32[2,5,96,128]{3,2,1,0:T(8,128)S(1)} %get-tuple-element.69.s_s) | copy-start | bytes 1474564
  54.7 9.2 %collective-permute-start.8 = (f32[80,512]{1,0:T(8,128)S(1)}, f32[80,512]{1,0:T(8,128)S(1)}, u32[]{:S(2)}, u32[]{:S(2)}) collective-permute-start(f32[80,512]{1,0:T(8,128)S(1)} %get-tuple-element.59), channel_id=1, source_target_pairs={{24,0},{0,24},{25,1},{1,25},{26,2},{2,26},{27,3},{3,27},{28,4},{4,... | collective-permute-start | bytes 491528 | tf_op jit(solution)/shard_map/ppermute | solution.py:958
  58.1 3.2 %copy-start.7 = (f32[256,512]{1,0:T(8,128)S(1)}, f32[256,512]{1,0:T(8,128)}, u32[]{:S(2)}) copy-start(f32[256,512]{1,0:T(8,128)} %base.7) | copy-start | bytes 1572868
  58.2 3.2 %copy-start.11 = (f32[256,512]{1,0:T(8,128)S(1)}, f32[256,512]{1,0:T(8,128)}, u32[]{:S(2)}) copy-start(f32[256,512]{1,0:T(8,128)} %copy-done.10) | copy-start | bytes 1572868
  59.4 0.7 copy-start.24
  60.1 6.7 %collective-permute-start.6 = (f32[80,512]{1,0:T(8,128)S(1)}, f32[80,512]{1,0:T(8,128)S(1)}, u32[]{:S(2)}, u32[]{:S(2)}) collective-permute-start(f32[80,512]{1,0:T(8,128)S(1)} %get-tuple-element.57), channel_id=1, source_target_pairs={{8,0},{16,24},{24,8},{0,16},{9,1},{17,25},{25,9},{1,17},{10,2},{18... | collective-permute-start | bytes 491528 | tf_op jit(solution)/shard_map/ppermute | solution.py:960
  60.1 8.6 %collective-permute-start.7 = (f32[80,512]{1,0:T(8,128)S(1)}, f32[80,512]{1,0:T(8,128)S(1)}, u32[]{:S(2)}, u32[]{:S(2)}) collective-permute-start(f32[80,512]{1,0:T(8,128)S(1)} %get-tuple-element.58), channel_id=1, source_target_pairs={{16,0},{8,24},{17,1},{9,25},{18,2},{10,26},{19,3},{11,27},{20,4},{... | collective-permute-start | bytes 491528 | tf_op jit(solution)/shard_map/ppermute | solution.py:959
  68.6 8.5 %copy-start.15 = (f32[2,5,96,128]{3,2,1,0:T(8,128)S(1)}, f32[2,5,96,128]{3,2,1,0:T(8,128)}, u32[]{:S(2)}) copy-start(f32[2,5,96,128]{3,2,1,0:T(8,128)} %copy-done.14) | copy-start | bytes 1474564
  68.6 8.5 %copy-start.17 = (f32[2,5,96,128]{3,2,1,0:T(8,128)S(1)}, f32[2,5,96,128]{3,2,1,0:T(8,128)}, u32[]{:S(2)}) copy-start(f32[2,5,96,128]{3,2,1,0:T(8,128)} %copy-done.16) | copy-start | bytes 1474564
  68.7 8.5 %copy-start.25 = (f32[2,5,8,512]{3,2,1,0:T(8,128)S(1)}, f32[2,5,8,512]{3,2,1,0:T(8,128)}, u32[]{:S(2)}) copy-start(f32[2,5,8,512]{3,2,1,0:T(8,128)} %copy-done.24) | copy-start | bytes 491524
  70.6 13.7 %all-to-all-start.1 = ((f32[32,1,128]{2,1,0:T(1,128)}), f32[32,1,128]{2,1,0:T(1,128)S(1)}, u32[]{:S(2)}, u32[]{:S(2)}) async-start(f32[32,1,128]{2,1,0:T(1,128)} %broadcast_in_dim.9), calls=%async_computation.1 | async-start | bytes 32768 | tf_op jit(solution)/shard_map/all_to_all | solution.py:978
  77.2 1.0 %copy-start.19 = (f32[2,5,96,128]{3,2,1,0:T(8,128)S(1)}, f32[2,5,96,128]{3,2,1,0:T(8,128)}, u32[]{:S(2)}) copy-start(f32[2,5,96,128]{3,2,1,0:T(8,128)} %copy-done.18) | copy-start | bytes 1474564
  78.2 1.0 %copy-start.21 = (f32[2,5,96,128]{3,2,1,0:T(8,128)S(1)}, f32[2,5,96,128]{3,2,1,0:T(8,128)}, u32[]{:S(2)}) copy-start(f32[2,5,96,128]{3,2,1,0:T(8,128)} %copy-done.20) | copy-start | bytes 1474564
  79.2 1.0 %copy-start.23 = (f32[2,5,96,128]{3,2,1,0:T(8,128)S(1)}, f32[2,5,96,128]{3,2,1,0:T(8,128)}, u32[]{:S(2)}) copy-start(f32[2,5,96,128]{3,2,1,0:T(8,128)} %copy-done.22) | copy-start | bytes 1474564

commit v8 on v7

--- a/solution.py
+++ b/solution.py
@@ -25,6 +25,9 @@
 GROUP = 4
 SKEW = 1
 NICE = 8
+FIRST = [(0, 1), (1, 0), (2, 3), (3, 2)]
+SECOND = [(0, 2), (2, 0), (1, 3), (3, 1)]
+DIAGONAL = [(0, 3), (3, 0), (1, 2), (2, 1)]
 NOC = 3
 
 
@@ -105,7 +108,7 @@
 
 def pack_rows(g_ref, base, depth, x0, cur, land, thick, iceb, vel, stress, wind,
               c, a, b, token, thick_s, depth_s, land_s, iceb_s, sems):
-    g = g_ref[0]
+    g = g_ref[0] & 3
     rows, cols = base.shape
     ice_rows = thick.shape[1]
     slab = ice_rows + 2 * SUB
@@ -174,8 +177,9 @@
         run([], [(a, True), (c, False)])
 
 
-def pack_own(g_ref, token, base, depth, x0, cur, land, thick, iceb, vel, stress, wind, gf, h, left, right):
+def pack_own(g_ref, token, base, depth, x0, cur, land, thick, iceb, vel, stress, wind, gf, h, inner, cross):
     cols = base.shape[1]
+    even = g_ref[0] < 4
     lane = lane_iota()
     slot = lane // EDGE
     state = {"n": 0, "l": None, "r": None}
@@ -192,8 +196,8 @@
             state["r"] = jnp.where(slot == s - 1, both, state["r"])
         if s == SLOTS - 1:
             k = n // SLOTS
-            left[tile(k), :] = state["l"]
-            right[tile(k), :] = state["r"]
+            inner[tile(k), :] = jnp.where(even, state["r"], state["l"])
+            cross[tile(k), :] = jnp.where(even, state["l"], state["r"])
         state["n"] = n + 1
 
     def emit_all(ref):
@@ -235,15 +239,15 @@
     return picked + [start + i * ocean_tiles + (ocean_tiles - 1 if last else 0) for i in range(NOC)]
 
 
-def pack_narrow(g_ref, from_left, from_right, h, gf, base, x0, vel, stress, wind, outer, narrow, d):
-    g = g_ref[0]
+def pack_narrow(g_ref, inner, cross, h, gf, base, x0, vel, stress, wind, outer, narrow, d):
+    g = g_ref[0] & 3
     rows, cols = base.shape
     ice_rows = h.shape[1]
     lane = lane_iota()
     count = sum(own_count(rows, ice_rows))
     batch = 32
     for n in range(0, count, batch):
-        made = [outer_columns(from_left, from_right, i, lane) for i in range(n, min(n + batch, count))]
+        made = [outer_columns(g_ref[0] < 4, inner, cross, i, lane) for i in range(n, min(n + batch, count))]
         for i, value in enumerate(made):
             outer[tile(n + i), :] = value
     packed = narrow.shape[1] // SUB
@@ -355,9 +359,11 @@
     return split(inner) + [wide_outer(packed, i, lane)]
 
 
-def outer_columns(from_left, from_right, n, lane):
+def outer_columns(even, inner, cross, n, lane):
     s, k = n % SLOTS, n // SLOTS
-    both = jnp.where(lane // EDGE == s, from_right[tile(k), :], from_left[tile(k), :])
+    from_right = jnp.where(even, inner[tile(k), :], cross[tile(k), :])
+    from_left = jnp.where(even, cross[tile(k), :], inner[tile(k), :])
+    both = jnp.where(lane // EDGE == s, from_right, from_left)
     both = pltpu.roll(both, LANES - EDGE * s, 1) if s else both
     return jnp.where((lane < EDGE) | (lane >= LANES - EDGE), both, 0.0)
 
@@ -491,7 +497,7 @@
 
 def ice_steps(g_ref, ra, rb, rc, nx, outer, h, vel, stress, wind, cur,
               u_s, v_s, p_s, q_s, s_s, p3, p2, p1, mine, kept, *rest):
-    g = g_ref[0]
+    g = g_ref[0] & 3
     state = (u_s, v_s, p_s, q_s, s_s)
     ice_rows, cols = h.shape[1:]
     rows = cur.shape[1]
@@ -571,8 +577,8 @@
 
     def put(block, north, south):
         p3[block] = jnp.where(g == 3, north, south)
-        p2[block] = jnp.where(g == 2, north, south)
-        p1[block] = jnp.where((g == 1) | (g == 3), north, south)
+        p2[block] = jnp.where((g == 2) | (g == 3), north, south)
+        p1[block] = jnp.where(g == 1, north, south)
         mine[block] = jnp.where(g == 0, north, south)
 
     for k in range(bands):
@@ -584,7 +590,7 @@
 
 
 def ice_late(g_ref, rd, ra, rb, nx, outer, h, vel, stress, wind, kept, p2_in, p1_in, p2, p1, fixed, *scratch):
-    g = g_ref[0]
+    g = g_ref[0] & 3
     state, rest = scratch[:5], scratch[5:]
     ice_rows, cols = h.shape[1:]
     regs = cols // LANES + 1
@@ -668,7 +674,7 @@
 
 
 def ice_results(g_ref, u_s, v_s, p_s, q_s, s_s, fixed, vel_out, stress_out):
-    g = g_ref[0]
+    g = g_ref[0] & 3
     per = vel_out.shape[2] // SUB
     regs = u_s.shape[1]
     for cap in range(2):
@@ -705,7 +711,7 @@
 
 
 def ocean_before(g_ref, ra, rc, rd, nx, outer, base, gf, x0, g_s, invd, ra_out, gx_s, x_s, b_s):
-    g = g_ref[0]
+    g = g_ref[0] & 3
     rows, cols = base.shape
     regs = cols // LANES + 1
     per = rows // SUB
@@ -740,7 +746,7 @@
 
 def ocean_basis(g_ref, gw, invd, ra, r1, r2, r3, mine, y0_out, y1_out, y2_out, sums,
                 sp, u0_s, u1_s, u2_s):
-    g = g_ref[0]
+    g = g_ref[0] & 3
     regs = gw.shape[0]
     ext = gw.shape[1] // SUB - 2
     slab = r1.shape[0] // SUB - 2
@@ -784,13 +790,13 @@
     @pl.when(g == 1)
     def _():
         clear(range(2, ext))
-        put(0, strip(r1, slab - 1))
-        put(1, strip(r1, slab))
+        put(0, strip(r2, slab - 1))
+        put(1, strip(r2, slab))
 
     @pl.when(g == 2)
     def _():
         clear(range(ext - 1))
-        put(ext - 1, strip(r1, 0))
+        put(ext - 1, strip(r2, 0))
 
     acc = [[zero] * (regs - 1) for _ in range(6)]
 
@@ -894,7 +900,8 @@
     groups = lax.axis_size("grp")
     tiles = lax.axis_size("tile")
     assert groups == 4
-    g = lax.axis_index("grp").astype(jnp.int32).reshape(1)
+    assert tiles % 2 == 0
+    g = (lax.axis_index("grp") + groups * (lax.axis_index("tile") & 1)).astype(jnp.int32).reshape(1)
     rows, cols = base_rhs.shape
     ice_rows = ice_thick.shape[1]
     assert rows == groups * ice_rows
@@ -911,31 +918,32 @@
         sems=48,
         hbm=True,
     )
-    rc = lax.ppermute(c, "grp", [(0, 3), (3, 0), (1, 2), (2, 1)])
-    ra = lax.ppermute(a, "grp", [(0, 1), (1, 0), (2, 3), (3, 2)])
-    rb = lax.ppermute(b, "grp", [(0, 2), (3, 1)])
+    rc = lax.ppermute(c, "grp", DIAGONAL)
+    ra = lax.ppermute(a, "grp", FIRST)
+    rb = lax.ppermute(b, "grp", SECOND)
 
     own = sum(own_count(rows, ice_rows))
     packed = (-(-own // SLOTS) * SUB, LANES)
-    gf, h, left, right = call(
+    gf, h, inner, cross = call(
         pack_own,
         [(rows, cols), (2, ice_rows, cols), packed, packed],
         [g, token, base_rhs, depth, ssh_prev, currents, land_blocks, ice_thick, ice_blocks, ice_vel, ice_stress,
          wind],
     )
-    from_left = lax.ppermute(right, "tile", [(i, i + 1) for i in range(tiles - 1)])
-    from_right = lax.ppermute(left, "tile", [(i + 1, i) for i in range(tiles - 1)])
+    inner = lax.ppermute(inner, "tile", [(i, i ^ 1) for i in range(tiles)])
+    odd = range(1, tiles - 1, 2)
+    cross = lax.ppermute(cross, "tile", [(i, i + 1) for i in odd] + [(i + 1, i) for i in odd])
     strip_tiles = 2 * (slab // SUB)
     narrow_rows = -(-strip_tiles // WIDE_SLOTS) * SUB
     tail = -(-narrow_rows * LANES // (SUB * cols)) * SUB
     outer, narrow, d = call(
         pack_narrow,
         [(own * SUB, LANES), (groups, narrow_rows, LANES), ((2 * NICE + 2) * SUB + tail, cols)],
-        [g, from_left, from_right, h, gf, base_rhs, ssh_prev, ice_vel, ice_stress, wind],
+        [g, inner, cross, h, gf, base_rhs, ssh_prev, ice_vel, ice_stress, wind],
     )
     nx = lax.all_to_all(narrow, "grp", 0, 0, tiled=True)
     d, nx = lax.optimization_barrier((d, nx))
-    rd = lax.ppermute(d, "grp", [(0, 1), (3, 2)])
+    rd = lax.ppermute(d, "grp", FIRST)
 
     back = (ice_rows + 2 * SUB, cols)
     regs = cols // LANES + 1
@@ -956,8 +964,8 @@
         flops=20000000,
     )
     r3 = lax.ppermute(p3, "grp", [(3, 0), (0, 3)])
-    r2 = lax.ppermute(p2, "grp", [(2, 0), (1, 3)])
-    r1 = lax.ppermute(p1, "grp", [(1, 0), (2, 3), (3, 1), (0, 2)])
+    r2 = lax.ppermute(p2, "grp", SECOND)
+    r1 = lax.ppermute(p1, "grp", FIRST)
     velocity, stress = call(ice_results, [ice_vel.shape, ice_stress.shape], [g, *state, fixed], flops=10000000)
 
     field = (regs, rows + 4 * SUB, LANES)

time: 86 us -> 82.1 us (0.955)
  waiting for transfers between devices: 27.5 us -> 24.1 us
    ppermute x8, starting transfers between devices: 14.1 us -> 8.72 us  [the longest x1 2.02 us: shards(): ra = lax.ppermute(a, 'grp', FIRST)]
    ppermute x8, waiting for transfers between devices: 23.8 us -> 19.7 us  [the longest x1 14.8 us: shards(): rc = lax.ppermute(c, 'grp', DIAGONAL)]
    all_to_all x1, starting transfers between devices: 6.49 us -> 10.1 us  [shards(): lax.all_to_all(jnp.broadcast_to(sums[None], (devices, 1, LANES)), ('grp',...]
    all_to_all x1, waiting for transfers between devices: 0.01 us -> 1.51 us  [shards(): nx = lax.all_to_all(narrow, 'grp', 0, 0, tiled=True)]
    all_to_all x1, starting transfers between devices: 3.9 us -> 5.08 us  [shards(): nx = lax.all_to_all(narrow, 'grp', 0, 0, tiled=True)]
  transfers between devices with their start and end apart: 11 -> 11, of which waited for: 6 -> 6; matrix products, arithmetic and copies ran while one was open for 0% -> 0% of each run, Pallas kernels for 16% -> 17%
where the time goes in v8:
time: 82.1 us; the launch traced here: 81.5 us
  starting transfers between devices  27.5 us (33%)
  waiting for transfers between devices  24.1 us (29%)
  Pallas kernels  18.8 us (23%)
  local copies, waits for them, and re-layouts  10.1 us (12%)
  between operations  1.06 us (1%)
    pallas_call x9, Pallas kernels, call(): pl.pallas_call(body, out_shape=shapes, in_specs=specs, out_specs=tuple((v...  18.8 us
    ppermute x1, waiting for transfers between devices, shards(): rc = lax.ppermute(c, 'grp', DIAGONAL)  14.8 us
    all_to_all x1, starting transfers between devices, shards(): lax.all_to_all(jnp.broadcast_to(sums[None], (devices, 1, LANES)), ('grp',...  10.1 us
    unnamed x66, local copies, waits for them, and re-layouts  9.51 us
    all_to_all x1, starting transfers between devices, shards(): nx = lax.all_to_all(narrow, 'grp', 0, 0, tiled=True)  5.08 us
    ppermute x1, starting transfers between devices, shards(): r3 = lax.ppermute(p3, 'grp', [(3, 0), (0, 3)])  3.62 us
    all_to_all x1, waiting for transfers between devices, shards(): lax.all_to_all(jnp.broadcast_to(sums[None], (devices, 1, LANES)), ('grp',...  2.89 us
    ppermute x1, waiting for transfers between devices, shards(): r2 = lax.ppermute(p2, 'grp', SECOND)  2.59 us
  transfers between devices with their start and end apart: 11, of which 6 were waited for; matrix products, arithmetic and copies ran while one was open for 0% of the time, Pallas kernels for 17%

profile of v8, /device:TPU:0, one launch (start us, length us, event | category | flops | bytes accessed | tf_op | source)
XLA Modules:
  0.0 81.5 jit_solution(7412227603414357003)
XLA Ops:
  0.7 0.0 copy-start.4
  0.7 0.0 copy-start.6
  0.7 1.8 %shard_map.121 = (f32[144,512]{1,0:T(8,128)S(1)}, f32[160,512]{1,0:T(8,128)S(1)}, f32[160,512]{1,0:T(8,128)S(1)}, f32[8,128]{1,0:T(8,128)S(1)}) custom-call(s32[1]{0:T(128)} %bitcast.g_ref, f32[256,512]{1,0:T(8,128)} %base.7, f32[256,512]{1,0:T(8,128)} %depth.3, f32[256,512]{1,0:T(8,128)} %x0.9, f32[2,256,512]{2,1,0:T(8,128)} %cur.5, s32[32,64]{1,0:T(8,128)} %land.3, ...), custom_call_target="tpu_custom_call" | custom-call | flops 1000000 | bytes 4000000 | tf_op jit(solution)/shard_map/pallas_call | solution.py:49
  2.6 0.0 copy-start.29
  2.6 0.7 copy-done.29
  3.3 0.7 copy-done.30
  4.1 0.7 copy-done.32
  4.8 0.4 shard_map.122
  5.3 0.0 copy-start.10
  5.3 0.6 collective-permute-start.2
  5.8 0.7 collective-permute-start.3
  6.5 0.3 collective-permute-done.2.inner
  6.8 0.0 collective-permute-done.3.cross
  6.8 0.5 shard_map.123
  7.4 0.6 copy-done.26
  8.0 0.7 copy-done.31
  8.7 5.1 %all-to-all-start = ((f32[4,40,128]{2,1,0:T(8,128)}), f32[4,40,128]{2,1,0:T(8,128)}, u32[]{:S(2)}, u32[]{:S(2)}) async-start(f32[4,40,128]{2,1,0:T(8,128)} %copy-done.26), calls=%async_computation | async-start | bytes 163840 | tf_op jit(solution)/shard_map/all_to_all | solution.py:944
  13.8 2.0 %collective-permute-start = (f32[160,512]{1,0:T(8,128)}, f32[160,512]{1,0:T(8,128)}, u32[]{:S(2)}, u32[]{:S(2)}) collective-permute-start(f32[160,512]{1,0:T(8,128)} %copy-done.30), channel_id=1, source_target_pairs={{0,8},{8,0},{16,24},{24,16},{1,9},{9,1},{17,25},{25,17},{2,10},{10... | collective-permute-start | bytes 983048 | tf_op jit(solution)/shard_map/ppermute | solution.py:922
  15.8 1.5 %collective-permute-start.5 = (f32[160,512]{1,0:T(8,128)}, f32[160,512]{1,0:T(8,128)}, u32[]{:S(2)}, u32[]{:S(2)}) collective-permute-start(f32[160,512]{1,0:T(8,128)} %copy-done.29), channel_id=1, source_target_pairs={{0,16},{16,0},{8,24},{24,8},{1,17},{17,1},{9,25},{25,9},{2,18},{18... | collective-permute-start | bytes 983048 | tf_op jit(solution)/shard_map/ppermute | solution.py:923
  17.3 1.5 %all-to-all-done.nx = f32[4,40,128]{2,1,0:T(8,128)} async-done(((f32[4,40,128]{2,1,0:T(8,128)}), f32[4,40,128]{2,1,0:T(8,128)}, u32[]{:S(2)}, u32[]{:S(2)}) %all-to-all-start) | async-done | bytes 81952 | tf_op jit(solution)/shard_map/all_to_all | solution.py:944
  18.8 0.8 collective-permute-start.4
  19.6 1.5 %collective-permute-start.1 = (f32[144,512]{1,0:T(8,128)}, f32[144,512]{1,0:T(8,128)S(1)}, u32[]{:S(2)}, u32[]{:S(2)}) collective-permute-start(f32[144,512]{1,0:T(8,128)} %copy-done.32), channel_id=1, source_target_pairs={{0,24},{24,0},{8,16},{16,8},{1,25},{25,1},{9,17},{17,9},{2,26},{26... | collective-permute-start | bytes 884744 | tf_op jit(solution)/shard_map/ppermute | solution.py:921
  21.0 14.8 %collective-permute-done.1.rc = f32[144,512]{1,0:T(8,128)S(1)} collective-permute-done((f32[144,512]{1,0:T(8,128)}, f32[144,512]{1,0:T(8,128)S(1)}, u32[]{:S(2)}, u32[]{:S(2)}) %collective-permute-start.1) | collective-permute-done | bytes 294944 | tf_op jit(solution)/shard_map/ppermute | solution.py:921
  35.9 1.2 %copy-done.5 = f32[2,256,512]{2,1,0:T(8,128)S(1)} copy-done((f32[2,256,512]{2,1,0:T(8,128)S(1)}, f32[2,256,512]{2,1,0:T(8,128)}, u32[]{:S(2)}) %copy-start.5) | copy-done | bytes 1048600
  37.1 0.9 %copy-done.9 = f32[2,64,512]{2,1,0:T(8,128)S(1)} copy-done((f32[2,64,512]{2,1,0:T(8,128)S(1)}, f32[2,64,512]{2,1,0:T(8,128)}, u32[]{:S(2)}) %copy-start.9) | copy-done | bytes 262168
  38.0 9.5 %shard_map.125 = (f32[2,5,96,128]{3,2,1,0:T(8,128)S(1)}, f32[2,5,96,128]{3,2,1,0:T(8,128)S(1)}, f32[2,5,96,128]{3,2,1,0:T(8,128)S(1)}, f32[2,5,96,128]{3,2,1,0:T...) custom-call(s32[1]{0:T(128)} %bitcast.g_ref, ...), custom_call_target="tpu_custom_call" | custom-call | flops 20000000 | bytes 4000000 | tf_op jit(solution)/shard_map/pallas_call | solution.py:49
  47.5 0.0 copy-start.14
  47.5 0.0 copy-start.16
  47.6 3.6 %collective-permute-start.8 = (f32[80,512]{1,0:T(8,128)S(1)}, f32[80,512]{1,0:T(8,128)S(1)}, u32[]{:S(2)}, u32[]{:S(2)}) collective-permute-start(f32[80,512]{1,0:T(8,128)S(1)} %get-tuple-element.59), channel_id=1, source_target_pairs={{24,0},{0,24},{25,1},{1,25},{26,2},{2,26},{27,3},{3,27},{28,4},{4,... | collective-permute-start | bytes 491528 | tf_op jit(solution)/shard_map/ppermute | solution.py:966
  51.2 0.0 collective-permute-done.4.rd
  51.2 0.0 copy-start.7
  51.2 0.0 copy-start.11
  51.2 1.2 %shard_map.126 = (f32[80,512]{1,0:T(8,128)S(1)}, f32[80,512]{1,0:T(8,128)S(1)}, f32[2,5,8,512]{3,2,1,0:T(8,128)S(1)}) custom-call(s32[1]{0:T(128)} %bitcast.g_ref, f32[160,512]{1,0:T(8,128)S(1)} %collective-permute-done.4.rd, f32[160,512]{1,0:T(8,128)} %collective-permute-done.ra, f32[160,512]{1,0:T(8,128)} %collective-permute-done.5.rb, ...), custom_call_target="tpu_custom_call" | custom-call | flops 20000000 | bytes 4000000 | tf_op jit(solution)/shard_map/pallas_call | solution.py:49
  52.5 0.7 copy-done.24
  53.2 1.0 %collective-permute-start.6 = (f32[80,512]{1,0:T(8,128)S(1)}, f32[80,512]{1,0:T(8,128)S(1)}, u32[]{:S(2)}, u32[]{:S(2)}) collective-permute-start(f32[80,512]{1,0:T(8,128)S(1)} %get-tuple-element.57), channel_id=1, source_target_pairs={{0,8},{8,0},{16,24},{24,16},{1,9},{9,1},{17,25},{25,17},{2,10},{10... | collective-permute-start | bytes 491528 | tf_op jit(solution)/shard_map/ppermute | solution.py:968
  54.1 0.8 collective-permute-start.7
  54.9 1.8 %shard_map.124 = (f32[5,288,128]{2,1,0:T(8,128)S(1)}, f32[5,288,128]{2,1,0:T(8,128)S(1)}, f32[5,288,128]{2,1,0:T(8,128)S(1)}) custom-call(s32[1]{0:T(128)} %bitcast.g_ref, f32[160,512]{1,0:T(8,128)} %collective-permute-done.ra, f32[144,512]{1,0:T(8,128)S(1)} %collective-permute-done.1.rc, f32[160,512]{1,0:T(8,128)S(1)} %collective-permute-done.4.rd, ...), custom_call_target="tpu_custom_call" | custom-call | flops 20000000 | bytes 4000000 | tf_op jit(solution)/shard_map/pallas_call | solution.py:49
  56.7 1.9 %collective-permute-done.6.r1 = f32[80,512]{1,0:T(8,128)S(1)} collective-permute-done((f32[80,512]{1,0:T(8,128)S(1)}, f32[80,512]{1,0:T(8,128)S(1)}, u32[]{:S(2)}, u32[]{:S(2)}) %collective-permute-start.6) | collective-permute-done | bytes 163872 | tf_op jit(solution)/shard_map/ppermute | solution.py:968
  58.7 2.6 %collective-permute-done.7.r2 = f32[80,512]{1,0:T(8,128)S(1)} collective-permute-done((f32[80,512]{1,0:T(8,128)S(1)}, f32[80,512]{1,0:T(8,128)S(1)}, u32[]{:S(2)}, u32[]{:S(2)}) %collective-permute-start.7) | collective-permute-done | bytes 163872 | tf_op jit(solution)/shard_map/ppermute | solution.py:967
  61.2 1.4 %shard_map.127 = (f32[4,256,128]{2,1,0:T(8,128)S(1)}, f32[4,256,128]{2,1,0:T(8,128)S(1)}, f32[4,256,128]{2,1,0:T(8,128)S(1)}, f32[1,128]{1,0:T(1,128)S(1)}) custom-call(s32[1]{0:T(128)} %bitcast.g_ref, f32[5,288,128]{2,1,0:T(8,128)S(1)} %get-tuple-element.50.gw, f32[5,288,128]{2,1,0:T(8,128)S(1)} %get-tuple-element.51.invd, ...), custom_call_target="tpu_custom_call" | custom-call | flops 1000000 | bytes 4000000 | tf_op jit(solution)/shard_map/pallas_call | solution.py:49
  62.6 0.6 broadcast_in_dim.9
  63.2 10.1 %all-to-all-start.1 = ((f32[32,1,128]{2,1,0:T(1,128)}), f32[32,1,128]{2,1,0:T(1,128)S(1)}, u32[]{:S(2)}, u32[]{:S(2)}) async-start(f32[32,1,128]{2,1,0:T(1,128)} %broadcast_in_dim.9), calls=%async_computation.1 | async-start | bytes 32768 | tf_op jit(solution)/shard_map/all_to_all | solution.py:986
  73.3 1.0 %copy-done.19 = f32[2,5,96,128]{3,2,1,0:T(8,128)S(1)} copy-done((f32[2,5,96,128]{3,2,1,0:T(8,128)S(1)}, f32[2,5,96,128]{3,2,1,0:T(8,128)}, u32[]{:S(2)}) %copy-start.19) | copy-done | bytes 491544
  74.4 1.0 %copy-done.21 = f32[2,5,96,128]{3,2,1,0:T(8,128)S(1)} copy-done((f32[2,5,96,128]{3,2,1,0:T(8,128)S(1)}, f32[2,5,96,128]{3,2,1,0:T(8,128)}, u32[]{:S(2)}) %copy-start.21) | copy-done | bytes 491544
  75.4 1.0 %copy-done.23 = f32[2,5,96,128]{3,2,1,0:T(8,128)S(1)} copy-done((f32[2,5,96,128]{3,2,1,0:T(8,128)S(1)}, f32[2,5,96,128]{3,2,1,0:T(8,128)}, u32[]{:S(2)}) %copy-start.23) | copy-done | bytes 491544
  76.4 1.1 %shard_map.129 = (f32[2,2,64,512]{3,2,1,0:T(8,128)}, f32[3,2,64,512]{3,2,1,0:T(8,128)}) custom-call(s32[1]{0:T(128)} %bitcast.g_ref, f32[2,5,96,128]{3,2,1,0:T(8,128)S(1)} %copy-done.15, f32[2,5,96,128]{3,2,1,0:T(8,128)S(1)} %copy-done.17, f32[2,5,96,128]{3,2,1,0:T(8,128)S(1)} %copy-done.19, f32[2,5,96,128]{3,2,1,0:T(8,128)S(1)} %copy-done.21, ...), custom_call_target="tpu_custom_call" | custom-call | flops 10000000 | bytes 4000000 | tf_op jit(solution)/shard_map/pallas_call | solution.py:49
  77.6 2.9 %all-to-all-done.1.parts = f32[32,1,128]{2,1,0:T(1,128)S(1)} async-done(((f32[32,1,128]{2,1,0:T(1,128)}), f32[32,1,128]{2,1,0:T(1,128)S(1)}, u32[]{:S(2)}, u32[]{:S(2)}) %all-to-all-start.1) | async-done | bytes 16416 | tf_op jit(solution)/shard_map/all_to_all | solution.py:986
  80.5 1.1 %shard_map.128 = f32[256,512]{1,0:T(8,128)} custom-call(s32[1]{0:T(128)} %bitcast.g_ref, f32[32,1,128]{2,1,0:T(1,128)S(1)} %all-to-all-done.1.parts, f32[256,512]{1,0:T(8,128)S(1)} %copy-done.3, f32[4,256,128]{2,1,0:T(8,128)S(1)} %get-tuple-element.62.y0, f32[4,256,128]{2,1,0:T(8,128)S(1)} %get-tuple-element.63.y1, f32[4,256,128]{2,1,0:T(8,128)S(1)} %get-tuple-element.64.y2), custom_call_target="tpu_custom_call" | custom-call | flops 1000000 | bytes 4000000 | tf_op jit(solution)/shard_map/pallas_call | solution.py:49
  (50 shorter events, 0.1 us)
Async XLA Ops:
  0.6 4.1 %copy-start = (f32[3,2,64,512]{3,2,1,0:T(8,128)S(1)}, f32[3,2,64,512]{3,2,1,0:T(8,128)}, u32[]{:S(2)}) copy-start(f32[3,2,64,512]{3,2,1,0:T(8,128)} %stress.9) | copy-start | bytes 2359300
  0.7 4.1 %copy-start.1 = (f32[2,2,64,512]{3,2,1,0:T(8,128)S(1)}, f32[2,2,64,512]{3,2,1,0:T(8,128)}, u32[]{:S(2)}) copy-start(f32[2,2,64,512]{3,2,1,0:T(8,128)} %vel.9) | copy-start | bytes 1572868
  0.7 4.1 %copy-start.2 = (f32[2,2,64,512]{3,2,1,0:T(8,128)S(1)}, f32[2,2,64,512]{3,2,1,0:T(8,128)}, u32[]{:S(2)}) copy-start(f32[2,2,64,512]{3,2,1,0:T(8,128)} %wind.9) | copy-start | bytes 1572868
  0.7 4.1 %copy-start.3 = (f32[256,512]{1,0:T(8,128)S(1)}, f32[256,512]{1,0:T(8,128)}, u32[]{:S(2)}) copy-start(f32[256,512]{1,0:T(8,128)} %x0.9) | copy-start | bytes 1572868
  0.7 4.1 %copy-start.4 = (f32[2,256,512]{2,1,0:T(8,128)S(1)}, f32[2,256,512]{2,1,0:T(8,128)}, u32[]{:S(2)}) copy-start(f32[2,256,512]{2,1,0:T(8,128)} %cur.5) | copy-start | bytes 3145732
  0.7 4.1 %copy-start.6 = (f32[256,512]{1,0:T(8,128)S(1)}, f32[256,512]{1,0:T(8,128)}, u32[]{:S(2)}) copy-start(f32[256,512]{1,0:T(8,128)} %base.7) | copy-start | bytes 1572868
  0.7 4.1 %copy-start.12 = (f32[256,512]{1,0:T(8,128)S(1)}, f32[256,512]{1,0:T(8,128)}, u32[]{:S(2)}) copy-start(f32[256,512]{1,0:T(8,128)} %depth.3) | copy-start | bytes 1572868
  0.7 4.1 %copy-start.13 = (f32[2,64,512]{2,1,0:T(8,128)S(1)}, f32[2,64,512]{2,1,0:T(8,128)}, u32[]{:S(2)}) copy-start(f32[2,64,512]{2,1,0:T(8,128)} %thick.3) | copy-start | bytes 786436
  0.7 4.1 %copy-start.27 = (s32[32,64]{1,0:T(8,128)S(1)}, s32[32,64]{1,0:T(8,128)}, u32[]{:S(2)}) copy-start(s32[32,64]{1,0:T(8,128)} %land.3) | copy-start | bytes 24580
  0.7 4.1 %copy-start.28 = (s32[2,8,64]{2,1,0:T(8,128)S(1)}, s32[2,8,64]{2,1,0:T(8,128)}, u32[]{:S(2)}) copy-start(s32[2,8,64]{2,1,0:T(8,128)} %iceb.3) | copy-start | bytes 12292
  2.6 0.7 copy-start.29
  3.3 0.7 copy-start.30
  4.0 0.7 copy-start.32
  5.3 2.1 %copy-start.8 = (f32[2,64,512]{2,1,0:T(8,128)}, f32[2,64,512]{2,1,0:T(8,128)S(1)}, u32[]{:S(2)}) copy-start(f32[2,64,512]{2,1,0:T(8,128)S(1)} %get-tuple-element.43.h) | copy-start | bytes 786436
  5.3 2.1 %copy-start.10 = (f32[256,512]{1,0:T(8,128)}, f32[256,512]{1,0:T(8,128)S(1)}, u32[]{:S(2)}) copy-start(f32[256,512]{1,0:T(8,128)S(1)} %get-tuple-element.44.gf) | copy-start | bytes 1572868
  5.3 1.6 %collective-permute-start.2 = (f32[288,128]{1,0:T(8,128)S(1)}, f32[288,128]{1,0:T(8,128)S(1)}, u32[]{:S(2)}, u32[]{:S(2)}) collective-permute-start(f32[288,128]{1,0:T(8,128)S(1)} %get-tuple-element.41), channel_id=1, source_target_pairs={{0,1},{1,0},{2,3},{3,2},{4,5},{5,4},{6,7},{7,6},{8,9},{9,8},{10,11... | collective-permute-start | bytes 442376 | tf_op jit(solution)/shard_map/ppermute | solution.py:933
  5.8 1.0 %collective-permute-start.3 = (f32[288,128]{1,0:T(8,128)S(1)}, f32[288,128]{1,0:T(8,128)S(1)}, u32[]{:S(2)}, u32[]{:S(2)}) collective-permute-start(f32[288,128]{1,0:T(8,128)S(1)} %get-tuple-element.42), channel_id=1, source_target_pairs={{1,2},{3,4},{5,6},{2,1},{4,3},{6,5},{9,10},{11,12},{13,14},{10,9},... | collective-permute-start | bytes 442376 | tf_op jit(solution)/shard_map/ppermute | solution.py:935
  7.3 0.6 copy-start.26
  8.0 0.7 copy-start.31
  8.7 10.1 %all-to-all-start = ((f32[4,40,128]{2,1,0:T(8,128)}), f32[4,40,128]{2,1,0:T(8,128)}, u32[]{:S(2)}, u32[]{:S(2)}) async-start(f32[4,40,128]{2,1,0:T(8,128)} %copy-done.26), calls=%async_computation | async-start | bytes 163840 | tf_op jit(solution)/shard_map/all_to_all | solution.py:944
  13.8 22.1 %collective-permute-start = (f32[160,512]{1,0:T(8,128)}, f32[160,512]{1,0:T(8,128)}, u32[]{:S(2)}, u32[]{:S(2)}) collective-permute-start(f32[160,512]{1,0:T(8,128)} %copy-done.30), channel_id=1, source_target_pairs={{0,8},{8,0},{16,24},{24,16},{1,9},{9,1},{17,25},{25,17},{2,10},{10... | collective-permute-start | bytes 983048 | tf_op jit(solution)/shard_map/ppermute | solution.py:922
  15.8 20.1 %collective-permute-start.5 = (f32[160,512]{1,0:T(8,128)}, f32[160,512]{1,0:T(8,128)}, u32[]{:S(2)}, u32[]{:S(2)}) collective-permute-start(f32[160,512]{1,0:T(8,128)} %copy-done.29), channel_id=1, source_target_pairs={{0,16},{16,0},{8,24},{24,8},{1,17},{17,1},{9,25},{25,9},{2,18},{18... | collective-permute-start | bytes 983048 | tf_op jit(solution)/shard_map/ppermute | solution.py:923
  18.8 32.4 %collective-permute-start.4 = (f32[160,512]{1,0:T(8,128)}, f32[160,512]{1,0:T(8,128)S(1)}, u32[]{:S(2)}, u32[]{:S(2)}) collective-permute-start(f32[160,512]{1,0:T(8,128)} %copy-done.31), channel_id=1, source_target_pairs={{0,8},{8,0},{16,24},{24,16},{1,9},{9,1},{17,25},{25,17},{2,10},{10... | collective-permute-start | bytes 983048 | tf_op jit(solution)/shard_map/ppermute | solution.py:946
  19.6 16.3 %collective-permute-start.1 = (f32[144,512]{1,0:T(8,128)}, f32[144,512]{1,0:T(8,128)S(1)}, u32[]{:S(2)}, u32[]{:S(2)}) collective-permute-start(f32[144,512]{1,0:T(8,128)} %copy-done.32), channel_id=1, source_target_pairs={{0,24},{24,0},{8,16},{16,8},{1,25},{25,1},{9,17},{17,9},{2,26},{26... | collective-permute-start | bytes 884744 | tf_op jit(solution)/shard_map/ppermute | solution.py:921
  35.9 1.2 %copy-start.5 = (f32[2,256,512]{2,1,0:T(8,128)S(1)}, f32[2,256,512]{2,1,0:T(8,128)}, u32[]{:S(2)}) copy-start(f32[2,256,512]{2,1,0:T(8,128)} %cur.5) | copy-start | bytes 3145732
  37.1 0.9 %copy-start.9 = (f32[2,64,512]{2,1,0:T(8,128)S(1)}, f32[2,64,512]{2,1,0:T(8,128)}, u32[]{:S(2)}) copy-start(f32[2,64,512]{2,1,0:T(8,128)} %copy-done.8) | copy-start | bytes 786436
  47.5 4.9 %copy-start.14 = (f32[2,5,96,128]{3,2,1,0:T(8,128)}, f32[2,5,96,128]{3,2,1,0:T(8,128)S(1)}, u32[]{:S(2)}) copy-start(f32[2,5,96,128]{3,2,1,0:T(8,128)S(1)} %get-tuple-element.65.u_s) | copy-start | bytes 1474564
  47.5 4.9 %copy-start.16 = (f32[2,5,96,128]{3,2,1,0:T(8,128)}, f32[2,5,96,128]{3,2,1,0:T(8,128)S(1)}, u32[]{:S(2)}) copy-start(f32[2,5,96,128]{3,2,1,0:T(8,128)S(1)} %get-tuple-element.66.v_s) | copy-start | bytes 1474564
  47.5 4.9 %copy-start.18 = (f32[2,5,96,128]{3,2,1,0:T(8,128)}, f32[2,5,96,128]{3,2,1,0:T(8,128)S(1)}, u32[]{:S(2)}) copy-start(f32[2,5,96,128]{3,2,1,0:T(8,128)S(1)} %get-tuple-element.67.p_s) | copy-start | bytes 1474564
  47.5 4.9 %copy-start.20 = (f32[2,5,96,128]{3,2,1,0:T(8,128)}, f32[2,5,96,128]{3,2,1,0:T(8,128)S(1)}, u32[]{:S(2)}) copy-start(f32[2,5,96,128]{3,2,1,0:T(8,128)S(1)} %get-tuple-element.68.q_s) | copy-start | bytes 1474564
  47.6 4.9 %copy-start.22 = (f32[2,5,96,128]{3,2,1,0:T(8,128)}, f32[2,5,96,128]{3,2,1,0:T(8,128)S(1)}, u32[]{:S(2)}) copy-start(f32[2,5,96,128]{3,2,1,0:T(8,128)S(1)} %get-tuple-element.69.s_s) | copy-start | bytes 1474564
  47.6 9.2 %collective-permute-start.8 = (f32[80,512]{1,0:T(8,128)S(1)}, f32[80,512]{1,0:T(8,128)S(1)}, u32[]{:S(2)}, u32[]{:S(2)}) collective-permute-start(f32[80,512]{1,0:T(8,128)S(1)} %get-tuple-element.59), channel_id=1, source_target_pairs={{24,0},{0,24},{25,1},{1,25},{26,2},{2,26},{27,3},{3,27},{28,4},{4,... | collective-permute-start | bytes 491528 | tf_op jit(solution)/shard_map/ppermute | solution.py:966
  51.2 3.7 %copy-start.7 = (f32[256,512]{1,0:T(8,128)S(1)}, f32[256,512]{1,0:T(8,128)}, u32[]{:S(2)}) copy-start(f32[256,512]{1,0:T(8,128)} %base.7) | copy-start | bytes 1572868
  51.2 3.7 %copy-start.11 = (f32[256,512]{1,0:T(8,128)S(1)}, f32[256,512]{1,0:T(8,128)}, u32[]{:S(2)}) copy-start(f32[256,512]{1,0:T(8,128)} %copy-done.10) | copy-start | bytes 1572868
  52.5 0.7 copy-start.24
  53.2 5.5 %collective-permute-start.6 = (f32[80,512]{1,0:T(8,128)S(1)}, f32[80,512]{1,0:T(8,128)S(1)}, u32[]{:S(2)}, u32[]{:S(2)}) collective-permute-start(f32[80,512]{1,0:T(8,128)S(1)} %get-tuple-element.57), channel_id=1, source_target_pairs={{0,8},{8,0},{16,24},{24,16},{1,9},{9,1},{17,25},{25,17},{2,10},{10... | collective-permute-start | bytes 491528 | tf_op jit(solution)/shard_map/ppermute | solution.py:968
  54.1 7.1 %collective-permute-start.7 = (f32[80,512]{1,0:T(8,128)S(1)}, f32[80,512]{1,0:T(8,128)S(1)}, u32[]{:S(2)}, u32[]{:S(2)}) collective-permute-start(f32[80,512]{1,0:T(8,128)S(1)} %get-tuple-element.58), channel_id=1, source_target_pairs={{0,16},{16,0},{8,24},{24,8},{1,17},{17,1},{9,25},{25,9},{2,18},{18... | collective-permute-start | bytes 491528 | tf_op jit(solution)/shard_map/ppermute | solution.py:967
  61.2 12.1 %copy-start.15 = (f32[2,5,96,128]{3,2,1,0:T(8,128)S(1)}, f32[2,5,96,128]{3,2,1,0:T(8,128)}, u32[]{:S(2)}) copy-start(f32[2,5,96,128]{3,2,1,0:T(8,128)} %copy-done.14) | copy-start | bytes 1474564
  61.2 12.1 %copy-start.17 = (f32[2,5,96,128]{3,2,1,0:T(8,128)S(1)}, f32[2,5,96,128]{3,2,1,0:T(8,128)}, u32[]{:S(2)}) copy-start(f32[2,5,96,128]{3,2,1,0:T(8,128)} %copy-done.16) | copy-start | bytes 1474564
  61.2 12.1 %copy-start.25 = (f32[2,5,8,512]{3,2,1,0:T(8,128)S(1)}, f32[2,5,8,512]{3,2,1,0:T(8,128)}, u32[]{:S(2)}) copy-start(f32[2,5,8,512]{3,2,1,0:T(8,128)} %copy-done.24) | copy-start | bytes 491524
  63.2 17.2 %all-to-all-start.1 = ((f32[32,1,128]{2,1,0:T(1,128)}), f32[32,1,128]{2,1,0:T(1,128)S(1)}, u32[]{:S(2)}, u32[]{:S(2)}) async-start(f32[32,1,128]{2,1,0:T(1,128)} %broadcast_in_dim.9), calls=%async_computation.1 | async-start | bytes 32768 | tf_op jit(solution)/shard_map/all_to_all | solution.py:986
  73.3 1.0 %copy-start.19 = (f32[2,5,96,128]{3,2,1,0:T(8,128)S(1)}, f32[2,5,96,128]{3,2,1,0:T(8,128)}, u32[]{:S(2)}) copy-start(f32[2,5,96,128]{3,2,1,0:T(8,128)} %copy-done.18) | copy-start | bytes 1474564
  74.4 1.0 %copy-start.21 = (f32[2,5,96,128]{3,2,1,0:T(8,128)S(1)}, f32[2,5,96,128]{3,2,1,0:T(8,128)}, u32[]{:S(2)}) copy-start(f32[2,5,96,128]{3,2,1,0:T(8,128)} %copy-done.20) | copy-start | bytes 1474564
  75.4 1.0 %copy-start.23 = (f32[2,5,96,128]{3,2,1,0:T(8,128)S(1)}, f32[2,5,96,128]{3,2,1,0:T(8,128)}, u32[]{:S(2)}) copy-start(f32[2,5,96,128]{3,2,1,0:T(8,128)} %copy-done.22) | copy-start | bytes 1474564

commit v9 on v8

--- a/solution.py
+++ b/solution.py
@@ -489,6 +489,19 @@
     return d0, d1
 
 
+def tail_regs(per, inner):
+    used = -(-(per + 1) // WIDE_SLOTS) + 1
+    return -(-used // inner) * inner
+
+
+def stacked_rows(values):
+    row = row_iota(LANES)
+    total = jnp.where(row == 0, values[0], 0.0)
+    for c in range(1, len(values)):
+        total = total + jnp.where(row == c, pltpu.roll(values[c], c, 0), 0.0)
+    return total
+
+
 def packed_edge(edge, k, lane):
     edge = jnp.where((lane < EDGE) | (lane >= LANES - EDGE), edge, 0.0)
     i = k % WIDE_SLOTS
@@ -581,12 +594,14 @@
         p1[block] = jnp.where(g == 1, north, south)
         mine[block] = jnp.where(g == 0, north, south)
 
-    for k in range(bands):
+    for k in range(per):
         for c in range(regs - 1):
             put((tile(k), slice(c * LANES, (c + 1) * LANES)), spreads[0][k][c], spreads[1][k][c])
-    for c in range(regs - 1):
+    for cap in range(2):
+        packs[cap].append(stacked_rows(spreads[cap][per][: regs - 1]))
+    for c in range(tail_regs(per, regs - 1)):
         pair = [pack[c] if c < len(pack) else zero for pack in packs]
-        put((tile(bands), slice(c * LANES, (c + 1) * LANES)), *pair)
+        put((tile(per + c // (regs - 1)), slice(c % (regs - 1) * LANES, (c % (regs - 1) + 1) * LANES)), *pair)
 
 
 def ice_late(g_ref, rd, ra, rb, nx, outer, h, vel, stress, wind, kept, p2_in, p1_in, p2, p1, fixed, *scratch):
@@ -596,7 +611,6 @@
     regs = cols // LANES + 1
     per = ice_rows // SUB
     ext = per + 2
-    bands = per + 1
     lane = lane_iota()
     row = row_iota(LANES)
     zero = jnp.zeros((SUB, LANES), F32)
@@ -651,18 +665,25 @@
                     fixed[cap, 4, :, cut] = state[4][cap, c, at(1), :]
             out = outs[cap]
             k = 0 if group == 1 else per - 1
+
+            def spot(c):
+                c, t = c % (regs - 1), c // (regs - 1)
+                return tile(per + t), slice(c * LANES, (c + 1) * LANES)
+
             for c in range(regs - 1):
                 cut = slice(c * LANES, (c + 1) * LANES)
                 out[tile(k), cut] = bits[c][0]
-                out[tile(k + 1), cut] = out[tile(k + 1), cut] + bits[c][1] if group == 1 else bits[c][1]
+                if group == 1:
+                    out[tile(k + 1), cut] = out[tile(k + 1), cut] + bits[c][1]
+            if group == 2:
+                out[spot(-(-(per + 1) // WIDE_SLOTS))] = stacked_rows([b[1] for b in bits[: regs - 1]])
             for n, add in ((k, False), (k + 1, group == 1)):
                 c = n // WIDE_SLOTS
-                cut = slice(c * LANES, (c + 1) * LANES)
                 edge = packed_edge(bits[regs - 1][n - k], n, lane)
                 start = (2 * EDGE * (n % WIDE_SLOTS) - EDGE) % LANES
                 inside = (lane - start) % LANES < 2 * EDGE if start else lane < 2 * EDGE
-                old = out[tile(bands), cut]
-                out[tile(bands), cut] = old + edge if add else jnp.where(inside, edge, old)
+                old = out[spot(c)]
+                out[spot(c)] = old + edge if add else jnp.where(inside, edge, old)
 
     @pl.when(g == 1)
     def _():
@@ -749,14 +770,22 @@
     g = g_ref[0] & 3
     regs = gw.shape[0]
     ext = gw.shape[1] // SUB - 2
-    slab = r1.shape[0] // SUB - 2
+    inner = regs - 1
+    slab = (gw.shape[1] // SUB - 4) // 4
+    row = row_iota(LANES)
     lane = lane_iota()
     zero = jnp.zeros((SUB, LANES), F32)
     clear_ends((u0_s, u1_s, u2_s), ext)
 
     def strip(ref, k):
-        n, i = k // WIDE_SLOTS, k % WIDE_SLOTS
-        return split(ref[tile(k), :]) + [wide_outer(ref[tile(slab + 1), n * LANES : (n + 1) * LANES], i, lane)]
+        def spot(c):
+            return ref[tile(slab + c // inner), c % inner * LANES : (c % inner + 1) * LANES]
+
+        edge = wide_outer(spot(k // WIDE_SLOTS), k % WIDE_SLOTS, lane)
+        if k < slab:
+            return split(ref[tile(k), :]) + [edge]
+        below = spot(-(-(slab + 1) // WIDE_SLOTS))
+        return [jnp.where(row == 0, pltpu.roll(below, SUB - c, 0) if c else below, 0.0) for c in range(inner)] + [edge]
 
     def put(j, values):
         for c in range(regs):
@@ -945,8 +974,8 @@
     d, nx = lax.optimization_barrier((d, nx))
     rd = lax.ppermute(d, "grp", FIRST)
 
-    back = (ice_rows + 2 * SUB, cols)
     regs = cols // LANES + 1
+    back = (ice_rows + tail_regs(ice_rows // SUB, regs - 1) // (regs - 1) * SUB, cols)
     held = (2, regs, slab + 2 * SUB, LANES)
     *state, p3, p2, p1, mine, kept = call(
         ice_steps,

time: 82.1 us -> 81.7 us (level)
  no operation moved by 1% of the time
where the time goes in v9:
time: 81.7 us; the launch traced here: 81.2 us
  starting transfers between devices  27.9 us (34%)
  waiting for transfers between devices  23.4 us (29%)
  Pallas kernels  18.7 us (23%)
  local copies, waits for them, and re-layouts  10.1 us (12%)
  between operations  1.06 us (1%)
    pallas_call x9, Pallas kernels, call(): pl.pallas_call(body, out_shape=shapes, in_specs=specs, out_specs=tuple((v...  18.7 us
    ppermute x1, waiting for transfers between devices, shards(): rc = lax.ppermute(c, 'grp', DIAGONAL)  14.8 us
    all_to_all x1, starting transfers between devices, shards(): lax.all_to_all(jnp.broadcast_to(sums[None], (devices, 1, LANES)), ('grp',...  10.4 us
    unnamed x66, local copies, waits for them, and re-layouts  9.51 us
    all_to_all x1, starting transfers between devices, shards(): nx = lax.all_to_all(narrow, 'grp', 0, 0, tiled=True)  5.08 us
    ppermute x1, starting transfers between devices, shards(): r3 = lax.ppermute(p3, 'grp', [(3, 0), (0, 3)])  3.62 us
    all_to_all x1, waiting for transfers between devices, shards(): lax.all_to_all(jnp.broadcast_to(sums[None], (devices, 1, LANES)), ('grp',...  2.89 us
    ppermute x1, waiting for transfers between devices, shards(): r2 = lax.ppermute(p2, 'grp', SECOND)  2.28 us
  transfers between devices with their start and end apart: 11, of which 6 were waited for; matrix products, arithmetic and copies ran while one was open for 0% of the time, Pallas kernels for 17%

profile of v9, /device:TPU:0, one launch (start us, length us, event | category | flops | bytes accessed | tf_op | source)
XLA Modules:
  0.0 81.2 jit_solution(1852104686066545910)
XLA Ops:
  0.7 0.0 copy-start.4
  0.7 0.0 copy-start.6
  0.7 1.8 %shard_map.121 = (f32[144,512]{1,0:T(8,128)S(1)}, f32[160,512]{1,0:T(8,128)S(1)}, f32[160,512]{1,0:T(8,128)S(1)}, f32[8,128]{1,0:T(8,128)S(1)}) custom-call(s32[1]{0:T(128)} %bitcast.g_ref, f32[256,512]{1,0:T(8,128)} %base.7, f32[256,512]{1,0:T(8,128)} %depth.3, f32[256,512]{1,0:T(8,128)} %x0.9, f32[2,256,512]{2,1,0:T(8,128)} %cur.5, s32[32,64]{1,0:T(8,128)} %land.3, ...), custom_call_target="tpu_custom_call" | custom-call | flops 1000000 | bytes 4000000 | tf_op jit(solution)/shard_map/pallas_call | solution.py:49
  2.6 0.0 copy-start.29
  2.6 0.7 copy-done.29
  3.3 0.7 copy-done.30
  4.1 0.7 copy-done.32
  4.8 0.4 shard_map.122
  5.3 0.0 copy-start.10
  5.3 0.6 collective-permute-start.2
  5.8 0.7 collective-permute-start.3
  6.5 0.3 collective-permute-done.2.inner
  6.8 0.0 collective-permute-done.3.cross
  6.8 0.5 shard_map.123
  7.4 0.6 copy-done.26
  8.0 0.7 copy-done.31
  8.7 5.1 %all-to-all-start = ((f32[4,40,128]{2,1,0:T(8,128)}), f32[4,40,128]{2,1,0:T(8,128)}, u32[]{:S(2)}, u32[]{:S(2)}) async-start(f32[4,40,128]{2,1,0:T(8,128)} %copy-done.26), calls=%async_computation | async-start | bytes 163840 | tf_op jit(solution)/shard_map/all_to_all | solution.py:973
  13.8 2.0 %collective-permute-start = (f32[160,512]{1,0:T(8,128)}, f32[160,512]{1,0:T(8,128)}, u32[]{:S(2)}, u32[]{:S(2)}) collective-permute-start(f32[160,512]{1,0:T(8,128)} %copy-done.30), channel_id=1, source_target_pairs={{0,8},{8,0},{16,24},{24,16},{1,9},{9,1},{17,25},{25,17},{2,10},{10... | collective-permute-start | bytes 983048 | tf_op jit(solution)/shard_map/ppermute | solution.py:951
  15.8 1.5 %collective-permute-start.5 = (f32[160,512]{1,0:T(8,128)}, f32[160,512]{1,0:T(8,128)}, u32[]{:S(2)}, u32[]{:S(2)}) collective-permute-start(f32[160,512]{1,0:T(8,128)} %copy-done.29), channel_id=1, source_target_pairs={{0,16},{16,0},{8,24},{24,8},{1,17},{17,1},{9,25},{25,9},{2,18},{18... | collective-permute-start | bytes 983048 | tf_op jit(solution)/shard_map/ppermute | solution.py:952
  17.3 1.5 %all-to-all-done.nx = f32[4,40,128]{2,1,0:T(8,128)} async-done(((f32[4,40,128]{2,1,0:T(8,128)}), f32[4,40,128]{2,1,0:T(8,128)}, u32[]{:S(2)}, u32[]{:S(2)}) %all-to-all-start) | async-done | bytes 81952 | tf_op jit(solution)/shard_map/all_to_all | solution.py:973
  18.8 0.8 collective-permute-start.4
  19.6 1.5 %collective-permute-start.1 = (f32[144,512]{1,0:T(8,128)}, f32[144,512]{1,0:T(8,128)S(1)}, u32[]{:S(2)}, u32[]{:S(2)}) collective-permute-start(f32[144,512]{1,0:T(8,128)} %copy-done.32), channel_id=1, source_target_pairs={{0,24},{24,0},{8,16},{16,8},{1,25},{25,1},{9,17},{17,9},{2,26},{26... | collective-permute-start | bytes 884744 | tf_op jit(solution)/shard_map/ppermute | solution.py:950
  21.0 14.8 %collective-permute-done.1.rc = f32[144,512]{1,0:T(8,128)S(1)} collective-permute-done((f32[144,512]{1,0:T(8,128)}, f32[144,512]{1,0:T(8,128)S(1)}, u32[]{:S(2)}, u32[]{:S(2)}) %collective-permute-start.1) | collective-permute-done | bytes 294944 | tf_op jit(solution)/shard_map/ppermute | solution.py:950
  35.9 0.0 collective-permute-done.ra
  35.9 1.2 %copy-done.5 = f32[2,256,512]{2,1,0:T(8,128)S(1)} copy-done((f32[2,256,512]{2,1,0:T(8,128)S(1)}, f32[2,256,512]{2,1,0:T(8,128)}, u32[]{:S(2)}) %copy-start.5) | copy-done | bytes 1048600
  37.1 0.9 %copy-done.9 = f32[2,64,512]{2,1,0:T(8,128)S(1)} copy-done((f32[2,64,512]{2,1,0:T(8,128)S(1)}, f32[2,64,512]{2,1,0:T(8,128)}, u32[]{:S(2)}) %copy-start.9) | copy-done | bytes 262168
  38.0 9.4 %shard_map.125 = (f32[2,5,96,128]{3,2,1,0:T(8,128)S(1)}, f32[2,5,96,128]{3,2,1,0:T(8,128)S(1)}, f32[2,5,96,128]{3,2,1,0:T(8,128)S(1)}, f32[2,5,96,128]{3,2,1,0:T...) custom-call(s32[1]{0:T(128)} %bitcast.g_ref, ...), custom_call_target="tpu_custom_call" | custom-call | flops 20000000 | bytes 4000000 | tf_op jit(solution)/shard_map/pallas_call | solution.py:49
  47.4 0.0 copy-start.14
  47.5 0.0 copy-start.16
  47.5 3.6 %collective-permute-start.8 = (f32[72,512]{1,0:T(8,128)S(1)}, f32[72,512]{1,0:T(8,128)S(1)}, u32[]{:S(2)}, u32[]{:S(2)}) collective-permute-start(f32[72,512]{1,0:T(8,128)S(1)} %get-tuple-element.59), channel_id=1, source_target_pairs={{24,0},{0,24},{25,1},{1,25},{26,2},{2,26},{27,3},{3,27},{28,4},{4,... | collective-permute-start | bytes 442376 | tf_op jit(solution)/shard_map/ppermute | solution.py:995
  51.1 0.0 copy-start.7
  51.1 0.0 copy-start.11
  51.2 1.2 %shard_map.126 = (f32[72,512]{1,0:T(8,128)S(1)}, f32[72,512]{1,0:T(8,128)S(1)}, f32[2,5,8,512]{3,2,1,0:T(8,128)S(1)}) custom-call(s32[1]{0:T(128)} %bitcast.g_ref, f32[160,512]{1,0:T(8,128)S(1)} %collective-permute-done.4.rd, f32[160,512]{1,0:T(8,128)} %collective-permute-done.ra, f32[160,512]{1,0:T(8,128)} %collective-permute-done.5.rb, ...), custom_call_target="tpu_custom_call" | custom-call | flops 20000000 | bytes 4000000 | tf_op jit(solution)/shard_map/pallas_call | solution.py:49
  52.4 0.7 copy-done.24
  53.1 1.0 %collective-permute-start.6 = (f32[72,512]{1,0:T(8,128)S(1)}, f32[72,512]{1,0:T(8,128)S(1)}, u32[]{:S(2)}, u32[]{:S(2)}) collective-permute-start(f32[72,512]{1,0:T(8,128)S(1)} %get-tuple-element.57), channel_id=1, source_target_pairs={{0,8},{8,0},{16,24},{24,16},{1,9},{9,1},{17,25},{25,17},{2,10},{10... | collective-permute-start | bytes 442376 | tf_op jit(solution)/shard_map/ppermute | solution.py:997
  54.1 0.8 collective-permute-start.7
  54.9 1.8 %shard_map.124 = (f32[5,288,128]{2,1,0:T(8,128)S(1)}, f32[5,288,128]{2,1,0:T(8,128)S(1)}, f32[5,288,128]{2,1,0:T(8,128)S(1)}) custom-call(s32[1]{0:T(128)} %bitcast.g_ref, f32[160,512]{1,0:T(8,128)} %collective-permute-done.ra, f32[144,512]{1,0:T(8,128)S(1)} %collective-permute-done.1.rc, f32[160,512]{1,0:T(8,128)S(1)} %collective-permute-done.4.rd, ...), custom_call_target="tpu_custom_call" | custom-call | flops 20000000 | bytes 4000000 | tf_op jit(solution)/shard_map/pallas_call | solution.py:49
  56.7 1.6 %collective-permute-done.6.r1 = f32[72,512]{1,0:T(8,128)S(1)} collective-permute-done((f32[72,512]{1,0:T(8,128)S(1)}, f32[72,512]{1,0:T(8,128)S(1)}, u32[]{:S(2)}, u32[]{:S(2)}) %collective-permute-start.6) | collective-permute-done | bytes 147488 | tf_op jit(solution)/shard_map/ppermute | solution.py:997
  58.2 2.3 %collective-permute-done.7.r2 = f32[72,512]{1,0:T(8,128)S(1)} collective-permute-done((f32[72,512]{1,0:T(8,128)S(1)}, f32[72,512]{1,0:T(8,128)S(1)}, u32[]{:S(2)}, u32[]{:S(2)}) %collective-permute-start.7) | collective-permute-done | bytes 147488 | tf_op jit(solution)/shard_map/ppermute | solution.py:996
  60.5 1.4 %shard_map.127 = (f32[4,256,128]{2,1,0:T(8,128)S(1)}, f32[4,256,128]{2,1,0:T(8,128)S(1)}, f32[4,256,128]{2,1,0:T(8,128)S(1)}, f32[1,128]{1,0:T(1,128)S(1)}) custom-call(s32[1]{0:T(128)} %bitcast.g_ref, f32[5,288,128]{2,1,0:T(8,128)S(1)} %get-tuple-element.50.gw, f32[5,288,128]{2,1,0:T(8,128)S(1)} %get-tuple-element.51.invd, ...), custom_call_target="tpu_custom_call" | custom-call | flops 1000000 | bytes 4000000 | tf_op jit(solution)/shard_map/pallas_call | solution.py:49
  61.9 0.6 broadcast_in_dim.9
  62.5 10.4 %all-to-all-start.1 = ((f32[32,1,128]{2,1,0:T(1,128)}), f32[32,1,128]{2,1,0:T(1,128)S(1)}, u32[]{:S(2)}, u32[]{:S(2)}) async-start(f32[32,1,128]{2,1,0:T(1,128)} %broadcast_in_dim.9), calls=%async_computation.1 | async-start | bytes 32768 | tf_op jit(solution)/shard_map/all_to_all | solution.py:1015
  73.0 1.0 %copy-done.19 = f32[2,5,96,128]{3,2,1,0:T(8,128)S(1)} copy-done((f32[2,5,96,128]{3,2,1,0:T(8,128)S(1)}, f32[2,5,96,128]{3,2,1,0:T(8,128)}, u32[]{:S(2)}) %copy-start.19) | copy-done | bytes 491544
  74.0 1.0 %copy-done.21 = f32[2,5,96,128]{3,2,1,0:T(8,128)S(1)} copy-done((f32[2,5,96,128]{3,2,1,0:T(8,128)S(1)}, f32[2,5,96,128]{3,2,1,0:T(8,128)}, u32[]{:S(2)}) %copy-start.21) | copy-done | bytes 491544
  75.0 1.0 %copy-done.23 = f32[2,5,96,128]{3,2,1,0:T(8,128)S(1)} copy-done((f32[2,5,96,128]{3,2,1,0:T(8,128)S(1)}, f32[2,5,96,128]{3,2,1,0:T(8,128)}, u32[]{:S(2)}) %copy-start.23) | copy-done | bytes 491544
  76.0 1.1 %shard_map.129 = (f32[2,2,64,512]{3,2,1,0:T(8,128)}, f32[3,2,64,512]{3,2,1,0:T(8,128)}) custom-call(s32[1]{0:T(128)} %bitcast.g_ref, f32[2,5,96,128]{3,2,1,0:T(8,128)S(1)} %copy-done.15, f32[2,5,96,128]{3,2,1,0:T(8,128)S(1)} %copy-done.17, f32[2,5,96,128]{3,2,1,0:T(8,128)S(1)} %copy-done.19, f32[2,5,96,128]{3,2,1,0:T(8,128)S(1)} %copy-done.21, ...), custom_call_target="tpu_custom_call" | custom-call | flops 10000000 | bytes 4000000 | tf_op jit(solution)/shard_map/pallas_call | solution.py:49
  77.2 2.9 %all-to-all-done.1.parts = f32[32,1,128]{2,1,0:T(1,128)S(1)} async-done(((f32[32,1,128]{2,1,0:T(1,128)}), f32[32,1,128]{2,1,0:T(1,128)S(1)}, u32[]{:S(2)}, u32[]{:S(2)}) %all-to-all-start.1) | async-done | bytes 16416 | tf_op jit(solution)/shard_map/all_to_all | solution.py:1015
  80.1 1.1 %shard_map.128 = f32[256,512]{1,0:T(8,128)} custom-call(s32[1]{0:T(128)} %bitcast.g_ref, f32[32,1,128]{2,1,0:T(1,128)S(1)} %all-to-all-done.1.parts, f32[256,512]{1,0:T(8,128)S(1)} %copy-done.3, f32[4,256,128]{2,1,0:T(8,128)S(1)} %get-tuple-element.62.y0, f32[4,256,128]{2,1,0:T(8,128)S(1)} %get-tuple-element.63.y1, f32[4,256,128]{2,1,0:T(8,128)S(1)} %get-tuple-element.64.y2), custom_call_target="tpu_custom_call" | custom-call | flops 1000000 | bytes 4000000 | tf_op jit(solution)/shard_map/pallas_call | solution.py:49
  (50 shorter events, 0.1 us)
Async XLA Ops:
  0.6 4.1 %copy-start = (f32[3,2,64,512]{3,2,1,0:T(8,128)S(1)}, f32[3,2,64,512]{3,2,1,0:T(8,128)}, u32[]{:S(2)}) copy-start(f32[3,2,64,512]{3,2,1,0:T(8,128)} %stress.9) | copy-start | bytes 2359300
  0.7 4.1 %copy-start.1 = (f32[2,2,64,512]{3,2,1,0:T(8,128)S(1)}, f32[2,2,64,512]{3,2,1,0:T(8,128)}, u32[]{:S(2)}) copy-start(f32[2,2,64,512]{3,2,1,0:T(8,128)} %vel.9) | copy-start | bytes 1572868
  0.7 4.1 %copy-start.2 = (f32[2,2,64,512]{3,2,1,0:T(8,128)S(1)}, f32[2,2,64,512]{3,2,1,0:T(8,128)}, u32[]{:S(2)}) copy-start(f32[2,2,64,512]{3,2,1,0:T(8,128)} %wind.9) | copy-start | bytes 1572868
  0.7 4.1 %copy-start.3 = (f32[256,512]{1,0:T(8,128)S(1)}, f32[256,512]{1,0:T(8,128)}, u32[]{:S(2)}) copy-start(f32[256,512]{1,0:T(8,128)} %x0.9) | copy-start | bytes 1572868
  0.7 4.1 %copy-start.4 = (f32[2,256,512]{2,1,0:T(8,128)S(1)}, f32[2,256,512]{2,1,0:T(8,128)}, u32[]{:S(2)}) copy-start(f32[2,256,512]{2,1,0:T(8,128)} %cur.5) | copy-start | bytes 3145732
  0.7 4.1 %copy-start.6 = (f32[256,512]{1,0:T(8,128)S(1)}, f32[256,512]{1,0:T(8,128)}, u32[]{:S(2)}) copy-start(f32[256,512]{1,0:T(8,128)} %base.7) | copy-start | bytes 1572868
  0.7 4.1 %copy-start.12 = (f32[256,512]{1,0:T(8,128)S(1)}, f32[256,512]{1,0:T(8,128)}, u32[]{:S(2)}) copy-start(f32[256,512]{1,0:T(8,128)} %depth.3) | copy-start | bytes 1572868
  0.7 4.1 %copy-start.13 = (f32[2,64,512]{2,1,0:T(8,128)S(1)}, f32[2,64,512]{2,1,0:T(8,128)}, u32[]{:S(2)}) copy-start(f32[2,64,512]{2,1,0:T(8,128)} %thick.3) | copy-start | bytes 786436
  0.7 4.1 %copy-start.27 = (s32[32,64]{1,0:T(8,128)S(1)}, s32[32,64]{1,0:T(8,128)}, u32[]{:S(2)}) copy-start(s32[32,64]{1,0:T(8,128)} %land.3) | copy-start | bytes 24580
  0.7 4.1 %copy-start.28 = (s32[2,8,64]{2,1,0:T(8,128)S(1)}, s32[2,8,64]{2,1,0:T(8,128)}, u32[]{:S(2)}) copy-start(s32[2,8,64]{2,1,0:T(8,128)} %iceb.3) | copy-start | bytes 12292
  2.6 0.7 copy-start.29
  3.3 0.7 copy-start.30
  4.0 0.7 copy-start.32
  5.3 2.1 %copy-start.8 = (f32[2,64,512]{2,1,0:T(8,128)}, f32[2,64,512]{2,1,0:T(8,128)S(1)}, u32[]{:S(2)}) copy-start(f32[2,64,512]{2,1,0:T(8,128)S(1)} %get-tuple-element.43.h) | copy-start | bytes 786436
  5.3 2.1 %copy-start.10 = (f32[256,512]{1,0:T(8,128)}, f32[256,512]{1,0:T(8,128)S(1)}, u32[]{:S(2)}) copy-start(f32[256,512]{1,0:T(8,128)S(1)} %get-tuple-element.44.gf) | copy-start | bytes 1572868
  5.3 1.6 %collective-permute-start.2 = (f32[288,128]{1,0:T(8,128)S(1)}, f32[288,128]{1,0:T(8,128)S(1)}, u32[]{:S(2)}, u32[]{:S(2)}) collective-permute-start(f32[288,128]{1,0:T(8,128)S(1)} %get-tuple-element.41), channel_id=1, source_target_pairs={{0,1},{1,0},{2,3},{3,2},{4,5},{5,4},{6,7},{7,6},{8,9},{9,8},{10,11... | collective-permute-start | bytes 442376 | tf_op jit(solution)/shard_map/ppermute | solution.py:962
  5.8 1.0 %collective-permute-start.3 = (f32[288,128]{1,0:T(8,128)S(1)}, f32[288,128]{1,0:T(8,128)S(1)}, u32[]{:S(2)}, u32[]{:S(2)}) collective-permute-start(f32[288,128]{1,0:T(8,128)S(1)} %get-tuple-element.42), channel_id=1, source_target_pairs={{1,2},{3,4},{5,6},{2,1},{4,3},{6,5},{9,10},{11,12},{13,14},{10,9},... | collective-permute-start | bytes 442376 | tf_op jit(solution)/shard_map/ppermute | solution.py:964
  7.3 0.6 copy-start.26
  8.0 0.7 copy-start.31
  8.7 10.1 %all-to-all-start = ((f32[4,40,128]{2,1,0:T(8,128)}), f32[4,40,128]{2,1,0:T(8,128)}, u32[]{:S(2)}, u32[]{:S(2)}) async-start(f32[4,40,128]{2,1,0:T(8,128)} %copy-done.26), calls=%async_computation | async-start | bytes 163840 | tf_op jit(solution)/shard_map/all_to_all | solution.py:973
  13.8 22.1 %collective-permute-start = (f32[160,512]{1,0:T(8,128)}, f32[160,512]{1,0:T(8,128)}, u32[]{:S(2)}, u32[]{:S(2)}) collective-permute-start(f32[160,512]{1,0:T(8,128)} %copy-done.30), channel_id=1, source_target_pairs={{0,8},{8,0},{16,24},{24,16},{1,9},{9,1},{17,25},{25,17},{2,10},{10... | collective-permute-start | bytes 983048 | tf_op jit(solution)/shard_map/ppermute | solution.py:951
  15.8 20.1 %collective-permute-start.5 = (f32[160,512]{1,0:T(8,128)}, f32[160,512]{1,0:T(8,128)}, u32[]{:S(2)}, u32[]{:S(2)}) collective-permute-start(f32[160,512]{1,0:T(8,128)} %copy-done.29), channel_id=1, source_target_pairs={{0,16},{16,0},{8,24},{24,8},{1,17},{17,1},{9,25},{25,9},{2,18},{18... | collective-permute-start | bytes 983048 | tf_op jit(solution)/shard_map/ppermute | solution.py:952
  18.8 32.4 %collective-permute-start.4 = (f32[160,512]{1,0:T(8,128)}, f32[160,512]{1,0:T(8,128)S(1)}, u32[]{:S(2)}, u32[]{:S(2)}) collective-permute-start(f32[160,512]{1,0:T(8,128)} %copy-done.31), channel_id=1, source_target_pairs={{0,8},{8,0},{16,24},{24,16},{1,9},{9,1},{17,25},{25,17},{2,10},{10... | collective-permute-start | bytes 983048 | tf_op jit(solution)/shard_map/ppermute | solution.py:975
  19.6 16.3 %collective-permute-start.1 = (f32[144,512]{1,0:T(8,128)}, f32[144,512]{1,0:T(8,128)S(1)}, u32[]{:S(2)}, u32[]{:S(2)}) collective-permute-start(f32[144,512]{1,0:T(8,128)} %copy-done.32), channel_id=1, source_target_pairs={{0,24},{24,0},{8,16},{16,8},{1,25},{25,1},{9,17},{17,9},{2,26},{26... | collective-permute-start | bytes 884744 | tf_op jit(solution)/shard_map/ppermute | solution.py:950
  35.9 1.2 %copy-start.5 = (f32[2,256,512]{2,1,0:T(8,128)S(1)}, f32[2,256,512]{2,1,0:T(8,128)}, u32[]{:S(2)}) copy-start(f32[2,256,512]{2,1,0:T(8,128)} %cur.5) | copy-start | bytes 3145732
  37.1 0.9 %copy-start.9 = (f32[2,64,512]{2,1,0:T(8,128)S(1)}, f32[2,64,512]{2,1,0:T(8,128)}, u32[]{:S(2)}) copy-start(f32[2,64,512]{2,1,0:T(8,128)} %copy-done.8) | copy-start | bytes 786436
  47.4 4.9 %copy-start.14 = (f32[2,5,96,128]{3,2,1,0:T(8,128)}, f32[2,5,96,128]{3,2,1,0:T(8,128)S(1)}, u32[]{:S(2)}) copy-start(f32[2,5,96,128]{3,2,1,0:T(8,128)S(1)} %get-tuple-element.65.u_s) | copy-start | bytes 1474564
  47.5 4.9 %copy-start.16 = (f32[2,5,96,128]{3,2,1,0:T(8,128)}, f32[2,5,96,128]{3,2,1,0:T(8,128)S(1)}, u32[]{:S(2)}) copy-start(f32[2,5,96,128]{3,2,1,0:T(8,128)S(1)} %get-tuple-element.66.v_s) | copy-start | bytes 1474564
  47.5 4.9 %copy-start.18 = (f32[2,5,96,128]{3,2,1,0:T(8,128)}, f32[2,5,96,128]{3,2,1,0:T(8,128)S(1)}, u32[]{:S(2)}) copy-start(f32[2,5,96,128]{3,2,1,0:T(8,128)S(1)} %get-tuple-element.67.p_s) | copy-start | bytes 1474564
  47.5 4.9 %copy-start.20 = (f32[2,5,96,128]{3,2,1,0:T(8,128)}, f32[2,5,96,128]{3,2,1,0:T(8,128)S(1)}, u32[]{:S(2)}) copy-start(f32[2,5,96,128]{3,2,1,0:T(8,128)S(1)} %get-tuple-element.68.q_s) | copy-start | bytes 1474564
  47.5 4.9 %copy-start.22 = (f32[2,5,96,128]{3,2,1,0:T(8,128)}, f32[2,5,96,128]{3,2,1,0:T(8,128)S(1)}, u32[]{:S(2)}) copy-start(f32[2,5,96,128]{3,2,1,0:T(8,128)S(1)} %get-tuple-element.69.s_s) | copy-start | bytes 1474564
  47.5 9.2 %collective-permute-start.8 = (f32[72,512]{1,0:T(8,128)S(1)}, f32[72,512]{1,0:T(8,128)S(1)}, u32[]{:S(2)}, u32[]{:S(2)}) collective-permute-start(f32[72,512]{1,0:T(8,128)S(1)} %get-tuple-element.59), channel_id=1, source_target_pairs={{24,0},{0,24},{25,1},{1,25},{26,2},{2,26},{27,3},{3,27},{28,4},{4,... | collective-permute-start | bytes 442376 | tf_op jit(solution)/shard_map/ppermute | solution.py:995
  51.1 3.7 %copy-start.7 = (f32[256,512]{1,0:T(8,128)S(1)}, f32[256,512]{1,0:T(8,128)}, u32[]{:S(2)}) copy-start(f32[256,512]{1,0:T(8,128)} %base.7) | copy-start | bytes 1572868
  51.1 3.7 %copy-start.11 = (f32[256,512]{1,0:T(8,128)S(1)}, f32[256,512]{1,0:T(8,128)}, u32[]{:S(2)}) copy-start(f32[256,512]{1,0:T(8,128)} %copy-done.10) | copy-start | bytes 1572868
  52.4 0.7 copy-start.24
  53.1 5.1 %collective-permute-start.6 = (f32[72,512]{1,0:T(8,128)S(1)}, f32[72,512]{1,0:T(8,128)S(1)}, u32[]{:S(2)}, u32[]{:S(2)}) collective-permute-start(f32[72,512]{1,0:T(8,128)S(1)} %get-tuple-element.57), channel_id=1, source_target_pairs={{0,8},{8,0},{16,24},{24,16},{1,9},{9,1},{17,25},{25,17},{2,10},{10... | collective-permute-start | bytes 442376 | tf_op jit(solution)/shard_map/ppermute | solution.py:997
  54.1 6.4 %collective-permute-start.7 = (f32[72,512]{1,0:T(8,128)S(1)}, f32[72,512]{1,0:T(8,128)S(1)}, u32[]{:S(2)}, u32[]{:S(2)}) collective-permute-start(f32[72,512]{1,0:T(8,128)S(1)} %get-tuple-element.58), channel_id=1, source_target_pairs={{0,16},{16,0},{8,24},{24,8},{1,17},{17,1},{9,25},{25,9},{2,18},{18... | collective-permute-start | bytes 442376 | tf_op jit(solution)/shard_map/ppermute | solution.py:996
  60.5 12.4 %copy-start.15 = (f32[2,5,96,128]{3,2,1,0:T(8,128)S(1)}, f32[2,5,96,128]{3,2,1,0:T(8,128)}, u32[]{:S(2)}) copy-start(f32[2,5,96,128]{3,2,1,0:T(8,128)} %copy-done.14) | copy-start | bytes 1474564
  60.5 12.4 %copy-start.17 = (f32[2,5,96,128]{3,2,1,0:T(8,128)S(1)}, f32[2,5,96,128]{3,2,1,0:T(8,128)}, u32[]{:S(2)}) copy-start(f32[2,5,96,128]{3,2,1,0:T(8,128)} %copy-done.16) | copy-start | bytes 1474564
  60.5 12.4 %copy-start.25 = (f32[2,5,8,512]{3,2,1,0:T(8,128)S(1)}, f32[2,5,8,512]{3,2,1,0:T(8,128)}, u32[]{:S(2)}) copy-start(f32[2,5,8,512]{3,2,1,0:T(8,128)} %copy-done.24) | copy-start | bytes 491524
  62.5 17.6 %all-to-all-start.1 = ((f32[32,1,128]{2,1,0:T(1,128)}), f32[32,1,128]{2,1,0:T(1,128)S(1)}, u32[]{:S(2)}, u32[]{:S(2)}) async-start(f32[32,1,128]{2,1,0:T(1,128)} %broadcast_in_dim.9), calls=%async_computation.1 | async-start | bytes 32768 | tf_op jit(solution)/shard_map/all_to_all | solution.py:1015
  72.9 1.0 %copy-start.19 = (f32[2,5,96,128]{3,2,1,0:T(8,128)S(1)}, f32[2,5,96,128]{3,2,1,0:T(8,128)}, u32[]{:S(2)}) copy-start(f32[2,5,96,128]{3,2,1,0:T(8,128)} %copy-done.18) | copy-start | bytes 1474564
  74.0 1.0 %copy-start.21 = (f32[2,5,96,128]{3,2,1,0:T(8,128)S(1)}, f32[2,5,96,128]{3,2,1,0:T(8,128)}, u32[]{:S(2)}) copy-start(f32[2,5,96,128]{3,2,1,0:T(8,128)} %copy-done.20) | copy-start | bytes 1474564
  75.0 1.0 %copy-start.23 = (f32[2,5,96,128]{3,2,1,0:T(8,128)S(1)}, f32[2,5,96,128]{3,2,1,0:T(8,128)}, u32[]{:S(2)}) copy-start(f32[2,5,96,128]{3,2,1,0:T(8,128)} %copy-done.22) | copy-start | bytes 1474564
